TPU v7x, 32 devices: a whole 2x2x4 slice. The times are simulated.
32 devices in a mesh: rep: 2 (over y), shard: 16 (over z, x, core).
Axes of the slice: x: 2, y: 2, z: 4, core: 2. Of those that a mesh axis runs over, the one named last changes fastest.
Arguments:
- hidden: bfloat16 [8192, 1536], P(('rep', 'shard')), may hold values from -6 to 6
- text_states: bfloat16 [7, 64, 1536], replicated, may hold values from -6 to 6
- clip_index: int32 [8192], P(('rep', 'shard')), may hold values from 0 to 6, as said below
- frame_offset: int32 [8192], P(('rep', 'shard')), may hold values from 0 to 1279, as said below
- self_gain: bfloat16 [1536], P('shard'), may hold values from 0.5 to 1.5
- self_bias: bfloat16 [1536], P('shard'), may hold values from -2.5 to 2.5
- w_query: bfloat16 [1536, 1536], P('shard'), may hold values from -0.15625 to 0.15625
- w_key: bfloat16 [1536, 1536], P('shard'), may hold values from -0.15625 to 0.15625
- w_value: bfloat16 [1536, 1536], P('shard'), may hold values from -0.15625 to 0.15625
- w_output: bfloat16 [1536, 1536], P('shard'), may hold values from -1.75 to 1.75
- cross_gain: bfloat16 [1536], P('shard'), may hold values from 0.5 to 1.5
- cross_bias: bfloat16 [1536], P('shard'), may hold values from -2.5 to 2.5
- x_query: bfloat16 [1536, 1536], P('shard'), may hold values from -0.15625 to 0.15625
- x_key: bfloat16 [1536, 1536], P('shard'), may hold values from -0.15625 to 0.15625
- x_value: bfloat16 [1536, 1536], P('shard'), may hold values from -0.15625 to 0.15625
- x_output: bfloat16 [1536, 1536], P('shard'), may hold values from -0.625 to 0.625
- final_gain: bfloat16 [1536], P('shard'), may hold values from 0.5 to 1.5
- final_bias: bfloat16 [1536], P('shard'), may hold values from -2.5 to 2.5
- w_up: bfloat16 [1536, 6144], P('shard'), may hold values from -0.15625 to 0.15625
- w_down: bfloat16 [6144, 1536], P('shard'), may hold values from -0.078125 to 0.078125
- cotangent: bfloat16 [8192, 1536], P(('rep', 'shard')), may hold values from -6 to 6
Outputs:
- block_out: bfloat16 [8192, 1536], P(('rep', 'shard'))
- grad_hidden: bfloat16 [8192, 1536], P(('rep', 'shard'))
- grad_text: float32 [7, 64, 1536], replicated
- grad_self_gain: float32 [1536], P('shard')
- grad_self_bias: float32 [1536], P('shard')
- grad_w_query: float32 [1536, 1536], P('shard')
- grad_w_key: float32 [1536, 1536], P('shard')
- grad_w_value: float32 [1536, 1536], P('shard')
- grad_w_output: float32 [1536, 1536], P('shard')
- grad_cross_gain: float32 [1536], P('shard')
- grad_cross_bias: float32 [1536], P('shard')
- grad_x_query: float32 [1536, 1536], P('shard')
- grad_x_key: float32 [1536, 1536], P('shard')
- grad_x_value: float32 [1536, 1536], P('shard')
- grad_x_output: float32 [1536, 1536], P('shard')
- grad_final_gain: float32 [1536], P('shard')
- grad_final_bias: float32 [1536], P('shard')
- grad_w_up: float32 [1536, 6144], P('shard')
- grad_w_down: float32 [6144, 1536], P('shard')
Inputs may be any that keep to these rules, and one draw needn't show every extreme that they name: `clip_index`: clip of each token in order: 0 at the first token, rising by one at each clip's first token. Every clip holds at most 1280 tokens, the first exactly 1280, and every clip but the last more than 256. `frame_offset`: position of each token inside its clip, counted from 0 at the clip's first token.
All inputs are finite; a program needn't handle non-finite values.
Results may differ from a plain program's by a relative error of at most 0.017.
Values may be sent and summed in bfloat16 or wider, within the bound.
A program may use at most 384 MiB of HBM per device.

v0:
```python
import math

import jax
import jax.numpy as jnp
from jax import lax
from jax.sharding import PartitionSpec as P

HD = 64
CLIP_MAX = 1280


EPSILON = 1e-05
NEGATIVE = -1e30


def shifted(array, axis, by):
    length = lax.axis_size(axis)
    pairs = [(i, i + by) for i in range(length) if 0 <= i + by < length]
    return lax.ppermute(array, axis, pairs)


def normalize(values):
    centre = values - jnp.mean(values, axis=-1, keepdims=True)
    spread = jnp.mean(centre * centre, axis=-1, keepdims=True)
    return centre * lax.rsqrt(spread + EPSILON)


def scaled_norm(values, scale_vec):
    return normalize(values) * scale_vec


def exact_gelu(values):
    return jax.nn.gelu(values, approximate=False)


def matmul(left, right):
    return jnp.dot(left, right, preferred_element_type=jnp.float32)


def left_t(left, right):
    return lax.dot_general(
        left, right, (((0,), (0,)), ((), ())), preferred_element_type=jnp.float32
    )


def right_t(left, right):
    return lax.dot_general(
        left, right, (((1,), (1,)), ((), ())), preferred_element_type=jnp.float32
    )


def norm_back(values, scale_vec, upstream):
    _, pull = jax.vjp(scaled_norm, values, scale_vec.astype(jnp.float32))
    grad_values, grad_scale = pull(upstream)
    return (grad_values, grad_scale, jnp.sum(upstream, axis=0))


def on_device(
    hidden,
    text_states,
    clip_index,
    frame_offset,
    self_gain,
    self_bias,
    w_query,
    w_key,
    w_value,
    w_output,
    cross_gain,
    cross_bias,
    x_query,
    x_key,
    x_value,
    x_output,
    final_gain,
    final_bias,
    w_up,
    w_down,
    cotangent,
):
    tok_rows, model_width = hidden.shape
    head_count = model_width // HD
    group_size = math.gcd(head_count, 8)
    group_count = head_count // group_size
    shard_reach = (CLIP_MAX - 2) // tok_rows + 1
    context = (shard_reach + 1) * tok_rows
    key_scale = HD ** (-0.5)
    clip_total = text_states.shape[0]
    text_rows = text_states.shape[1]
    (
        full_query,
        full_key,
        full_value,
        full_output,
        full_xquery,
        full_xkey,
        full_xvalue,
        full_xoutput,
        full_up,
        full_down,
        gain_one,
        bias_one,
        gain_two,
        bias_two,
        gain_three,
        bias_three,
    ) = (
        lax.all_gather(w_query, "shard", axis=0, tiled=True),
        lax.all_gather(w_key, "shard", axis=0, tiled=True),
        lax.all_gather(w_value, "shard", axis=0, tiled=True),
        lax.all_gather(w_output, "shard", axis=0, tiled=True),
        lax.all_gather(x_query, "shard", axis=0, tiled=True),
        lax.all_gather(x_key, "shard", axis=0, tiled=True),
        lax.all_gather(x_value, "shard", axis=0, tiled=True),
        lax.all_gather(x_output, "shard", axis=0, tiled=True),
        lax.all_gather(w_up, "shard", axis=0, tiled=True),
        lax.all_gather(w_down, "shard", axis=0, tiled=True),
        lax.all_gather(self_gain, "shard", axis=0, tiled=True),
        lax.all_gather(self_bias, "shard", axis=0, tiled=True),
        lax.all_gather(cross_gain, "shard", axis=0, tiled=True),
        lax.all_gather(cross_bias, "shard", axis=0, tiled=True),
        lax.all_gather(final_gain, "shard", axis=0, tiled=True),
        lax.all_gather(final_bias, "shard", axis=0, tiled=True),
    )
    resid = hidden.astype(jnp.float32)
    normed_one = (
        scaled_norm(resid, gain_one.astype(jnp.float32)) + bias_one.astype(jnp.float32)
    ).astype(jnp.bfloat16)
    queries = matmul(normed_one, full_query).astype(jnp.bfloat16)
    keys_now = matmul(normed_one, full_key).astype(jnp.bfloat16)
    values_now = matmul(normed_one, full_value).astype(jnp.bfloat16)
    paired = jnp.stack([keys_now, values_now])
    pieces = []
    for distance in range(shard_reach, 0, -1):
        pieces.append(shifted(paired, ("rep", "shard"), distance))
    pieces.append(paired)
    window = jnp.concatenate(pieces, axis=1)
    keys_all = window[0].reshape(context, head_count, HD)
    values_all = window[1].reshape(context, head_count, HD)
    query_heads = queries.reshape(tok_rows, head_count, HD)
    row_index = jnp.arange(tok_rows, dtype=jnp.int32)[:, None]
    col_index = jnp.arange(context, dtype=jnp.int32)[None, :]
    gap_rows = row_index + shard_reach * tok_rows - col_index
    allowed = (gap_rows >= 0) & (gap_rows <= frame_offset[:, None])

    def head_parts(index):
        start = index * group_size
        return (
            lax.dynamic_slice_in_dim(query_heads, start, group_size, 1),
            lax.dynamic_slice_in_dim(keys_all, start, group_size, 1),
            lax.dynamic_slice_in_dim(values_all, start, group_size, 1),
        )

    def masked_scores(query_part, key_part):
        scores = (
            jnp.einsum("thd,khd->htk", query_part, key_part, preferred_element_type=jnp.float32)
            * key_scale
        )
        return jnp.where(allowed[None], scores, NEGATIVE)

    def attend(index):
        query_part, key_part, value_part = head_parts(index)
        scores = masked_scores(query_part, key_part)
        peak = jnp.max(scores, axis=2, keepdims=True)
        expo = jnp.exp(scores - peak)
        total = jnp.sum(expo, axis=2, keepdims=True)
        probs = (expo / total).astype(jnp.bfloat16)
        mixed = jnp.einsum("htk,khd->thd", probs, value_part, preferred_element_type=jnp.float32)
        return (mixed, peak[:, :, 0] + jnp.log(total[:, :, 0]))

    mixed_parts, log_totals = lax.map(attend, jnp.arange(group_count, dtype=jnp.int32))
    attended = (
        jnp.transpose(mixed_parts, (1, 0, 2, 3)).reshape(tok_rows, model_width).astype(jnp.bfloat16)
    )
    after_self = resid + matmul(attended, full_output)
    normed_two = (
        scaled_norm(after_self, gain_two.astype(jnp.float32)) + bias_two.astype(jnp.float32)
    ).astype(jnp.bfloat16)
    cross_q = matmul(normed_two, full_xquery).astype(jnp.bfloat16)
    first = clip_index[0]
    second = jnp.minimum(first + 1, clip_total - 1)
    chosen = jnp.concatenate(
        [
            lax.dynamic_index_in_dim(text_states, first, 0, False),
            lax.dynamic_index_in_dim(text_states, second, 0, False),
        ],
        axis=0,
    )
    cross_k = matmul(chosen, full_xkey).astype(jnp.bfloat16)
    cross_v = matmul(chosen, full_xvalue).astype(jnp.bfloat16)
    slot = jnp.arange(2 * text_rows, dtype=jnp.int32) // text_rows
    slot_clip = jnp.where(slot == 0, first, second)
    open_slot = (slot == 0) | (second != first)
    cross_mask = (clip_index[:, None] == slot_clip[None, :]) & open_slot[None, :]
    cq_heads = cross_q.reshape(tok_rows, head_count, HD)
    ck_heads = cross_k.reshape(2 * text_rows, head_count, HD)
    cv_heads = cross_v.reshape(2 * text_rows, head_count, HD)
    cross_scores = (
        jnp.einsum("thd,khd->htk", cq_heads, ck_heads, preferred_element_type=jnp.float32)
        * key_scale
    )
    cross_scores = jnp.where(cross_mask[None], cross_scores, NEGATIVE)
    cross_probs = jax.nn.softmax(cross_scores, axis=2)
    cross_low = cross_probs.astype(jnp.bfloat16)
    cross_mix = (
        jnp.einsum("htk,khd->thd", cross_low, cv_heads, preferred_element_type=jnp.float32)
        .reshape(tok_rows, model_width)
        .astype(jnp.bfloat16)
    )
    after_cross = after_self + matmul(cross_mix, full_xoutput)
    normed_three = (
        scaled_norm(after_cross, gain_three.astype(jnp.float32)) + bias_three.astype(jnp.float32)
    ).astype(jnp.bfloat16)
    pre_act = matmul(normed_three, full_up)
    activ = exact_gelu(pre_act).astype(jnp.bfloat16)
    block_out = (after_cross + matmul(activ, full_down)).astype(jnp.bfloat16)
    (
        back_query,
        back_key,
        back_value,
        back_output,
        back_xquery,
        back_xoutput,
        back_up,
        back_down,
        back_gain_one,
        back_gain_two,
        back_gain_three,
    ) = (
        lax.all_gather(w_query, "shard", axis=0, tiled=True),
        lax.all_gather(w_key, "shard", axis=0, tiled=True),
        lax.all_gather(w_value, "shard", axis=0, tiled=True),
        lax.all_gather(w_output, "shard", axis=0, tiled=True),
        lax.all_gather(x_query, "shard", axis=0, tiled=True),
        lax.all_gather(x_output, "shard", axis=0, tiled=True),
        lax.all_gather(w_up, "shard", axis=0, tiled=True),
        lax.all_gather(w_down, "shard", axis=0, tiled=True),
        lax.all_gather(self_gain, "shard", axis=0, tiled=True),
        lax.all_gather(cross_gain, "shard", axis=0, tiled=True),
        lax.all_gather(final_gain, "shard", axis=0, tiled=True),
    )
    grad_down = left_t(activ, cotangent)
    grad_act = right_t(cotangent, back_down)
    _, gelu_pull = jax.vjp(exact_gelu, pre_act)
    grad_pre = gelu_pull(grad_act)[0].astype(jnp.bfloat16)
    grad_up = left_t(normed_three, grad_pre)
    grad_norm_three = right_t(grad_pre, back_up)
    norm_three_part, grad_gain_three, grad_bias_three = norm_back(
        after_cross, back_gain_three, grad_norm_three
    )
    grad_cross_res = cotangent.astype(jnp.float32) + norm_three_part
    sum_up, sum_down, sum_gain_three, sum_bias_three = (
        lax.psum_scatter(grad_up, "shard", scatter_dimension=0, tiled=True),
        lax.psum_scatter(grad_down, "shard", scatter_dimension=0, tiled=True),
        lax.psum_scatter(grad_gain_three, "shard", scatter_dimension=0, tiled=True),
        lax.psum_scatter(grad_bias_three, "shard", scatter_dimension=0, tiled=True),
    )
    branch_two = grad_cross_res.astype(jnp.bfloat16)
    grad_xoutput = left_t(cross_mix, branch_two)
    grad_cmix = (
        right_t(branch_two, back_xoutput).astype(jnp.bfloat16).reshape(tok_rows, head_count, HD)
    )
    grad_cprob = jnp.einsum("thd,khd->htk", grad_cmix, cv_heads, preferred_element_type=jnp.float32)
    cross_inner = jnp.sum(cross_probs * grad_cprob, axis=2, keepdims=True)
    grad_cscore = (cross_probs * (grad_cprob - cross_inner)).astype(jnp.bfloat16)
    grad_cq = (
        (
            jnp.einsum("htk,khd->thd", grad_cscore, ck_heads, preferred_element_type=jnp.float32)
            * key_scale
        )
        .reshape(tok_rows, model_width)
        .astype(jnp.bfloat16)
    )
    grad_ck = (
        jnp.einsum("htk,thd->khd", grad_cscore, cq_heads, preferred_element_type=jnp.float32)
        * key_scale
    ).reshape(2 * text_rows, model_width)
    grad_cv = jnp.einsum(
        "htk,thd->khd", cross_low, grad_cmix, preferred_element_type=jnp.float32
    ).reshape(2 * text_rows, model_width)
    grad_xquery = left_t(normed_two, grad_cq)
    grad_norm_two = right_t(grad_cq, back_xquery)
    norm_two_part, grad_gain_two, grad_bias_two = norm_back(
        after_self, back_gain_two, grad_norm_two
    )
    grad_self_res = grad_cross_res + norm_two_part
    sum_xquery, sum_xoutput, sum_gain_two, sum_bias_two = (
        lax.psum_scatter(grad_xquery, "shard", scatter_dimension=0, tiled=True),
        lax.psum_scatter(grad_xoutput, "shard", scatter_dimension=0, tiled=True),
        lax.psum_scatter(grad_gain_two, "shard", scatter_dimension=0, tiled=True),
        lax.psum_scatter(grad_bias_two, "shard", scatter_dimension=0, tiled=True),
    )
    empty_slots = jnp.zeros((clip_total, text_rows, model_width), jnp.float32)
    key_slots = empty_slots.at[first].add(grad_ck[:text_rows]).at[second].add(grad_ck[text_rows:])
    value_slots = empty_slots.at[first].add(grad_cv[:text_rows]).at[second].add(grad_cv[text_rows:])
    key_total, value_total = lax.psum((key_slots, value_slots), ("rep", "shard"))
    key_round = key_total.reshape(clip_total * text_rows, model_width).astype(jnp.bfloat16)
    value_round = value_total.reshape(clip_total * text_rows, model_width).astype(jnp.bfloat16)
    shard_rows = x_key.shape[0]
    col_start = lax.axis_index("shard") * shard_rows
    text_flat = text_states.reshape(clip_total * text_rows, model_width)
    text_slice = lax.dynamic_slice_in_dim(text_flat, col_start, shard_rows, 1)
    grad_xkey = left_t(text_slice, key_round)
    grad_xvalue = left_t(text_slice, value_round)
    text_part = right_t(key_round, x_key) + right_t(value_round, x_value)
    grad_text = lax.all_gather(text_part, "shard", axis=1, tiled=True).reshape(
        clip_total, text_rows, model_width
    )
    branch_one = grad_self_res.astype(jnp.bfloat16)
    grad_output = left_t(attended, branch_one)
    grad_heads = (
        right_t(branch_one, back_output).astype(jnp.bfloat16).reshape(tok_rows, head_count, HD)
    )

    def attend_back(index):
        query_part, key_part, value_part = head_parts(index)
        grad_part = lax.dynamic_slice_in_dim(grad_heads, index * group_size, group_size, 1)
        scores = masked_scores(query_part, key_part)
        probs = jnp.exp(scores - log_totals[index][:, :, None])
        probs_low = probs.astype(jnp.bfloat16)
        grad_probs = jnp.einsum(
            "thd,khd->htk", grad_part, value_part, preferred_element_type=jnp.float32
        )
        inner = jnp.sum(probs * grad_probs, axis=2, keepdims=True)
        grad_scores = (probs * (grad_probs - inner)).astype(jnp.bfloat16)
        grad_q = (
            jnp.einsum("htk,khd->thd", grad_scores, key_part, preferred_element_type=jnp.float32)
            * key_scale
        )
        grad_k = (
            jnp.einsum("htk,thd->khd", grad_scores, query_part, preferred_element_type=jnp.float32)
            * key_scale
        )
        grad_v = jnp.einsum(
            "htk,thd->khd", probs_low, grad_part, preferred_element_type=jnp.float32
        )
        return (grad_q, grad_k, grad_v)

    q_parts, k_parts, v_parts = lax.map(attend_back, jnp.arange(group_count, dtype=jnp.int32))
    grad_queries = (
        jnp.transpose(q_parts, (1, 0, 2, 3)).reshape(tok_rows, model_width).astype(jnp.bfloat16)
    )
    grad_window = jnp.stack(
        [
            jnp.transpose(k_parts, (1, 0, 2, 3)).reshape(context, model_width),
            jnp.transpose(v_parts, (1, 0, 2, 3)).reshape(context, model_width),
        ]
    )
    own_grads = grad_window[:, shard_reach * tok_rows :]
    for distance in range(1, shard_reach + 1):
        low_edge = (shard_reach - distance) * tok_rows
        own_grads = own_grads + shifted(
            grad_window[:, low_edge : low_edge + tok_rows], ("rep", "shard"), -distance
        )
    grad_keys = own_grads[0].astype(jnp.bfloat16)
    grad_values = own_grads[1].astype(jnp.bfloat16)
    grad_query = left_t(normed_one, grad_queries)
    grad_key = left_t(normed_one, grad_keys)
    grad_value = left_t(normed_one, grad_values)
    grad_norm_one = (
        right_t(grad_queries, back_query)
        + right_t(grad_keys, back_key)
        + right_t(grad_values, back_value)
    )
    norm_one_part, grad_gain_one, grad_bias_one = norm_back(resid, back_gain_one, grad_norm_one)
    grad_hidden = (grad_self_res + norm_one_part).astype(jnp.bfloat16)
    sum_query, sum_key, sum_value, sum_output, sum_gain_one, sum_bias_one = (
        lax.psum_scatter(grad_query, "shard", scatter_dimension=0, tiled=True),
        lax.psum_scatter(grad_key, "shard", scatter_dimension=0, tiled=True),
        lax.psum_scatter(grad_value, "shard", scatter_dimension=0, tiled=True),
        lax.psum_scatter(grad_output, "shard", scatter_dimension=0, tiled=True),
        lax.psum_scatter(grad_gain_one, "shard", scatter_dimension=0, tiled=True),
        lax.psum_scatter(grad_bias_one, "shard", scatter_dimension=0, tiled=True),
    )
    (
        fin_query,
        fin_key,
        fin_value,
        fin_output,
        fin_xquery,
        fin_xoutput,
        fin_up,
        fin_down,
        fin_gain_one,
        fin_bias_one,
        fin_gain_two,
        fin_bias_two,
        fin_gain_three,
        fin_bias_three,
    ) = lax.psum(
        (
            sum_query,
            sum_key,
            sum_value,
            sum_output,
            sum_xquery,
            sum_xoutput,
            sum_up,
            sum_down,
            sum_gain_one,
            sum_bias_one,
            sum_gain_two,
            sum_bias_two,
            sum_gain_three,
            sum_bias_three,
        ),
        "rep",
    )
    return (
        block_out,
        grad_hidden,
        grad_text,
        fin_gain_one,
        fin_bias_one,
        fin_query,
        fin_key,
        fin_value,
        fin_output,
        fin_gain_two,
        fin_bias_two,
        fin_xquery,
        grad_xkey,
        grad_xvalue,
        fin_xoutput,
        fin_gain_three,
        fin_bias_three,
        fin_up,
        fin_down,
    )


def solution(mesh):
    placed = (
        P(("rep", "shard"), None),
        P(),
        P(("rep", "shard")),
        P(("rep", "shard")),
        P("shard"),
        P("shard"),
        P("shard", None),
        P("shard", None),
        P("shard", None),
        P("shard", None),
        P("shard"),
        P("shard"),
        P("shard", None),
        P("shard", None),
        P("shard", None),
        P("shard", None),
        P("shard"),
        P("shard"),
        P("shard", None),
        P("shard", None),
        P(("rep", "shard"), None),
    )
    return jax.shard_map(
        on_device,
        mesh=mesh,
        in_specs=placed,
        out_specs=(
            P(("rep", "shard"), None),
            P(("rep", "shard"), None),
            P(),
            P("shard"),
            P("shard"),
            P("shard", None),
            P("shard", None),
            P("shard", None),
            P("shard", None),
            P("shard"),
            P("shard"),
            P("shard", None),
            P("shard", None),
            P("shard", None),
            P("shard", None),
            P("shard"),
            P("shard"),
            P("shard", None),
            P("shard", None),
        ),
        check_vma=False,
    )
```

profile of v0, /device:TPU:0, one launch (start us, length us, event | category | flops | bytes accessed | tf_op | source)
XLA Modules:
  0.0 3024.4 jit_solution(13819163257135578216)
XLA Ops:
  16.9 64.6 %all-reduce.16 = (bf16[1536]{0:T(1024)(128)(2,1)S(1)}, bf16[1536]{0:T(1024)(128)(2,1)S(1)}, bf16[1536]{0:T(1024)(128)(2,1)S(1)}, bf16[1536]{0:T(1024)(128)(2,1)S...) all-reduce(bf16[1536]{0:T(1024)(128)(2,1)S(1)} %dynamic-update-slic, ...), channel_id=1, replica_groups=mesh['rep'=2,'shard'=16] {'shard'}, use_global_device_ids=true, to_apply=%add.1 | all-reduce | flops 9216 | bytes 36864
  88.5 32.3 %all-gather.12.cloned.1.call-done = bf16[1536,1536]{1,0:T(8,128)(2,1)} async-done(((bf16[96,1536]{1,0:T(8,128)(2,1)}), bf16[1536,1536]{1,0:T(8,128)(2,1)}) %all-gather.12.cloned.1.call-update) | async-done | bytes 4718608 | tf_op jit(solution)/shard_map/all_gather | solution.py:109
  125.8 4.5 collective-permute-start
  136.6 4.0 collective-permute-start.1
  148.9 180.9 %all-gather.16.cloned.1.call-done = bf16[1536,1536]{1,0:T(8,128)(2,1)} async-done(((bf16[96,1536]{1,0:T(8,128)(2,1)}), bf16[1536,1536]{1,0:T(8,128)(2,1)}) %all-gather.16.cloned.1.call-update) | async-done | bytes 4718608 | tf_op jit(solution)/shard_map/all_gather | solution.py:108
  329.8 4.7 convolution_convert_fusion.3
  334.5 50.8 %all-gather.20.cloned.1.call-done = bf16[1536,1536]{1,0:T(8,128)(2,1)} async-done(((bf16[96,1536]{1,0:T(8,128)(2,1)}), bf16[1536,1536]{1,0:T(8,128)(2,1)}) %all-gather.20.cloned.1.call-update) | async-done | bytes 4718608 | tf_op jit(solution)/shard_map/all_gather | solution.py:114
  385.2 3.9 convolution_convert_fusion.7
  392.4 46.6 %all-gather.24.cloned.1.call-done = bf16[1536,1536]{1,0:T(8,128)(2,1)} async-done(((bf16[96,1536]{1,0:T(8,128)(2,1)}), bf16[1536,1536]{1,0:T(8,128)(2,1)}) %all-gather.24.cloned.1.call-update) | async-done | bytes 4718608 | tf_op jit(solution)/shard_map/all_gather | solution.py:113
  439.1 4.0 convolution_convert_fusion.6
  459.6 8.0 fusion.137
  467.7 7.1 copy.77
  474.8 6.7 copy.79
  482.4 44.0 %while.32 = (s32[]{:T(128)}, bf16[3,256,8,64]{1,3,2,0:T(8,128)(2,1)}, f32[3,8,256]{2,1,0:T(8,128)S(1)}, s32[3]{0:T(128)S(1)}, bf16[1536,24,64]{0,2,1:T(8,128)(2,...) while((s32[]{:T(128)}, ...), condition=%wide.region_5.6_spmd.clone, body=%wide.region_2.5_spmd.clone.sunk | while | flops 844625920 | bytes 43322572 | solution.py:171
  491.5 5.5 fusion.224
  506.2 5.5 fusion.224
  520.7 5.5 fusion.224
  526.5 4.1 fusion.141
  531.0 15.7 all-gather.22.cloned.1.call-done
  546.7 4.7 convolution_convert_fusion.2
  552.8 4.1 fusion.142
  559.4 41.3 %all-gather.26.cloned.1.call-done = bf16[1536,1536]{1,0:T(8,128)(2,1)} async-done(((bf16[96,1536]{1,0:T(8,128)(2,1)}), bf16[1536,1536]{1,0:T(8,128)(2,1)}) %all-gather.26.cloned.1.call-update) | async-done | bytes 4718608 | tf_op jit(solution)/shard_map/all_gather | solution.py:115
  600.7 3.8 fusion.143
  606.0 93.7 %all-gather.28.cloned.1.call-done = bf16[1536,6144]{1,0:T(8,128)(2,1)} async-done(((bf16[96,6144]{1,0:T(8,128)(2,1)}), bf16[1536,6144]{1,0:T(8,128)(2,1)}) %all-gather.28.cloned.1.call-update) | async-done | bytes 18874384 | tf_op jit(solution)/shard_map/all_gather | solution.py:116
  699.8 11.1 fusion.125
  710.9 89.2 %all-gather.30.cloned.1.call-done = bf16[6144,1536]{1,0:T(8,128)(2,1)} async-done(((bf16[384,1536]{1,0:T(8,128)(2,1)}), bf16[6144,1536]{1,0:T(8,128)(2,1)}) %all-gather.30.cloned.1.call-update) | async-done | bytes 18874384 | tf_op jit(solution)/shard_map/all_gather | solution.py:117
  800.1 22.9 add_convert_fusion
  823.0 11.4 multiply_reduce_fusion.2
  837.2 4.7 convolution_convert_fusion.1
  849.5 5.1 multiply_reduce_fusion.3
  860.2 107.6 %while.33 = (s32[]{:T(128)}, bf16[3,256,8,64]{1,3,2,0:T(8,128)(2,1)}, f32[3,1536,8,64]{1,3,2,0:T(8,128)}, f32[3,1536,8,64]{1,3,2,0:T(8,128)}, s32[3]{0:T(128)S(1...) while((s32[]{:T(128)}, ...), condition=%wide.region_19.20_spmd.clone, body=%wide.region_17.19_spmd.clone.sunk | while | flops 2044065792 | bytes 183284208 | solution.py:339
  862.1 7.8 fusion.233
  872.6 8.3 multiply_reduce_fusion.9
  884.6 6.1 fusion.235
  897.8 7.8 fusion.233
  908.3 8.3 multiply_reduce_fusion.9
  920.3 6.1 fusion.235
  933.5 7.8 fusion.233
  944.0 8.3 multiply_reduce_fusion.9
  955.9 6.1 fusion.235
  967.8 6.5 fusion.128
  975.9 5.0 fusion.104
  982.8 5.9 fusion.123
  990.3 5.7 fusion.146
  996.1 10.5 fusion.74
  1013.5 132.7 %collective-permute-done.9 = f32[2,256,1536]{1,2,0:T(8,128)S(1)} collective-permute-done((f32[2,256,1536]{1,2,0:T(8,128)}, f32[2,256,1536]{1,2,0:T(8,128)S(1)}, u32[]{:S(2)}, u32[]{:S(2)}) %collective-permute-start.9) | collective-permute-done | bytes 3145760 | tf_op jit(solution)/shard_map/ppermute | solution.py:19
  1151.4 7.0 fusion.77
  1158.5 5.2 fusion.100
  1163.7 5.2 fusion.101
  1170.3 16.8 fusion.124
  1187.4 5.7 multiply_convert_fusion.1
  1194.9 14.8 fusion.147
  1233.0 388.3 %all-reduce.21 = (bf16[7,64,1536]{2,1,0:T(8,128)(2,1)}, bf16[7,64,1536]{2,1,0:T(8,128)(2,1)}) all-reduce(f32[7,64,1536]{2,1,0:T(8,128)} %get-tuple-element.382, f32[7,64,1536]{2,1,0:T(8,128)} %get-tuple-element.383), channel_id=1, replica_groups=mesh['rep'=2,'shard'=16] {'rep','shard'}, use_global_device_ids=true, to_apply=%region_24.25 | all-reduce | flops 1376256 | bytes 8257536 | tf_op jit(solution)/shard_map/psum | solution.py:296
  1626.1 54.6 %reduce-scatter.17.cloned.1.call-done = f32[96,1536]{1,0:T(8,128)} async-done(((f32[1536,1536]{1,0:T(8,128)}), f32[96,1536]{1,0:T(8,128)}) %reduce-scatter.17.cloned.1.call-update) | async-done | bytes 589840 | tf_op jit(solution)/shard_map/reduce_scatter | solution.py:288
  1680.7 114.8 %reduce-scatter.19.cloned.1.call-done = f32[96,1536]{1,0:T(8,128)} async-done(((f32[1536,1536]{1,0:T(8,128)}), f32[96,1536]{1,0:T(8,128)}) %reduce-scatter.19.cloned.1.call-update) | async-done | bytes 589840 | tf_op jit(solution)/shard_map/reduce_scatter | solution.py:289
  1795.6 114.8 %reduce-scatter.11.cloned.1.call-done = f32[96,1536]{1,0:T(8,128)} async-done(((f32[1536,1536]{1,0:T(8,128)}), f32[96,1536]{1,0:T(8,128)}) %reduce-scatter.11.cloned.1.call-update) | async-done | bytes 589840 | tf_op jit(solution)/shard_map/reduce_scatter | solution.py:369
  1910.4 114.8 %reduce-scatter.13.cloned.1.call-done = f32[96,1536]{1,0:T(8,128)} async-done(((f32[1536,1536]{1,0:T(8,128)}), f32[96,1536]{1,0:T(8,128)}) %reduce-scatter.13.cloned.1.call-update) | async-done | bytes 589840 | tf_op jit(solution)/shard_map/reduce_scatter | solution.py:370
  2025.3 368.3 %reduce-scatter.21.cloned.1.call-done = f32[96,6144]{1,0:T(8,128)} async-done(((f32[1536,6144]{1,0:T(8,128)}), f32[96,6144]{1,0:T(8,128)}) %reduce-scatter.21.cloned.1.call-update) | async-done | bytes 2359312 | tf_op jit(solution)/shard_map/reduce_scatter | solution.py:253
  2393.6 367.9 %reduce-scatter.23.cloned.1.call-done = f32[384,1536]{1,0:T(8,128)} async-done(((f32[6144,1536]{1,0:T(8,128)}), f32[384,1536]{1,0:T(8,128)}) %reduce-scatter.23.cloned.1.call-update) | async-done | bytes 2359312 | tf_op jit(solution)/shard_map/reduce_scatter | solution.py:254
  2767.7 3.9 fusion.144
  2771.7 11.3 fusion.78
  2788.2 60.3 %all-reduce.13 = (f32[1536]{0:T(1024)S(1)}, f32[1536]{0:T(1024)S(1)}, f32[1536]{0:T(1024)S(1)}, f32[1536]{0:T(1024)S(1)}, f32[1536]{0:T(1024)S(1)}, /*index=5*/f32[1536]{0:T(1024)S(1)}) all-reduce(f32[1536]{0:T(1024)S(1)} %get-tuple-element.268, ...), channel_id=2, replica_groups=mesh['rep'=2,'shard'=16] {'shard'}, use_global_device_ids=true, to_apply=%region_27.28.clone | all-reduce | flops 9216 | bytes 73728
  2849.0 5.6 all-reduce.14
  2860.9 144.9 %all-reduce.20.cloned.1.call-done = (f32[96,1536]{1,0:T(8,128)}, f32[96,1536]{1,0:T(8,128)}, f32[96,1536]{1,0:T(8,128)}, f32[96,1536]{1,0:T(8,128)}, f32[96,1536...) async-done(((f32[96,1536]{1,0:T(8,128)}, f32[96,1536]{1,0:T(8,128)}, f32[96,1536]{1,0:T(8,128)}, f32[96,1536]{1,0:T(8,128)}, ...) | async-done | bytes 8257552 | tf_op jit(solution)/shard_map/psum | solution.py:390
  (457 shorter events, 209.3 us)
Async XLA Ops:
  7.3 74.3 %copy-start.87 = (s32[256]{0:T(256)S(1)}, s32[256]{0:T(256)}, u32[]{:S(2)}) copy-start(s32[256]{0:T(256)} %param.35) | copy-start | bytes 3076
  7.3 76.8 %copy-start.1 = (bf16[256,1536]{1,0:T(8,128)(2,1)S(1)}, bf16[256,1536]{1,0:T(8,128)(2,1)}, u32[]{:S(2)}) copy-start(bf16[256,1536]{1,0:T(8,128)(2,1)} %param.33) | copy-start | bytes 2359300
  7.3 77.4 %all-gather.14.cloned.1.call-start = ((), (), s32[]{:S(2)}) async-start(), calls=%async_computation.9 | async-start | bytes 5013504 | tf_op jit(solution)/shard_map/all_gather | solution.py:110
  8.0 112.7 %all-gather.12.cloned.1.call-start = ((), (), s32[]{:S(2)}) async-start(), calls=%async_computation.8 | async-start | bytes 5013504 | tf_op jit(solution)/shard_map/all_gather | solution.py:109
  8.8 321.0 %all-gather.16.cloned.1.call-start = ((), (), s32[]{:S(2)}) async-start(), calls=%async_computation.10 | async-start | bytes 5013504 | tf_op jit(solution)/shard_map/all_gather | solution.py:108
  9.5 375.7 %all-gather.20.cloned.1.call-start = ((), (), s32[]{:S(2)}) async-start(), calls=%async_computation.12 | async-start | bytes 5013504 | tf_op jit(solution)/shard_map/all_gather | solution.py:114
  10.1 429.0 %all-gather.24.cloned.1.call-start = ((), (), s32[]{:S(2)}) async-start(), calls=%async_computation.14 | async-start | bytes 5013504 | tf_op jit(solution)/shard_map/all_gather | solution.py:113
  10.7 515.8 %all-gather.18.cloned.1.call-start = ((), (), s32[]{:S(2)}) async-start(), calls=%async_computation.11 | async-start | bytes 5013504 | tf_op jit(solution)/shard_map/all_gather | solution.py:111
  11.2 535.5 %all-gather.22.cloned.1.call-start = ((), (), s32[]{:S(2)}) async-start(), calls=%async_computation.13 | async-start | bytes 5013504 | tf_op jit(solution)/shard_map/all_gather | solution.py:112
  12.0 588.7 %all-gather.26.cloned.1.call-start = ((), (), s32[]{:S(2)}) async-start(), calls=%async_computation.15 | async-start | bytes 5013504 | tf_op jit(solution)/shard_map/all_gather | solution.py:115
  12.7 687.0 %all-gather.28.cloned.1.call-start = ((), (), s32[]{:S(2)}) async-start(), calls=%async_computation.16 | async-start | bytes 20054016 | tf_op jit(solution)/shard_map/all_gather | solution.py:116
  13.5 786.7 %all-gather.30.cloned.1.call-start = ((), (), s32[]{:S(2)}) async-start(), calls=%async_computation.17 | async-start | bytes 20054016 | tf_op jit(solution)/shard_map/all_gather | solution.py:117
  14.1 1612.0 %reduce-scatter.9.cloned.1.call-start = ((), (), s32[]{:S(2)}) async-start(), calls=%async_computation.19 | async-start | bytes 10027008 | tf_op jit(solution)/shard_map/reduce_scatter | solution.py:368
  81.5 248.2 %copy-start.57 = (f32[1536]{0:T(1024)}, f32[1536]{0:T(1024)S(1)}, u32[]{:S(2)}) copy-start(f32[1536]{0:T(1024)S(1)} %convert_element_type.151) | copy-start | bytes 18436
  81.6 248.2 %copy-start.53 = (f32[1536]{0:T(1024)}, f32[1536]{0:T(1024)S(1)}, u32[]{:S(2)}) copy-start(f32[1536]{0:T(1024)S(1)} %convert_element_type.150) | copy-start | bytes 18436
  84.3 245.5 %copy-start.64 = (f32[256]{0:T(256)}, f32[256]{0:T(256)S(1)}, u32[]{:S(2)}) copy-start(f32[256]{0:T(256)S(1)} %broadcast_multiply_fusion.2) | copy-start | bytes 3076
  84.6 245.2 %copy-start.66 = (f32[256]{0:T(256)}, f32[256]{0:T(256)S(1)}, u32[]{:S(2)}) copy-start(f32[256]{0:T(256)S(1)} %fusion.115) | copy-start | bytes 3076
  125.8 319.1 %collective-permute-start = (bf16[2,256,1536]{2,1,0:T(8,128)(2,1)}, bf16[2,256,1536]{2,1,0:T(8,128)(2,1)}, u32[]{:S(2)}, u32[]{:S(2)}) collective-permute-start(bf16[2,256,1536]{2,1,0:T(8,128)(2,1)} %pad_maximum_fusion.1), channel_id=1, source_target_pairs={{0,5},{1,6},{2,7},{3,8},{4,9},{5,10},{6,11},{7,12},{8,13},{9,14},{... | collective-permute-start | bytes 4718600 | tf_op jit(solution)/shard_map/ppermute | solution.py:19
  136.5 248.7 %copy-start.41 = (bf16[64,1536]{1,0:T(8,128)(2,1)}, bf16[64,1536]{1,0:T(8,128)(2,1)S(1)}, u32[]{:S(2)}) copy-start(bf16[64,1536]{1,0:T(8,128)(2,1)S(1)} %get-tuple-element.364) | copy-start | bytes 589828
  136.6 311.1 %collective-permute-start.1 = (bf16[2,256,1536]{2,1,0:T(8,128)(2,1)}, bf16[2,256,1536]{2,1,0:T(8,128)(2,1)}, u32[]{:S(2)}, u32[]{:S(2)}) collective-permute-start(bf16[2,256,1536]{2,1,0:T(8,128)(2,1)} %pad_maximum_fusion.1), channel_id=1, source_target_pairs={{0,4},{1,5},{2,6},{3,7},{4,8},{5,9},{6,10},{7,11},{8,12},{9,13},{1... | collective-permute-start | bytes 4718600 | tf_op jit(solution)/shard_map/ppermute | solution.py:19
  140.5 309.9 %collective-permute-start.2 = (bf16[2,256,1536]{2,1,0:T(8,128)(2,1)}, bf16[2,256,1536]{2,1,0:T(8,128)(2,1)}, u32[]{:S(2)}, u32[]{:S(2)}) collective-permute-start(bf16[2,256,1536]{2,1,0:T(8,128)(2,1)} %pad_maximum_fusion.1), channel_id=1, source_target_pairs={{0,3},{1,4},{2,5},{3,6},{4,7},{5,8},{6,9},{7,10},{8,11},{9,12},{10... | collective-permute-start | bytes 4718600 | tf_op jit(solution)/shard_map/ppermute | solution.py:19
  143.7 309.4 %collective-permute-start.3 = (bf16[2,256,1536]{2,1,0:T(8,128)(2,1)}, bf16[2,256,1536]{2,1,0:T(8,128)(2,1)}, u32[]{:S(2)}, u32[]{:S(2)}) collective-permute-start(bf16[2,256,1536]{2,1,0:T(8,128)(2,1)} %pad_maximum_fusion.1), channel_id=1, source_target_pairs={{0,2},{1,3},{2,4},{3,5},{4,6},{5,7},{6,8},{7,9},{8,10},{9,11},{10,... | collective-permute-start | bytes 4718600 | tf_op jit(solution)/shard_map/ppermute | solution.py:19
  146.1 309.6 %collective-permute-start.4 = (bf16[2,256,1536]{2,1,0:T(8,128)(2,1)}, bf16[2,256,1536]{2,1,0:T(8,128)(2,1)}, u32[]{:S(2)}, u32[]{:S(2)}) collective-permute-start(bf16[2,256,1536]{2,1,0:T(8,128)(2,1)} %pad_maximum_fusion.1), channel_id=1, source_target_pairs={{0,1},{1,2},{2,3},{3,4},{4,5},{5,6},{6,7},{7,8},{8,9},{9,10},{10,1... | collective-permute-start | bytes 4718600 | tf_op jit(solution)/shard_map/ppermute | solution.py:19
  526.5 20.3 copy-start.61
  526.5 20.3 copy-start.68
  530.6 324.0 %copy-start.3 = (f32[256,1536]{1,0:T(8,128)}, f32[256,1536]{1,0:T(8,128)S(1)}, u32[]{:S(2)}) copy-start(f32[256,1536]{1,0:T(8,128)S(1)} %get-tuple-element.372) | copy-start | bytes 4718596
  530.6 324.0 %copy-start.75 = (f32[256]{0:T(256)}, f32[256]{0:T(256)S(1)}, u32[]{:S(2)}) copy-start(f32[256]{0:T(256)S(1)} %broadcast_multiply_fusion.1) | copy-start | bytes 3076
  530.9 323.7 %copy-start.78 = (f32[256]{0:T(256)}, f32[256]{0:T(256)S(1)}, u32[]{:S(2)}) copy-start(f32[256]{0:T(256)S(1)} %fusion.116) | copy-start | bytes 3076
  531.0 21.8 copy-start.72
  556.9 290.3 %copy-start.77 = (f32[24,256]{1,0:T(8,128)}, f32[24,256]{1,0:T(8,128)S(1)}, u32[]{:S(2)}) copy-start(f32[24,256]{1,0:T(8,128)S(1)} %get-tuple-element.373) | copy-start | bytes 73732
  559.4 45.2 %copy-start.48 = (bf16[24,64,256]{2,1,0:T(8,128)(2,1)}, bf16[24,64,256]{2,1,0:T(8,128)(2,1)S(1)}, u32[]{:S(2)}) copy-start(bf16[24,64,256]{2,1,0:T(8,128)(2,1)S(1)} %convolution_convert_fusion.8) | copy-start | bytes 2359300
  600.7 99.1 %copy-start.55 = (f32[1536]{0:T(1024)S(1)}, f32[1536]{0:T(1024)}, u32[]{:S(2)}) copy-start(f32[1536]{0:T(1024)} %convert_element_type.169) | copy-start | bytes 18436
  600.7 99.1 %copy-start.59 = (f32[1536]{0:T(1024)S(1)}, f32[1536]{0:T(1024)}, u32[]{:S(2)}) copy-start(f32[1536]{0:T(1024)} %convert_element_type.170) | copy-start | bytes 18436
  604.6 229.8 %copy-start.70 = (f32[256]{0:T(256)}, f32[256]{0:T(256)S(1)}, u32[]{:S(2)}) copy-start(f32[256]{0:T(256)S(1)} %broadcast_multiply_fusion) | copy-start | bytes 3076
  606.0 228.4 %copy-start.73 = (f32[256]{0:T(256)}, f32[256]{0:T(256)S(1)}, u32[]{:S(2)}) copy-start(f32[256]{0:T(256)S(1)} %fusion.117) | copy-start | bytes 3076
  606.0 194.1 %copy-start.21 = (bf16[256,1536]{1,0:T(8,128)(2,1)S(1)}, bf16[256,1536]{1,0:T(8,128)(2,1)}, u32[]{:S(2)}) copy-start(bf16[256,1536]{1,0:T(8,128)(2,1)} %param.53) | copy-start | bytes 2359300
  800.1 22.9 copy-start.12
  860.2 107.6 %copy-start.54 = (f32[1536]{0:T(1024)S(1)}, f32[1536]{0:T(1024)}, u32[]{:S(2)}) copy-start(f32[1536]{0:T(1024)} %copy-done.53) | copy-start | bytes 18436
  860.2 107.6 %copy-start.58 = (f32[1536]{0:T(1024)S(1)}, f32[1536]{0:T(1024)}, u32[]{:S(2)}) copy-start(f32[1536]{0:T(1024)} %copy-done.57) | copy-start | bytes 18436
  860.2 107.6 %copy-start.65 = (f32[256]{0:T(256)S(1)}, f32[256]{0:T(256)}, u32[]{:S(2)}) copy-start(f32[256]{0:T(256)} %copy-done.64) | copy-start | bytes 3076
  860.2 107.6 %copy-start.67 = (f32[256]{0:T(256)S(1)}, f32[256]{0:T(256)}, u32[]{:S(2)}) copy-start(f32[256]{0:T(256)} %copy-done.66) | copy-start | bytes 3076
  974.3 651.8 %reduce-scatter.15.cloned.1.call-start = ((), (), s32[]{:S(2)}) async-start(), calls=%async_computation.22 | async-start | bytes 10027008 | tf_op jit(solution)/shard_map/reduce_scatter | solution.py:371
  981.0 699.8 %reduce-scatter.17.cloned.1.call-start = ((), (), s32[]{:S(2)}) async-start(), calls=%async_computation.23 | async-start | bytes 10027008 | tf_op jit(solution)/shard_map/reduce_scatter | solution.py:288
  988.7 806.8 %reduce-scatter.19.cloned.1.call-start = ((), (), s32[]{:S(2)}) async-start(), calls=%async_computation.24 | async-start | bytes 10027008 | tf_op jit(solution)/shard_map/reduce_scatter | solution.py:289
  996.0 914.4 %reduce-scatter.11.cloned.1.call-start = ((), (), s32[]{:S(2)}) async-start(), calls=%async_computation.20 | async-start | bytes 10027008 | tf_op jit(solution)/shard_map/reduce_scatter | solution.py:369
  996.0 155.3 %slice-start.3 = ((s8[9437184]{0:T(1024)(128)(4,1)}), s8[4194304]{0:T(1024)(128)(4,1)S(1)}, s32[]{:S(2)}) async-start(s8[9437184]{0:T(1024)(128)(4,1)} %bitcast.169), calls=%async_computation.31 | async-start | bytes 8388608
  996.0 155.3 %slice-start.4 = ((s8[9437184]{0:T(1024)(128)(4,1)}), s8[4194304]{0:T(1024)(128)(4,1)S(1)}, s32[]{:S(2)}) async-start(s8[9437184]{0:T(1024)(128)(4,1)} %bitcast.169), calls=%async_computation.32 | async-start | bytes 8388608
  996.1 155.3 %slice-start.5 = ((s8[9437184]{0:T(1024)(128)(4,1)}), s8[1048576]{0:T(1024)(128)(4,1)S(1)}, s32[]{:S(2)}) async-start(s8[9437184]{0:T(1024)(128)(4,1)} %bitcast.169), calls=%async_computation.33 | async-start | bytes 2097152
  1006.6 139.6 %collective-permute-start.9 = (f32[2,256,1536]{1,2,0:T(8,128)}, f32[2,256,1536]{1,2,0:T(8,128)S(1)}, u32[]{:S(2)}, u32[]{:S(2)}) collective-permute-start(f32[2,256,1536]{1,2,0:T(8,128)} %get-tuple-element.359), channel_id=1, source_target_pairs={{5,0},{6,1},{7,2},{8,3},{9,4},{10,5},{11,6},{12,7},{13,8},{14,9},{... | collective-permute-start | bytes 9437192 | tf_op jit(solution)/shard_map/ppermute | solution.py:19
  1008.1 138.8 %collective-permute-start.8 = (f32[2,256,1536]{1,2,0:T(8,128)}, f32[2,256,1536]{1,2,0:T(8,128)S(1)}, u32[]{:S(2)}, u32[]{:S(2)}) collective-permute-start(f32[2,256,1536]{1,2,0:T(8,128)} %get-tuple-element.360), channel_id=1, source_target_pairs={{4,0},{5,1},{6,2},{7,3},{8,4},{9,5},{10,6},{11,7},{12,8},{13,9},{1... | collective-permute-start | bytes 9437192 | tf_op jit(solution)/shard_map/ppermute | solution.py:19
  1009.4 137.5 %collective-permute-start.7 = (f32[2,256,1536]{1,2,0:T(8,128)}, f32[2,256,1536]{1,2,0:T(8,128)S(1)}, u32[]{:S(2)}, u32[]{:S(2)}) collective-permute-start(f32[2,256,1536]{1,2,0:T(8,128)} %get-tuple-element.358), channel_id=1, source_target_pairs={{3,0},{4,1},{5,2},{6,3},{7,4},{8,5},{9,6},{10,7},{11,8},{12,9},{13... | collective-permute-start | bytes 9437192 | tf_op jit(solution)/shard_map/ppermute | solution.py:19
  1010.7 136.2 %collective-permute-start.6 = (f32[2,256,1536]{1,2,0:T(8,128)S(1)}, f32[2,256,1536]{1,2,0:T(8,128)S(1)}, u32[]{:S(2)}, u32[]{:S(2)}) collective-permute-start(f32[2,256,1536]{1,2,0:T(8,128)S(1)} %get-tuple-element.357), channel_id=1, source_target_pairs={{2,0},{3,1},{4,2},{5,3},{6,4},{7,5},{8,6},{9,7},{10,8},{11,9},{12,... | collective-permute-start | bytes 9437192 | tf_op jit(solution)/shard_map/ppermute | solution.py:19
  1012.0 146.4 %copy-start.2 = (bf16[256,1536]{1,0:T(8,128)(2,1)S(1)}, bf16[256,1536]{1,0:T(8,128)(2,1)}, u32[]{:S(2)}) copy-start(bf16[256,1536]{1,0:T(8,128)(2,1)} %param.33) | copy-start | bytes 2359300
  1012.0 139.4 %collective-permute-start.5 = (f32[2,256,1536]{1,2,0:T(8,128)S(1)}, f32[2,256,1536]{1,2,0:T(8,128)}, u32[]{:S(2)}, u32[]{:S(2)}) collective-permute-start(f32[2,256,1536]{1,2,0:T(8,128)S(1)} %get-tuple-element.356), channel_id=1, source_target_pairs={{1,0},{2,1},{3,2},{4,3},{5,4},{6,5},{7,6},{8,7},{9,8},{10,9},{11,1... | collective-permute-start | bytes 9437192 | tf_op jit(solution)/shard_map/ppermute | solution.py:19
  1163.6 861.6 %reduce-scatter.13.cloned.1.call-start = ((), (), s32[]{:S(2)}) async-start(), calls=%async_computation.21 | async-start | bytes 10027008 | tf_op jit(solution)/shard_map/reduce_scatter | solution.py:370
  1169.0 1224.6 %reduce-scatter.21.cloned.1.call-start = ((), (), s32[]{:S(2)}) async-start(), calls=%async_computation.25 | async-start | bytes 40108032 | tf_op jit(solution)/shard_map/reduce_scatter | solution.py:253
  1187.1 1574.3 %reduce-scatter.23.cloned.1.call-start = ((), (), s32[]{:S(2)}) async-start(), calls=%async_computation.26 | async-start | bytes 40108032 | tf_op jit(solution)/shard_map/reduce_scatter | solution.py:254
  1209.6 1647.8 %all-gather.32.cloned.1.call-start = ((), (), s32[]{:S(2)}) async-start(), calls=%async_computation.18 | async-start | bytes 3342336 | tf_op jit(solution)/shard_map/all_gather | solution.py:306
  1232.9 388.3 %copy-start.46 = (bf16[96,1536]{1,0:T(8,128)(2,1)S(1)}, bf16[96,1536]{1,0:T(8,128)(2,1)}, u32[]{:S(2)}) copy-start(bf16[96,1536]{1,0:T(8,128)(2,1)} %param.46) | copy-start | bytes 884740
  1233.0 390.2 %copy-start.47 = (bf16[96,1536]{1,0:T(8,128)(2,1)S(1)}, bf16[96,1536]{1,0:T(8,128)(2,1)}, u32[]{:S(2)}) copy-start(bf16[96,1536]{1,0:T(8,128)(2,1)} %param.47) | copy-start | bytes 884740
  1625.7 1380.1 %all-reduce.20.cloned.1.call-start = ((), (), s32[]{:S(2)}) async-start(), calls=%async_computation.27 | async-start | bytes 16515072 | tf_op jit(solution)/shard_map/psum | solution.py:390
  2767.7 15.3 slice-start.10
  2767.7 16.7 slice-start.8
  2786.3 68.3 %copy-start.16 = (f32[256,1536]{1,0:T(8,128)S(1)}, f32[256,1536]{1,0:T(8,128)}, u32[]{:S(2)}) copy-start(f32[256,1536]{1,0:T(8,128)} %copy-done.14) | copy-start | bytes 4718596
  (89 other events, 448.0 us)
Sparse Core Ops, SparseCore 0:
  10.4 56.4 all-gather.13
  69.1 51.5 all-gather.11
  123.1 206.6 all-gather.15
  331.9 53.2 all-gather.19
  387.4 51.6 all-gather.23
  441.2 51.6 all-gather.17
  495.2 51.4 all-gather.21
  549.0 51.6 all-gather.25
  602.3 97.4 all-gather.27
  701.2 98.8 all-gather.29
  974.4 455.2 reduce-scatter.8
  1433.7 128.8 reduce-scatter.14
  1566.7 114.0 reduce-scatter.16
  1684.7 110.8 reduce-scatter.18
  1799.5 110.8 reduce-scatter.10
  1914.4 110.8 reduce-scatter.12
  2029.3 364.1 reduce-scatter.20
  2397.7 363.7 reduce-scatter.22
  2764.3 44.8 all-gather.31
  2812.0 193.7 all-reduce.19
where the time goes:
time: 3030 us; the launch traced here: 3020 us
  waiting for transfers between devices  1970 us (65%)
  blocking collectives  519 us (17%)
  matrix products  309 us (10%)
  local copies, waits for them, and re-layouts  100 us (3%)
  other arithmetic  69.3 us (2%)
    psum x1, blocking collectives, on_device(): lax.psum((key_slots, value_slots), ('rep', 'shard'))  388 us
    reduce_scatter x1, waiting for transfers between devices, on_device(): lax.psum_scatter(grad_up, 'shard', scatter_dimension=0, tiled=True)  368 us
    reduce_scatter x1, waiting for transfers between devices, on_device(): lax.psum_scatter(grad_down, 'shard', scatter_dimension=0, tiled=True)  368 us
    all_gather x1, waiting for transfers between devices, on_device(): lax.all_gather(w_query, 'shard', axis=0, tiled=True)  181 us
    psum x1, waiting for transfers between devices, on_device(): lax.psum((sum_query, sum_key, sum_value, sum_output, sum_xquery, sum_xout...  145 us
    ppermute x10, waiting for transfers between devices, shifted(): return lax.ppermute(array, axis, pairs)  133 us
    unnamed x2, blocking collectives  125 us
    reduce_scatter x1, waiting for transfers between devices, on_device(): lax.psum_scatter(grad_value, 'shard', scatter_dimension=0, tiled=True)  115 us
  transfers between devices with their start and end apart: 30, of which 17 were waited for; matrix products, arithmetic and copies ran while one was open for 9% of the time, Pallas kernels for 0%

commit v1 on v0

v1 whole, which is shorter than its diff:
```python
import functools

import jax
import jax.numpy as jnp
from jax import lax
from jax.experimental import pallas as pl
from jax.experimental.pallas import tpu as pltpu
from jax.sharding import PartitionSpec as P

HD = 64
CLIP_MAX = 1280
EPSILON = 1e-05
NEGATIVE = -1e30
BLOCK = 256
BOTH = ("rep", "shard")
LOW = jnp.bfloat16
WIDE = jnp.float32


def normalize(values):
    centre = values - jnp.mean(values, axis=-1, keepdims=True)
    spread = jnp.mean(centre * centre, axis=-1, keepdims=True)
    return centre * lax.rsqrt(spread + EPSILON)


def scaled_norm(values, scale_vec):
    return normalize(values) * scale_vec


def exact_gelu(values):
    return jax.nn.gelu(values, approximate=False)


def matmul(left, right):
    return jnp.dot(left, right, preferred_element_type=WIDE)


def left_t(left, right):
    return lax.dot_general(left, right, (((0,), (0,)), ((), ())), preferred_element_type=WIDE)


def right_t(left, right):
    return lax.dot_general(left, right, (((1,), (1,)), ((), ())), preferred_element_type=WIDE)


def norm_back(values, scale_vec, upstream):
    _, pull = jax.vjp(scaled_norm, values, scale_vec.astype(WIDE))
    grad_values, grad_scale = pull(upstream)
    return (grad_values, grad_scale, jnp.sum(upstream, axis=0))


def pick(array, index, axis):
    return lax.dynamic_index_in_dim(array, index, axis, False)


def axis_length(axis):
    return lax.axis_size(axis)


def swap(array, axis, pairing):
    length = axis_length(axis)
    pairs = [(i, pairing(i)) for i in range(length)]
    return lax.ppermute(array, axis, [(i, j) for i, j in pairs if 0 <= j < length])


def add_low(left, right):
    return (left.astype(WIDE) + right.astype(WIDE)).astype(LOW)


def gather_rows(array):
    return lax.all_gather(array, "shard", axis=0, tiled=True)


def joined(parts):
    return parts[0] if len(parts) == 1 else jnp.concatenate(parts, axis=-1)


def staged_total(grads):
    index = lax.axis_index("shard")
    core, side, level, rep = index % 2, (index // 2) % 2, index // 4, lax.axis_index("rep")
    rows = grads[0].shape[0] // 16
    parts = [grad.reshape(8, 2, rows, grad.shape[1]) for grad in grads]
    away = joined([pick(part, 1 - core, 1) for part in parts])
    held = joined([pick(part, core, 1) for part in parts])
    width = held.shape[-1]
    half = width // 2
    held = add_low(held, swap(away, "shard", lambda i: i ^ 1))
    held = held.reshape(4, 2, rows, width)
    first = held[..., :half]
    first = add_low(
        pick(first, side, 1),
        swap(pick(first, 1 - side, 1), "shard", lambda i: i ^ 2),
    ).reshape(4, 2, rows // 2, half)
    second = held[..., half:].reshape(4, 2, 2, rows // 2, width - half)
    second = add_low(
        pick(second, rep, 2),
        swap(pick(second, 1 - rep, 2), "rep", lambda i: i ^ 1),
    )
    first = add_low(pick(first, rep, 1), swap(pick(first, 1 - rep, 1), "rep", lambda i: i ^ 1))
    second = add_low(
        pick(second, side, 1),
        swap(pick(second, 1 - side, 1), "shard", lambda i: i ^ 2),
    )
    both = jnp.concatenate([first, second], axis=2)
    total = pick(both, level, 0).astype(WIDE)
    for step in range(1, 4):
        total = total + swap(
            pick(both, (level + step) % 4, 0), "shard", lambda i: (i + 4 * step) % 16
        ).astype(WIDE)
    own = total.astype(LOW)
    other = swap(own, "rep", lambda i: i ^ 1)
    low, high = jnp.where(rep == 0, own, other), jnp.where(rep == 0, other, own)
    return jnp.concatenate([low, high], axis=0).astype(WIDE)


def summed_rows(grads):
    grads = [grad.astype(LOW) for grad in grads]
    widths = [grad.shape[1] for grad in grads]
    if axis_length("shard") == 16 and axis_length("rep") == 2:
        whole = staged_total(grads)
    else:
        share = lax.psum_scatter(joined(grads), "shard", scatter_dimension=0, tiled=True)
        whole = lax.psum(share.astype(WIDE), "rep")
    out, start = [], 0
    for width in widths:
        out.append(whole[:, start : start + width])
        start += width
    return out


def summed_vectors(stack):
    if axis_length("shard") != 16 or axis_length("rep") != 2:
        return lax.psum(stack, BOTH)
    for bit in (1, 2, 4, 8):
        stack = stack + swap(stack, "shard", lambda i: i ^ bit)
    return stack + swap(stack, "rep", lambda i: i ^ 1)


def head_lanes(which):
    lane = lax.broadcasted_iota(jnp.int32, (BLOCK, 2 * HD), 1)
    return lane < HD if which == 0 else lane >= HD


def open_pairs(offsets, step, reach):
    base = (reach - step) * BLOCK
    keys = lax.broadcasted_iota(jnp.int32, (BLOCK, BLOCK), 0)
    column = lax.broadcasted_iota(jnp.int32, (1, BLOCK), 1)
    allowed = keys >= (column - offsets) + base
    if base == 0:
        allowed = allowed & (keys <= lax.broadcasted_iota(jnp.int32, (BLOCK, BLOCK), 1))
    return allowed


def attend_kernel(reach, offset_ref, query_ref, window_ref, out_ref, log_ref, held):
    start = pl.program_id(1) * BLOCK
    offsets = offset_ref[...]
    scaled = query_ref[...] * jnp.asarray(HD**-0.5, LOW)
    mixed = []
    for head in range(2):
        query = jnp.where(head_lanes(head), scaled, jnp.zeros_like(scaled))
        peak = jnp.full((1, BLOCK), NEGATIVE, WIDE)
        for step in range(reach + 1):
            rows = pl.ds(pl.multiple_of(start + step * BLOCK, BLOCK), BLOCK)
            scores = right_t(window_ref[0, rows, :], query)
            scores = jnp.where(open_pairs(offsets, step, reach), scores, NEGATIVE)
            held[head, step] = scores
            peak = jnp.maximum(peak, jnp.max(scores, axis=0, keepdims=True))
        total = jnp.zeros((1, BLOCK), WIDE)
        blend = jnp.zeros((2 * HD, BLOCK), WIDE)
        for step in range(reach + 1):
            rows = pl.ds(pl.multiple_of(start + step * BLOCK, BLOCK), BLOCK)
            expo = jnp.exp(held[head, step] - peak)
            total = total + jnp.sum(expo, axis=0, keepdims=True)
            blend = blend + left_t(window_ref[1, rows, :], expo.astype(LOW))
        mixed.append((blend / total)[head * HD : (head + 1) * HD])
        log_ref[0, pl.ds(head, 1), :] = peak + jnp.log(total)
    out_ref[...] = jnp.concatenate(mixed, axis=0).T.astype(LOW)


def attend(offsets, queries, window, reach):
    rows, width = queries.shape
    pairs, blocks, context = width // (2 * HD), rows // BLOCK, window.shape[1]
    work = pairs * 2 * rows * (reach + 1) * BLOCK
    return pl.pallas_call(
        functools.partial(attend_kernel, reach),
        grid=(pairs, blocks),
        in_specs=[
            pl.BlockSpec((1, BLOCK), lambda p, b: (0, b)),
            pl.BlockSpec((BLOCK, 2 * HD), lambda p, b: (b, p)),
            pl.BlockSpec((2, context, 2 * HD), lambda p, b: (0, 0, p)),
        ],
        out_specs=[
            pl.BlockSpec((BLOCK, 2 * HD), lambda p, b: (b, p)),
            pl.BlockSpec((1, 2, BLOCK), lambda p, b: (p, 0, b)),
        ],
        out_shape=[
            jax.ShapeDtypeStruct((rows, width), LOW),
            jax.ShapeDtypeStruct((pairs, 2, rows), WIDE),
        ],
        scratch_shapes=[pltpu.VMEM((2, reach + 1, BLOCK, BLOCK), WIDE)],
        cost_estimate=pl.CostEstimate(
            flops=16 * HD * work, transcendentals=work, bytes_accessed=8 * rows * width
        ),
        name="attend_forward",
    )(offsets, queries, window)


def attend_back_kernel(
    reach,
    offset_ref,
    query_ref,
    window_ref,
    out_ref,
    log_ref,
    grad_ref,
    grad_query_ref,
    grad_window_ref,
    grad_keys,
    grad_values,
):
    block = pl.program_id(1)
    start = block * BLOCK

    @pl.when(block == 0)
    def _():
        grad_keys[...] = jnp.zeros_like(grad_keys)
        grad_values[...] = jnp.zeros_like(grad_values)

    offsets = offset_ref[...]
    scaled = query_ref[...] * jnp.asarray(HD**-0.5, LOW)
    grads = grad_ref[...]
    inner = (grads.astype(WIDE) * out_ref[...].astype(WIDE)).T
    query, grad, inners, logs = [], [], [], []
    for head in range(2):
        lanes = head_lanes(head)
        query.append(jnp.where(lanes, scaled, jnp.zeros_like(scaled)))
        grad.append(jnp.where(lanes, grads, jnp.zeros_like(grads)))
        inners.append(jnp.sum(inner[head * HD : (head + 1) * HD], axis=0, keepdims=True))
        logs.append(log_ref[0, pl.ds(head, 1), :])
    back = [jnp.zeros((2 * HD, BLOCK), WIDE) for _ in range(2)]
    for step in range(reach + 1):
        rows = pl.ds(pl.multiple_of(start + step * BLOCK, BLOCK), BLOCK)
        key, value = window_ref[0, rows, :], window_ref[1, rows, :]
        allowed = open_pairs(offsets, step, reach)
        to_key = jnp.zeros((BLOCK, 2 * HD), WIDE)
        to_value = jnp.zeros((BLOCK, 2 * HD), WIDE)
        for head in range(2):
            scores = jnp.where(allowed, right_t(key, query[head]), NEGATIVE)
            probs = jnp.exp(scores - logs[head])
            to_value = to_value + matmul(probs.astype(LOW), grad[head])
            grad_probs = right_t(value, grad[head])
            grad_scores = (probs * (grad_probs - inners[head])).astype(LOW)
            to_key = to_key + matmul(grad_scores, query[head])
            back[head] = back[head] + left_t(key, grad_scores)
        grad_keys[rows, :] += to_key
        grad_values[rows, :] += to_value
    back = jnp.concatenate([back[0][:HD], back[1][HD:]], axis=0) * (HD**-0.5)
    grad_query_ref[...] = back.T.astype(LOW)

    @pl.when(block == pl.num_programs(1) - 1)
    def _():
        grad_window_ref[0] = grad_keys[...].astype(LOW)
        grad_window_ref[1] = grad_values[...].astype(LOW)


def attend_back(offsets, queries, window, out, logs, grads, reach):
    rows, width = queries.shape
    pairs, blocks, context = width // (2 * HD), rows // BLOCK, window.shape[1]
    work = pairs * 2 * rows * (reach + 1) * BLOCK
    row_block = pl.BlockSpec((BLOCK, 2 * HD), lambda p, b: (b, p))
    window_block = pl.BlockSpec((2, context, 2 * HD), lambda p, b: (0, 0, p))
    return pl.pallas_call(
        functools.partial(attend_back_kernel, reach),
        grid=(pairs, blocks),
        in_specs=[
            pl.BlockSpec((1, BLOCK), lambda p, b: (0, b)),
            row_block,
            window_block,
            row_block,
            pl.BlockSpec((1, 2, BLOCK), lambda p, b: (p, 0, b)),
            row_block,
        ],
        out_specs=[row_block, window_block],
        out_shape=[
            jax.ShapeDtypeStruct((rows, width), LOW),
            jax.ShapeDtypeStruct(window.shape, LOW),
        ],
        scratch_shapes=[
            pltpu.VMEM((context, 2 * HD), WIDE),
            pltpu.VMEM((context, 2 * HD), WIDE),
        ],
        cost_estimate=pl.CostEstimate(
            flops=40 * HD * work, transcendentals=work, bytes_accessed=16 * rows * width
        ),
        name="attend_backward",
    )(offsets, queries, window, out, logs, grads)


def core_pair(own, got, core, axis):
    return jnp.where(
        core == 0,
        jnp.concatenate([own, got], axis=axis),
        jnp.concatenate([got, own], axis=axis),
    )


def on_device(
    hidden,
    text_states,
    clip_index,
    frame_offset,
    self_gain,
    self_bias,
    w_query,
    w_key,
    w_value,
    w_output,
    cross_gain,
    cross_bias,
    x_query,
    x_key,
    x_value,
    x_output,
    final_gain,
    final_bias,
    w_up,
    w_down,
    cotangent,
):
    tok_rows, model_width = hidden.shape
    head_count = model_width // HD
    half_width = model_width // 2
    reach = (CLIP_MAX - 2) // tok_rows + 1
    key_scale = HD ** (-0.5)
    clip_total = text_states.shape[0]
    text_rows = text_states.shape[1]
    shard_count, rep_count = axis_length("shard"), axis_length("rep")
    device_count = shard_count * rep_count
    place = lax.axis_index("rep") * shard_count + lax.axis_index("shard")
    core, side = place % 2, (place // 2) % 2

    params = jnp.stack(
        [self_gain, self_bias, cross_gain, cross_bias, final_gain, final_bias], axis=1
    )
    params = jnp.pad(params, ((0, 0), (0, 128 - params.shape[1])))
    split = [w[:, h : h + half_width] for h in (0, half_width) for w in (w_query, w_key, w_value)]
    first_group = gather_rows(jnp.concatenate(split + [params], axis=1))
    full_qkv = first_group[:, : 3 * model_width]
    gain_one, bias_one, gain_two, bias_two, gain_three, bias_three = (
        first_group[:, 3 * model_width + i].astype(WIDE) for i in range(6)
    )
    second_group = gather_rows(
        jnp.concatenate([w_output, x_query, x_key, x_value, x_output], axis=1)
    )
    full_output, full_xquery, full_xkey, full_xvalue, full_xoutput = (
        second_group[:, i * model_width : (i + 1) * model_width] for i in range(5)
    )
    full_up = gather_rows(w_up)
    full_down = gather_rows(w_down)

    offsets = core_pair(frame_offset, swap(frame_offset, BOTH, lambda i: i ^ 1), core, 0)[None, :]
    resid = hidden.astype(WIDE)
    normed_one = (scaled_norm(resid, gain_one) + bias_one).astype(LOW)
    projected = matmul(normed_one, full_qkv)
    projected = projected.astype(LOW).reshape(tok_rows, 2, 3, half_width)
    projected = jnp.transpose(projected, (1, 2, 0, 3))
    got = swap(pick(projected, 1 - core, 0), BOTH, lambda i: i ^ 1)
    chip_qkv = core_pair(pick(projected, core, 0), got, core, 1)
    queries, own_unit = chip_qkv[0], chip_qkv[1:]
    below = swap(own_unit, BOTH, lambda i: i + 4)
    far = swap(own_unit[:, tok_rows:], BOTH, lambda i: i + 8 if i % 4 >= 2 else -1)
    message = jnp.concatenate(
        [
            jnp.where(side == 0, own_unit, below),
            jnp.where(side == 0, below[:, tok_rows:], far),
        ],
        axis=1,
    )
    across = swap(message, BOTH, lambda i: i ^ 2)
    chip_rows = 2 * tok_rows
    window = jnp.concatenate(
        [across[:, chip_rows:], below, across[:, :chip_rows], own_unit], axis=1
    )
    chip_mixed, logs = attend(offsets, queries, window, reach)

    def to_tokens(chip_rows_array):
        mine = lax.dynamic_slice_in_dim(chip_rows_array, core * tok_rows, tok_rows, 0)
        away = lax.dynamic_slice_in_dim(chip_rows_array, (1 - core) * tok_rows, tok_rows, 0)
        return core_pair(mine, swap(away, BOTH, lambda i: i ^ 1), core, 1)

    attended = to_tokens(chip_mixed)
    after_self = resid + matmul(attended, full_output)
    normed_two = (scaled_norm(after_self, gain_two) + bias_two).astype(LOW)
    cross_q = matmul(normed_two, full_xquery).astype(LOW)
    first = clip_index[0]
    second = jnp.minimum(first + 1, clip_total - 1)
    chosen = jnp.concatenate(
        [
            lax.dynamic_index_in_dim(text_states, first, 0, False),
            lax.dynamic_index_in_dim(text_states, second, 0, False),
        ],
        axis=0,
    )
    cross_k = matmul(chosen, full_xkey).astype(LOW)
    cross_v = matmul(chosen, full_xvalue).astype(LOW)
    slot = jnp.arange(2 * text_rows, dtype=jnp.int32) // text_rows
    slot_clip = jnp.where(slot == 0, first, second)
    open_slot = (slot == 0) | (second != first)
    cross_mask = (clip_index[:, None] == slot_clip[None, :]) & open_slot[None, :]
    cq_heads = cross_q.reshape(tok_rows, head_count, HD)
    ck_heads = cross_k.reshape(2 * text_rows, head_count, HD)
    cv_heads = cross_v.reshape(2 * text_rows, head_count, HD)
    cross_scores = (
        jnp.einsum("thd,khd->htk", cq_heads, ck_heads, preferred_element_type=WIDE) * key_scale
    )
    cross_scores = jnp.where(cross_mask[None], cross_scores, NEGATIVE)
    cross_probs = jax.nn.softmax(cross_scores, axis=2)
    cross_low = cross_probs.astype(LOW)
    cross_mix = (
        jnp.einsum("htk,khd->thd", cross_low, cv_heads, preferred_element_type=WIDE)
        .reshape(tok_rows, model_width)
        .astype(LOW)
    )
    after_cross = after_self + matmul(cross_mix, full_xoutput)
    normed_three = (scaled_norm(after_cross, gain_three) + bias_three).astype(LOW)
    pre_act = matmul(normed_three, full_up)
    activ = exact_gelu(pre_act).astype(LOW)
    grad_down = left_t(activ, cotangent)
    (fin_down,) = summed_rows([grad_down])
    block_out = (after_cross + matmul(activ, full_down)).astype(LOW)
    grad_act = right_t(cotangent, full_down)
    _, gelu_pull = jax.vjp(exact_gelu, pre_act)
    grad_pre = gelu_pull(grad_act)[0].astype(LOW)
    grad_up = left_t(normed_three, grad_pre)
    (fin_up,) = summed_rows([grad_up])
    grad_norm_three = right_t(grad_pre, full_up)
    norm_three_part, grad_gain_three, grad_bias_three = norm_back(
        after_cross, gain_three, grad_norm_three
    )
    grad_cross_res = cotangent.astype(WIDE) + norm_three_part
    branch_two = grad_cross_res.astype(LOW)
    grad_xoutput = left_t(cross_mix, branch_two)
    grad_cmix = right_t(branch_two, full_xoutput).astype(LOW)
    grad_cmix = grad_cmix.reshape(tok_rows, head_count, HD)
    grad_cprob = jnp.einsum("thd,khd->htk", grad_cmix, cv_heads, preferred_element_type=WIDE)
    cross_inner = jnp.sum(cross_probs * grad_cprob, axis=2, keepdims=True)
    grad_cscore = (cross_probs * (grad_cprob - cross_inner)).astype(LOW)
    grad_cq = (
        (jnp.einsum("htk,khd->thd", grad_cscore, ck_heads, preferred_element_type=WIDE) * key_scale)
        .reshape(tok_rows, model_width)
        .astype(LOW)
    )
    grad_ck = (
        jnp.einsum("htk,thd->khd", grad_cscore, cq_heads, preferred_element_type=WIDE) * key_scale
    ).reshape(2 * text_rows, model_width)
    grad_cv = jnp.einsum(
        "htk,thd->khd", cross_low, grad_cmix, preferred_element_type=WIDE
    ).reshape(2 * text_rows, model_width)
    grad_xquery = left_t(normed_two, grad_cq)
    grad_norm_two = right_t(grad_cq, full_xquery)
    norm_two_part, grad_gain_two, grad_bias_two = norm_back(after_self, gain_two, grad_norm_two)
    grad_self_res = grad_cross_res + norm_two_part
    branch_one = grad_self_res.astype(LOW)
    grad_output = left_t(attended, branch_one)
    fin_xoutput, fin_xquery, fin_output = summed_rows([grad_xoutput, grad_xquery, grad_output])

    slots = jnp.arange(clip_total, dtype=jnp.int32)
    in_first = (slots == first).astype(WIDE)[None, :, None, None]
    in_second = (slots == second).astype(WIDE)[None, :, None, None]
    pair = jnp.stack([grad_ck, grad_cv]).reshape(2, 2, text_rows, model_width)
    sums = (pair[:, None, 0] * in_first + pair[:, None, 1] * in_second).astype(LOW)
    sums = sums.reshape(2 * clip_total * text_rows, model_width)
    text_total = sums.shape[0]
    padded = -(-text_total // (16 * device_count)) * 16 * device_count
    sums = jnp.pad(sums, ((0, padded - text_total), (0, 0)))
    share = lax.psum_scatter(sums, BOTH, scatter_dimension=0, tiled=True)
    sums = lax.all_gather(share, BOTH, axis=0, tiled=True)
    flat_rows = clip_total * text_rows
    key_round, value_round = sums[:flat_rows], sums[flat_rows:text_total]
    shard_rows = x_key.shape[0]
    col_start = lax.axis_index("shard") * shard_rows
    text_flat = text_states.reshape(flat_rows, model_width)
    text_slice = lax.dynamic_slice_in_dim(text_flat, col_start, shard_rows, 1)
    grad_xkey = left_t(text_slice, key_round)
    grad_xvalue = left_t(text_slice, value_round)
    grad_text = right_t(key_round, full_xkey) + right_t(value_round, full_xvalue)
    grad_text = grad_text.reshape(clip_total, text_rows, model_width)

    grad_attended = right_t(branch_one, full_output).astype(LOW)
    halves = jnp.transpose(grad_attended.reshape(tok_rows, 2, half_width), (1, 0, 2))
    chip_grad = core_pair(
        pick(halves, core, 0),
        swap(pick(halves, 1 - core, 0), BOTH, lambda i: i ^ 1),
        core,
        0,
    )
    chip_dq, grad_window = attend_back(offsets, queries, window, chip_mixed, logs, chip_grad, reach)
    far_part = grad_window[:, :tok_rows]
    below_part = grad_window[:, tok_rows : tok_rows + chip_rows]
    across_part = grad_window[:, tok_rows + chip_rows : tok_rows + 2 * chip_rows]
    own_part = grad_window[:, tok_rows + 2 * chip_rows :]
    back = swap(jnp.concatenate([across_part, far_part], axis=1), BOTH, lambda i: i ^ 2)
    back_unit, back_half = back[:, :chip_rows], back[:, chip_rows:]
    nothing = jnp.zeros_like(back_half)
    low_half = jnp.concatenate([nothing, back_half], axis=1)
    to_below = add_low(below_part, jnp.where(side == 0, low_half, back_unit))
    own_sum = own_part.astype(WIDE) + jnp.where(side == 0, back_unit, jnp.zeros_like(back_unit))
    own_sum = own_sum + swap(to_below, BOTH, lambda i: i - 4).astype(WIDE)
    from_far = swap(back_half, BOTH, lambda i: i - 8 if i % 4 >= 2 else -1)
    own_sum = own_sum + jnp.concatenate([nothing, from_far], axis=1).astype(WIDE)
    chip_grads = jnp.concatenate([chip_dq[None], own_sum.astype(LOW)], axis=0)
    mine = lax.dynamic_slice_in_dim(chip_grads, core * tok_rows, tok_rows, 1)
    away = lax.dynamic_slice_in_dim(chip_grads, (1 - core) * tok_rows, tok_rows, 1)
    got = swap(away, BOTH, lambda i: i ^ 1)
    pieces = core_pair(mine, got, core, 0)
    grad_qkv = jnp.concatenate([pieces[i] for i in range(6)], axis=1)
    grad_weights = left_t(normed_one, grad_qkv)
    (fin_qkv,) = summed_rows([grad_weights])
    grad_norm_one = right_t(grad_qkv, full_qkv)
    norm_one_part, grad_gain_one, grad_bias_one = norm_back(resid, gain_one, grad_norm_one)
    grad_hidden = (grad_self_res + norm_one_part).astype(LOW)
    fin_query, fin_key, fin_value = (
        jnp.concatenate(
            [
                fin_qkv[:, i * half_width : (i + 1) * half_width],
                fin_qkv[:, (i + 3) * half_width : (i + 4) * half_width],
            ],
            axis=1,
        )
        for i in range(3)
    )
    vectors = summed_vectors(
        jnp.stack(
            [
                grad_gain_one,
                grad_bias_one,
                grad_gain_two,
                grad_bias_two,
                grad_gain_three,
                grad_bias_three,
            ]
        ),
    )
    fin_gain_one, fin_bias_one, fin_gain_two, fin_bias_two, fin_gain_three, fin_bias_three = (
        lax.dynamic_slice_in_dim(vectors, col_start, shard_rows, 1)
    )
    return (
        block_out,
        grad_hidden,
        grad_text,
        fin_gain_one,
        fin_bias_one,
        fin_query,
        fin_key,
        fin_value,
        fin_output,
        fin_gain_two,
        fin_bias_two,
        fin_xquery,
        grad_xkey,
        grad_xvalue,
        fin_xoutput,
        fin_gain_three,
        fin_bias_three,
        fin_up,
        fin_down,
    )


def solution(mesh):
    rows, vector, tokens = P("shard", None), P("shard"), P(BOTH, None)
    placed = (
        (tokens, P(), P(BOTH), P(BOTH))
        + (vector, vector, rows, rows, rows, rows)
        + (vector, vector, rows, rows, rows, rows)
        + (vector, vector, rows, rows, tokens)
    )
    return jax.shard_map(
        on_device,
        mesh=mesh,
        in_specs=placed,
        out_specs=(
            (tokens, tokens, P())
            + (vector, vector, rows, rows, rows, rows)
            + (vector, vector, rows, rows, rows, rows)
            + (vector, vector, rows, rows)
        ),
        check_vma=False,
    )
```

time: 3030 us -> 1350 us (0.45)
  waiting for transfers between devices: 1970 us -> 609 us
  blocking collectives: 519 us -> 0 us
  starting transfers between devices: 25.1 us -> 194 us
  matrix products: 309 us -> 181 us
  Pallas kernels: 0 us -> 71.2 us
  local copies, waits for them, and re-layouts: 100 us -> 149 us
  other arithmetic: 69.3 us -> 108 us
    reduce_scatter x8 -> x1, waiting for transfers between devices: 1140 us -> 0.01 us  [on_device(): share = lax.psum_scatter(sums, BOTH, scatter_dimension=0, tiled=True)]
    psum x2 -> x0, blocking collectives: 394 us -> none  [the longest x1 388 us: on_device(): lax.psum((key_slots, value_slots), ('rep', 'shard'))]
    all_gather x11 -> x5, waiting for transfers between devices: 551 us -> 207 us  [the longest x4 207 us: gather_rows(): return lax.all_gather(array, 'shard', axis=0, tiled=True)]
    ppermute x10 -> x52, waiting for transfers between devices: 133 us -> 401 us  [swap(): lax.ppermute(array, axis, [(i, j) for i, j in pairs if 0 <= j < length])]
    ppermute x10 -> x52, starting transfers between devices: 23.7 us -> 193 us  [swap(): lax.ppermute(array, axis, [(i, j) for i, j in pairs if 0 <= j < length])]
    psum x1 -> x0, waiting for transfers between devices: 145 us -> none  [on_device(): lax.psum((sum_query, sum_key, sum_value, sum_output, sum_xquery, sum_xout...]
    unnamed x2 -> x0, blocking collectives: 125 us -> none
    dot_general x34 -> x11, matrix products: 175 us -> 61.1 us  [the longest x8 54.2 us: matmul(): return jnp.dot(left, right, preferred_element_type=WIDE)]
  transfers between devices with their start and end apart: 30 -> 58, of which waited for: 17 -> 24; matrix products, arithmetic and copies ran while one was open for 9% -> 24% of each run, Pallas kernels for 0% -> 5%
where the time goes in v1:
time: 1350 us; the launch traced here: 1330 us
  waiting for transfers between devices  609 us (45%)
  starting transfers between devices  194 us (14%)
  matrix products  181 us (13%)
  local copies, waits for them, and re-layouts  149 us (11%)
  other arithmetic  108 us (8%)
  Pallas kernels  71.2 us (5%)
  between operations  19.5 us (1%)
    ppermute x52, waiting for transfers between devices, swap(): lax.ppermute(array, axis, [(i, j) for i, j in pairs if 0 <= j < length])  401 us
    all_gather x4, waiting for transfers between devices, gather_rows(): return lax.all_gather(array, 'shard', axis=0, tiled=True)  207 us
    ppermute x52, starting transfers between devices, swap(): lax.ppermute(array, axis, [(i, j) for i, j in pairs if 0 <= j < length])  193 us
    dot_general x8, matrix products, right_t(): lax.dot_general(left, right, (((1,), (1,)), ((), ())), preferred_element_...  67.9 us
    dot_general x8, matrix products, matmul(): return jnp.dot(left, right, preferred_element_type=WIDE)  54.2 us
    convert_element_type x21, other arithmetic, add_low(): return (left.astype(WIDE) + right.astype(WIDE)).astype(LOW)  52.6 us
    pallas_call x1, Pallas kernels, attend_back(): pl.pallas_call(functools.partial(attend_back_kernel, reach), grid=(pairs,...  45.3 us
    dot_general x8, matrix products, left_t(): lax.dot_general(left, right, (((0,), (0,)), ((), ())), preferred_element_...  45.2 us
  transfers between devices with their start and end apart: 58, of which 24 were waited for; matrix products, arithmetic and copies ran while one was open for 24% of the time, Pallas kernels for 5%

profile of v1, /device:TPU:0, one launch (start us, length us, event | category | flops | bytes accessed | tf_op | source)
XLA Modules:
  0.0 1330.6 jit_solution(13278441256670104665)
XLA Ops:
  18.8 111.5 %all-gather.6.cloned.1.call-done = bf16[1536,4736]{1,0:T(8,128)(2,1)} async-done(((bf16[96,4736]{1,0:T(8,128)(2,1)}), bf16[1536,4736]{1,0:T(8,128)(2,1)}) %all-gather.6.cloned.1.call-update) | async-done | bytes 14549008 | tf_op jit(solution)/shard_map/all_gather | solution.py:71
  130.2 4.0 convert_reduce_fusion.2
  134.2 11.4 fusion.8
  166.2 64.9 %collective-permute-done.2 = bf16[2,512,768]{2,1,0:T(8,128)(2,1)} collective-permute-done((bf16[2,512,768]{2,1,0:T(8,128)(2,1)}, bf16[2,512,768]{2,1,0:T(8,128)(2,1)}, u32[]{:S(2)}, u32[]{:S(2)}) %collective-permute-start.2) | collective-permute-done | bytes 1572896 | tf_op jit(solution)/shard_map/ppermute | solution.py:63
  234.1 35.7 %collective-permute-start.4 = (bf16[2,768,768]{2,1,0:T(8,128)(2,1)}, bf16[2,768,768]{2,1,0:T(8,128)(2,1)}, u32[]{:S(2)}, u32[]{:S(2)}) collective-permute-start(bf16[2,768,768]{2,1,0:T(8,128)(2,1)} %pad_maximum_fusion.2), channel_id=1, source_target_pairs={{0,2},{1,3},{2,0},{3,1},{4,6},{5,7},{6,4},{7,5},{8,10},{9,11},{10,... | collective-permute-start | bytes 7077896 | tf_op jit(solution)/shard_map/ppermute | solution.py:63
  285.3 76.3 %collective-permute-done.4 = bf16[2,768,768]{2,1,0:T(8,128)(2,1)} collective-permute-done((bf16[2,768,768]{2,1,0:T(8,128)(2,1)}, bf16[2,768,768]{2,1,0:T(8,128)(2,1)}, u32[]{:S(2)}, u32[]{:S(2)}) %collective-permute-start.4) | collective-permute-done | bytes 2359328 | tf_op jit(solution)/shard_map/ppermute | solution.py:63
  364.3 5.3 pad_maximum_fusion.1.window_ref
  369.6 25.9 %attend_forward.1 = (bf16[512,768]{1,0:T(8,128)(2,1)}, f32[6,2,512]{2,1,0:T(2,128)}) custom-call(s32[1,512]{1,0:T(1,128)} %broadcast_select_fusion.9.offset_ref, bf16[512,768]{1,0:T(8,128)(2,1)} %slice_bitcast_fusion.query_ref, bf16[2,1792,768]{2,1,0:T(8,128)(2,1)} %pad_maximum_fusion.1.window_ref), custom_call_target="tpu_custom_call" | custom-call | flops 9663676416 | bytes 3145728 | tf_op jit(solution)/shard_map/attend_forward/pallas_call | solution.py:184
  405.3 4.1 fusion.192
  420.6 4.2 fusion.194
  427.0 7.8 all-gather.10.cloned.1.call-done
  434.8 13.6 %fusion.181 = f32[256,6144]{1,0:T(8,128)} fusion(bf16[1536,6144]{1,0:T(8,128)(2,1)} %all-gather.10.cloned.1.call-done, f32[256,1536]{1,0:T(8,128)S(1)} %get-tuple-element.123, f32[1536]{0:T(1024)} %get-tuple-element.28, f32[1536]{0:T(1024)S(1)} %get-tuple-element.27, f32[256]{0:T(256)} %fusion.171, f32[256]{0:T(256)} %copy-done.77), kind=kOutput, calls=%fused_computation.398 | convolution fusion | flops 4833804288 | bytes 26753024 | tf_op jit(solution)/shard_map/dot_general | solution.py:35
  448.3 87.4 %all-gather.12.cloned.1.call-done = bf16[6144,1536]{1,0:T(8,128)(2,1)} async-done(((bf16[384,1536]{1,0:T(8,128)(2,1)}), bf16[6144,1536]{1,0:T(8,128)(2,1)}) %all-gather.12.cloned.1.call-update) | async-done | bytes 18874384 | tf_op jit(solution)/shard_map/all_gather | solution.py:71
  535.7 23.4 %add_convert_fusion.1 = (bf16[256,6144]{1,0:T(8,128)(2,1)S(1)}, f32[256,6144]{1,0:T(8,128)}) fusion(f32[256,6144]{1,0:T(8,128)} %fusion.181, bf16[256,1536]{1,0:T(8,128)(2,1)} %param.41, bf16[6144,1536]{1,0:T(8,128)(2,1)} %all-gather.12.cloned.1.call-done), kind=kOutput, calls=%fused_computation.25 | convolution fusion | flops 4945084416 | bytes 35389440 | tf_op jit(solution)/shard_map/dot_general | solution.py:43
  559.1 11.3 multiply_reduce_fusion.1
  573.3 4.6 fusion.63
  592.3 9.3 convolution_convert_fusion.1
  610.0 4.9 convolution_convert_fusion.4
  614.9 4.7 multiply_reduce_fusion.2
  621.6 4.3 fusion.57
  632.1 4.7 convolution_convert_fusion.3
  638.0 45.3 %attend_backward.1 = (bf16[512,768]{1,0:T(8,128)(2,1)}, bf16[2,1792,768]{2,1,0:T(8,128)(2,1)}) custom-call(s32[1,512]{1,0:T(1,128)} %broadcast_select_fusion.9.offset_ref, bf16[512,768]{1,0:T(8,128)(2,1)} %slice_bitcast_fusion.query_ref, bf16[2,1792,768]{2,1,0:T(8,128)(2,1)} %pad_maximum_fusion.1.window_ref, bf16[512,768]{1,0:T(8,128)(2,1)} %get-tuple-element.23.out_ref, ...), custom_call_target="tpu_custom_call" | custom-call | flops 24159191040 | bytes 6291456 | tf_op jit(solution)/shard_map/attend_backward/pallas_call | solution.py:272
  688.9 5.3 dynamic-slice_bitcast_fusion.10
  694.3 5.3 dynamic-slice_bitcast_fusion.8
  699.7 5.9 multiply_convert_fusion
  705.6 37.8 %collective-permute-done.7 = bf16[2,768,768]{2,1,0:T(8,128)(2,1)} collective-permute-done((bf16[2,768,768]{2,1,0:T(8,128)(2,1)}, bf16[2,768,768]{2,1,0:T(8,128)(2,1)}, u32[]{:S(2)}, u32[]{:S(2)}) %collective-permute-start.7) | collective-permute-done | bytes 2359328 | tf_op jit(solution)/shard_map/ppermute | solution.py:63
  755.7 8.5 dynamic-slice_bitcast_fusion.1
  764.7 22.6 %collective-permute-done.8 = bf16[2,512,768]{2,1,0:T(8,128)(2,1)} collective-permute-done((bf16[2,512,768]{2,1,0:T(8,128)(2,1)}, bf16[2,512,768]{2,1,0:T(8,128)(2,1)}, u32[]{:S(2)}, u32[]{:S(2)}) %collective-permute-start.8) | collective-permute-done | bytes 1572896 | tf_op jit(solution)/shard_map/ppermute | solution.py:63
  792.3 9.4 convolution_convert_fusion
  801.6 7.9 dynamic-slice_bitcast_fusion
  813.0 8.1 fusion.182
  823.2 10.6 fusion.56
  833.9 35.9 %collective-permute-start.12 = (f32[6,1536]{1,0:T(8,128)S(1)}, f32[6,1536]{1,0:T(8,128)S(1)}, u32[]{:S(2)}, u32[]{:S(2)}) collective-permute-start(f32[6,1536]{1,0:T(8,128)S(1)} %add.447), channel_id=1, source_target_pairs={{0,2},{1,3},{2,0},{3,1},{4,6},{5,7},{6,4},{7,5},{8,10},{9,11},{10,... | collective-permute-start | bytes 110600 | tf_op jit(solution)/shard_map/ppermute | solution.py:63
  869.9 9.0 convolution_convert_fusion.2
  879.0 4.7 add_convert_fusion
  889.3 6.5 dynamic-slice_bitcast_fusion.2
  895.8 5.0 collective-permute-start.14
  911.1 27.4 %collective-permute-done.26 = bf16[4,96,2304]{2,1,0:T(8,128)(2,1)S(1)} collective-permute-done((bf16[4,96,2304]{2,1,0:T(8,128)(2,1)}, bf16[4,96,2304]{2,1,0:T(8,128)(2,1)S(1)}, u32[]{:S(2)}, u32[]{:S(2)}) %collective-permute-start.26) | collective-permute-done | bytes 1769504 | tf_op jit(solution)/shard_map/ppermute | solution.py:63
  942.9 11.2 collective-permute-done.28
  958.6 9.7 fusion.2
  968.3 5.5 fusion.1
  973.9 8.5 fusion.187
  982.4 4.3 constant_dynamic-slice_fusion.3
  1000.0 4.6 fusion.186
  1014.0 12.0 collective-permute-done.31
  1030.1 5.2 fusion.27
  1035.4 6.3 fusion.47
  1046.2 26.8 %collective-permute-done.33 = bf16[48,4608]{1,0:T(8,128)(2,1)S(1)} collective-permute-done((bf16[48,4608]{1,0:T(8,128)(2,1)S(1)}, bf16[48,4608]{1,0:T(8,128)(2,1)S(1)}, u32[]{:S(2)}, u32[]{:S(2)}) %collective-permute-start.33) | collective-permute-done | bytes 442400 | tf_op jit(solution)/shard_map/ppermute | solution.py:63
  1087.3 7.4 collective-permute-done.44
  1099.1 28.0 %collective-permute-done.46 = bf16[4,2,192,768]{3,2,0,1:T(8,128)(2,1)S(1)} collective-permute-done((bf16[4,2,192,768]{3,2,0,1:T(8,128)(2,1)S(1)}, bf16[4,2,192,768]{3,2,0,1:T(8,128)(2,1)S(1)}, u32[]{:S(2)}, u32[]{:S(2)}) %collective-permute-start.46) | collective-permute-done | bytes 2359328 | tf_op jit(solution)/shard_map/ppermute | solution.py:63
  1130.5 10.0 fusion.3
  1145.6 6.9 collective-permute-done.36
  1156.0 7.9 collective-permute-start.39
  1167.1 5.4 collective-permute-done.45
  1177.5 16.4 %collective-permute-start.48 = (bf16[192,1536]{1,0:T(8,128)(2,1)S(1)}, bf16[192,1536]{1,0:T(8,128)(2,1)S(1)}, u32[]{:S(2)}, u32[]{:S(2)}) collective-permute-start(bf16[192,1536]{1,0:T(8,128)(2,1)S(1)} %get-tuple-element.71), channel_id=1, source_target_pairs={{0,4},{1,5},{2,6},{3,7},{4,8},{5,9},{6,10},{7,11},{8,12},{9,13},{1... | collective-permute-start | bytes 1769480 | tf_op jit(solution)/shard_map/ppermute | solution.py:63
  1193.9 6.7 collective-permute-done.40
  1200.6 31.6 %collective-permute-start.50 = (bf16[192,1536]{1,0:T(8,128)(2,1)S(1)}, bf16[192,1536]{1,0:T(8,128)(2,1)S(1)}, u32[]{:S(2)}, u32[]{:S(2)}) collective-permute-start(bf16[192,1536]{1,0:T(8,128)(2,1)S(1)} %get-tuple-element.73), channel_id=1, source_target_pairs={{0,12},{1,13},{2,14},{3,15},{4,0},{5,1},{6,2},{7,3},{8,4},{9,5},{1... | collective-permute-start | bytes 1769480 | tf_op jit(solution)/shard_map/ppermute | solution.py:63
  1233.8 10.0 collective-permute-done.50
  1248.3 27.0 %collective-permute-done.18 = bf16[4,48,2304]{2,1,0:T(8,128)(2,1)S(1)} collective-permute-done((bf16[4,48,2304]{2,1,0:T(8,128)(2,1)S(1)}, bf16[4,48,2304]{2,1,0:T(8,128)(2,1)S(1)}, u32[]{:S(2)}, u32[]{:S(2)}) %collective-permute-start.18) | collective-permute-done | bytes 884768 | tf_op jit(solution)/shard_map/ppermute | solution.py:63
  1275.9 10.7 collective-permute-start.21
  1293.1 4.1 collective-permute-done.21
  1297.2 9.5 collective-permute-done.22
  1306.7 5.7 collective-permute-done.23
  1315.1 6.1 collective-permute-done.24
  (520 shorter events, 249.2 us)
Async XLA Ops:
  7.2 123.0 %all-gather.6.cloned.1.call-start = ((), (), s32[]{:S(2)}) async-start(), calls=%async_computation.1 | async-start | bytes 15458304 | tf_op jit(solution)/shard_map/all_gather | solution.py:71
  14.8 382.1 %all-gather.8.cloned.1.call-start = ((), (), s32[]{:S(2)}) async-start(), calls=%async_computation.2 | async-start | bytes 25067520 | tf_op jit(solution)/shard_map/all_gather | solution.py:71
  16.2 418.5 %all-gather.10.cloned.1.call-start = ((), (), s32[]{:S(2)}) async-start(), calls=%async_computation.3 | async-start | bytes 20054016 | tf_op jit(solution)/shard_map/all_gather | solution.py:71
  17.0 518.7 %all-gather.12.cloned.1.call-start = ((), (), s32[]{:S(2)}) async-start(), calls=%async_computation.4 | async-start | bytes 20054016 | tf_op jit(solution)/shard_map/all_gather | solution.py:71
  17.5 816.3 %reduce-scatter.2.cloned.1.call-start = ((), (), s32[]{:S(2)}) async-start(), calls=%async_computation.5 | async-start | bytes 3244032 | tf_op jit(solution)/shard_map/reduce_scatter | solution.py:476
  17.8 127.8 %copy-start.80 = (f32[256]{0:T(256)}, f32[256]{0:T(256)S(1)}, u32[]{:S(2)}) copy-start(f32[256]{0:T(256)S(1)} %broadcast_multiply_fusion.2) | copy-start | bytes 3076
  18.8 126.8 %copy-start.86 = (f32[256]{0:T(256)}, f32[256]{0:T(256)S(1)}, u32[]{:S(2)}) copy-start(f32[256]{0:T(256)S(1)} %fusion.169) | copy-start | bytes 3076
  152.5 3.1 collective-permute-start.1
  160.6 70.6 %collective-permute-start.2 = (bf16[2,512,768]{2,1,0:T(8,128)(2,1)}, bf16[2,512,768]{2,1,0:T(8,128)(2,1)}, u32[]{:S(2)}, u32[]{:S(2)}) collective-permute-start(bf16[2,512,768]{2,1,0:T(8,128)(2,1)} %slice.237), channel_id=1, source_target_pairs={{0,4},{1,5},{2,6},{3,7},{4,8},{5,9},{6,10},{7,11},{8,12},{9,13},{1... | collective-permute-start | bytes 4718600 | tf_op jit(solution)/shard_map/ppermute | solution.py:63
  164.7 1.6 collective-permute-start.3
  234.1 127.5 %collective-permute-start.4 = (bf16[2,768,768]{2,1,0:T(8,128)(2,1)}, bf16[2,768,768]{2,1,0:T(8,128)(2,1)}, u32[]{:S(2)}, u32[]{:S(2)}) collective-permute-start(bf16[2,768,768]{2,1,0:T(8,128)(2,1)} %pad_maximum_fusion.2), channel_id=1, source_target_pairs={{0,2},{1,3},{2,0},{3,1},{4,6},{5,7},{6,4},{7,5},{8,10},{9,11},{10,... | collective-permute-start | bytes 7077896 | tf_op jit(solution)/shard_map/ppermute | solution.py:63
  269.8 13.2 collective-permute-start
  396.8 7.7 collective-permute-start.5
  424.8 167.4 %copy-start.7 = (f32[256,1536]{1,0:T(8,128)}, f32[256,1536]{1,0:T(8,128)S(1)}, u32[]{:S(2)}) copy-start(f32[256,1536]{1,0:T(8,128)S(1)} %get-tuple-element.123) | copy-start | bytes 4718596
  627.8 8.9 collective-permute-start.6
  631.1 399.0 %all-gather.14.cloned.1.call-start = ((), (), s32[]{:S(2)}) async-start(), calls=%async_computation.6 | async-start | bytes 3244032 | tf_op jit(solution)/shard_map/all_gather | solution.py:477
  687.6 55.8 %collective-permute-start.7 = (bf16[2,768,768]{2,1,0:T(8,128)(2,1)}, bf16[2,768,768]{2,1,0:T(8,128)(2,1)}, u32[]{:S(2)}, u32[]{:S(2)}) collective-permute-start(bf16[2,768,768]{2,1,0:T(8,128)(2,1)} %pad_maximum_fusion.3), channel_id=1, source_target_pairs={{0,2},{1,3},{2,0},{3,1},{4,6},{5,7},{6,4},{7,5},{8,10},{9,11},{10,... | collective-permute-start | bytes 7077896 | tf_op jit(solution)/shard_map/ppermute | solution.py:63
  705.6 86.7 %copy-start.4 = (bf16[256,6144]{1,0:T(8,128)(2,1)}, bf16[256,6144]{1,0:T(8,128)(2,1)S(1)}, u32[]{:S(2)}) copy-start(bf16[256,6144]{1,0:T(8,128)(2,1)S(1)} %multiply_convert_fusion) | copy-start | bytes 9437188
  749.4 37.9 %collective-permute-start.8 = (bf16[2,512,768]{2,1,0:T(8,128)(2,1)}, bf16[2,512,768]{2,1,0:T(8,128)(2,1)}, u32[]{:S(2)}, u32[]{:S(2)}) collective-permute-start(bf16[2,512,768]{2,1,0:T(8,128)(2,1)} %add_convert_fusion.3), channel_id=1, source_target_pairs={{4,0},{5,1},{6,2},{7,3},{8,4},{9,5},{10,6},{11,7},{12,8},{13,9},{1... | collective-permute-start | bytes 4718600 | tf_op jit(solution)/shard_map/ppermute | solution.py:63
  754.1 124.8 %collective-permute-start.25 = (bf16[8,96,4608]{2,1,0:T(8,128)(2,1)}, bf16[8,96,4608]{2,1,0:T(8,128)(2,1)}, u32[]{:S(2)}, u32[]{:S(2)}) collective-permute-start(bf16[8,96,4608]{2,1,0:T(8,128)(2,1)} %pad_maximum_fusion), channel_id=1, source_target_pairs={{0,1},{1,0},{2,3},{3,2},{4,5},{5,4},{6,7},{7,6},{8,9},{9,8},{10,11... | collective-permute-start | bytes 21233672 | tf_op jit(solution)/shard_map/ppermute | solution.py:63
  754.1 10.6 collective-permute-start.9
  764.2 194.4 %collective-permute-start.34 = (bf16[8,96,6144]{2,1,0:T(8,128)(2,1)}, bf16[8,96,6144]{2,1,0:T(8,128)(2,1)}, u32[]{:S(2)}, u32[]{:S(2)}) collective-permute-start(bf16[8,96,6144]{2,1,0:T(8,128)(2,1)} %dynamic-slice_bitcast_fusion.1), channel_id=1, source_target_pairs={{0,1},{1,0},{2,3},{3,2},{4,5},{5,4},{6,7},{7,6},{8,9},{9,8},{10,11... | collective-permute-start | bytes 28311560 | tf_op jit(solution)/shard_map/ppermute | solution.py:63
  792.2 17.8 %collective-permute-start.10 = (bf16[3,256,768]{2,1,0:T(8,128)(2,1)}, bf16[3,256,768]{2,1,0:T(8,128)(2,1)}, u32[]{:S(2)}, u32[]{:S(2)}) collective-permute-start(bf16[3,256,768]{2,1,0:T(8,128)(2,1)} %get-tuple-element.78), channel_id=1, source_target_pairs={{0,1},{1,0},{2,3},{3,2},{4,5},{5,4},{6,7},{7,6},{8,9},{9,8},{10,11... | collective-permute-start | bytes 3538952 | tf_op jit(solution)/shard_map/ppermute | solution.py:63
  809.5 158.8 %collective-permute-start.43 = (bf16[8,384,1536]{2,1,0:T(8,128)(2,1)}, bf16[8,384,1536]{2,1,0:T(8,128)(2,1)}, u32[]{:S(2)}, u32[]{:S(2)}) collective-permute-start(bf16[8,384,1536]{2,1,0:T(8,128)(2,1)} %dynamic-slice_bitcast_fusion), channel_id=1, source_target_pairs={{0,1},{1,0},{2,3},{3,2},{4,5},{5,4},{6,7},{7,6},{8,9},{9,8},{10,11... | collective-permute-start | bytes 28311560 | tf_op jit(solution)/shard_map/ppermute | solution.py:63
  823.1 10.8 collective-permute-start.11
  833.9 44.9 %collective-permute-start.12 = (f32[6,1536]{1,0:T(8,128)S(1)}, f32[6,1536]{1,0:T(8,128)S(1)}, u32[]{:S(2)}, u32[]{:S(2)}) collective-permute-start(f32[6,1536]{1,0:T(8,128)S(1)} %add.447), channel_id=1, source_target_pairs={{0,2},{1,3},{2,0},{3,1},{4,6},{5,7},{6,4},{7,5},{8,10},{9,11},{10,... | collective-permute-start | bytes 110600 | tf_op jit(solution)/shard_map/ppermute | solution.py:63
  878.9 16.9 %collective-permute-start.13 = (f32[6,1536]{1,0:T(8,128)S(1)}, f32[6,1536]{1,0:T(8,128)S(1)}, u32[]{:S(2)}, u32[]{:S(2)}) collective-permute-start(f32[6,1536]{1,0:T(8,128)S(1)} %add.448), channel_id=1, source_target_pairs={{0,4},{1,5},{2,6},{3,7},{4,0},{5,1},{6,2},{7,3},{8,12},{9,13},{10,... | collective-permute-start | bytes 110600 | tf_op jit(solution)/shard_map/ppermute | solution.py:63
  883.7 74.9 %slice-start.5 = ((s8[18874368]{0:T(1024)(128)(4,1)}), s8[2097152]{0:T(1024)(128)(4,1)S(1)}, s32[]{:S(2)}) async-start(s8[18874368]{0:T(1024)(128)(4,1)} %bitcast.323), calls=%async_computation.12 | async-start | bytes 4194304
  883.7 74.9 %slice-start.6 = ((s8[18874368]{0:T(1024)(128)(4,1)}), s8[4194304]{0:T(1024)(128)(4,1)S(1)}, s32[]{:S(2)}) async-start(s8[18874368]{0:T(1024)(128)(4,1)} %bitcast.323), calls=%async_computation.13 | async-start | bytes 8388608
  889.1 49.3 %collective-permute-start.26 = (bf16[4,96,2304]{2,1,0:T(8,128)(2,1)}, bf16[4,96,2304]{2,1,0:T(8,128)(2,1)S(1)}, u32[]{:S(2)}, u32[]{:S(2)}) collective-permute-start(bf16[4,96,2304]{2,1,0:T(8,128)(2,1)} %dynamic-slice_bitcast_fusion.11), channel_id=1, source_target_pairs={{0,2},{1,3},{2,0},{3,1},{4,6},{5,7},{6,4},{7,5},{8,10},{9,11},{10,... | collective-permute-start | bytes 5308424 | tf_op jit(solution)/shard_map/ppermute | solution.py:63
  895.8 8.4 collective-permute-start.14
  904.3 6.2 collective-permute-start.15
  906.9 47.2 %collective-permute-start.28 = (bf16[4,2,48,2304]{3,2,0,1:T(8,128)(2,1)S(1)}, bf16[4,2,48,2304]{3,2,0,1:T(8,128)(2,1)S(1)}, u32[]{:S(2)}, u32[]{:S(2)}) collective-permute-start(bf16[4,2,48,2304]{3,2,0,1:T(8,128)(2,1)S(1)} %bitcast.363), channel_id=1, source_target_pairs={{0,16},{16,0},{1,17},{17,1},{2,18},{18,2},{3,19},{19,3},{4,20},{20... | collective-permute-start | bytes 5308424 | tf_op jit(solution)/shard_map/ppermute | solution.py:63
  910.5 220.0 %collective-permute-start.16 = (bf16[8,96,4608]{2,1,0:T(8,128)(2,1)}, bf16[8,96,4608]{2,1,0:T(8,128)(2,1)}, u32[]{:S(2)}, u32[]{:S(2)}) collective-permute-start(bf16[8,96,4608]{2,1,0:T(8,128)(2,1)} %dynamic-slice_bitcast_fusion.2), channel_id=1, source_target_pairs={{0,1},{1,0},{2,3},{3,2},{4,5},{5,4},{6,7},{7,6},{8,9},{9,8},{10,11... | collective-permute-start | bytes 21233672 | tf_op jit(solution)/shard_map/ppermute | solution.py:63
  941.1 49.1 %collective-permute-start.27 = (bf16[4,48,2304]{2,1,0:T(8,128)(2,1)}, bf16[4,48,2304]{2,1,0:T(8,128)(2,1)}, u32[]{:S(2)}, u32[]{:S(2)}) collective-permute-start(bf16[4,48,2304]{2,1,0:T(8,128)(2,1)} %dynamic-slice_bitcast_fusion.18), channel_id=1, source_target_pairs={{0,16},{16,0},{1,17},{17,1},{2,18},{18,2},{3,19},{19,3},{4,20},{20... | collective-permute-start | bytes 2654216 | tf_op jit(solution)/shard_map/ppermute | solution.py:63
  956.8 35.1 %collective-permute-start.29 = (bf16[4,48,2304]{2,1,0:T(8,128)(2,1)}, bf16[4,48,2304]{2,1,0:T(8,128)(2,1)}, u32[]{:S(2)}, u32[]{:S(2)}) collective-permute-start(bf16[4,48,2304]{2,1,0:T(8,128)(2,1)} %dynamic-slice_bitcast_fusion.17), channel_id=1, source_target_pairs={{0,2},{1,3},{2,0},{3,1},{4,6},{5,7},{6,4},{7,5},{8,10},{9,11},{10,... | collective-permute-start | bytes 2654216 | tf_op jit(solution)/shard_map/ppermute | solution.py:63
  989.7 86.7 %collective-permute-start.35 = (bf16[4,96,3072]{2,1,0:T(8,128)(2,1)}, bf16[4,96,3072]{2,1,0:T(8,128)(2,1)}, u32[]{:S(2)}, u32[]{:S(2)}) collective-permute-start(bf16[4,96,3072]{2,1,0:T(8,128)(2,1)} %dynamic-slice_bitcast_fusion.4), channel_id=1, source_target_pairs={{0,2},{1,3},{2,0},{3,1},{4,6},{5,7},{6,4},{7,5},{8,10},{9,11},{10,... | collective-permute-start | bytes 7077896 | tf_op jit(solution)/shard_map/ppermute | solution.py:63
  994.8 17.2 %collective-permute-start.30 = (bf16[48,4608]{1,0:T(8,128)(2,1)}, bf16[48,4608]{1,0:T(8,128)(2,1)}, u32[]{:S(2)}, u32[]{:S(2)}) collective-permute-start(bf16[48,4608]{1,0:T(8,128)(2,1)} %get-tuple-element.84), channel_id=1, source_target_pairs={{0,4},{1,5},{2,6},{3,7},{4,8},{5,9},{6,10},{7,11},{8,12},{9,13},{1... | collective-permute-start | bytes 1327112 | tf_op jit(solution)/shard_map/ppermute | solution.py:63
  995.1 30.9 %collective-permute-start.31 = (bf16[48,4608]{1,0:T(8,128)(2,1)}, bf16[48,4608]{1,0:T(8,128)(2,1)}, u32[]{:S(2)}, u32[]{:S(2)}) collective-permute-start(bf16[48,4608]{1,0:T(8,128)(2,1)} %get-tuple-element.85), channel_id=1, source_target_pairs={{0,8},{1,9},{2,10},{3,11},{4,12},{5,13},{6,14},{7,15},{8,0},{9,1},... | collective-permute-start | bytes 1327112 | tf_op jit(solution)/shard_map/ppermute | solution.py:63
  997.7 29.4 %collective-permute-start.32 = (bf16[48,4608]{1,0:T(8,128)(2,1)S(1)}, bf16[48,4608]{1,0:T(8,128)(2,1)}, u32[]{:S(2)}, u32[]{:S(2)}) collective-permute-start(bf16[48,4608]{1,0:T(8,128)(2,1)S(1)} %get-tuple-element.86), channel_id=1, source_target_pairs={{0,12},{1,13},{2,14},{3,15},{4,0},{5,1},{6,2},{7,3},{8,4},{9,5},{1... | collective-permute-start | bytes 1327112 | tf_op jit(solution)/shard_map/ppermute | solution.py:63
  1012.0 68.2 %collective-permute-start.37 = (bf16[4,2,48,3072]{3,2,0,1:T(8,128)(2,1)}, bf16[4,2,48,3072]{3,2,0,1:T(8,128)(2,1)}, u32[]{:S(2)}, u32[]{:S(2)}) collective-permute-start(bf16[4,2,48,3072]{3,2,0,1:T(8,128)(2,1)} %bitcast.313), channel_id=1, source_target_pairs={{0,16},{16,0},{1,17},{17,1},{2,18},{18,2},{3,19},{19,3},{4,20},{20... | collective-permute-start | bytes 7077896 | tf_op jit(solution)/shard_map/ppermute | solution.py:63
  1026.0 68.7 %collective-permute-start.44 = (bf16[4,384,768]{2,1,0:T(8,128)(2,1)}, bf16[4,384,768]{2,1,0:T(8,128)(2,1)}, u32[]{:S(2)}, u32[]{:S(2)}) collective-permute-start(bf16[4,384,768]{2,1,0:T(8,128)(2,1)} %dynamic-slice_bitcast_fusion.3), channel_id=1, source_target_pairs={{0,2},{1,3},{2,0},{3,1},{4,6},{5,7},{6,4},{7,5},{8,10},{9,11},{10,... | collective-permute-start | bytes 7077896 | tf_op jit(solution)/shard_map/ppermute | solution.py:63
  1028.6 44.4 %collective-permute-start.33 = (bf16[48,4608]{1,0:T(8,128)(2,1)S(1)}, bf16[48,4608]{1,0:T(8,128)(2,1)S(1)}, u32[]{:S(2)}, u32[]{:S(2)}) collective-permute-start(bf16[48,4608]{1,0:T(8,128)(2,1)S(1)} %fusion.113), channel_id=1, source_target_pairs={{0,16},{16,0},{1,17},{17,1},{2,18},{18,2},{3,19},{19,3},{4,20},{20... | collective-permute-start | bytes 1327112 | tf_op jit(solution)/shard_map/ppermute | solution.py:63
  1073.0 54.1 %collective-permute-start.46 = (bf16[4,2,192,768]{3,2,0,1:T(8,128)(2,1)S(1)}, bf16[4,2,192,768]{3,2,0,1:T(8,128)(2,1)S(1)}, u32[]{:S(2)}, u32[]{:S(2)}) collective-permute-start(bf16[4,2,192,768]{3,2,0,1:T(8,128)(2,1)S(1)} %bitcast.359), channel_id=1, source_target_pairs={{0,16},{16,0},{1,17},{17,1},{2,18},{18,2},{3,19},{19,3},{4,20},{20... | collective-permute-start | bytes 7077896 | tf_op jit(solution)/shard_map/ppermute | solution.py:63
  1080.2 72.3 %collective-permute-start.36 = (bf16[4,48,3072]{2,1,0:T(8,128)(2,1)}, bf16[4,48,3072]{2,1,0:T(8,128)(2,1)}, u32[]{:S(2)}, u32[]{:S(2)}) collective-permute-start(bf16[4,48,3072]{2,1,0:T(8,128)(2,1)} %dynamic-slice_bitcast_fusion.16), channel_id=1, source_target_pairs={{0,16},{16,0},{1,17},{17,1},{2,18},{18,2},{3,19},{19,3},{4,20},{20... | collective-permute-start | bytes 3538952 | tf_op jit(solution)/shard_map/ppermute | solution.py:63
  1086.1 68.1 %collective-permute-start.38 = (bf16[4,48,3072]{2,1,0:T(8,128)(2,1)}, bf16[4,48,3072]{2,1,0:T(8,128)(2,1)}, u32[]{:S(2)}, u32[]{:S(2)}) collective-permute-start(bf16[4,48,3072]{2,1,0:T(8,128)(2,1)} %dynamic-slice_bitcast_fusion.15), channel_id=1, source_target_pairs={{0,2},{1,3},{2,0},{3,1},{4,6},{5,7},{6,4},{7,5},{8,10},{9,11},{10,... | collective-permute-start | bytes 3538952 | tf_op jit(solution)/shard_map/ppermute | solution.py:63
  1097.1 75.4 %collective-permute-start.45 = (bf16[4,192,768]{2,1,0:T(8,128)(2,1)S(1)}, bf16[4,192,768]{2,1,0:T(8,128)(2,1)}, u32[]{:S(2)}, u32[]{:S(2)}) collective-permute-start(bf16[4,192,768]{2,1,0:T(8,128)(2,1)S(1)} %dynamic-slice_bitcast_fusion.14), channel_id=1, source_target_pairs={{0,16},{16,0},{1,17},{17,1},{2,18},{18,2},{3,19},{19,3},{4,20},{20... | collective-permute-start | bytes 3538952 | tf_op jit(solution)/shard_map/ppermute | solution.py:63
  1129.2 45.7 %collective-permute-start.47 = (bf16[4,192,768]{2,1,0:T(8,128)(2,1)S(1)}, bf16[4,192,768]{2,1,0:T(8,128)(2,1)S(1)}, u32[]{:S(2)}, u32[]{:S(2)}) collective-permute-start(bf16[4,192,768]{2,1,0:T(8,128)(2,1)S(1)} %dynamic-slice_bitcast_fusion.13), channel_id=1, source_target_pairs={{0,2},{1,3},{2,0},{3,1},{4,6},{5,7},{6,4},{7,5},{8,10},{9,11},{10,... | collective-permute-start | bytes 3538952 | tf_op jit(solution)/shard_map/ppermute | solution.py:63
  1144.7 100.3 %collective-permute-start.17 = (bf16[4,96,2304]{2,1,0:T(8,128)(2,1)S(1)}, bf16[4,96,2304]{2,1,0:T(8,128)(2,1)S(1)}, u32[]{:S(2)}, u32[]{:S(2)}) collective-permute-start(bf16[4,96,2304]{2,1,0:T(8,128)(2,1)S(1)} %dynamic-slice_bitcast_fusion.12), channel_id=1, source_target_pairs={{0,2},{1,3},{2,0},{3,1},{4,6},{5,7},{6,4},{7,5},{8,10},{9,11},{10,... | collective-permute-start | bytes 5308424 | tf_op jit(solution)/shard_map/ppermute | solution.py:63
  1156.0 21.4 %collective-permute-start.39 = (bf16[48,6144]{1,0:T(8,128)(2,1)S(1)}, bf16[48,6144]{1,0:T(8,128)(2,1)S(1)}, u32[]{:S(2)}, u32[]{:S(2)}) collective-permute-start(bf16[48,6144]{1,0:T(8,128)(2,1)S(1)} %get-tuple-element.74), channel_id=1, source_target_pairs={{0,4},{1,5},{2,6},{3,7},{4,8},{5,9},{6,10},{7,11},{8,12},{9,13},{1... | collective-permute-start | bytes 1769480 | tf_op jit(solution)/shard_map/ppermute | solution.py:63
  1164.0 36.6 %collective-permute-start.40 = (bf16[48,6144]{1,0:T(8,128)(2,1)S(1)}, bf16[48,6144]{1,0:T(8,128)(2,1)S(1)}, u32[]{:S(2)}, u32[]{:S(2)}) collective-permute-start(bf16[48,6144]{1,0:T(8,128)(2,1)S(1)} %get-tuple-element.75), channel_id=1, source_target_pairs={{0,8},{1,9},{2,10},{3,11},{4,12},{5,13},{6,14},{7,15},{8,0},{9,1},... | collective-permute-start | bytes 1769480 | tf_op jit(solution)/shard_map/ppermute | solution.py:63
  1172.5 28.1 %collective-permute-start.41 = (bf16[48,6144]{1,0:T(8,128)(2,1)S(1)}, bf16[48,6144]{1,0:T(8,128)(2,1)S(1)}, u32[]{:S(2)}, u32[]{:S(2)}) collective-permute-start(bf16[48,6144]{1,0:T(8,128)(2,1)S(1)} %get-tuple-element.76), channel_id=1, source_target_pairs={{0,12},{1,13},{2,14},{3,15},{4,0},{5,1},{6,2},{7,3},{8,4},{9,5},{1... | collective-permute-start | bytes 1769480 | tf_op jit(solution)/shard_map/ppermute | solution.py:63
  1174.9 71.9 %collective-permute-start.19 = (bf16[4,2,48,2304]{3,2,0,1:T(8,128)(2,1)S(1)}, bf16[4,2,48,2304]{3,2,0,1:T(8,128)(2,1)S(1)}, u32[]{:S(2)}, u32[]{:S(2)}) collective-permute-start(bf16[4,2,48,2304]{3,2,0,1:T(8,128)(2,1)S(1)} %bitcast.362), channel_id=1, source_target_pairs={{0,16},{16,0},{1,17},{17,1},{2,18},{18,2},{3,19},{19,3},{4,20},{20... | collective-permute-start | bytes 5308424 | tf_op jit(solution)/shard_map/ppermute | solution.py:63
  1177.5 55.0 %collective-permute-start.48 = (bf16[192,1536]{1,0:T(8,128)(2,1)S(1)}, bf16[192,1536]{1,0:T(8,128)(2,1)S(1)}, u32[]{:S(2)}, u32[]{:S(2)}) collective-permute-start(bf16[192,1536]{1,0:T(8,128)(2,1)S(1)} %get-tuple-element.71), channel_id=1, source_target_pairs={{0,4},{1,5},{2,6},{3,7},{4,8},{5,9},{6,10},{7,11},{8,12},{9,13},{1... | collective-permute-start | bytes 1769480 | tf_op jit(solution)/shard_map/ppermute | solution.py:63
  1200.6 33.2 %collective-permute-start.49 = (bf16[192,1536]{1,0:T(8,128)(2,1)S(1)}, bf16[192,1536]{1,0:T(8,128)(2,1)S(1)}, u32[]{:S(2)}, u32[]{:S(2)}) collective-permute-start(bf16[192,1536]{1,0:T(8,128)(2,1)S(1)} %get-tuple-element.72), channel_id=1, source_target_pairs={{0,8},{1,9},{2,10},{3,11},{4,12},{5,13},{6,14},{7,15},{8,0},{9,1},... | collective-permute-start | bytes 1769480 | tf_op jit(solution)/shard_map/ppermute | solution.py:63
  1200.6 43.2 %collective-permute-start.50 = (bf16[192,1536]{1,0:T(8,128)(2,1)S(1)}, bf16[192,1536]{1,0:T(8,128)(2,1)S(1)}, u32[]{:S(2)}, u32[]{:S(2)}) collective-permute-start(bf16[192,1536]{1,0:T(8,128)(2,1)S(1)} %get-tuple-element.73), channel_id=1, source_target_pairs={{0,12},{1,13},{2,14},{3,15},{4,0},{5,1},{6,2},{7,3},{8,4},{9,5},{1... | collective-permute-start | bytes 1769480 | tf_op jit(solution)/shard_map/ppermute | solution.py:63
  1232.5 15.7 %collective-permute-start.42 = (bf16[48,6144]{1,0:T(8,128)(2,1)S(1)}, bf16[48,6144]{1,0:T(8,128)(2,1)S(1)}, u32[]{:S(2)}, u32[]{:S(2)}) collective-permute-start(bf16[48,6144]{1,0:T(8,128)(2,1)S(1)} %fusion.109), channel_id=1, source_target_pairs={{0,16},{16,0},{1,17},{17,1},{2,18},{18,2},{3,19},{19,3},{4,20},{20... | collective-permute-start | bytes 1769480 | tf_op jit(solution)/shard_map/ppermute | solution.py:63
  1244.1 69.2 %collective-permute-start.51 = (bf16[192,1536]{1,0:T(8,128)(2,1)S(1)}, bf16[192,1536]{1,0:T(8,128)(2,1)S(1)}, u32[]{:S(2)}, u32[]{:S(2)}) collective-permute-start(bf16[192,1536]{1,0:T(8,128)(2,1)S(1)} %fusion.106), channel_id=1, source_target_pairs={{0,16},{16,0},{1,17},{17,1},{2,18},{18,2},{3,19},{19,3},{4,20},{20... | collective-permute-start | bytes 1769480 | tf_op jit(solution)/shard_map/ppermute | solution.py:63
  1245.6 29.7 %collective-permute-start.18 = (bf16[4,48,2304]{2,1,0:T(8,128)(2,1)S(1)}, bf16[4,48,2304]{2,1,0:T(8,128)(2,1)S(1)}, u32[]{:S(2)}, u32[]{:S(2)}) collective-permute-start(bf16[4,48,2304]{2,1,0:T(8,128)(2,1)S(1)} %dynamic-slice_bitcast_fusion.20), channel_id=1, source_target_pairs={{0,16},{16,0},{1,17},{17,1},{2,18},{18,2},{3,19},{19,3},{4,20},{20... | collective-permute-start | bytes 2654216 | tf_op jit(solution)/shard_map/ppermute | solution.py:63
  1247.3 28.3 %collective-permute-start.20 = (bf16[4,48,2304]{2,1,0:T(8,128)(2,1)S(1)}, bf16[4,48,2304]{2,1,0:T(8,128)(2,1)S(1)}, u32[]{:S(2)}, u32[]{:S(2)}) collective-permute-start(bf16[4,48,2304]{2,1,0:T(8,128)(2,1)S(1)} %dynamic-slice_bitcast_fusion.19), channel_id=1, source_target_pairs={{0,2},{1,3},{2,0},{3,1},{4,6},{5,7},{6,4},{7,5},{8,10},{9,11},{10,... | collective-permute-start | bytes 2654216 | tf_op jit(solution)/shard_map/ppermute | solution.py:63
  1275.9 21.3 %collective-permute-start.21 = (bf16[48,4608]{1,0:T(8,128)(2,1)S(1)}, bf16[48,4608]{1,0:T(8,128)(2,1)S(1)}, u32[]{:S(2)}, u32[]{:S(2)}) collective-permute-start(bf16[48,4608]{1,0:T(8,128)(2,1)S(1)} %get-tuple-element.93), channel_id=1, source_target_pairs={{0,4},{1,5},{2,6},{3,7},{4,8},{5,9},{6,10},{7,11},{8,12},{9,13},{1... | collective-permute-start | bytes 1327112 | tf_op jit(solution)/shard_map/ppermute | solution.py:63
  1286.6 20.1 %collective-permute-start.22 = (bf16[48,4608]{1,0:T(8,128)(2,1)S(1)}, bf16[48,4608]{1,0:T(8,128)(2,1)S(1)}, u32[]{:S(2)}, u32[]{:S(2)}) collective-permute-start(bf16[48,4608]{1,0:T(8,128)(2,1)S(1)} %get-tuple-element.94), channel_id=1, source_target_pairs={{0,8},{1,9},{2,10},{3,11},{4,12},{5,13},{6,14},{7,15},{8,0},{9,1},... | collective-permute-start | bytes 1327112 | tf_op jit(solution)/shard_map/ppermute | solution.py:63
  1288.6 23.8 %collective-permute-start.23 = (bf16[48,4608]{1,0:T(8,128)(2,1)S(1)}, bf16[48,4608]{1,0:T(8,128)(2,1)S(1)}, u32[]{:S(2)}, u32[]{:S(2)}) collective-permute-start(bf16[48,4608]{1,0:T(8,128)(2,1)S(1)} %get-tuple-element.95), channel_id=1, source_target_pairs={{0,12},{1,13},{2,14},{3,15},{4,0},{5,1},{6,2},{7,3},{8,4},{9,5},{1... | collective-permute-start | bytes 1327112 | tf_op jit(solution)/shard_map/ppermute | solution.py:63
  1312.7 8.5 collective-permute-start.24
  (117 other events, 1174.4 us)
Sparse Core Ops, SparseCore 0:
  14.9 115.2 all-gather.5
  132.4 188.8 all-gather.7
  322.9 111.7 all-gather.9
  436.2 99.4 all-gather.11
  631.3 101.8 reduce-scatter.1
  834.0 100.7 all-gather.13

commit v2 on v1

--- a/solution.py
+++ b/solution.py
@@ -6,6 +6,7 @@
 from jax.experimental import pallas as pl
 from jax.experimental.pallas import tpu as pltpu
 from jax.sharding import PartitionSpec as P
+
 
 HD = 64
 CLIP_MAX = 1280
@@ -75,57 +76,104 @@
     return parts[0] if len(parts) == 1 else jnp.concatenate(parts, axis=-1)
 
 
-def staged_total(grads):
-    index = lax.axis_index("shard")
-    core, side, level, rep = index % 2, (index // 2) % 2, index // 4, lax.axis_index("rep")
+def positions(grads):
+    index, rep = lax.axis_index("shard"), lax.axis_index("rep")
+    grads, index, rep = lax.optimization_barrier((grads, index, rep))
+    return grads, index % 2, (index // 2) % 2, index // 4, rep
+
+
+def across_cores(grads, core):
     rows = grads[0].shape[0] // 16
     parts = [grad.reshape(8, 2, rows, grad.shape[1]) for grad in grads]
     away = joined([pick(part, 1 - core, 1) for part in parts])
     held = joined([pick(part, core, 1) for part in parts])
-    width = held.shape[-1]
-    half = width // 2
-    held = add_low(held, swap(away, "shard", lambda i: i ^ 1))
-    held = held.reshape(4, 2, rows, width)
-    first = held[..., :half]
-    first = add_low(
-        pick(first, side, 1),
-        swap(pick(first, 1 - side, 1), "shard", lambda i: i ^ 2),
-    ).reshape(4, 2, rows // 2, half)
-    second = held[..., half:].reshape(4, 2, 2, rows // 2, width - half)
-    second = add_low(
-        pick(second, rep, 2),
-        swap(pick(second, 1 - rep, 2), "rep", lambda i: i ^ 1),
-    )
-    first = add_low(pick(first, rep, 1), swap(pick(first, 1 - rep, 1), "rep", lambda i: i ^ 1))
-    second = add_low(
-        pick(second, side, 1),
-        swap(pick(second, 1 - side, 1), "shard", lambda i: i ^ 2),
-    )
-    both = jnp.concatenate([first, second], axis=2)
+    return add_low(held, swap(away, "shard", lambda i: i ^ 1))
+
+
+def down_levels(both, level):
     total = pick(both, level, 0).astype(WIDE)
     for step in range(1, 4):
         total = total + swap(
             pick(both, (level + step) % 4, 0), "shard", lambda i: (i + 4 * step) % 16
         ).astype(WIDE)
-    own = total.astype(LOW)
+    return total.astype(LOW)
+
+
+def box_total(held, side, level, rep):
+    rows, width = held.shape[-2:]
+    held = held.reshape(4, 2, rows, width)
+    half = width // 2
+    first = held[..., :half]
+    second = held[..., half:].reshape(4, 2, 2, rows // 2, width - half)
+    second = add_low(
+        pick(second, rep, 2),
+        swap(pick(second, 1 - rep, 2), "rep", lambda i: i ^ 1),
+    )
+    first = add_low(
+        pick(first, side, 1),
+        swap(pick(first, 1 - side, 1), "shard", lambda i: i ^ 2),
+    ).reshape(4, 2, rows // 2, half)
+    first = add_low(pick(first, rep, 1), swap(pick(first, 1 - rep, 1), "rep", lambda i: i ^ 1))
+    second = add_low(
+        pick(second, side, 1),
+        swap(pick(second, 1 - side, 1), "shard", lambda i: i ^ 2),
+    )
+    own = down_levels(jnp.concatenate([first, second], axis=2), level)
     other = swap(own, "rep", lambda i: i ^ 1)
     low, high = jnp.where(rep == 0, own, other), jnp.where(rep == 0, other, own)
-    return jnp.concatenate([low, high], axis=0).astype(WIDE)
+    return jnp.concatenate([low, high], axis=0)
+
+
+def plane_total(grads):
+    if axis_length("shard") != 16:
+        return lax.psum_scatter(joined(grads), "shard", scatter_dimension=0, tiled=True)
+    grads, core, side, level, _ = positions(grads)
+    held = across_cores(grads, core)
+    held = held.reshape(4, 2, *held.shape[1:])
+    held = add_low(
+        pick(held, side, 1),
+        swap(pick(held, 1 - side, 1), "shard", lambda i: i ^ 2),
+    )
+    return down_levels(held, level)
+
+
+def rep_pair(own):
+    other = swap(own, "rep", lambda i: i ^ 1)
+    rep = lax.axis_index("rep")
+    return jnp.where(rep == 0, own, other), jnp.where(rep == 0, other, own)
 
 
 def summed_rows(grads):
     grads = [grad.astype(LOW) for grad in grads]
     widths = [grad.shape[1] for grad in grads]
     if axis_length("shard") == 16 and axis_length("rep") == 2:
-        whole = staged_total(grads)
+        grads, core, side, level, rep = positions(grads)
+        whole = box_total(across_cores(grads, core), side, level, rep)
     else:
         share = lax.psum_scatter(joined(grads), "shard", scatter_dimension=0, tiled=True)
         whole = lax.psum(share.astype(WIDE), "rep")
+    whole = whole.astype(WIDE)
     out, start = [], 0
     for width in widths:
         out.append(whole[:, start : start + width])
         start += width
     return out
+
+
+def summed_halves(grads):
+    width = sum(grad.shape[1] for grad in grads)
+    grad = joined([grad.astype(LOW) for grad in grads])
+    if axis_length("shard") == 16 and axis_length("rep") == 2:
+        grad, core, side, level, rep = positions(grad)
+        whole = box_total(grad.reshape(8, -1, width), side, level, rep)
+        rows = whole.shape[0] // 2
+        parts = whole.reshape(2, rows, width)
+        got = swap(pick(parts, 1 - core, 0), "shard", lambda i: i ^ 1)
+        return core_pair(pick(parts, core, 0), got, core, 1).astype(WIDE)
+    core = lax.axis_index("shard") % 2
+    grad = core_pair(grad, jnp.zeros_like(grad), core, 1)
+    share = lax.psum_scatter(grad, "shard", scatter_dimension=0, tiled=True)
+    return lax.psum(share.astype(WIDE), "rep")
 
 
 def summed_vectors(stack):
@@ -263,12 +311,13 @@
         grad_window_ref[1] = grad_values[...].astype(LOW)
 
 
-def attend_back(offsets, queries, window, out, logs, grads, reach):
-    rows, width = queries.shape
-    pairs, blocks, context = width // (2 * HD), rows // BLOCK, window.shape[1]
+def attend_back(offsets, queries, window, out, logs, grads, reach, begin, pairs):
+    rows = queries.shape[0]
+    width = pairs * 2 * HD
+    blocks, context = rows // BLOCK, window.shape[1]
     work = pairs * 2 * rows * (reach + 1) * BLOCK
-    row_block = pl.BlockSpec((BLOCK, 2 * HD), lambda p, b: (b, p))
-    window_block = pl.BlockSpec((2, context, 2 * HD), lambda p, b: (0, 0, p))
+    row_block = pl.BlockSpec((BLOCK, 2 * HD), lambda p, b: (b, p + begin))
+    window_block = pl.BlockSpec((2, context, 2 * HD), lambda p, b: (0, 0, p + begin))
     return pl.pallas_call(
         functools.partial(attend_back_kernel, reach),
         grid=(pairs, blocks),
@@ -277,13 +326,16 @@
             row_block,
             window_block,
             row_block,
-            pl.BlockSpec((1, 2, BLOCK), lambda p, b: (p, 0, b)),
+            pl.BlockSpec((1, 2, BLOCK), lambda p, b: (p + begin, 0, b)),
             row_block,
         ],
-        out_specs=[row_block, window_block],
+        out_specs=[
+            pl.BlockSpec((BLOCK, 2 * HD), lambda p, b: (b, p)),
+            pl.BlockSpec((2, context, 2 * HD), lambda p, b: (0, 0, p)),
+        ],
         out_shape=[
             jax.ShapeDtypeStruct((rows, width), LOW),
-            jax.ShapeDtypeStruct(window.shape, LOW),
+            jax.ShapeDtypeStruct((2, context, width), LOW),
         ],
         scratch_shapes=[
             pltpu.VMEM((context, 2 * HD), WIDE),
@@ -344,42 +396,56 @@
     )
     params = jnp.pad(params, ((0, 0), (0, 128 - params.shape[1])))
     split = [w[:, h : h + half_width] for h in (0, half_width) for w in (w_query, w_key, w_value)]
-    first_group = gather_rows(jnp.concatenate(split + [params], axis=1))
-    full_qkv = first_group[:, : 3 * model_width]
+    first_group = gather_rows(jnp.concatenate(split + [w_output, params], axis=1))
+    full_output = first_group[:, 3 * model_width : 4 * model_width]
     gain_one, bias_one, gain_two, bias_two, gain_three, bias_three = (
-        first_group[:, 3 * model_width + i].astype(WIDE) for i in range(6)
-    )
-    second_group = gather_rows(
-        jnp.concatenate([w_output, x_query, x_key, x_value, x_output], axis=1)
-    )
-    full_output, full_xquery, full_xkey, full_xvalue, full_xoutput = (
-        second_group[:, i * model_width : (i + 1) * model_width] for i in range(5)
-    )
-    full_up = gather_rows(w_up)
-    full_down = gather_rows(w_down)
+        first_group[:, 4 * model_width + i].astype(WIDE) for i in range(6)
+    )
+    full_part = lax.dynamic_slice_in_dim(
+        first_group, core * (3 * half_width), 3 * half_width, 1
+    )
+    second_group = gather_rows(jnp.concatenate([x_query, x_key, x_value, x_output], axis=1))
+    full_xquery, full_xkey, full_xvalue, full_xoutput = (
+        second_group[:, i * model_width : (i + 1) * model_width] for i in range(4)
+    )
+    rep_index = lax.axis_index("rep")
+    down_rows = w_down.shape[0]
+    chunk = down_rows // 4
+    some_up = pick(w_up.reshape(w_up.shape[0], shard_count, 2, 2, chunk), rep_index, 2)
+    some_up = jnp.transpose(some_up, (0, 2, 1, 3)).reshape(w_up.shape[0], -1)
+    some_down = pick(w_down.reshape(2, 2, chunk, model_width), rep_index, 0)
+    hidden_half = some_up.shape[1]
+    third_group = gather_rows(jnp.concatenate([some_up, some_down[0], some_down[1]], axis=1))
+    half_up = third_group[:, :hidden_half]
+    half_down = [
+        third_group[:, hidden_half + i * model_width : hidden_half + (i + 1) * model_width]
+        for i in range(2)
+    ]
+    upstream = jnp.concatenate([cotangent, swap(cotangent, "rep", lambda i: i ^ 1)], axis=0)
 
     offsets = core_pair(frame_offset, swap(frame_offset, BOTH, lambda i: i ^ 1), core, 0)[None, :]
     resid = hidden.astype(WIDE)
-    normed_one = (scaled_norm(resid, gain_one) + bias_one).astype(LOW)
-    projected = matmul(normed_one, full_qkv)
-    projected = projected.astype(LOW).reshape(tok_rows, 2, 3, half_width)
-    projected = jnp.transpose(projected, (1, 2, 0, 3))
-    got = swap(pick(projected, 1 - core, 0), BOTH, lambda i: i ^ 1)
-    chip_qkv = core_pair(pick(projected, core, 0), got, core, 1)
-    queries, own_unit = chip_qkv[0], chip_qkv[1:]
-    below = swap(own_unit, BOTH, lambda i: i + 4)
-    far = swap(own_unit[:, tok_rows:], BOTH, lambda i: i + 8 if i % 4 >= 2 else -1)
-    message = jnp.concatenate(
+    below = swap(hidden, BOTH, lambda i: i + 4)
+    far = swap(hidden, BOTH, lambda i: i + 8 if i % 4 == 3 else -1)
+    across = swap(jnp.where(side == 0, hidden, below), BOTH, lambda i: i ^ 2)
+    third = swap(jnp.where(side == 0, below, far), BOTH, lambda i: i ^ 2 if i % 2 == 1 else -1)
+    shards = jnp.stack([below, across, hidden, third])
+    partner = swap(shards, BOTH, lambda i: i ^ 1)
+    paired = core_pair(shards[:3], partner[:3], core, 1)
+    around = jnp.concatenate(
+        [jnp.where(core == 1, third, partner[3]), paired[0], paired[1], paired[2]], axis=0
+    )
+    chip_rows = 2 * tok_rows
+    halo_rows = tok_rows + 2 * chip_rows
+    around = around.astype(WIDE)
+    normed_around = (scaled_norm(around, gain_one) + bias_one).astype(LOW)
+    normed_chip = normed_around[halo_rows:]
+    queries = matmul(normed_chip, full_part[:, :half_width]).astype(LOW)
+    window = jnp.stack(
         [
-            jnp.where(side == 0, own_unit, below),
-            jnp.where(side == 0, below[:, tok_rows:], far),
-        ],
-        axis=1,
-    )
-    across = swap(message, BOTH, lambda i: i ^ 2)
-    chip_rows = 2 * tok_rows
-    window = jnp.concatenate(
-        [across[:, chip_rows:], below, across[:, :chip_rows], own_unit], axis=1
+            matmul(normed_around, full_part[:, half_width : 2 * half_width]).astype(LOW),
+            matmul(normed_around, full_part[:, 2 * half_width :]).astype(LOW),
+        ]
     )
     chip_mixed, logs = attend(offsets, queries, window, reach)
 
@@ -423,17 +489,40 @@
     )
     after_cross = after_self + matmul(cross_mix, full_xoutput)
     normed_three = (scaled_norm(after_cross, gain_three) + bias_three).astype(LOW)
-    pre_act = matmul(normed_three, full_up)
-    activ = exact_gelu(pre_act).astype(LOW)
-    grad_down = left_t(activ, cotangent)
-    (fin_down,) = summed_rows([grad_down])
-    block_out = (after_cross + matmul(activ, full_down)).astype(LOW)
-    grad_act = right_t(cotangent, full_down)
-    _, gelu_pull = jax.vjp(exact_gelu, pre_act)
-    grad_pre = gelu_pull(grad_act)[0].astype(LOW)
-    grad_up = left_t(normed_three, grad_pre)
-    (fin_up,) = summed_rows([grad_up])
-    grad_norm_three = right_t(grad_pre, full_up)
+    both_three = jnp.concatenate([normed_three, swap(normed_three, "rep", lambda i: i ^ 1)], axis=0)
+    pre_act = matmul(both_three, half_up)
+    activ, gelu_pull = jax.vjp(exact_gelu, pre_act)
+    activ = activ.astype(LOW)
+    slope = gelu_pull(jnp.ones_like(pre_act))[0]
+    activ, slope = lax.optimization_barrier((activ, slope))
+    grad_act = [right_t(upstream, part) for part in half_down]
+    grad_pre = (slope * jnp.concatenate(grad_act, axis=1)).astype(LOW)
+    grad_both = right_t(grad_pre, half_up)
+    grad_norm_three = grad_both[:tok_rows] + swap(
+        grad_both[tok_rows:].astype(LOW), "rep", lambda i: i ^ 1
+    ).astype(WIDE)
+    quarter = hidden_half // 2
+    grad_down = [
+        left_t(activ[:, i * quarter : (i + 1) * quarter], upstream).astype(LOW)
+        for i in range(2)
+    ]
+    grad_up = left_t(both_three, grad_pre).astype(LOW)
+    down_halves = rep_pair(plane_total(grad_down))
+    fin_down = jnp.concatenate(
+        [half[:, i * model_width : (i + 1) * model_width] for half in down_halves for i in range(2)],
+        axis=0,
+    ).astype(WIDE)
+    up_halves = rep_pair(plane_total([grad_up]))
+    fin_up = jnp.stack(
+        [half.reshape(w_up.shape[0], 2, shard_count, chunk) for half in up_halves], axis=1
+    )
+    fin_up = jnp.transpose(fin_up, (0, 3, 1, 2, 4)).reshape(w_up.shape).astype(WIDE)
+    mixed_both = matmul(activ[:, :quarter], half_down[0]) + matmul(activ[:, quarter:], half_down[1])
+    block_out = (
+        after_cross
+        + mixed_both[:tok_rows]
+        + swap(mixed_both[tok_rows:].astype(LOW), "rep", lambda i: i ^ 1).astype(WIDE)
+    ).astype(LOW)
     norm_three_part, grad_gain_three, grad_bias_three = norm_back(
         after_cross, gain_three, grad_norm_three
     )
@@ -494,31 +583,31 @@
         core,
         0,
     )
-    chip_dq, grad_window = attend_back(offsets, queries, window, chip_mixed, logs, chip_grad, reach)
-    far_part = grad_window[:, :tok_rows]
-    below_part = grad_window[:, tok_rows : tok_rows + chip_rows]
-    across_part = grad_window[:, tok_rows + chip_rows : tok_rows + 2 * chip_rows]
-    own_part = grad_window[:, tok_rows + 2 * chip_rows :]
-    back = swap(jnp.concatenate([across_part, far_part], axis=1), BOTH, lambda i: i ^ 2)
-    back_unit, back_half = back[:, :chip_rows], back[:, chip_rows:]
-    nothing = jnp.zeros_like(back_half)
-    low_half = jnp.concatenate([nothing, back_half], axis=1)
-    to_below = add_low(below_part, jnp.where(side == 0, low_half, back_unit))
-    own_sum = own_part.astype(WIDE) + jnp.where(side == 0, back_unit, jnp.zeros_like(back_unit))
-    own_sum = own_sum + swap(to_below, BOTH, lambda i: i - 4).astype(WIDE)
-    from_far = swap(back_half, BOTH, lambda i: i - 8 if i % 4 >= 2 else -1)
-    own_sum = own_sum + jnp.concatenate([nothing, from_far], axis=1).astype(WIDE)
-    chip_grads = jnp.concatenate([chip_dq[None], own_sum.astype(LOW)], axis=0)
-    mine = lax.dynamic_slice_in_dim(chip_grads, core * tok_rows, tok_rows, 1)
-    away = lax.dynamic_slice_in_dim(chip_grads, (1 - core) * tok_rows, tok_rows, 1)
-    got = swap(away, BOTH, lambda i: i ^ 1)
-    pieces = core_pair(mine, got, core, 0)
-    grad_qkv = jnp.concatenate([pieces[i] for i in range(6)], axis=1)
-    grad_weights = left_t(normed_one, grad_qkv)
-    (fin_qkv,) = summed_rows([grad_weights])
-    grad_norm_one = right_t(grad_qkv, full_qkv)
-    norm_one_part, grad_gain_one, grad_bias_one = norm_back(resid, gain_one, grad_norm_one)
-    grad_hidden = (grad_self_res + norm_one_part).astype(LOW)
+    pairs = head_count // 4
+    calls = 2 if pairs % 2 == 0 else 1
+    backs = []
+    for call in range(calls):
+        backs.append(
+            attend_back(
+                offsets,
+                queries,
+                window,
+                chip_mixed,
+                logs,
+                chip_grad,
+                reach,
+                call * pairs // calls,
+                pairs // calls,
+            )
+        )
+    chip_dq = jnp.concatenate([part[0] for part in backs], axis=1)
+    grad_window = jnp.concatenate([part[1] for part in backs], axis=2)
+    grad_weights = [
+        left_t(normed_chip, chip_dq),
+        left_t(normed_around, grad_window[0]),
+        left_t(normed_around, grad_window[1]),
+    ]
+    fin_qkv = summed_halves(grad_weights)
     fin_query, fin_key, fin_value = (
         jnp.concatenate(
             [
@@ -529,6 +618,30 @@
         )
         for i in range(3)
     )
+    grad_around = right_t(grad_window[0], full_part[:, half_width : 2 * half_width]) + right_t(
+        grad_window[1], full_part[:, 2 * half_width :]
+    )
+    grad_chip = grad_around[halo_rows:] + right_t(chip_dq, full_part[:, :half_width])
+    grad_halo = grad_around[:halo_rows].astype(LOW)
+    units = jnp.concatenate([grad_halo[tok_rows:], grad_chip.astype(LOW)], axis=0)
+    units = units.reshape(3, 2, tok_rows, model_width)
+    sent = jnp.concatenate([pick(units, 1 - core, 1), grad_halo[None, :tok_rows]], axis=0)
+    partner = swap(sent, BOTH, lambda i: i ^ 1)
+    sums = add_low(pick(units, core, 1), partner[:3])
+    low_sum = add_low(grad_halo[:tok_rows], partner[3])
+    back = swap(sums[1], BOTH, lambda i: i ^ 2).astype(WIDE)
+    back_half = swap(low_sum, BOTH, lambda i: i ^ 2 if i % 2 == 1 else -1)
+    to_below = (
+        sums[0].astype(WIDE) + jnp.where(side == 0, back_half.astype(WIDE), back)
+    ).astype(LOW)
+    grad_norm_one = (
+        sums[2].astype(WIDE)
+        + jnp.where(side == 0, back, 0.0)
+        + swap(to_below, BOTH, lambda i: i - 4).astype(WIDE)
+        + swap(back_half, BOTH, lambda i: i - 8 if i % 4 == 3 else -1).astype(WIDE)
+    )
+    norm_one_part, grad_gain_one, grad_bias_one = norm_back(resid, gain_one, grad_norm_one)
+    grad_hidden = (grad_self_res + norm_one_part).astype(LOW)
     vectors = summed_vectors(
         jnp.stack(
             [

time: 1350 us -> 1170 us (0.87)
  waiting for transfers between devices: 609 us -> 454 us
  starting transfers between devices: 194 us -> 148 us
  other arithmetic: 108 us -> 135 us
  matrix products: 181 us -> 207 us
  local copies, waits for them, and re-layouts: 149 us -> 126 us
    all_gather x4 -> x3, waiting for transfers between devices: 207 us -> 76.2 us  [gather_rows(): return lax.all_gather(array, 'shard', axis=0, tiled=True)]
    ppermute x52, starting transfers between devices: 193 us -> 148 us  [swap(): lax.ppermute(array, axis, [(i, j) for i, j in pairs if 0 <= j < length])]
    ppermute x52, waiting for transfers between devices: 401 us -> 378 us  [swap(): lax.ppermute(array, axis, [(i, j) for i, j in pairs if 0 <= j < length])]
    convert_element_type x11 -> x14, other arithmetic: 19.2 us -> 38.8 us  [the longest x1 11.3 us: on_device(): normed_around = (scaled_norm(around, gain_one) + bias_one).astype(LOW)]
    convert_element_type x21 -> x15, other arithmetic: 52.6 us -> 36.9 us  [add_low(): return (left.astype(WIDE) + right.astype(WIDE)).astype(LOW)]
    dot_general x8 -> x11, matrix products: 54.2 us -> 69.3 us  [matmul(): return jnp.dot(left, right, preferred_element_type=WIDE)]
    slice x11 -> x8, local copies, waits for them, and re-layouts: 28.6 us -> 13.9 us  [the longest x2 6.32 us: box_total(): second = held[..., half:].reshape(4, 2, 2, rows // 2, width - half)]
    dot_general x8 -> x11, matrix products: 45.2 us -> 52 us  [left_t(): lax.dot_general(left, right, (((0,), (0,)), ((), ())), preferred_element_...]
  transfers between devices with their start and end apart: 58 -> 57, of which waited for: 24 -> 27; matrix products, arithmetic and copies ran while one was open for 24% -> 33% of each run, Pallas kernels for 5% -> 6%
where the time goes in v2:
time: 1170 us; the launch traced here: 1160 us
  waiting for transfers between devices  454 us (39%)
  matrix products  207 us (18%)
  starting transfers between devices  148 us (13%)
  other arithmetic  135 us (12%)
  local copies, waits for them, and re-layouts  126 us (11%)
  Pallas kernels  73.5 us (6%)
  between operations  19.4 us (2%)
    ppermute x52, waiting for transfers between devices, swap(): lax.ppermute(array, axis, [(i, j) for i, j in pairs if 0 <= j < length])  378 us
    ppermute x52, starting transfers between devices, swap(): lax.ppermute(array, axis, [(i, j) for i, j in pairs if 0 <= j < length])  148 us
    all_gather x3, waiting for transfers between devices, gather_rows(): return lax.all_gather(array, 'shard', axis=0, tiled=True)  76.2 us
    dot_general x11, matrix products, right_t(): lax.dot_general(left, right, (((1,), (1,)), ((), ())), preferred_element_...  73 us
    dot_general x11, matrix products, matmul(): return jnp.dot(left, right, preferred_element_type=WIDE)  69.3 us
    dot_general x11, matrix products, left_t(): lax.dot_general(left, right, (((0,), (0,)), ((), ())), preferred_element_...  52 us
    pallas_call x2, Pallas kernels, attend_back(): pl.pallas_call(functools.partial(attend_back_kernel, reach), grid=(pairs,...  47.5 us
    convert_element_type x15, other arithmetic, add_low(): return (left.astype(WIDE) + right.astype(WIDE)).astype(LOW)  36.9 us
  transfers between devices with their start and end apart: 57, of which 27 were waited for; matrix products, arithmetic and copies ran while one was open for 33% of the time, Pallas kernels for 6%

profile of v2, /device:TPU:0, one launch (start us, length us, event | category | flops | bytes accessed | tf_op | source)
XLA Modules:
  0.0 1162.5 jit_solution(457710234545839383)
XLA Ops:
  17.2 5.0 collective-permute-start.1
  22.9 33.6 %collective-permute-done.1 = bf16[256,1536]{1,0:T(8,128)(2,1)S(1)} collective-permute-done((bf16[256,1536]{1,0:T(8,128)(2,1)S(1)}, bf16[256,1536]{1,0:T(8,128)(2,1)S(1)}, u32[]{:S(2)}, u32[]{:S(2)}) %collective-permute-start.1) | collective-permute-done | bytes 786464 | tf_op jit(solution)/shard_map/ppermute | solution.py:64
  59.5 25.5 %collective-permute-done.4 = bf16[256,1536]{1,0:T(8,128)(2,1)S(1)} collective-permute-done((bf16[256,1536]{1,0:T(8,128)(2,1)S(1)}, bf16[256,1536]{1,0:T(8,128)(2,1)S(1)}, u32[]{:S(2)}, u32[]{:S(2)}) %collective-permute-start.4) | collective-permute-done | bytes 786464 | tf_op jit(solution)/shard_map/ppermute | solution.py:64
  87.0 51.6 %collective-permute-start.5 = (bf16[4,256,1536]{2,1,0:T(8,128)(2,1)}, bf16[4,256,1536]{2,1,0:T(8,128)(2,1)}, u32[]{:S(2)}, u32[]{:S(2)}) collective-permute-start(bf16[4,256,1536]{2,1,0:T(8,128)(2,1)} %pad_maximum_fusion.6), channel_id=1, source_target_pairs={{0,1},{1,0},{2,3},{3,2},{4,5},{5,4},{6,7},{7,6},{8,9},{9,8},{10,11... | collective-permute-start | bytes 9437192 | tf_op jit(solution)/shard_map/ppermute | solution.py:64
  149.9 8.6 collective-permute-done.9
  166.2 9.2 fusion.3
  180.5 67.8 %all-gather.5.cloned.1.call-done = bf16[1536,6272]{1,0:T(8,128)(2,1)} async-done(((bf16[96,6272]{1,0:T(8,128)(2,1)}), bf16[1536,6272]{1,0:T(8,128)(2,1)}) %all-gather.5.cloned.1.call-update) | async-done | bytes 19267600 | tf_op jit(solution)/shard_map/all_gather | solution.py:72
  248.3 4.3 convert_reduce_fusion.3
  252.6 11.3 fusion.6
  263.9 5.8 fusion.118.query_ref
  269.7 6.7 fusion.63
  276.4 6.3 fusion.62
  285.6 26.0 %attend_forward.1 = (bf16[512,768]{1,0:T(8,128)(2,1)}, f32[6,2,512]{2,1,0:T(2,128)}) custom-call(s32[1,512]{1,0:T(1,128)} %broadcast_select_fusion.10.offset_ref, bf16[512,768]{1,0:T(8,128)(2,1)} %fusion.118.query_ref, bf16[2,1792,768]{2,1,0:T(8,128)(2,1)} %pad_maximum_fusion.3.window_ref), custom_call_target="tpu_custom_call" | custom-call | flops 9663676416 | bytes 3145728 | tf_op jit(solution)/shard_map/attend_forward/pallas_call | solution.py:232
  317.3 4.1 fusion.209
  332.6 4.1 fusion.211
  340.3 8.4 all-gather.9.cloned.1.call-done
  348.7 7.2 fusion.24
  355.9 6.8 fusion.28
  362.7 22.2 %multiply_add_fusion = (f32[512,3072]{1,0:T(8,128)S(1)}, f32[512,3072]{1,0:T(8,128)S(1)}, f32[512,3072]{1,0:T(8,128)}) fusion(bf16[1536,6144]{1,0:T(8,128)(2,1)} %all-gather.9.cloned.1.call-done, bf16[256,1536]{1,0:T(8,128)(2,1)} %collective-permute-done.7, bf16[256,1536]{1,0:T(8,128)(2,1)} %add_convert_fusion.3), kind=kOutput, calls=%fused_computation.30 | convolution fusion | flops 4941938688 | bytes 29884416 | tf_op jit(solution)/shard_map/dot_general | solution.py:36
  384.9 6.0 multiply_convert_fusion
  396.3 9.1 convolution_convert_fusion
  405.5 6.8 convolution_convert_fusion.2
  412.4 4.3 convolution_convert_fusion.1
  416.7 8.8 fusion.8
  428.0 4.5 fusion.26
  432.5 4.9 fusion.56
  440.6 4.8 dynamic-slice_bitcast_fusion
  445.4 6.8 dynamic-slice_bitcast_fusion.4
  457.6 5.8 collective-permute-done.8
  467.7 4.6 fusion.77
  489.5 4.7 multiply_reduce_fusion.2
  515.0 7.6 dynamic-slice_bitcast_fusion.10
  524.8 23.7 %attend_backward.2 = (bf16[512,384]{1,0:T(8,128)(2,1)}, bf16[2,1792,384]{2,1,0:T(8,128)(2,1)}) custom-call(s32[1,512]{1,0:T(1,128)} %broadcast_select_fusion.10.offset_ref, bf16[512,768]{1,0:T(8,128)(2,1)} %fusion.118.query_ref, bf16[2,1792,768]{2,1,0:T(8,128)(2,1)} %pad_maximum_fusion.3.window_ref, bf16[512,768]{1,0:T(8,128)(2,1)} %get-tuple-element.40.out_ref, ...), custom_call_target="tpu_custom_call" | custom-call | flops 12079595520 | bytes 3145728 | tf_op jit(solution)/shard_map/attend_backward/pallas_call | solution.py:321
  548.5 23.8 %attend_backward.3 = (bf16[512,384]{1,0:T(8,128)(2,1)}, bf16[2,1792,384]{2,1,0:T(8,128)(2,1)}) custom-call(s32[1,512]{1,0:T(1,128)} %broadcast_select_fusion.10.offset_ref, bf16[512,768]{1,0:T(8,128)(2,1)} %fusion.118.query_ref, bf16[2,1792,768]{2,1,0:T(8,128)(2,1)} %pad_maximum_fusion.3.window_ref, bf16[512,768]{1,0:T(8,128)(2,1)} %get-tuple-element.40.out_ref, ...), custom_call_target="tpu_custom_call" | custom-call | flops 12079595520 | bytes 3145728 | tf_op jit(solution)/shard_map/attend_backward/pallas_call | solution.py:321
  574.7 9.6 convolution_convert_fusion.7
  584.4 5.3 convolution_convert_fusion.8
  595.7 11.2 fusion.80
  606.9 10.4 fusion.212
  621.7 10.3 copy.100
  632.0 5.6 fusion.204
  646.7 4.2 fusion.64
  656.6 23.7 %collective-permute-done.22 = bf16[4,192,1152]{2,1,0:T(8,128)(2,1)} collective-permute-done((bf16[4,192,1152]{2,1,0:T(8,128)(2,1)}, bf16[4,192,1152]{2,1,0:T(8,128)(2,1)}, u32[]{:S(2)}, u32[]{:S(2)}) %collective-permute-start.22) | collective-permute-done | bytes 1769504 | tf_op jit(solution)/shard_map/ppermute | solution.py:64
  691.8 13.5 %collective-permute-done.23 = bf16[4,96,1152]{2,1,0:T(8,128)(2,1)} collective-permute-done((bf16[4,96,1152]{2,1,0:T(8,128)(2,1)}, bf16[4,96,1152]{2,1,0:T(8,128)(2,1)}, u32[]{:S(2)}, u32[]{:S(2)}) %collective-permute-start.23) | collective-permute-done | bytes 884768 | tf_op jit(solution)/shard_map/ppermute | solution.py:64
  720.6 5.9 collective-permute-done.28
  726.4 26.5 %collective-permute-done.27 = bf16[96,2304]{1,0:T(8,128)(2,1)} collective-permute-done((bf16[96,2304]{1,0:T(8,128)(2,1)S(1)}, bf16[96,2304]{1,0:T(8,128)(2,1)}, u32[]{:S(2)}, u32[]{:S(2)}) %collective-permute-start.27) | collective-permute-done | bytes 442400 | tf_op jit(solution)/shard_map/ppermute | solution.py:64
  769.0 5.7 fusion.7
  780.6 4.0 add_convert_fusion.1
  798.2 13.8 %collective-permute-done.15 = bf16[256,1536]{1,0:T(8,128)(2,1)} collective-permute-done((bf16[256,1536]{1,0:T(8,128)(2,1)}, bf16[256,1536]{1,0:T(8,128)(2,1)}, u32[]{:S(2)}, u32[]{:S(2)}) %collective-permute-start.15) | collective-permute-done | bytes 786464 | tf_op jit(solution)/shard_map/ppermute | solution.py:64
  819.2 18.7 %collective-permute-start.18 = (f32[6,1536]{1,0:T(8,128)S(1)}, f32[6,1536]{1,0:T(8,128)S(1)}, u32[]{:S(2)}, u32[]{:S(2)}) collective-permute-start(f32[6,1536]{1,0:T(8,128)S(1)} %add.571), channel_id=1, source_target_pairs={{0,2},{1,3},{2,0},{3,1},{4,6},{5,7},{6,4},{7,5},{8,10},{9,11},{10,... | collective-permute-start | bytes 110600 | tf_op jit(solution)/shard_map/ppermute | solution.py:64
  839.0 60.2 %collective-permute-done.18 = f32[6,1536]{1,0:T(8,128)S(1)} collective-permute-done((f32[6,1536]{1,0:T(8,128)S(1)}, f32[6,1536]{1,0:T(8,128)S(1)}, u32[]{:S(2)}, u32[]{:S(2)}) %collective-permute-start.18) | collective-permute-done | bytes 36896 | tf_op jit(solution)/shard_map/ppermute | solution.py:64
  925.7 10.1 collective-permute-done.44
  935.8 20.1 %collective-permute-start.49 = (bf16[96,3072]{1,0:T(8,128)(2,1)S(1)}, bf16[96,3072]{1,0:T(8,128)(2,1)S(1)}, u32[]{:S(2)}, u32[]{:S(2)}) collective-permute-start(bf16[96,3072]{1,0:T(8,128)(2,1)S(1)} %get-tuple-element.108), channel_id=1, source_target_pairs={{0,8},{1,9},{2,10},{3,11},{4,12},{5,13},{6,14},{7,15},{8,0},{9,1},... | collective-permute-start | bytes 1769480 | tf_op jit(solution)/shard_map/ppermute | solution.py:64
  955.9 34.1 %collective-permute-done.43 = bf16[96,3072]{1,0:T(8,128)(2,1)S(1)} collective-permute-done((bf16[96,3072]{1,0:T(8,128)(2,1)S(1)}, bf16[96,3072]{1,0:T(8,128)(2,1)S(1)}, u32[]{:S(2)}, u32[]{:S(2)}) %collective-permute-start.43) | collective-permute-done | bytes 589856 | tf_op jit(solution)/shard_map/ppermute | solution.py:64
  991.8 26.5 %collective-permute-done.49 = bf16[96,3072]{1,0:T(8,128)(2,1)S(1)} collective-permute-done((bf16[96,3072]{1,0:T(8,128)(2,1)S(1)}, bf16[96,3072]{1,0:T(8,128)(2,1)S(1)}, u32[]{:S(2)}, u32[]{:S(2)}) %collective-permute-start.49) | collective-permute-done | bytes 589856 | tf_op jit(solution)/shard_map/ppermute | solution.py:64
  1019.2 4.5 add_convert_fusion
  1027.4 7.6 collective-permute-done.51
  1037.0 24.6 %collective-permute-done.32 = bf16[4,96,2304]{2,1,0:T(8,128)(2,1)S(1)} collective-permute-done((bf16[4,96,2304]{2,1,0:T(8,128)(2,1)S(1)}, bf16[4,96,2304]{2,1,0:T(8,128)(2,1)S(1)}, u32[]{:S(2)}, u32[]{:S(2)}) %collective-permute-start.32) | collective-permute-done | bytes 1769504 | tf_op jit(solution)/shard_map/ppermute | solution.py:64
  1064.8 8.1 collective-permute-done.34
  1081.1 6.8 collective-permute-done.33
  1092.2 7.4 collective-permute-start.37
  1104.1 5.4 reshape.495
  1112.4 24.1 %collective-permute-done.37 = bf16[48,4608]{1,0:T(8,128)(2,1)} collective-permute-done((bf16[48,4608]{1,0:T(8,128)(2,1)}, bf16[48,4608]{1,0:T(8,128)(2,1)}, u32[]{:S(2)}, u32[]{:S(2)}) %collective-permute-start.37) | collective-permute-done | bytes 442400 | tf_op jit(solution)/shard_map/ppermute | solution.py:64
  1138.4 5.2 fusion.36
  1143.6 6.2 fusion.59
  (539 shorter events, 283.1 us)
Async XLA Ops:
  7.3 168.7 %all-gather.7.cloned.1.call-start = ((), (), s32[]{:S(2)}) async-start(), calls=%async_computation.2 | async-start | bytes 20054016 | tf_op jit(solution)/shard_map/all_gather | solution.py:72
  9.8 238.5 %all-gather.5.cloned.1.call-start = ((), (), s32[]{:S(2)}) async-start(), calls=%async_computation.1 | async-start | bytes 20471808 | tf_op jit(solution)/shard_map/all_gather | solution.py:72
  12.3 336.4 %all-gather.9.cloned.1.call-start = ((), (), s32[]{:S(2)}) async-start(), calls=%async_computation.3 | async-start | bytes 20054016 | tf_op jit(solution)/shard_map/all_gather | solution.py:72
  17.1 776.7 %reduce-scatter.2.cloned.1.call-start = ((), (), s32[]{:S(2)}) async-start(), calls=%async_computation.4 | async-start | bytes 3244032 | tf_op jit(solution)/shard_map/reduce_scatter | solution.py:565
  17.2 39.4 %collective-permute-start.1 = (bf16[256,1536]{1,0:T(8,128)(2,1)S(1)}, bf16[256,1536]{1,0:T(8,128)(2,1)S(1)}, u32[]{:S(2)}, u32[]{:S(2)}) collective-permute-start(bf16[256,1536]{1,0:T(8,128)(2,1)S(1)} %copy-done), channel_id=1, source_target_pairs={{0,4},{1,5},{2,6},{3,7},{4,8},{5,9},{6,10},{7,11},{8,12},{9,13},{1... | collective-permute-start | bytes 2359304 | tf_op jit(solution)/shard_map/ppermute | solution.py:64
  22.2 34.4 %collective-permute-start.2 = (bf16[256,1536]{1,0:T(8,128)(2,1)S(1)}, bf16[256,1536]{1,0:T(8,128)(2,1)S(1)}, u32[]{:S(2)}, u32[]{:S(2)}) collective-permute-start(bf16[256,1536]{1,0:T(8,128)(2,1)S(1)} %copy-done), channel_id=1, source_target_pairs={{3,11},{7,15},{11,19},{15,23},{19,27},{23,31}} | collective-permute-start | bytes 2359304 | tf_op jit(solution)/shard_map/ppermute | solution.py:64
  56.7 2.8 collective-permute-start.3
  57.6 27.4 %collective-permute-start.4 = (bf16[256,1536]{1,0:T(8,128)(2,1)S(1)}, bf16[256,1536]{1,0:T(8,128)(2,1)S(1)}, u32[]{:S(2)}, u32[]{:S(2)}) collective-permute-start(bf16[256,1536]{1,0:T(8,128)(2,1)S(1)} %get-tuple-element.148), channel_id=1, source_target_pairs={{0,2},{1,3},{2,0},{3,1},{4,6},{5,7},{6,4},{7,5},{8,10},{9,11},{10,... | collective-permute-start | bytes 2359304 | tf_op jit(solution)/shard_map/ppermute | solution.py:64
  85.0 53.5 %copy-start.113 = (s32[256]{0:T(256)S(1)}, s32[256]{0:T(256)}, u32[]{:S(2)}) copy-start(s32[256]{0:T(256)} %param.24) | copy-start | bytes 3076
  85.0 53.6 %copy-start.29 = (bf16[256,1536]{1,0:T(8,128)(2,1)S(1)}, bf16[256,1536]{1,0:T(8,128)(2,1)}, u32[]{:S(2)}) copy-start(bf16[256,1536]{1,0:T(8,128)(2,1)} %param.41) | copy-start | bytes 2359300
  85.0 53.6 %copy-start.112 = (s32[256]{0:T(256)S(1)}, s32[256]{0:T(256)}, u32[]{:S(2)}) copy-start(s32[256]{0:T(256)} %param.23) | copy-start | bytes 3076
  87.0 72.5 %collective-permute-start.5 = (bf16[4,256,1536]{2,1,0:T(8,128)(2,1)}, bf16[4,256,1536]{2,1,0:T(8,128)(2,1)}, u32[]{:S(2)}, u32[]{:S(2)}) collective-permute-start(bf16[4,256,1536]{2,1,0:T(8,128)(2,1)} %pad_maximum_fusion.6), channel_id=1, source_target_pairs={{0,1},{1,0},{2,3},{3,2},{4,5},{5,4},{6,7},{7,6},{8,9},{9,8},{10,11... | collective-permute-start | bytes 9437192 | tf_op jit(solution)/shard_map/ppermute | solution.py:64
  138.5 10.9 collective-permute-start
  138.6 19.9 %collective-permute-start.9 = (bf16[256,1536]{1,0:T(8,128)(2,1)S(1)}, bf16[256,1536]{1,0:T(8,128)(2,1)S(1)}, u32[]{:S(2)}, u32[]{:S(2)}) collective-permute-start(bf16[256,1536]{1,0:T(8,128)(2,1)S(1)} %copy-done.29), channel_id=1, source_target_pairs={{0,16},{16,0},{1,17},{17,1},{2,18},{18,2},{3,19},{19,3},{4,20},{20... | collective-permute-start | bytes 2359304 | tf_op jit(solution)/shard_map/ppermute | solution.py:64
  312.8 3.8 collective-permute-start.6
  338.9 23.8 %collective-permute-start.7 = (bf16[256,1536]{1,0:T(8,128)(2,1)}, bf16[256,1536]{1,0:T(8,128)(2,1)}, u32[]{:S(2)}, u32[]{:S(2)}) collective-permute-start(bf16[256,1536]{1,0:T(8,128)(2,1)} %add_convert_fusion.3), channel_id=1, source_target_pairs={{0,16},{16,0},{1,17},{17,1},{2,18},{18,2},{3,19},{19,3},{4,20},{20... | collective-permute-start | bytes 2359304 | tf_op jit(solution)/shard_map/ppermute | solution.py:64
  426.5 28.5 %collective-permute-start.10 = (bf16[256,1536]{1,0:T(8,128)(2,1)}, bf16[256,1536]{1,0:T(8,128)(2,1)}, u32[]{:S(2)}, u32[]{:S(2)}) collective-permute-start(bf16[256,1536]{1,0:T(8,128)(2,1)} %slice.483), channel_id=1, source_target_pairs={{0,16},{16,0},{1,17},{17,1},{2,18},{18,2},{3,19},{19,3},{4,20},{20... | collective-permute-start | bytes 2359304 | tf_op jit(solution)/shard_map/ppermute | solution.py:64
  440.1 23.3 %collective-permute-start.8 = (bf16[256,1536]{1,0:T(8,128)(2,1)}, bf16[256,1536]{1,0:T(8,128)(2,1)}, u32[]{:S(2)}, u32[]{:S(2)}) collective-permute-start(bf16[256,1536]{1,0:T(8,128)(2,1)} %slice.484), channel_id=1, source_target_pairs={{0,16},{16,0},{1,17},{17,1},{2,18},{18,2},{3,19},{19,3},{4,20},{20... | collective-permute-start | bytes 2359304 | tf_op jit(solution)/shard_map/ppermute | solution.py:64
  445.4 323.6 %collective-permute-start.40 = (bf16[8,96,3072]{2,1,0:T(8,128)(2,1)}, bf16[8,96,3072]{2,1,0:T(8,128)(2,1)}, u32[]{:S(2)}, u32[]{:S(2)}) collective-permute-start(bf16[8,96,3072]{2,1,0:T(8,128)(2,1)} %dynamic-slice_bitcast_fusion), channel_id=1, source_target_pairs={{0,1},{1,0},{2,3},{3,2},{4,5},{5,4},{6,7},{7,6},{8,9},{9,8},{10,11... | collective-permute-start | bytes 14155784 | tf_op jit(solution)/shard_map/ppermute | solution.py:64
  506.9 15.6 %collective-permute-start.11 = (bf16[256,768]{1,0:T(8,128)(2,1)}, bf16[256,768]{1,0:T(8,128)(2,1)}, u32[]{:S(2)}, u32[]{:S(2)}) collective-permute-start(bf16[256,768]{1,0:T(8,128)(2,1)} %bitcast.306), channel_id=1, source_target_pairs={{0,1},{1,0},{2,3},{3,2},{4,5},{5,4},{6,7},{7,6},{8,9},{9,8},{10,11... | collective-permute-start | bytes 1179656 | tf_op jit(solution)/shard_map/ppermute | solution.py:64
  513.1 625.3 %all-gather.11.cloned.1.call-start = ((), (), s32[]{:S(2)}) async-start(), calls=%async_computation.5 | async-start | bytes 3244032 | tf_op jit(solution)/shard_map/all_gather | solution.py:566
  639.1 41.3 %collective-permute-start.22 = (bf16[4,192,1152]{2,1,0:T(8,128)(2,1)}, bf16[4,192,1152]{2,1,0:T(8,128)(2,1)}, u32[]{:S(2)}, u32[]{:S(2)}) collective-permute-start(bf16[4,192,1152]{2,1,0:T(8,128)(2,1)} %dynamic-slice_bitcast_fusion.16), channel_id=1, source_target_pairs={{0,2},{1,3},{2,0},{3,1},{4,6},{5,7},{6,4},{7,5},{8,10},{9,11},{10,... | collective-permute-start | bytes 5308424 | tf_op jit(solution)/shard_map/ppermute | solution.py:64
  645.2 41.0 %collective-permute-start.24 = (bf16[4,2,96,1152]{3,2,0,1:T(8,128)(2,1)}, bf16[4,2,96,1152]{3,2,0,1:T(8,128)(2,1)}, u32[]{:S(2)}, u32[]{:S(2)}) collective-permute-start(bf16[4,2,96,1152]{3,2,0,1:T(8,128)(2,1)} %copy.102), channel_id=1, source_target_pairs={{0,16},{16,0},{1,17},{17,1},{2,18},{18,2},{3,19},{19,3},{4,20},{20... | collective-permute-start | bytes 5308424 | tf_op jit(solution)/shard_map/ppermute | solution.py:64
  654.6 35.3 %slice-start = ((s8[4718592]{0:T(1024)(128)(4,1)}), s8[524288]{0:T(1024)(128)(4,1)S(1)}, s32[]{:S(2)}) async-start(s8[4718592]{0:T(1024)(128)(4,1)} %bitcast.311), calls=%async_computation.6 | async-start | bytes 1048576
  656.6 99.8 %collective-permute-start.12 = (bf16[4,256,1536]{2,1,0:T(8,128)(2,1)}, bf16[4,256,1536]{2,1,0:T(8,128)(2,1)}, u32[]{:S(2)}, u32[]{:S(2)}) collective-permute-start(bf16[4,256,1536]{2,1,0:T(8,128)(2,1)} %pad_maximum_fusion.7), channel_id=1, source_target_pairs={{0,1},{1,0},{2,3},{3,2},{4,5},{5,4},{6,7},{7,6},{8,9},{9,8},{10,11... | collective-permute-start | bytes 9437192 | tf_op jit(solution)/shard_map/ppermute | solution.py:64
  656.6 33.4 %slice-start.1 = ((s8[4718592]{0:T(1024)(128)(4,1)}), s8[4194304]{0:T(1024)(128)(4,1)S(1)}, s32[]{:S(2)}) async-start(s8[4718592]{0:T(1024)(128)(4,1)} %bitcast.311), calls=%async_computation.7 | async-start | bytes 8388608
  683.9 21.5 %collective-permute-start.23 = (bf16[4,96,1152]{2,1,0:T(8,128)(2,1)}, bf16[4,96,1152]{2,1,0:T(8,128)(2,1)}, u32[]{:S(2)}, u32[]{:S(2)}) collective-permute-start(bf16[4,96,1152]{2,1,0:T(8,128)(2,1)} %dynamic-slice_bitcast_fusion.20), channel_id=1, source_target_pairs={{0,16},{16,0},{1,17},{17,1},{2,18},{18,2},{3,19},{19,3},{4,20},{20... | collective-permute-start | bytes 2654216 | tf_op jit(solution)/shard_map/ppermute | solution.py:64
  689.2 21.2 %collective-permute-start.25 = (bf16[4,96,1152]{2,1,0:T(8,128)(2,1)}, bf16[4,96,1152]{2,1,0:T(8,128)(2,1)}, u32[]{:S(2)}, u32[]{:S(2)}) collective-permute-start(bf16[4,96,1152]{2,1,0:T(8,128)(2,1)} %dynamic-slice_bitcast_fusion.19), channel_id=1, source_target_pairs={{0,2},{1,3},{2,0},{3,1},{4,6},{5,7},{6,4},{7,5},{8,10},{9,11},{10,... | collective-permute-start | bytes 2654216 | tf_op jit(solution)/shard_map/ppermute | solution.py:64
  712.8 13.6 %collective-permute-start.28 = (bf16[96,2304]{1,0:T(8,128)(2,1)}, bf16[96,2304]{1,0:T(8,128)(2,1)}, u32[]{:S(2)}, u32[]{:S(2)}) collective-permute-start(bf16[96,2304]{1,0:T(8,128)(2,1)} %get-tuple-element.126), channel_id=1, source_target_pairs={{0,12},{1,13},{2,14},{3,15},{4,0},{5,1},{6,2},{7,3},{8,4},{9,5},{1... | collective-permute-start | bytes 1327112 | tf_op jit(solution)/shard_map/ppermute | solution.py:64
  715.5 37.4 %collective-permute-start.27 = (bf16[96,2304]{1,0:T(8,128)(2,1)S(1)}, bf16[96,2304]{1,0:T(8,128)(2,1)}, u32[]{:S(2)}, u32[]{:S(2)}) collective-permute-start(bf16[96,2304]{1,0:T(8,128)(2,1)S(1)} %get-tuple-element.125), channel_id=1, source_target_pairs={{0,8},{1,9},{2,10},{3,11},{4,12},{5,13},{6,14},{7,15},{8,0},{9,1},... | collective-permute-start | bytes 1327112 | tf_op jit(solution)/shard_map/ppermute | solution.py:64
  715.8 37.2 %collective-permute-start.26 = (bf16[96,2304]{1,0:T(8,128)(2,1)S(1)}, bf16[96,2304]{1,0:T(8,128)(2,1)}, u32[]{:S(2)}, u32[]{:S(2)}) collective-permute-start(bf16[96,2304]{1,0:T(8,128)(2,1)S(1)} %get-tuple-element.124), channel_id=1, source_target_pairs={{0,4},{1,5},{2,6},{3,7},{4,8},{5,9},{6,10},{7,11},{8,12},{9,13},{1... | collective-permute-start | bytes 1327112 | tf_op jit(solution)/shard_map/ppermute | solution.py:64
  726.4 49.9 %collective-permute-start.46 = (bf16[8,96,3072]{2,1,0:T(8,128)(2,1)}, bf16[8,96,3072]{2,1,0:T(8,128)(2,1)S(1)}, u32[]{:S(2)}, u32[]{:S(2)}) collective-permute-start(bf16[8,96,3072]{2,1,0:T(8,128)(2,1)} %pad_maximum_fusion.5), channel_id=1, source_target_pairs={{0,1},{1,0},{2,3},{3,2},{4,5},{5,4},{6,7},{7,6},{8,9},{9,8},{10,11... | collective-permute-start | bytes 14155784 | tf_op jit(solution)/shard_map/ppermute | solution.py:64
  753.0 266.2 %collective-permute-start.31 = (bf16[8,96,4608]{2,1,0:T(8,128)(2,1)}, bf16[8,96,4608]{2,1,0:T(8,128)(2,1)}, u32[]{:S(2)}, u32[]{:S(2)}) collective-permute-start(bf16[8,96,4608]{2,1,0:T(8,128)(2,1)} %pad_maximum_fusion.1), channel_id=1, source_target_pairs={{0,1},{1,0},{2,3},{3,2},{4,5},{5,4},{6,7},{7,6},{8,9},{9,8},{10,11... | collective-permute-start | bytes 21233672 | tf_op jit(solution)/shard_map/ppermute | solution.py:64
  754.6 12.6 %collective-permute-start.29 = (bf16[96,2304]{1,0:T(8,128)(2,1)S(1)}, bf16[96,2304]{1,0:T(8,128)(2,1)S(1)}, u32[]{:S(2)}, u32[]{:S(2)}) collective-permute-start(bf16[96,2304]{1,0:T(8,128)(2,1)S(1)} %fusion.147), channel_id=1, source_target_pairs={{0,16},{16,0},{1,17},{17,1},{2,18},{18,2},{3,19},{19,3},{4,20},{20... | collective-permute-start | bytes 1327112 | tf_op jit(solution)/shard_map/ppermute | solution.py:64
  758.8 25.8 %collective-permute-start.14 = (bf16[256,1536]{1,0:T(8,128)(2,1)}, bf16[256,1536]{1,0:T(8,128)(2,1)}, u32[]{:S(2)}, u32[]{:S(2)}) collective-permute-start(bf16[256,1536]{1,0:T(8,128)(2,1)} %fusion.114), channel_id=1, source_target_pairs={{1,3},{3,1},{5,7},{7,5},{9,11},{11,9},{13,15},{15,13},{17,19},{19,... | collective-permute-start | bytes 2359304 | tf_op jit(solution)/shard_map/ppermute | solution.py:64
  767.2 20.6 %collective-permute-start.13 = (bf16[256,1536]{1,0:T(8,128)(2,1)}, bf16[256,1536]{1,0:T(8,128)(2,1)S(1)}, u32[]{:S(2)}, u32[]{:S(2)}) collective-permute-start(bf16[256,1536]{1,0:T(8,128)(2,1)} %slice_bitcast_fusion.11), channel_id=1, source_target_pairs={{0,2},{1,3},{2,0},{3,1},{4,6},{5,7},{6,4},{7,5},{8,10},{9,11},{10,... | collective-permute-start | bytes 2359304 | tf_op jit(solution)/shard_map/ppermute | solution.py:64
  769.0 24.8 %collective-permute-start.30 = (bf16[96,2304]{1,0:T(8,128)(2,1)}, bf16[96,2304]{1,0:T(8,128)(2,1)}, u32[]{:S(2)}, u32[]{:S(2)}) collective-permute-start(bf16[96,2304]{1,0:T(8,128)(2,1)} %get-tuple-element.141), channel_id=1, source_target_pairs={{0,1},{1,0},{2,3},{3,2},{4,5},{5,4},{6,7},{7,6},{8,9},{9,8},{10,11... | collective-permute-start | bytes 1327112 | tf_op jit(solution)/shard_map/ppermute | solution.py:64
  776.4 137.4 %collective-permute-start.41 = (bf16[4,96,3072]{2,1,0:T(8,128)(2,1)}, bf16[4,96,3072]{2,1,0:T(8,128)(2,1)}, u32[]{:S(2)}, u32[]{:S(2)}) collective-permute-start(bf16[4,96,3072]{2,1,0:T(8,128)(2,1)} %dynamic-slice_bitcast_fusion.6), channel_id=1, source_target_pairs={{0,2},{1,3},{2,0},{3,1},{4,6},{5,7},{6,4},{7,5},{8,10},{9,11},{10,... | collective-permute-start | bytes 7077896 | tf_op jit(solution)/shard_map/ppermute | solution.py:64
  790.2 21.9 %collective-permute-start.15 = (bf16[256,1536]{1,0:T(8,128)(2,1)}, bf16[256,1536]{1,0:T(8,128)(2,1)}, u32[]{:S(2)}, u32[]{:S(2)}) collective-permute-start(bf16[256,1536]{1,0:T(8,128)(2,1)} %fusion.107), channel_id=1, source_target_pairs={{4,0},{5,1},{6,2},{7,3},{8,4},{9,5},{10,6},{11,7},{12,8},{13,9},{1... | collective-permute-start | bytes 2359304 | tf_op jit(solution)/shard_map/ppermute | solution.py:64
  791.5 5.9 collective-permute-start.16
  793.9 127.1 %collective-permute-start.47 = (bf16[4,96,3072]{2,1,0:T(8,128)(2,1)}, bf16[4,96,3072]{2,1,0:T(8,128)(2,1)}, u32[]{:S(2)}, u32[]{:S(2)}) collective-permute-start(bf16[4,96,3072]{2,1,0:T(8,128)(2,1)} %dynamic-slice_bitcast_fusion.1), channel_id=1, source_target_pairs={{0,2},{1,3},{2,0},{3,1},{4,6},{5,7},{6,4},{7,5},{8,10},{9,11},{10,... | collective-permute-start | bytes 7077896 | tf_op jit(solution)/shard_map/ppermute | solution.py:64
  815.4 3.8 collective-permute-start.17
  819.2 90.7 %copy-start.36 = (f32[256,1536]{1,0:T(8,128)S(1)}, f32[256,1536]{1,0:T(8,128)}, u32[]{:S(2)}) copy-start(f32[256,1536]{1,0:T(8,128)} %copy-done.35) | copy-start | bytes 4718596
  819.2 80.0 %collective-permute-start.18 = (f32[6,1536]{1,0:T(8,128)S(1)}, f32[6,1536]{1,0:T(8,128)S(1)}, u32[]{:S(2)}, u32[]{:S(2)}) collective-permute-start(f32[6,1536]{1,0:T(8,128)S(1)} %add.571), channel_id=1, source_target_pairs={{0,2},{1,3},{2,0},{3,1},{4,6},{5,7},{6,4},{7,5},{8,10},{9,11},{10,... | collective-permute-start | bytes 110600 | tf_op jit(solution)/shard_map/ppermute | solution.py:64
  899.2 4.6 collective-permute-start.19
  903.8 5.2 collective-permute-start.20
  909.0 4.2 collective-permute-start.21
  917.3 18.5 %collective-permute-start.44 = (bf16[96,3072]{1,0:T(8,128)(2,1)S(1)}, bf16[96,3072]{1,0:T(8,128)(2,1)S(1)}, u32[]{:S(2)}, u32[]{:S(2)}) collective-permute-start(bf16[96,3072]{1,0:T(8,128)(2,1)S(1)} %get-tuple-element.110), channel_id=1, source_target_pairs={{0,12},{1,13},{2,14},{3,15},{4,0},{5,1},{6,2},{7,3},{8,4},{9,5},{1... | collective-permute-start | bytes 1769480 | tf_op jit(solution)/shard_map/ppermute | solution.py:64
  919.1 70.9 %collective-permute-start.43 = (bf16[96,3072]{1,0:T(8,128)(2,1)S(1)}, bf16[96,3072]{1,0:T(8,128)(2,1)S(1)}, u32[]{:S(2)}, u32[]{:S(2)}) collective-permute-start(bf16[96,3072]{1,0:T(8,128)(2,1)S(1)} %get-tuple-element.111), channel_id=1, source_target_pairs={{0,8},{1,9},{2,10},{3,11},{4,12},{5,13},{6,14},{7,15},{8,0},{9,1},... | collective-permute-start | bytes 1769480 | tf_op jit(solution)/shard_map/ppermute | solution.py:64
  919.1 71.1 %collective-permute-start.42 = (bf16[96,3072]{1,0:T(8,128)(2,1)S(1)}, bf16[96,3072]{1,0:T(8,128)(2,1)S(1)}, u32[]{:S(2)}, u32[]{:S(2)}) collective-permute-start(bf16[96,3072]{1,0:T(8,128)(2,1)S(1)} %get-tuple-element.109), channel_id=1, source_target_pairs={{0,4},{1,5},{2,6},{3,7},{4,8},{5,9},{6,10},{7,11},{8,12},{9,13},{1... | collective-permute-start | bytes 1769480 | tf_op jit(solution)/shard_map/ppermute | solution.py:64
  923.5 95.7 %copy-start.19 = (bf16[8,96,1536]{2,1,0:T(8,128)(2,1)S(1)}, bf16[8,96,1536]{2,1,0:T(8,128)(2,1)}, u32[]{:S(2)}) copy-start(bf16[8,96,1536]{2,1,0:T(8,128)(2,1)} %get-tuple-element.93) | copy-start | bytes 7077892
  923.7 68.2 %collective-permute-start.50 = (bf16[96,3072]{1,0:T(8,128)(2,1)S(1)}, bf16[96,3072]{1,0:T(8,128)(2,1)S(1)}, u32[]{:S(2)}, u32[]{:S(2)}) collective-permute-start(bf16[96,3072]{1,0:T(8,128)(2,1)S(1)} %get-tuple-element.107), channel_id=1, source_target_pairs={{0,12},{1,13},{2,14},{3,15},{4,0},{5,1},{6,2},{7,3},{8,4},{9,5},{1... | collective-permute-start | bytes 1769480 | tf_op jit(solution)/shard_map/ppermute | solution.py:64
  935.8 82.6 %collective-permute-start.49 = (bf16[96,3072]{1,0:T(8,128)(2,1)S(1)}, bf16[96,3072]{1,0:T(8,128)(2,1)S(1)}, u32[]{:S(2)}, u32[]{:S(2)}) collective-permute-start(bf16[96,3072]{1,0:T(8,128)(2,1)S(1)} %get-tuple-element.108), channel_id=1, source_target_pairs={{0,8},{1,9},{2,10},{3,11},{4,12},{5,13},{6,14},{7,15},{8,0},{9,1},... | collective-permute-start | bytes 1769480 | tf_op jit(solution)/shard_map/ppermute | solution.py:64
  990.0 28.4 %collective-permute-start.48 = (bf16[96,3072]{1,0:T(8,128)(2,1)S(1)}, bf16[96,3072]{1,0:T(8,128)(2,1)S(1)}, u32[]{:S(2)}, u32[]{:S(2)}) collective-permute-start(bf16[96,3072]{1,0:T(8,128)(2,1)S(1)} %get-tuple-element.106), channel_id=1, source_target_pairs={{0,4},{1,5},{2,6},{3,7},{4,8},{5,9},{6,10},{7,11},{8,12},{9,13},{1... | collective-permute-start | bytes 1769480 | tf_op jit(solution)/shard_map/ppermute | solution.py:64
  990.6 45.4 %collective-permute-start.45 = (bf16[96,3072]{1,0:T(8,128)(2,1)S(1)}, bf16[96,3072]{1,0:T(8,128)(2,1)S(1)}, u32[]{:S(2)}, u32[]{:S(2)}) collective-permute-start(bf16[96,3072]{1,0:T(8,128)(2,1)S(1)} %fusion.139), channel_id=1, source_target_pairs={{0,16},{16,0},{1,17},{17,1},{2,18},{18,2},{3,19},{19,3},{4,20},{20... | collective-permute-start | bytes 1769480 | tf_op jit(solution)/shard_map/ppermute | solution.py:64
  1018.7 16.3 %collective-permute-start.51 = (bf16[96,3072]{1,0:T(8,128)(2,1)S(1)}, bf16[96,3072]{1,0:T(8,128)(2,1)S(1)}, u32[]{:S(2)}, u32[]{:S(2)}) collective-permute-start(bf16[96,3072]{1,0:T(8,128)(2,1)S(1)} %fusion.136), channel_id=1, source_target_pairs={{0,16},{16,0},{1,17},{17,1},{2,18},{18,2},{3,19},{19,3},{4,20},{20... | collective-permute-start | bytes 1769480 | tf_op jit(solution)/shard_map/ppermute | solution.py:64
  1024.6 37.1 %collective-permute-start.32 = (bf16[4,96,2304]{2,1,0:T(8,128)(2,1)S(1)}, bf16[4,96,2304]{2,1,0:T(8,128)(2,1)S(1)}, u32[]{:S(2)}, u32[]{:S(2)}) collective-permute-start(bf16[4,96,2304]{2,1,0:T(8,128)(2,1)S(1)} %dynamic-slice_bitcast_fusion.14), channel_id=1, source_target_pairs={{0,2},{1,3},{2,0},{3,1},{4,6},{5,7},{6,4},{7,5},{8,10},{9,11},{10,... | collective-permute-start | bytes 5308424 | tf_op jit(solution)/shard_map/ppermute | solution.py:64
  1025.6 47.3 %collective-permute-start.34 = (bf16[4,2,48,2304]{3,2,0,1:T(8,128)(2,1)S(1)}, bf16[4,2,48,2304]{3,2,0,1:T(8,128)(2,1)S(1)}, u32[]{:S(2)}, u32[]{:S(2)}) collective-permute-start(bf16[4,2,48,2304]{3,2,0,1:T(8,128)(2,1)S(1)} %bitcast.352), channel_id=1, source_target_pairs={{0,16},{16,0},{1,17},{17,1},{2,18},{18,2},{3,19},{19,3},{4,20},{20... | collective-permute-start | bytes 5308424 | tf_op jit(solution)/shard_map/ppermute | solution.py:64
  1063.1 24.8 %collective-permute-start.33 = (bf16[4,48,2304]{2,1,0:T(8,128)(2,1)}, bf16[4,48,2304]{2,1,0:T(8,128)(2,1)}, u32[]{:S(2)}, u32[]{:S(2)}) collective-permute-start(bf16[4,48,2304]{2,1,0:T(8,128)(2,1)} %dynamic-slice_bitcast_fusion.18), channel_id=1, source_target_pairs={{0,16},{16,0},{1,17},{17,1},{2,18},{18,2},{3,19},{19,3},{4,20},{20... | collective-permute-start | bytes 2654216 | tf_op jit(solution)/shard_map/ppermute | solution.py:64
  1074.3 15.0 %collective-permute-start.35 = (bf16[4,48,2304]{2,1,0:T(8,128)(2,1)}, bf16[4,48,2304]{2,1,0:T(8,128)(2,1)}, u32[]{:S(2)}, u32[]{:S(2)}) collective-permute-start(bf16[4,48,2304]{2,1,0:T(8,128)(2,1)} %dynamic-slice_bitcast_fusion.17), channel_id=1, source_target_pairs={{0,2},{1,3},{2,0},{3,1},{4,6},{5,7},{6,4},{7,5},{8,10},{9,11},{10,... | collective-permute-start | bytes 2654216 | tf_op jit(solution)/shard_map/ppermute | solution.py:64
  1092.2 20.2 %collective-permute-start.38 = (bf16[48,4608]{1,0:T(8,128)(2,1)}, bf16[48,4608]{1,0:T(8,128)(2,1)}, u32[]{:S(2)}, u32[]{:S(2)}) collective-permute-start(bf16[48,4608]{1,0:T(8,128)(2,1)} %get-tuple-element.117), channel_id=1, source_target_pairs={{0,12},{1,13},{2,14},{3,15},{4,0},{5,1},{6,2},{7,3},{8,4},{9,5},{1... | collective-permute-start | bytes 1327112 | tf_op jit(solution)/shard_map/ppermute | solution.py:64
  1092.2 44.3 %collective-permute-start.37 = (bf16[48,4608]{1,0:T(8,128)(2,1)}, bf16[48,4608]{1,0:T(8,128)(2,1)}, u32[]{:S(2)}, u32[]{:S(2)}) collective-permute-start(bf16[48,4608]{1,0:T(8,128)(2,1)} %get-tuple-element.116), channel_id=1, source_target_pairs={{0,8},{1,9},{2,10},{3,11},{4,12},{5,13},{6,14},{7,15},{8,0},{9,1},... | collective-permute-start | bytes 1327112 | tf_op jit(solution)/shard_map/ppermute | solution.py:64
  1099.6 36.9 %collective-permute-start.36 = (bf16[48,4608]{1,0:T(8,128)(2,1)}, bf16[48,4608]{1,0:T(8,128)(2,1)}, u32[]{:S(2)}, u32[]{:S(2)}) collective-permute-start(bf16[48,4608]{1,0:T(8,128)(2,1)} %get-tuple-element.115), channel_id=1, source_target_pairs={{0,4},{1,5},{2,6},{3,7},{4,8},{5,9},{6,10},{7,11},{8,12},{9,13},{1... | collective-permute-start | bytes 1327112 | tf_op jit(solution)/shard_map/ppermute | solution.py:64
  1138.0 16.2 %collective-permute-start.39 = (bf16[48,4608]{1,0:T(8,128)(2,1)S(1)}, bf16[48,4608]{1,0:T(8,128)(2,1)S(1)}, u32[]{:S(2)}, u32[]{:S(2)}) collective-permute-start(bf16[48,4608]{1,0:T(8,128)(2,1)S(1)} %fusion.144), channel_id=1, source_target_pairs={{0,16},{16,0},{1,17},{17,1},{2,18},{18,2},{3,19},{19,3},{4,20},{20... | collective-permute-start | bytes 1327112 | tf_op jit(solution)/shard_map/ppermute | solution.py:64
  (123 other events, 837.5 us)
Sparse Core Ops, SparseCore 0:
  9.9 139.8 all-gather.6
  151.4 96.8 all-gather.4
  249.9 98.7 all-gather.8
  513.2 102.2 reduce-scatter.1
  794.0 75.9 all-gather.10

commit v3 on v2

--- a/solution.py
+++ b/solution.py
@@ -91,28 +91,28 @@
 
 
 def down_levels(both, level):
-    total = pick(both, level, 0).astype(WIDE)
+    axis = both.ndim - 3
+    total = pick(both, level, axis).astype(WIDE)
     for step in range(1, 4):
         total = total + swap(
-            pick(both, (level + step) % 4, 0), "shard", lambda i: (i + 4 * step) % 16
+            pick(both, (level + step) % 4, axis), "shard", lambda i: (i + 4 * step) % 16
         ).astype(WIDE)
     return total.astype(LOW)
 
 
-def box_total(held, side, level, rep):
-    rows, width = held.shape[-2:]
-    held = held.reshape(4, 2, rows, width)
-    half = width // 2
-    first = held[..., :half]
-    second = held[..., half:].reshape(4, 2, 2, rows // 2, width - half)
+def box_total(firsts, seconds, side, level, rep):
+    rows = firsts[0].shape[-2]
+    firsts = [part.reshape(4, 2, *part.shape[-2:]) for part in firsts]
+    seconds = [part.reshape(4, 2, 2, rows // 2, part.shape[-1]) for part in seconds]
     second = add_low(
-        pick(second, rep, 2),
-        swap(pick(second, 1 - rep, 2), "rep", lambda i: i ^ 1),
+        joined([pick(part, rep, 2) for part in seconds]),
+        swap(joined([pick(part, 1 - rep, 2) for part in seconds]), "rep", lambda i: i ^ 1),
     )
     first = add_low(
-        pick(first, side, 1),
-        swap(pick(first, 1 - side, 1), "shard", lambda i: i ^ 2),
-    ).reshape(4, 2, rows // 2, half)
+        joined([pick(part, side, 1) for part in firsts]),
+        swap(joined([pick(part, 1 - side, 1) for part in firsts]), "shard", lambda i: i ^ 2),
+    )
+    first = first.reshape(4, 2, rows // 2, first.shape[-1])
     first = add_low(pick(first, rep, 1), swap(pick(first, 1 - rep, 1), "rep", lambda i: i ^ 1))
     second = add_low(
         pick(second, side, 1),
@@ -124,15 +124,19 @@
     return jnp.concatenate([low, high], axis=0)
 
 
-def plane_total(grads):
+def plane_total(grad):
     if axis_length("shard") != 16:
-        return lax.psum_scatter(joined(grads), "shard", scatter_dimension=0, tiled=True)
-    grads, core, side, level, _ = positions(grads)
-    held = across_cores(grads, core)
-    held = held.reshape(4, 2, *held.shape[1:])
+        return lax.psum_scatter(grad, "shard", scatter_dimension=1, tiled=True)
+    grad, core, side, level, _ = positions(grad)
+    count, rows, width = grad.shape[0], grad.shape[1] // 16, grad.shape[2]
+    parts = grad.reshape(count, 8, 2, rows, width)
     held = add_low(
-        pick(held, side, 1),
-        swap(pick(held, 1 - side, 1), "shard", lambda i: i ^ 2),
+        pick(parts, core, 2),
+        swap(pick(parts, 1 - core, 2), "shard", lambda i: i ^ 1),
+    ).reshape(count, 4, 2, rows, width)
+    held = add_low(
+        pick(held, side, 2),
+        swap(pick(held, 1 - side, 2), "shard", lambda i: i ^ 2),
     )
     return down_levels(held, level)
 
@@ -148,7 +152,9 @@
     widths = [grad.shape[1] for grad in grads]
     if axis_length("shard") == 16 and axis_length("rep") == 2:
         grads, core, side, level, rep = positions(grads)
-        whole = box_total(across_cores(grads, core), side, level, rep)
+        held = across_cores(grads, core)
+        half = held.shape[-1] // 2
+        whole = box_total([held[..., :half]], [held[..., half:]], side, level, rep)
     else:
         share = lax.psum_scatter(joined(grads), "shard", scatter_dimension=0, tiled=True)
         whole = lax.psum(share.astype(WIDE), "rep")
@@ -160,28 +166,26 @@
     return out
 
 
-def summed_halves(grads):
-    width = sum(grad.shape[1] for grad in grads)
-    grad = joined([grad.astype(LOW) for grad in grads])
+def summed_halves(wide, narrow):
+    wide, narrow = wide.astype(LOW), narrow.astype(LOW)
+    width = wide.shape[1] + narrow.shape[1]
     if axis_length("shard") == 16 and axis_length("rep") == 2:
-        grad, core, side, level, rep = positions(grad)
-        whole = box_total(grad.reshape(8, -1, width), side, level, rep)
-        rows = whole.shape[0] // 2
-        parts = whole.reshape(2, rows, width)
+        (wide, narrow), core, side, level, rep = positions((wide, narrow))
+        wide, narrow = (part.reshape(8, -1, part.shape[1]) for part in (wide, narrow))
+        half = width // 2
+        whole = box_total([wide[..., :half]], [wide[..., half:], narrow], side, level, rep)
+        parts = whole.reshape(2, -1, width)
         got = swap(pick(parts, 1 - core, 0), "shard", lambda i: i ^ 1)
         return core_pair(pick(parts, core, 0), got, core, 1).astype(WIDE)
     core = lax.axis_index("shard") % 2
+    grad = joined([wide, narrow])
     grad = core_pair(grad, jnp.zeros_like(grad), core, 1)
     share = lax.psum_scatter(grad, "shard", scatter_dimension=0, tiled=True)
     return lax.psum(share.astype(WIDE), "rep")
 
 
 def summed_vectors(stack):
-    if axis_length("shard") != 16 or axis_length("rep") != 2:
-        return lax.psum(stack, BOTH)
-    for bit in (1, 2, 4, 8):
-        stack = stack + swap(stack, "shard", lambda i: i ^ bit)
-    return stack + swap(stack, "rep", lambda i: i ^ 1)
+    return jnp.sum(lax.all_gather(stack, BOTH), axis=0)
 
 
 def head_lanes(which):
@@ -209,7 +213,7 @@
         peak = jnp.full((1, BLOCK), NEGATIVE, WIDE)
         for step in range(reach + 1):
             rows = pl.ds(pl.multiple_of(start + step * BLOCK, BLOCK), BLOCK)
-            scores = right_t(window_ref[0, rows, :], query)
+            scores = right_t(window_ref[rows, : 2 * HD], query)
             scores = jnp.where(open_pairs(offsets, step, reach), scores, NEGATIVE)
             held[head, step] = scores
             peak = jnp.maximum(peak, jnp.max(scores, axis=0, keepdims=True))
@@ -219,7 +223,7 @@
             rows = pl.ds(pl.multiple_of(start + step * BLOCK, BLOCK), BLOCK)
             expo = jnp.exp(held[head, step] - peak)
             total = total + jnp.sum(expo, axis=0, keepdims=True)
-            blend = blend + left_t(window_ref[1, rows, :], expo.astype(LOW))
+            blend = blend + left_t(window_ref[rows, 2 * HD :], expo.astype(LOW))
         mixed.append((blend / total)[head * HD : (head + 1) * HD])
         log_ref[0, pl.ds(head, 1), :] = peak + jnp.log(total)
     out_ref[...] = jnp.concatenate(mixed, axis=0).T.astype(LOW)
@@ -227,7 +231,7 @@
 
 def attend(offsets, queries, window, reach):
     rows, width = queries.shape
-    pairs, blocks, context = width // (2 * HD), rows // BLOCK, window.shape[1]
+    pairs, blocks, context = width // (2 * HD), rows // BLOCK, window.shape[0]
     work = pairs * 2 * rows * (reach + 1) * BLOCK
     return pl.pallas_call(
         functools.partial(attend_kernel, reach),
@@ -235,7 +239,7 @@
         in_specs=[
             pl.BlockSpec((1, BLOCK), lambda p, b: (0, b)),
             pl.BlockSpec((BLOCK, 2 * HD), lambda p, b: (b, p)),
-            pl.BlockSpec((2, context, 2 * HD), lambda p, b: (0, 0, p)),
+            pl.BlockSpec((context, 4 * HD), lambda p, b: (0, p)),
         ],
         out_specs=[
             pl.BlockSpec((BLOCK, 2 * HD), lambda p, b: (b, p)),
@@ -261,11 +265,9 @@
     out_ref,
     log_ref,
     grad_ref,
-    grad_query_ref,
-    grad_window_ref,
-    grad_keys,
-    grad_values,
+    *rest,
 ):
+    grad_query_ref, grad_window_ref, grad_keys, grad_values = rest[-4:]
     block = pl.program_id(1)
     start = block * BLOCK
 
@@ -288,7 +290,7 @@
     back = [jnp.zeros((2 * HD, BLOCK), WIDE) for _ in range(2)]
     for step in range(reach + 1):
         rows = pl.ds(pl.multiple_of(start + step * BLOCK, BLOCK), BLOCK)
-        key, value = window_ref[0, rows, :], window_ref[1, rows, :]
+        key, value = window_ref[rows, : 2 * HD], window_ref[rows, 2 * HD :]
         allowed = open_pairs(offsets, step, reach)
         to_key = jnp.zeros((BLOCK, 2 * HD), WIDE)
         to_value = jnp.zeros((BLOCK, 2 * HD), WIDE)
@@ -307,17 +309,16 @@
 
     @pl.when(block == pl.num_programs(1) - 1)
     def _():
-        grad_window_ref[0] = grad_keys[...].astype(LOW)
-        grad_window_ref[1] = grad_values[...].astype(LOW)
-
-
-def attend_back(offsets, queries, window, out, logs, grads, reach, begin, pairs):
-    rows = queries.shape[0]
-    width = pairs * 2 * HD
-    blocks, context = rows // BLOCK, window.shape[1]
+        grad_window_ref[:, : 2 * HD] = grad_keys[...].astype(LOW)
+        grad_window_ref[:, 2 * HD :] = grad_values[...].astype(LOW)
+
+
+def attend_back(offsets, queries, window, out, logs, grads, reach, begin, pairs, filled):
+    rows, width = queries.shape
+    blocks, context = rows // BLOCK, window.shape[0]
     work = pairs * 2 * rows * (reach + 1) * BLOCK
     row_block = pl.BlockSpec((BLOCK, 2 * HD), lambda p, b: (b, p + begin))
-    window_block = pl.BlockSpec((2, context, 2 * HD), lambda p, b: (0, 0, p + begin))
+    window_block = pl.BlockSpec((context, 4 * HD), lambda p, b: (0, p + begin))
     return pl.pallas_call(
         functools.partial(attend_back_kernel, reach),
         grid=(pairs, blocks),
@@ -328,15 +329,14 @@
             row_block,
             pl.BlockSpec((1, 2, BLOCK), lambda p, b: (p + begin, 0, b)),
             row_block,
-        ],
-        out_specs=[
-            pl.BlockSpec((BLOCK, 2 * HD), lambda p, b: (b, p)),
-            pl.BlockSpec((2, context, 2 * HD), lambda p, b: (0, 0, p)),
-        ],
+        ]
+        + [pl.BlockSpec(memory_space=pl.ANY)] * len(filled),
+        out_specs=[row_block, window_block],
         out_shape=[
             jax.ShapeDtypeStruct((rows, width), LOW),
-            jax.ShapeDtypeStruct((2, context, width), LOW),
+            jax.ShapeDtypeStruct(window.shape, LOW),
         ],
+        input_output_aliases={6 + i: i for i in range(len(filled))},
         scratch_shapes=[
             pltpu.VMEM((context, 2 * HD), WIDE),
             pltpu.VMEM((context, 2 * HD), WIDE),
@@ -345,7 +345,7 @@
             flops=40 * HD * work, transcendentals=work, bytes_accessed=16 * rows * width
         ),
         name="attend_backward",
-    )(offsets, queries, window, out, logs, grads)
+    )(offsets, queries, window, out, logs, grads, *filled)
 
 
 def core_pair(own, got, core, axis):
@@ -386,8 +386,8 @@
     key_scale = HD ** (-0.5)
     clip_total = text_states.shape[0]
     text_rows = text_states.shape[1]
-    shard_count, rep_count = axis_length("shard"), axis_length("rep")
-    device_count = shard_count * rep_count
+    shard_count = axis_length("shard")
+    shard_rows = x_key.shape[0]
     place = lax.axis_index("rep") * shard_count + lax.axis_index("shard")
     core, side = place % 2, (place // 2) % 2
 
@@ -395,14 +395,28 @@
         [self_gain, self_bias, cross_gain, cross_bias, final_gain, final_bias], axis=1
     )
     params = jnp.pad(params, ((0, 0), (0, 128 - params.shape[1])))
-    split = [w[:, h : h + half_width] for h in (0, half_width) for w in (w_query, w_key, w_value)]
-    first_group = gather_rows(jnp.concatenate(split + [w_output, params], axis=1))
+    pairs = head_count // 4
+    pair_split = (shard_rows, 2, pairs, 1, 2 * HD)
+    key_value = jnp.concatenate([w_key.reshape(pair_split), w_value.reshape(pair_split)], axis=3)
+    key_value = key_value.reshape(shard_rows, 2, model_width)
+    first_group = gather_rows(
+        jnp.concatenate(
+            [
+                part
+                for h in range(2)
+                for part in (w_query[:, h * half_width : (h + 1) * half_width], key_value[:, h])
+            ]
+            + [w_output, params],
+            axis=1,
+        ),
+    )
     full_output = first_group[:, 3 * model_width : 4 * model_width]
     gain_one, bias_one, gain_two, bias_two, gain_three, bias_three = (
         first_group[:, 4 * model_width + i].astype(WIDE) for i in range(6)
     )
-    full_part = lax.dynamic_slice_in_dim(
-        first_group, core * (3 * half_width), 3 * half_width, 1
+    part_query, part_pair = (
+        lax.dynamic_slice_in_dim(first_group, core * (3 * half_width) + begin, width, 1)
+        for begin, width in ((0, half_width), (half_width, model_width))
     )
     second_group = gather_rows(jnp.concatenate([x_query, x_key, x_value, x_output], axis=1))
     full_xquery, full_xkey, full_xvalue, full_xoutput = (
@@ -437,16 +451,11 @@
     )
     chip_rows = 2 * tok_rows
     halo_rows = tok_rows + 2 * chip_rows
-    around = around.astype(WIDE)
-    normed_around = (scaled_norm(around, gain_one) + bias_one).astype(LOW)
+    normed_plain = normalize(around.astype(WIDE))
+    normed_around = (normed_plain * gain_one + bias_one).astype(LOW)
     normed_chip = normed_around[halo_rows:]
-    queries = matmul(normed_chip, full_part[:, :half_width]).astype(LOW)
-    window = jnp.stack(
-        [
-            matmul(normed_around, full_part[:, half_width : 2 * half_width]).astype(LOW),
-            matmul(normed_around, full_part[:, 2 * half_width :]).astype(LOW),
-        ]
-    )
+    window = matmul(normed_around, part_pair).astype(LOW)
+    queries = matmul(normed_chip, part_query).astype(LOW)
     chip_mixed, logs = attend(offsets, queries, window, reach)
 
     def to_tokens(chip_rows_array):
@@ -490,39 +499,26 @@
     after_cross = after_self + matmul(cross_mix, full_xoutput)
     normed_three = (scaled_norm(after_cross, gain_three) + bias_three).astype(LOW)
     both_three = jnp.concatenate([normed_three, swap(normed_three, "rep", lambda i: i ^ 1)], axis=0)
-    pre_act = matmul(both_three, half_up)
-    activ, gelu_pull = jax.vjp(exact_gelu, pre_act)
-    activ = activ.astype(LOW)
-    slope = gelu_pull(jnp.ones_like(pre_act))[0]
-    activ, slope = lax.optimization_barrier((activ, slope))
-    grad_act = [right_t(upstream, part) for part in half_down]
-    grad_pre = (slope * jnp.concatenate(grad_act, axis=1)).astype(LOW)
+    quarter = hidden_half // 2
+    activ, slope, grad_pre = [], [], []
+    for i in range(2):
+        pre_act = matmul(both_three, half_up[:, i * quarter : (i + 1) * quarter])
+        shaped, gelu_pull = jax.vjp(exact_gelu, pre_act)
+        shaped, steep = shaped.astype(LOW), gelu_pull(jnp.ones_like(pre_act))[0]
+        shaped, steep = lax.optimization_barrier((shaped, steep))
+        activ.append(shaped)
+        slope.append(steep)
+    for i in range(2):
+        grad_pre.append((slope[i] * right_t(upstream, half_down[i])).astype(LOW))
+    activ, grad_pre = jnp.concatenate(activ, axis=1), jnp.concatenate(grad_pre, axis=1)
     grad_both = right_t(grad_pre, half_up)
     grad_norm_three = grad_both[:tok_rows] + swap(
         grad_both[tok_rows:].astype(LOW), "rep", lambda i: i ^ 1
     ).astype(WIDE)
-    quarter = hidden_half // 2
-    grad_down = [
-        left_t(activ[:, i * quarter : (i + 1) * quarter], upstream).astype(LOW)
-        for i in range(2)
-    ]
+    grad_down = left_t(activ, upstream).astype(LOW).reshape(2, -1, model_width)
     grad_up = left_t(both_three, grad_pre).astype(LOW)
-    down_halves = rep_pair(plane_total(grad_down))
-    fin_down = jnp.concatenate(
-        [half[:, i * model_width : (i + 1) * model_width] for half in down_halves for i in range(2)],
-        axis=0,
-    ).astype(WIDE)
-    up_halves = rep_pair(plane_total([grad_up]))
-    fin_up = jnp.stack(
-        [half.reshape(w_up.shape[0], 2, shard_count, chunk) for half in up_halves], axis=1
-    )
-    fin_up = jnp.transpose(fin_up, (0, 3, 1, 2, 4)).reshape(w_up.shape).astype(WIDE)
-    mixed_both = matmul(activ[:, :quarter], half_down[0]) + matmul(activ[:, quarter:], half_down[1])
-    block_out = (
-        after_cross
-        + mixed_both[:tok_rows]
-        + swap(mixed_both[tok_rows:].astype(LOW), "rep", lambda i: i ^ 1).astype(WIDE)
-    ).astype(LOW)
+    own_down = plane_total(grad_down)
+    own_up = plane_total(grad_up[None])
     norm_three_part, grad_gain_three, grad_bias_three = norm_back(
         after_cross, gain_three, grad_norm_three
     )
@@ -540,40 +536,33 @@
         .astype(LOW)
     )
     grad_ck = (
-        jnp.einsum("htk,thd->khd", grad_cscore, cq_heads, preferred_element_type=WIDE) * key_scale
-    ).reshape(2 * text_rows, model_width)
+        jnp.einsum("htk,thd->hdk", grad_cscore, cq_heads, preferred_element_type=WIDE) * key_scale
+    ).reshape(model_width, 2, text_rows)
     grad_cv = jnp.einsum(
-        "htk,thd->khd", cross_low, grad_cmix, preferred_element_type=WIDE
-    ).reshape(2 * text_rows, model_width)
+        "htk,thd->hdk", cross_low, grad_cmix, preferred_element_type=WIDE
+    ).reshape(model_width, 2, text_rows)
+    slots = jnp.arange(clip_total, dtype=jnp.int32)
+    in_first, in_second = (
+        (slots == clip).astype(WIDE)[None, :, None] for clip in (first, second)
+    )
+    text_sums = [
+        (part[:, :1] * in_first + part[:, 1:] * in_second).reshape(model_width, -1)
+        for part in (grad_ck, grad_cv)
+    ]
+    text_sums = jnp.concatenate(text_sums, axis=1)
+    text_cols = text_sums.shape[1]
+    text_sums = jnp.pad(text_sums, ((0, 0), (0, -text_cols % 256)))
     grad_xquery = left_t(normed_two, grad_cq)
     grad_norm_two = right_t(grad_cq, full_xquery)
     norm_two_part, grad_gain_two, grad_bias_two = norm_back(after_self, gain_two, grad_norm_two)
     grad_self_res = grad_cross_res + norm_two_part
     branch_one = grad_self_res.astype(LOW)
     grad_output = left_t(attended, branch_one)
-    fin_xoutput, fin_xquery, fin_output = summed_rows([grad_xoutput, grad_xquery, grad_output])
-
-    slots = jnp.arange(clip_total, dtype=jnp.int32)
-    in_first = (slots == first).astype(WIDE)[None, :, None, None]
-    in_second = (slots == second).astype(WIDE)[None, :, None, None]
-    pair = jnp.stack([grad_ck, grad_cv]).reshape(2, 2, text_rows, model_width)
-    sums = (pair[:, None, 0] * in_first + pair[:, None, 1] * in_second).astype(LOW)
-    sums = sums.reshape(2 * clip_total * text_rows, model_width)
-    text_total = sums.shape[0]
-    padded = -(-text_total // (16 * device_count)) * 16 * device_count
-    sums = jnp.pad(sums, ((0, padded - text_total), (0, 0)))
-    share = lax.psum_scatter(sums, BOTH, scatter_dimension=0, tiled=True)
-    sums = lax.all_gather(share, BOTH, axis=0, tiled=True)
+    fin_xoutput, fin_xquery, fin_output, text_share = summed_rows(
+        [grad_xoutput, grad_xquery, grad_output, text_sums]
+    )
+    text_whole = lax.all_gather(text_share.astype(LOW), "shard", axis=0, tiled=True)
     flat_rows = clip_total * text_rows
-    key_round, value_round = sums[:flat_rows], sums[flat_rows:text_total]
-    shard_rows = x_key.shape[0]
-    col_start = lax.axis_index("shard") * shard_rows
-    text_flat = text_states.reshape(flat_rows, model_width)
-    text_slice = lax.dynamic_slice_in_dim(text_flat, col_start, shard_rows, 1)
-    grad_xkey = left_t(text_slice, key_round)
-    grad_xvalue = left_t(text_slice, value_round)
-    grad_text = right_t(key_round, full_xkey) + right_t(value_round, full_xvalue)
-    grad_text = grad_text.reshape(clip_total, text_rows, model_width)
 
     grad_attended = right_t(branch_one, full_output).astype(LOW)
     halves = jnp.transpose(grad_attended.reshape(tok_rows, 2, half_width), (1, 0, 2))
@@ -583,46 +572,73 @@
         core,
         0,
     )
-    pairs = head_count // 4
     calls = 2 if pairs % 2 == 0 else 1
-    backs = []
+    backs = ()
     for call in range(calls):
-        backs.append(
-            attend_back(
-                offsets,
-                queries,
-                window,
-                chip_mixed,
-                logs,
-                chip_grad,
-                reach,
-                call * pairs // calls,
-                pairs // calls,
-            )
+        backs = attend_back(
+            offsets,
+            queries,
+            window,
+            chip_mixed,
+            logs,
+            chip_grad,
+            reach,
+            call * pairs // calls,
+            pairs // calls,
+            tuple(backs),
         )
-    chip_dq = jnp.concatenate([part[0] for part in backs], axis=1)
-    grad_window = jnp.concatenate([part[1] for part in backs], axis=2)
-    grad_weights = [
-        left_t(normed_chip, chip_dq),
-        left_t(normed_around, grad_window[0]),
-        left_t(normed_around, grad_window[1]),
+    chip_dq, grad_window = backs
+    grad_pair = left_t(normed_around, grad_window)
+    grad_wq = left_t(normed_chip, chip_dq)
+    _, own_down, own_up, after_late, activ_late = lax.optimization_barrier(
+        (grad_wq, own_down, own_up, after_cross, activ)
+    )
+    down_halves = rep_pair(own_down)
+    fin_down = jnp.concatenate(down_halves, axis=0).reshape(w_down.shape).astype(WIDE)
+    up_halves = rep_pair(own_up)
+    fin_up = jnp.stack(
+        [half.reshape(w_up.shape[0], 2, shard_count, chunk) for half in up_halves], axis=1
+    )
+    fin_up = jnp.transpose(fin_up, (0, 3, 1, 2, 4)).reshape(w_up.shape).astype(WIDE)
+    mixed_both = matmul(activ_late[:, :quarter], half_down[0]) + matmul(
+        activ_late[:, quarter:], half_down[1]
+    )
+    block_out = (
+        after_late
+        + mixed_both[:tok_rows]
+        + swap(mixed_both[tok_rows:].astype(LOW), "rep", lambda i: i ^ 1).astype(WIDE)
+    ).astype(LOW)
+    fin_halves = summed_halves(grad_pair, grad_wq).reshape(shard_rows, 2, 3 * half_width)
+    fin_pair = fin_halves[:, :, :model_width].reshape(shard_rows, 2, pairs, 2, 2 * HD)
+    fin_query = fin_halves[:, :, model_width:].reshape(w_query.shape)
+    fin_key = fin_pair[:, :, :, 0].reshape(w_query.shape)
+    fin_value = fin_pair[:, :, :, 1].reshape(w_query.shape)
+    grad_around = right_t(grad_window, part_pair)
+    grad_chip = grad_around[halo_rows:] + right_t(chip_dq, part_query)
+    around_sums = [
+        jnp.sum(grad_around[:halo_rows] * normed_plain[:halo_rows], axis=0)
+        + jnp.sum(grad_chip * normed_plain[halo_rows:], axis=0),
+        jnp.sum(grad_around[:halo_rows], axis=0) + jnp.sum(grad_chip, axis=0),
     ]
-    fin_qkv = summed_halves(grad_weights)
-    fin_query, fin_key, fin_value = (
-        jnp.concatenate(
-            [
-                fin_qkv[:, i * half_width : (i + 1) * half_width],
-                fin_qkv[:, (i + 3) * half_width : (i + 4) * half_width],
-            ],
-            axis=1,
+    grad_halo = grad_around[:halo_rows].astype(LOW)
+    _, text_whole = lax.optimization_barrier((grad_halo, text_whole))
+    key_round, value_round = (
+        text_whole[:, :flat_rows],
+        text_whole[:, flat_rows : 2 * flat_rows],
+    )
+    col_start = lax.axis_index("shard") * shard_rows
+    text_flat = text_states.reshape(flat_rows, model_width)
+    text_slice = lax.dynamic_slice_in_dim(text_flat, col_start, shard_rows, 1)
+
+    def mixed_dims(left, right):
+        return lax.dot_general(
+            left, right, (((0,), (1,)), ((), ())), preferred_element_type=WIDE
         )
-        for i in range(3)
-    )
-    grad_around = right_t(grad_window[0], full_part[:, half_width : 2 * half_width]) + right_t(
-        grad_window[1], full_part[:, 2 * half_width :]
-    )
-    grad_chip = grad_around[halo_rows:] + right_t(chip_dq, full_part[:, :half_width])
-    grad_halo = grad_around[:halo_rows].astype(LOW)
+
+    grad_xkey = mixed_dims(text_slice, key_round)
+    grad_xvalue = mixed_dims(text_slice, value_round)
+    grad_text = mixed_dims(key_round, full_xkey) + mixed_dims(value_round, full_xvalue)
+    grad_text = grad_text.reshape(clip_total, text_rows, model_width)
     units = jnp.concatenate([grad_halo[tok_rows:], grad_chip.astype(LOW)], axis=0)
     units = units.reshape(3, 2, tok_rows, model_width)
     sent = jnp.concatenate([pick(units, 1 - core, 1), grad_halo[None, :tok_rows]], axis=0)
@@ -640,7 +656,8 @@
         + swap(to_below, BOTH, lambda i: i - 4).astype(WIDE)
         + swap(back_half, BOTH, lambda i: i - 8 if i % 4 == 3 else -1).astype(WIDE)
     )
-    norm_one_part, grad_gain_one, grad_bias_one = norm_back(resid, gain_one, grad_norm_one)
+    norm_one_part, _, _ = norm_back(resid, gain_one, grad_norm_one)
+    grad_gain_one, grad_bias_one = around_sums
     grad_hidden = (grad_self_res + norm_one_part).astype(LOW)
     vectors = summed_vectors(
         jnp.stack(

time: 1170 us -> 1130 us (0.966)
  the two profiles are of different devices: /device:TPU:0 before, /device:TPU:9 now
where the time goes in v3:
time: 1130 us; the launch traced here: 1120 us
  waiting for transfers between devices  458 us (41%)
  matrix products  196 us (17%)
  local copies, waits for them, and re-layouts  142 us (13%)
  other arithmetic  128 us (11%)
  starting transfers between devices  104 us (9%)
  Pallas kernels  73.5 us (7%)
  between operations  19.4 us (2%)
    ppermute x47, waiting for transfers between devices, swap(): lax.ppermute(array, axis, [(i, j) for i, j in pairs if 0 <= j < length])  354 us
    ppermute x47, starting transfers between devices, swap(): lax.ppermute(array, axis, [(i, j) for i, j in pairs if 0 <= j < length])  104 us
    all_gather x3, waiting for transfers between devices, gather_rows(): return lax.all_gather(array, 'shard', axis=0, tiled=True)  104 us
    dot_general x11, matrix products, matmul(): return jnp.dot(left, right, preferred_element_type=WIDE)  71.5 us
    dot_general x8, matrix products, right_t(): lax.dot_general(left, right, (((1,), (1,)), ((), ())), preferred_element_...  47.6 us
    pallas_call x2, Pallas kernels, attend_back(): pl.pallas_call(functools.partial(attend_back_kernel, reach), grid=(pairs,...  47.4 us
    dot_general x7, matrix products, left_t(): lax.dot_general(left, right, (((0,), (0,)), ((), ())), preferred_element_...  45.6 us
    convert_element_type x15, other arithmetic, add_low(): return (left.astype(WIDE) + right.astype(WIDE)).astype(LOW)  34.5 us
  transfers between devices with their start and end apart: 52, of which 26 were waited for; matrix products, arithmetic and copies ran while one was open for 34% of the time, Pallas kernels for 7%

profile of v3, /device:TPU:9, one launch (start us, length us, event | category | flops | bytes accessed | tf_op | source)
XLA Modules:
  0.0 1120.6 jit_solution(10388960931759654082)
XLA Ops:
  23.0 34.2 %collective-permute-done = bf16[256,1536]{1,0:T(8,128)(2,1)S(1)} collective-permute-done((bf16[256,1536]{1,0:T(8,128)(2,1)S(1)}, bf16[256,1536]{1,0:T(8,128)(2,1)S(1)}, u32[]{:S(2)}, u32[]{:S(2)}) %collective-permute-start) | collective-permute-done | bytes 786464 | tf_op jit(solution)/shard_map/ppermute | solution.py:64
  57.4 34.3 %collective-permute-start.3 = (bf16[256,1536]{1,0:T(8,128)(2,1)S(1)}, bf16[256,1536]{1,0:T(8,128)(2,1)S(1)}, u32[]{:S(2)}, u32[]{:S(2)}) collective-permute-start(bf16[256,1536]{1,0:T(8,128)(2,1)S(1)} %get-tuple-element.166), channel_id=1, source_target_pairs={{0,2},{1,3},{2,0},{3,1},{4,6},{5,7},{6,4},{7,5},{8,10},{9,11},{10,... | collective-permute-start | bytes 2359304 | tf_op jit(solution)/shard_map/ppermute | solution.py:64
  94.2 7.3 collective-permute-done.3
  101.5 8.4 collective-permute-done.2
  128.6 9.2 fusion.3
  139.6 3.9 fusion.107
  144.7 102.3 %all-gather.8.cloned.1.call-done = bf16[1536,6272]{1,0:T(8,128)(2,1)} async-done(((bf16[96,6272]{1,0:T(8,128)(2,1)}), bf16[1536,6272]{1,0:T(8,128)(2,1)}) %all-gather.8.cloned.1.call-update) | async-done | bytes 19267600 | tf_op jit(solution)/shard_map/all_gather | solution.py:72
  247.1 4.6 convert_reduce_fusion.2
  251.6 13.3 %add_convert_fusion.1 = (bf16[1792,1536]{1,0:T(8,128)(2,1)S(1)}, f32[1792,1536]{1,0:T(8,128)}) fusion(f32[1536]{0:T(1024)S(1)} %get-tuple-element.81, f32[1536]{0:T(1024)S(1)} %get-tuple-element.82, f32[1792]{0:T(1024)} %add_rsqrt_fusion, f32[1792]{0:T(1024)} %copy-done.74, bf16[512,1536]{1,0:T(8,128)(2,1)S(1)} %copy-done.5, bf16[512,1536]{1,0:T(8,128)(2,1)} %copy-done.6, ...), kind=kLoop, calls=%fused_computation.9 | loop fusion | flops 35782656 | bytes 22046720 | tf_op jit(solution)/shard_map/convert_element_type | solution.py:455
  264.9 5.7 fusion.137.query_ref
  270.7 12.9 %convolution_convert_fusion.5.window_ref = bf16[1792,1536]{1,0:T(8,128)(2,1)} fusion(bf16[1792,1536]{1,0:T(8,128)(2,1)S(1)} %get-tuple-element.105, bf16[1536,6272]{1,0:T(8,128)(2,1)} %all-gather.8.cloned.1.call-done, s32[]{:T(128)S(6)} %select_n.463), kind=kOutput, calls=%fused_computation.23 | convolution fusion | flops 8458469376 | bytes 15728644 | tf_op jit(solution)/shard_map/dot_general | solution.py:36
  283.6 26.1 %attend_forward.1 = (bf16[512,768]{1,0:T(8,128)(2,1)}, f32[6,2,512]{2,1,0:T(2,128)}) custom-call(s32[1,512]{1,0:T(1,128)} %broadcast_select_fusion.10.offset_ref, bf16[512,768]{1,0:T(8,128)(2,1)} %fusion.137.query_ref, bf16[1792,1536]{1,0:T(8,128)(2,1)} %convolution_convert_fusion.5.window_ref), custom_call_target="tpu_custom_call" | custom-call | flops 9663676416 | bytes 3145728 | tf_op jit(solution)/shard_map/attend_forward/pallas_call | solution.py:236
  316.1 4.2 fusion.225
  321.3 3.8 fusion.98
  325.4 3.7 fusion.226
  331.6 4.2 fusion.227
  347.6 9.9 collective-permute-done.7
  357.5 11.8 %multiply_add_fusion.1 = (f32[512,1536]{1,0:T(8,128)S(1)}, f32[512,1536]{1,0:T(8,128)S(1)}, f32[512,1536]{1,0:T(8,128)S(1)}) fusion(bf16[1536,6144]{1,0:T(8,128)(2,1)} %all-gather.12.cloned.1.call-done, bf16[256,1536]{1,0:T(8,128)(2,1)} %collective-permute-done.7, bf16[256,1536]{1,0:T(8,128)(2,1)} %add_convert_fusion.4), kind=kOutput, calls=%fused_computation.114 | convolution fusion | flops 2472542208 | bytes 15728640 | tf_op jit(solution)/shard_map/dot_general | solution.py:36
  370.1 12.2 %multiply_add_fusion = (f32[512,1536]{1,0:T(8,128)}, f32[512,1536]{1,0:T(8,128)S(1)}, f32[512,1536]{1,0:T(8,128)S(1)}) fusion(bf16[1536,6144]{1,0:T(8,128)(2,1)S(1)} %copy-done.107, bf16[256,1536]{1,0:T(8,128)(2,1)} %collective-permute-done.7, bf16[256,1536]{1,0:T(8,128)(2,1)} %add_convert_fusion.4), kind=kOutput, calls=%fused_computation.100 | convolution fusion | flops 2472542208 | bytes 15728640 | tf_op jit(solution)/shard_map/dot_general | solution.py:36
  383.5 10.0 convolution_convert_fusion.1
  393.5 4.1 fusion.82
  397.5 5.6 fusion.79
  403.2 6.5 fusion.5
  413.4 9.3 fusion.4
  422.8 4.9 dynamic-slice_bitcast_fusion
  438.0 4.7 fusion.101
  455.6 3.7 convolution_convert_fusion.3
  459.3 4.7 multiply_reduce_fusion.2
  489.1 5.1 fusion.95
  497.2 3.9 constant_dynamic-slice_fusion.8
  506.7 8.3 dynamic-slice_bitcast_fusion.5
  522.2 23.7 %attend_backward.2 = (bf16[512,768]{1,0:T(8,128)(2,1)}, bf16[1792,1536]{1,0:T(8,128)(2,1)}) custom-call(s32[1,512]{1,0:T(1,128)} %broadcast_select_fusion.10.offset_ref, bf16[512,768]{1,0:T(8,128)(2,1)} %fusion.137.query_ref, bf16[1792,1536]{1,0:T(8,128)(2,1)} %convolution_convert_fusion.5.window_ref, bf16[512,768]{1,0:T(8,128)(2,1)} %get-tuple-element.48.out_ref, ...), custom_call_target="tpu_custom_call" | custom-call | flops 12079595520 | bytes 6291456 | tf_op jit(solution)/shard_map/attend_backward/pallas_call | solution.py:322
  545.9 23.7 %attend_backward.3 = (bf16[512,768]{1,0:T(8,128)(2,1)}, bf16[1792,1536]{1,0:T(8,128)(2,1)}) custom-call(s32[1,512]{1,0:T(1,128)} %broadcast_select_fusion.10.offset_ref, bf16[512,768]{1,0:T(8,128)(2,1)} %fusion.137.query_ref, bf16[1792,1536]{1,0:T(8,128)(2,1)} %convolution_convert_fusion.5.window_ref, ...), custom_call_target="tpu_custom_call", output_to_operand_aliasing={{0}: (6, {}), {1}: (7, {})} | custom-call | flops 12079595520 | bytes 6291456 | tf_op jit(solution)/shard_map/attend_backward/pallas_call | solution.py:322
  572.9 12.3 %convolution_convert_fusion.6 = bf16[1536,1536]{1,0:T(8,128)(2,1)} fusion(bf16[1792,1536]{1,0:T(8,128)(2,1)} %copy-done.29, bf16[1792,1536]{1,0:T(8,128)(2,1)S(1)} %copy-done.110), kind=kOutput, calls=%fused_computation.24 | convolution fusion | flops 8458076160 | bytes 15728640 | tf_op jit(solution)/shard_map/dot_general | solution.py:40
  586.6 4.0 slice.315
  599.3 12.5 %fusion.49 = f32[1792,1536]{1,0:T(8,128)S(1)} fusion(bf16[1792,1536]{1,0:T(8,128)(2,1)} %get-tuple-element.63, bf16[1536,6272]{1,0:T(8,128)(2,1)} %all-gather.8.cloned.1.call-done, s32[]{:T(128)S(6)} %select_n.463), kind=kOutput, calls=%fused_computation.79 | convolution fusion | flops 8455716864 | bytes 21233668 | tf_op jit(solution)/shard_map/dot_general | solution.py:44
  615.7 4.5 fusion.213
  627.2 7.6 collective-permute-done.38
  645.6 13.3 %collective-permute-done.39 = bf16[4,96,1152]{2,1,0:T(8,128)(2,1)S(1)} collective-permute-done((bf16[4,96,1152]{2,1,0:T(8,128)(2,1)S(1)}, bf16[4,96,1152]{2,1,0:T(8,128)(2,1)S(1)}, u32[]{:S(2)}, u32[]{:S(2)}) %collective-permute-start.39) | collective-permute-done | bytes 884768 | tf_op jit(solution)/shard_map/ppermute | solution.py:64
  665.8 6.9 pad_maximum_fusion
  675.9 4.0 collective-permute-done.40
  687.2 20.1 %collective-permute-done.41 = bf16[96,2304]{1,0:T(8,128)(2,1)S(1)} collective-permute-done((bf16[96,2304]{1,0:T(8,128)(2,1)S(1)}, bf16[96,2304]{1,0:T(8,128)(2,1)S(1)}, u32[]{:S(2)}, u32[]{:S(2)}) %collective-permute-start.41) | collective-permute-done | bytes 442400 | tf_op jit(solution)/shard_map/ppermute | solution.py:64
  725.2 6.5 fusion.7
  735.5 3.8 fusion.8
  741.8 6.3 collective-permute-done.24
  759.6 3.6 fusion.224
  775.2 5.5 add_convert_fusion
  785.9 13.9 %collective-permute-start.28 = (bf16[4,96,2816]{2,1,0:T(8,128)(2,1)S(1)}, bf16[4,96,2816]{2,1,0:T(8,128)(2,1)S(1)}, u32[]{:S(2)}, u32[]{:S(2)}) collective-permute-start(bf16[4,96,2816]{2,1,0:T(8,128)(2,1)S(1)} %dynamic-slice_bitcast_fusion.11), channel_id=1, source_target_pairs={{0,2},{1,3},{2,0},{3,1},{4,6},{5,7},{6,4},{7,5},{8,10},{9,11},{10,... | collective-permute-start | bytes 6488072 | tf_op jit(solution)/shard_map/ppermute | solution.py:64
  803.4 21.8 %collective-permute-done.30 = bf16[4,2,48,2816]{3,2,0,1:T(8,128)(2,1)S(1)} collective-permute-done((bf16[4,2,48,2816]{3,2,0,1:T(8,128)(2,1)S(1)}, bf16[4,2,48,2816]{3,2,0,1:T(8,128)(2,1)S(1)}, u32[]{:S(2)}, u32[]{:S(2)}) %collective-permute-start.30) | collective-permute-done | bytes 2162720 | tf_op jit(solution)/shard_map/ppermute | solution.py:64
  826.8 68.6 %collective-permute-done.28 = bf16[4,96,2816]{2,1,0:T(8,128)(2,1)S(1)} collective-permute-done((bf16[4,96,2816]{2,1,0:T(8,128)(2,1)S(1)}, bf16[4,96,2816]{2,1,0:T(8,128)(2,1)S(1)}, u32[]{:S(2)}, u32[]{:S(2)}) %collective-permute-start.28) | collective-permute-done | bytes 2162720 | tf_op jit(solution)/shard_map/ppermute | solution.py:64
  899.9 13.4 %collective-permute-done.31 = bf16[4,48,2816]{2,1,0:T(8,128)(2,1)S(1)} collective-permute-done((bf16[4,48,2816]{2,1,0:T(8,128)(2,1)S(1)}, bf16[4,48,2816]{2,1,0:T(8,128)(2,1)S(1)}, u32[]{:S(2)}, u32[]{:S(2)}) %collective-permute-start.31) | collective-permute-done | bytes 1081376 | tf_op jit(solution)/shard_map/ppermute | solution.py:64
  922.2 57.5 %collective-permute-done.32 = bf16[48,5632]{1,0:T(8,128)(2,1)S(1)} collective-permute-done((bf16[48,5632]{1,0:T(8,128)(2,1)S(1)}, bf16[48,5632]{1,0:T(8,128)(2,1)S(1)}, u32[]{:S(2)}, u32[]{:S(2)}) %collective-permute-start.32) | collective-permute-done | bytes 540704 | tf_op jit(solution)/shard_map/ppermute | solution.py:64
  979.7 24.2 %collective-permute-done.33 = bf16[48,5632]{1,0:T(8,128)(2,1)S(1)} collective-permute-done((bf16[48,5632]{1,0:T(8,128)(2,1)S(1)}, bf16[48,5632]{1,0:T(8,128)(2,1)S(1)}, u32[]{:S(2)}, u32[]{:S(2)}) %collective-permute-start.33) | collective-permute-done | bytes 540704 | tf_op jit(solution)/shard_map/ppermute | solution.py:64
  1010.0 7.0 collective-permute-done.35
  1018.7 15.0 %collective-permute-done.13 = bf16[2,96,1536]{2,1,0:T(8,128)(2,1)} collective-permute-done((bf16[2,96,1536]{2,1,0:T(8,128)(2,1)}, bf16[2,96,1536]{2,1,0:T(8,128)(2,1)}, u32[]{:S(2)}, u32[]{:S(2)}) %collective-permute-start.13) | collective-permute-done | bytes 589856 | tf_op jit(solution)/shard_map/ppermute | solution.py:64
  1033.7 8.5 collective-permute-done.14
  1042.2 4.0 collective-permute-done.15
  1050.2 5.0 fusion.21
  1055.2 4.6 fusion.59
  1062.0 15.0 %collective-permute-done.45 = bf16[1,96,3072]{2,1,0:T(8,128)(2,1)S(1)} collective-permute-done((bf16[1,96,3072]{2,1,0:T(8,128)(2,1)S(1)}, bf16[1,96,3072]{2,1,0:T(8,128)(2,1)S(1)}, u32[]{:S(2)}, u32[]{:S(2)}) %collective-permute-start.45) | collective-permute-done | bytes 589856 | tf_op jit(solution)/shard_map/ppermute | solution.py:64
  1080.9 5.6 reshape.601
  1094.9 3.6 fusion.143
  1101.6 5.1 fusion.33
  1106.7 7.1 fusion.76
  (537 shorter events, 280.0 us)
Async XLA Ops:
  7.2 132.4 %all-gather.10.cloned.1.call-start = ((), (), s32[]{:S(2)}) async-start(), calls=%async_computation.1 | async-start | bytes 20054016 | tf_op jit(solution)/shard_map/all_gather | solution.py:72
  9.7 237.3 %all-gather.8.cloned.1.call-start = ((), (), s32[]{:S(2)}) async-start(), calls=%async_computation | async-start | bytes 20471808 | tf_op jit(solution)/shard_map/all_gather | solution.py:72
  14.2 333.3 %all-gather.12.cloned.1.call-start = ((), (), s32[]{:S(2)}) async-start(), calls=%async_computation.2 | async-start | bytes 20054016 | tf_op jit(solution)/shard_map/all_gather | solution.py:72
  19.0 664.7 %all-gather.16.cloned.1.call-start = ((), (), s32[]{:S(2)}) async-start(), calls=%async_computation.4 | async-start | bytes 1622016 | tf_op jit(solution)/shard_map/all_gather | solution.py:188
  19.1 38.2 %collective-permute-start = (bf16[256,1536]{1,0:T(8,128)(2,1)S(1)}, bf16[256,1536]{1,0:T(8,128)(2,1)S(1)}, u32[]{:S(2)}, u32[]{:S(2)}) collective-permute-start(bf16[256,1536]{1,0:T(8,128)(2,1)S(1)} %copy-done.2), channel_id=1, source_target_pairs={{0,4},{1,5},{2,6},{3,7},{4,8},{5,9},{6,10},{7,11},{8,12},{9,13},{1... | collective-permute-start | bytes 2359304 | tf_op jit(solution)/shard_map/ppermute | solution.py:64
  22.3 35.0 %collective-permute-start.1 = (bf16[256,1536]{1,0:T(8,128)(2,1)S(1)}, bf16[256,1536]{1,0:T(8,128)(2,1)S(1)}, u32[]{:S(2)}, u32[]{:S(2)}) collective-permute-start(bf16[256,1536]{1,0:T(8,128)(2,1)S(1)} %copy-done.2), channel_id=1, source_target_pairs={{3,11},{7,15},{11,19},{15,23},{19,27},{23,31}} | collective-permute-start | bytes 2359304 | tf_op jit(solution)/shard_map/ppermute | solution.py:64
  57.4 44.1 %collective-permute-start.3 = (bf16[256,1536]{1,0:T(8,128)(2,1)S(1)}, bf16[256,1536]{1,0:T(8,128)(2,1)S(1)}, u32[]{:S(2)}, u32[]{:S(2)}) collective-permute-start(bf16[256,1536]{1,0:T(8,128)(2,1)S(1)} %get-tuple-element.166), channel_id=1, source_target_pairs={{0,2},{1,3},{2,0},{3,1},{4,6},{5,7},{6,4},{7,5},{8,10},{9,11},{10,... | collective-permute-start | bytes 2359304 | tf_op jit(solution)/shard_map/ppermute | solution.py:64
  91.7 18.2 %collective-permute-start.2 = (bf16[256,1536]{1,0:T(8,128)(2,1)S(1)}, bf16[256,1536]{1,0:T(8,128)(2,1)S(1)}, u32[]{:S(2)}, u32[]{:S(2)}) collective-permute-start(bf16[256,1536]{1,0:T(8,128)(2,1)S(1)} %get-tuple-element.167), channel_id=1, source_target_pairs={{1,3},{3,1},{5,7},{7,5},{9,11},{11,9},{13,15},{15,13},{17,19},{19,... | collective-permute-start | bytes 2359304 | tf_op jit(solution)/shard_map/ppermute | solution.py:64
  111.9 10.1 collective-permute-start.4
  111.9 9.5 collective-permute-start.5
  112.4 232.9 %collective-permute-start.8 = (bf16[256,1536]{1,0:T(8,128)(2,1)}, bf16[256,1536]{1,0:T(8,128)(2,1)}, u32[]{:S(2)}, u32[]{:S(2)}) collective-permute-start(bf16[256,1536]{1,0:T(8,128)(2,1)} %param.41), channel_id=1, source_target_pairs={{0,16},{16,0},{1,17},{17,1},{2,18},{18,2},{3,19},{19,3},{4,20},{20... | collective-permute-start | bytes 2359304 | tf_op jit(solution)/shard_map/ppermute | solution.py:64
  120.6 19.0 %copy-start.66 = (bf16[64,1536]{1,0:T(8,128)(2,1)}, bf16[64,1536]{1,0:T(8,128)(2,1)S(1)}, u32[]{:S(2)}) copy-start(bf16[64,1536]{1,0:T(8,128)(2,1)S(1)} %get-tuple-element.144) | copy-start | bytes 589828
  120.6 19.0 %copy-start.68 = (bf16[64,1536]{1,0:T(8,128)(2,1)}, bf16[64,1536]{1,0:T(8,128)(2,1)S(1)}, u32[]{:S(2)}) copy-start(bf16[64,1536]{1,0:T(8,128)(2,1)S(1)} %get-tuple-element.145) | copy-start | bytes 589828
  283.6 27.7 %copy-start.67 = (bf16[64,1536]{1,0:T(8,128)(2,1)S(1)}, bf16[64,1536]{1,0:T(8,128)(2,1)}, u32[]{:S(2)}) copy-start(bf16[64,1536]{1,0:T(8,128)(2,1)} %copy-done.66) | copy-start | bytes 589828
  283.6 27.7 %copy-start.69 = (bf16[64,1536]{1,0:T(8,128)(2,1)S(1)}, bf16[64,1536]{1,0:T(8,128)(2,1)}, u32[]{:S(2)}) copy-start(bf16[64,1536]{1,0:T(8,128)(2,1)} %copy-done.68) | copy-start | bytes 589828
  310.8 4.5 collective-permute-start.6
  335.8 97.9 %copy-start = (f32[256,1536]{1,0:T(8,128)}, f32[256,1536]{1,0:T(8,128)S(1)}, u32[]{:S(2)}) copy-start(f32[256,1536]{1,0:T(8,128)S(1)} %get-tuple-element.61) | copy-start | bytes 4718596
  338.1 19.4 %collective-permute-start.7 = (bf16[256,1536]{1,0:T(8,128)(2,1)}, bf16[256,1536]{1,0:T(8,128)(2,1)}, u32[]{:S(2)}, u32[]{:S(2)}) collective-permute-start(bf16[256,1536]{1,0:T(8,128)(2,1)} %add_convert_fusion.4), channel_id=1, source_target_pairs={{0,16},{16,0},{1,17},{17,1},{2,18},{18,2},{3,19},{19,3},{4,20},{20... | collective-permute-start | bytes 2359304 | tf_op jit(solution)/shard_map/ppermute | solution.py:64
  412.3 18.5 %collective-permute-start.9 = (bf16[256,1536]{1,0:T(8,128)(2,1)}, bf16[256,1536]{1,0:T(8,128)(2,1)}, u32[]{:S(2)}, u32[]{:S(2)}) collective-permute-start(bf16[256,1536]{1,0:T(8,128)(2,1)} %slice.472), channel_id=1, source_target_pairs={{0,16},{16,0},{1,17},{17,1},{2,18},{18,2},{3,19},{19,3},{4,20},{20... | collective-permute-start | bytes 2359304 | tf_op jit(solution)/shard_map/ppermute | solution.py:64
  427.6 295.9 %collective-permute-start.16 = (bf16[1,8,96,3072]{3,2,1,0:T(8,128)(2,1)}, bf16[1,8,96,3072]{3,2,1,0:T(8,128)(2,1)}, u32[]{:S(2)}, u32[]{:S(2)}) collective-permute-start(bf16[1,8,96,3072]{3,2,1,0:T(8,128)(2,1)} %dynamic-slice_bitcast_fusion), channel_id=1, source_target_pairs={{0,1},{1,0},{2,3},{3,2},{4,5},{5,4},{6,7},{7,6},{8,9},{9,8},{10,11... | collective-permute-start | bytes 14155784 | tf_op jit(solution)/shard_map/ppermute | solution.py:64
  501.8 19.2 %collective-permute-start.10 = (bf16[256,768]{1,0:T(8,128)(2,1)}, bf16[256,768]{1,0:T(8,128)(2,1)S(1)}, u32[]{:S(2)}, u32[]{:S(2)}) collective-permute-start(bf16[256,768]{1,0:T(8,128)(2,1)} %bitcast.329), channel_id=1, source_target_pairs={{0,1},{1,0},{2,3},{3,2},{4,5},{5,4},{6,7},{7,6},{8,9},{9,8},{10,11... | collective-permute-start | bytes 1179656 | tf_op jit(solution)/shard_map/ppermute | solution.py:64
  593.0 21.4 %slice-start = ((s8[11010048]{0:T(1024)(128)(4,1)}), s8[2621440]{0:T(1024)(128)(4,1)S(1)}, s32[]{:S(2)}) async-start(s8[11010048]{0:T(1024)(128)(4,1)} %bitcast.331), calls=%async_computation.5 | async-start | bytes 5242880
  594.4 40.5 %collective-permute-start.38 = (bf16[4,2,96,1152]{3,2,0,1:T(8,128)(2,1)}, bf16[4,2,96,1152]{3,2,0,1:T(8,128)(2,1)}, u32[]{:S(2)}, u32[]{:S(2)}) collective-permute-start(bf16[4,2,96,1152]{3,2,0,1:T(8,128)(2,1)} %pad_maximum_fusion.8), channel_id=1, source_target_pairs={{0,16},{16,0},{1,17},{17,1},{2,18},{18,2},{3,19},{19,3},{4,20},{20... | collective-permute-start | bytes 5308424 | tf_op jit(solution)/shard_map/ppermute | solution.py:64
  598.4 16.0 %slice-start.1 = ((s8[11010048]{0:T(1024)(128)(4,1)}), s8[4194304]{0:T(1024)(128)(4,1)S(1)}, s32[]{:S(2)}) async-start(s8[11010048]{0:T(1024)(128)(4,1)} %bitcast.331), calls=%async_computation.6 | async-start | bytes 8388608
  598.4 16.0 %slice-start.2 = ((s8[11010048]{0:T(1024)(128)(4,1)}), s8[4194304]{0:T(1024)(128)(4,1)S(1)}, s32[]{:S(2)}) async-start(s8[11010048]{0:T(1024)(128)(4,1)} %bitcast.331), calls=%async_computation.7 | async-start | bytes 8388608
  598.4 40.6 %collective-permute-start.36 = (bf16[4,192,1152]{2,1,0:T(8,128)(2,1)}, bf16[4,192,1152]{2,1,0:T(8,128)(2,1)}, u32[]{:S(2)}, u32[]{:S(2)}) collective-permute-start(bf16[4,192,1152]{2,1,0:T(8,128)(2,1)} %dynamic-slice_bitcast_fusion.12), channel_id=1, source_target_pairs={{0,2},{1,3},{2,0},{3,1},{4,6},{5,7},{6,4},{7,5},{8,10},{9,11},{10,... | collective-permute-start | bytes 5308424 | tf_op jit(solution)/shard_map/ppermute | solution.py:64
  624.9 470.0 %all-gather.14.cloned.1.call-start = ((), (), s32[]{:S(2)}) async-start(), calls=%async_computation.3 | async-start | bytes 3342336 | tf_op jit(solution)/shard_map/all_gather | solution.py:564
  637.0 21.9 %collective-permute-start.39 = (bf16[4,96,1152]{2,1,0:T(8,128)(2,1)S(1)}, bf16[4,96,1152]{2,1,0:T(8,128)(2,1)S(1)}, u32[]{:S(2)}, u32[]{:S(2)}) collective-permute-start(bf16[4,96,1152]{2,1,0:T(8,128)(2,1)S(1)} %dynamic-slice_bitcast_fusion.17), channel_id=1, source_target_pairs={{0,2},{1,3},{2,0},{3,1},{4,6},{5,7},{6,4},{7,5},{8,10},{9,11},{10,... | collective-permute-start | bytes 2654216 | tf_op jit(solution)/shard_map/ppermute | solution.py:64
  641.9 21.1 %collective-permute-start.37 = (bf16[4,96,1152]{2,1,0:T(8,128)(2,1)}, bf16[4,96,1152]{2,1,0:T(8,128)(2,1)}, u32[]{:S(2)}, u32[]{:S(2)}) collective-permute-start(bf16[4,96,1152]{2,1,0:T(8,128)(2,1)} %dynamic-slice_bitcast_fusion.18), channel_id=1, source_target_pairs={{0,16},{16,0},{1,17},{17,1},{2,18},{18,2},{3,19},{19,3},{4,20},{20... | collective-permute-start | bytes 2654216 | tf_op jit(solution)/shard_map/ppermute | solution.py:64
  644.2 66.2 %collective-permute-start.22 = (bf16[4,256,1536]{2,1,0:T(8,128)(2,1)}, bf16[4,256,1536]{2,1,0:T(8,128)(2,1)}, u32[]{:S(2)}, u32[]{:S(2)}) collective-permute-start(bf16[4,256,1536]{2,1,0:T(8,128)(2,1)} %pad_maximum_fusion.5), channel_id=1, source_target_pairs={{0,1},{1,0},{2,3},{3,2},{4,5},{5,4},{6,7},{7,6},{8,9},{9,8},{10,11... | collective-permute-start | bytes 9437192 | tf_op jit(solution)/shard_map/ppermute | solution.py:64
  664.5 15.4 %collective-permute-start.40 = (bf16[96,2304]{1,0:T(8,128)(2,1)S(1)}, bf16[96,2304]{1,0:T(8,128)(2,1)S(1)}, u32[]{:S(2)}, u32[]{:S(2)}) collective-permute-start(bf16[96,2304]{1,0:T(8,128)(2,1)S(1)} %get-tuple-element.137), channel_id=1, source_target_pairs={{0,4},{1,5},{2,6},{3,7},{4,8},{5,9},{6,10},{7,11},{8,12},{9,13},{1... | collective-permute-start | bytes 1327112 | tf_op jit(solution)/shard_map/ppermute | solution.py:64
  672.7 102.5 %collective-permute-start.27 = (bf16[8,96,5632]{2,1,0:T(8,128)(2,1)}, bf16[8,96,5632]{2,1,0:T(8,128)(2,1)}, u32[]{:S(2)}, u32[]{:S(2)}) collective-permute-start(bf16[8,96,5632]{2,1,0:T(8,128)(2,1)} %pad_maximum_fusion), channel_id=1, source_target_pairs={{0,1},{1,0},{2,3},{3,2},{4,5},{5,4},{6,7},{7,6},{8,9},{9,8},{10,11... | collective-permute-start | bytes 25952264 | tf_op jit(solution)/shard_map/ppermute | solution.py:64
  674.8 32.6 %collective-permute-start.41 = (bf16[96,2304]{1,0:T(8,128)(2,1)S(1)}, bf16[96,2304]{1,0:T(8,128)(2,1)S(1)}, u32[]{:S(2)}, u32[]{:S(2)}) collective-permute-start(bf16[96,2304]{1,0:T(8,128)(2,1)S(1)} %get-tuple-element.138), channel_id=1, source_target_pairs={{0,8},{1,9},{2,10},{3,11},{4,12},{5,13},{6,14},{7,15},{8,0},{9,1},... | collective-permute-start | bytes 1327112 | tf_op jit(solution)/shard_map/ppermute | solution.py:64
  679.9 28.9 %collective-permute-start.42 = (bf16[96,2304]{1,0:T(8,128)(2,1)S(1)}, bf16[96,2304]{1,0:T(8,128)(2,1)}, u32[]{:S(2)}, u32[]{:S(2)}) collective-permute-start(bf16[96,2304]{1,0:T(8,128)(2,1)S(1)} %get-tuple-element.139), channel_id=1, source_target_pairs={{0,12},{1,13},{2,14},{3,15},{4,0},{5,1},{6,2},{7,3},{8,4},{9,5},{1... | collective-permute-start | bytes 1327112 | tf_op jit(solution)/shard_map/ppermute | solution.py:64
  707.3 26.1 %collective-permute-start.11 = (bf16[2,8,96,1536]{3,2,1,0:T(8,128)(2,1)}, bf16[2,8,96,1536]{3,2,1,0:T(8,128)(2,1)}, u32[]{:S(2)}, u32[]{:S(2)}) collective-permute-start(bf16[2,8,96,1536]{3,2,1,0:T(8,128)(2,1)} %dynamic-slice_bitcast_fusion.1), channel_id=1, source_target_pairs={{0,1},{1,0},{2,3},{3,2},{4,5},{5,4},{6,7},{7,6},{8,9},{9,8},{10,11... | collective-permute-start | bytes 14155784 | tf_op jit(solution)/shard_map/ppermute | solution.py:64
  710.0 9.7 collective-permute-start.43
  714.5 26.6 %collective-permute-start.23 = (bf16[256,1536]{1,0:T(8,128)(2,1)}, bf16[256,1536]{1,0:T(8,128)(2,1)S(1)}, u32[]{:S(2)}, u32[]{:S(2)}) collective-permute-start(bf16[256,1536]{1,0:T(8,128)(2,1)} %slice_bitcast_fusion.5), channel_id=1, source_target_pairs={{0,2},{1,3},{2,0},{3,1},{4,6},{5,7},{6,4},{7,5},{8,10},{9,11},{10,... | collective-permute-start | bytes 2359304 | tf_op jit(solution)/shard_map/ppermute | solution.py:64
  719.7 28.3 %collective-permute-start.24 = (bf16[256,1536]{1,0:T(8,128)(2,1)}, bf16[256,1536]{1,0:T(8,128)(2,1)}, u32[]{:S(2)}, u32[]{:S(2)}) collective-permute-start(bf16[256,1536]{1,0:T(8,128)(2,1)} %fusion.131), channel_id=1, source_target_pairs={{1,3},{3,1},{5,7},{7,5},{9,11},{11,9},{13,15},{15,13},{17,19},{19,... | collective-permute-start | bytes 2359304 | tf_op jit(solution)/shard_map/ppermute | solution.py:64
  723.6 28.7 %collective-permute-start.44 = (bf16[96,2304]{1,0:T(8,128)(2,1)}, bf16[96,2304]{1,0:T(8,128)(2,1)S(1)}, u32[]{:S(2)}, u32[]{:S(2)}) collective-permute-start(bf16[96,2304]{1,0:T(8,128)(2,1)} %get-tuple-element.159), channel_id=1, source_target_pairs={{0,1},{1,0},{2,3},{3,2},{4,5},{5,4},{6,7},{7,6},{8,9},{9,8},{10,11... | collective-permute-start | bytes 1327112 | tf_op jit(solution)/shard_map/ppermute | solution.py:64
  734.6 66.2 %collective-permute-start.17 = (bf16[1,4,96,3072]{3,2,1,0:T(8,128)(2,1)}, bf16[1,4,96,3072]{3,2,1,0:T(8,128)(2,1)}, u32[]{:S(2)}, u32[]{:S(2)}) collective-permute-start(bf16[1,4,96,3072]{3,2,1,0:T(8,128)(2,1)} %dynamic-slice_bitcast_fusion.9), channel_id=1, source_target_pairs={{0,2},{1,3},{2,0},{3,1},{4,6},{5,7},{6,4},{7,5},{8,10},{9,11},{10,... | collective-permute-start | bytes 7077896 | tf_op jit(solution)/shard_map/ppermute | solution.py:64
  741.1 176.1 %collective-permute-start.12 = (bf16[2,4,96,1536]{3,2,1,0:T(8,128)(2,1)}, bf16[2,4,96,1536]{3,2,1,0:T(8,128)(2,1)}, u32[]{:S(2)}, u32[]{:S(2)}) collective-permute-start(bf16[2,4,96,1536]{3,2,1,0:T(8,128)(2,1)} %dynamic-slice_bitcast_fusion.10), channel_id=1, source_target_pairs={{0,2},{1,3},{2,0},{3,1},{4,6},{5,7},{6,4},{7,5},{8,10},{9,11},{10,... | collective-permute-start | bytes 7077896 | tf_op jit(solution)/shard_map/ppermute | solution.py:64
  750.3 22.1 %collective-permute-start.25 = (bf16[256,1536]{1,0:T(8,128)(2,1)}, bf16[256,1536]{1,0:T(8,128)(2,1)}, u32[]{:S(2)}, u32[]{:S(2)}) collective-permute-start(bf16[256,1536]{1,0:T(8,128)(2,1)} %fusion.126), channel_id=1, source_target_pairs={{4,0},{5,1},{6,2},{7,3},{8,4},{9,5},{10,6},{11,7},{12,8},{13,9},{1... | collective-permute-start | bytes 2359304 | tf_op jit(solution)/shard_map/ppermute | solution.py:64
  752.3 20.2 %collective-permute-start.26 = (bf16[256,1536]{1,0:T(8,128)(2,1)}, bf16[256,1536]{1,0:T(8,128)(2,1)}, u32[]{:S(2)}, u32[]{:S(2)}) collective-permute-start(bf16[256,1536]{1,0:T(8,128)(2,1)} %collective-permute-done.24), channel_id=1, source_target_pairs={{11,3},{15,7},{19,11},{23,15},{27,19},{31,23}} | collective-permute-start | bytes 2359304 | tf_op jit(solution)/shard_map/ppermute | solution.py:64
  781.8 43.4 %collective-permute-start.30 = (bf16[4,2,48,2816]{3,2,0,1:T(8,128)(2,1)S(1)}, bf16[4,2,48,2816]{3,2,0,1:T(8,128)(2,1)S(1)}, u32[]{:S(2)}, u32[]{:S(2)}) collective-permute-start(bf16[4,2,48,2816]{3,2,0,1:T(8,128)(2,1)S(1)} %bitcast.387), channel_id=1, source_target_pairs={{0,16},{16,0},{1,17},{17,1},{2,18},{18,2},{3,19},{19,3},{4,20},{20... | collective-permute-start | bytes 6488072 | tf_op jit(solution)/shard_map/ppermute | solution.py:64
  783.2 17.6 %slice-start.8 = ((s8[4718592]{0:T(1024)(128)(4,1)}), s8[4194304]{0:T(1024)(128)(4,1)S(1)}, s32[]{:S(2)}) async-start(s8[4718592]{0:T(1024)(128)(4,1)} %bitcast.346), calls=%async_computation.13 | async-start | bytes 8388608
  785.9 109.5 %collective-permute-start.28 = (bf16[4,96,2816]{2,1,0:T(8,128)(2,1)S(1)}, bf16[4,96,2816]{2,1,0:T(8,128)(2,1)S(1)}, u32[]{:S(2)}, u32[]{:S(2)}) collective-permute-start(bf16[4,96,2816]{2,1,0:T(8,128)(2,1)S(1)} %dynamic-slice_bitcast_fusion.11), channel_id=1, source_target_pairs={{0,2},{1,3},{2,0},{3,1},{4,6},{5,7},{6,4},{7,5},{8,10},{9,11},{10,... | collective-permute-start | bytes 6488072 | tf_op jit(solution)/shard_map/ppermute | solution.py:64
  825.8 87.6 %collective-permute-start.31 = (bf16[4,48,2816]{2,1,0:T(8,128)(2,1)S(1)}, bf16[4,48,2816]{2,1,0:T(8,128)(2,1)S(1)}, u32[]{:S(2)}, u32[]{:S(2)}) collective-permute-start(bf16[4,48,2816]{2,1,0:T(8,128)(2,1)S(1)} %dynamic-slice_bitcast_fusion.15), channel_id=1, source_target_pairs={{0,2},{1,3},{2,0},{3,1},{4,6},{5,7},{6,4},{7,5},{8,10},{9,11},{10,... | collective-permute-start | bytes 3244040 | tf_op jit(solution)/shard_map/ppermute | solution.py:64
  895.9 22.7 %slice-start.6 = ((s8[4718592]{0:T(1024)(128)(4,1)}), s8[4194304]{0:T(1024)(128)(4,1)S(1)}, s32[]{:S(2)}) async-start(s8[4718592]{0:T(1024)(128)(4,1)} %bitcast.342), calls=%async_computation.11 | async-start | bytes 8388608
  896.0 17.6 %collective-permute-start.29 = (bf16[4,48,2816]{2,1,0:T(8,128)(2,1)S(1)}, bf16[4,48,2816]{2,1,0:T(8,128)(2,1)S(1)}, u32[]{:S(2)}, u32[]{:S(2)}) collective-permute-start(bf16[4,48,2816]{2,1,0:T(8,128)(2,1)S(1)} %dynamic-slice_bitcast_fusion.16), channel_id=1, source_target_pairs={{0,16},{16,0},{1,17},{17,1},{2,18},{18,2},{3,19},{19,3},{4,20},{20... | collective-permute-start | bytes 3244040 | tf_op jit(solution)/shard_map/ppermute | solution.py:64
  897.6 109.4 %collective-permute-start.18 = (bf16[1,96,3072]{2,1,0:T(8,128)(2,1)S(1)}, bf16[1,96,3072]{2,1,0:T(8,128)(2,1)S(1)}, u32[]{:S(2)}, u32[]{:S(2)}) collective-permute-start(bf16[1,96,3072]{2,1,0:T(8,128)(2,1)S(1)} %get-tuple-element.125), channel_id=1, source_target_pairs={{0,4},{1,5},{2,6},{3,7},{4,8},{5,9},{6,10},{7,11},{8,12},{9,13},{1... | collective-permute-start | bytes 1769480 | tf_op jit(solution)/shard_map/ppermute | solution.py:64
  897.7 21.0 %slice-start.7 = ((s8[4718592]{0:T(1024)(128)(4,1)}), s8[524288]{0:T(1024)(128)(4,1)S(1)}, s32[]{:S(2)}) async-start(s8[4718592]{0:T(1024)(128)(4,1)} %bitcast.342), calls=%async_computation.12 | async-start | bytes 1048576
  897.7 111.1 %collective-permute-start.19 = (bf16[1,96,3072]{2,1,0:T(8,128)(2,1)S(1)}, bf16[1,96,3072]{2,1,0:T(8,128)(2,1)S(1)}, u32[]{:S(2)}, u32[]{:S(2)}) collective-permute-start(bf16[1,96,3072]{2,1,0:T(8,128)(2,1)S(1)} %get-tuple-element.127), channel_id=1, source_target_pairs={{0,8},{1,9},{2,10},{3,11},{4,12},{5,13},{6,14},{7,15},{8,0},{9,1},... | collective-permute-start | bytes 1769480 | tf_op jit(solution)/shard_map/ppermute | solution.py:64
  914.0 65.6 %collective-permute-start.32 = (bf16[48,5632]{1,0:T(8,128)(2,1)S(1)}, bf16[48,5632]{1,0:T(8,128)(2,1)S(1)}, u32[]{:S(2)}, u32[]{:S(2)}) collective-permute-start(bf16[48,5632]{1,0:T(8,128)(2,1)S(1)} %get-tuple-element.134), channel_id=1, source_target_pairs={{0,4},{1,5},{2,6},{3,7},{4,8},{5,9},{6,10},{7,11},{8,12},{9,13},{1... | collective-permute-start | bytes 1622024 | tf_op jit(solution)/shard_map/ppermute | solution.py:64
  914.2 89.7 %collective-permute-start.33 = (bf16[48,5632]{1,0:T(8,128)(2,1)S(1)}, bf16[48,5632]{1,0:T(8,128)(2,1)S(1)}, u32[]{:S(2)}, u32[]{:S(2)}) collective-permute-start(bf16[48,5632]{1,0:T(8,128)(2,1)S(1)} %get-tuple-element.135), channel_id=1, source_target_pairs={{0,8},{1,9},{2,10},{3,11},{4,12},{5,13},{6,14},{7,15},{8,0},{9,1},... | collective-permute-start | bytes 1622024 | tf_op jit(solution)/shard_map/ppermute | solution.py:64
  917.3 86.6 %collective-permute-start.34 = (bf16[48,5632]{1,0:T(8,128)(2,1)S(1)}, bf16[48,5632]{1,0:T(8,128)(2,1)S(1)}, u32[]{:S(2)}, u32[]{:S(2)}) collective-permute-start(bf16[48,5632]{1,0:T(8,128)(2,1)S(1)} %get-tuple-element.136), channel_id=1, source_target_pairs={{0,12},{1,13},{2,14},{3,15},{4,0},{5,1},{6,2},{7,3},{8,4},{9,5},{1... | collective-permute-start | bytes 1622024 | tf_op jit(solution)/shard_map/ppermute | solution.py:64
  979.7 29.9 %collective-permute-start.20 = (bf16[1,96,3072]{2,1,0:T(8,128)(2,1)S(1)}, bf16[1,96,3072]{2,1,0:T(8,128)(2,1)S(1)}, u32[]{:S(2)}, u32[]{:S(2)}) collective-permute-start(bf16[1,96,3072]{2,1,0:T(8,128)(2,1)S(1)} %get-tuple-element.126), channel_id=1, source_target_pairs={{0,12},{1,13},{2,14},{3,15},{4,0},{5,1},{6,2},{7,3},{8,4},{9,5},{1... | collective-permute-start | bytes 1769480 | tf_op jit(solution)/shard_map/ppermute | solution.py:64
  1003.9 29.8 %collective-permute-start.13 = (bf16[2,96,1536]{2,1,0:T(8,128)(2,1)}, bf16[2,96,1536]{2,1,0:T(8,128)(2,1)}, u32[]{:S(2)}, u32[]{:S(2)}) collective-permute-start(bf16[2,96,1536]{2,1,0:T(8,128)(2,1)} %get-tuple-element.128), channel_id=1, source_target_pairs={{0,4},{1,5},{2,6},{3,7},{4,8},{5,9},{6,10},{7,11},{8,12},{9,13},{1... | collective-permute-start | bytes 1769480 | tf_op jit(solution)/shard_map/ppermute | solution.py:64
  1003.9 38.3 %collective-permute-start.14 = (bf16[2,96,1536]{2,1,0:T(8,128)(2,1)}, bf16[2,96,1536]{2,1,0:T(8,128)(2,1)}, u32[]{:S(2)}, u32[]{:S(2)}) collective-permute-start(bf16[2,96,1536]{2,1,0:T(8,128)(2,1)} %get-tuple-element.130), channel_id=1, source_target_pairs={{0,8},{1,9},{2,10},{3,11},{4,12},{5,13},{6,14},{7,15},{8,0},{9,1},... | collective-permute-start | bytes 1769480 | tf_op jit(solution)/shard_map/ppermute | solution.py:64
  1007.0 39.2 %collective-permute-start.15 = (bf16[2,96,1536]{2,1,0:T(8,128)(2,1)S(1)}, bf16[2,96,1536]{2,1,0:T(8,128)(2,1)}, u32[]{:S(2)}, u32[]{:S(2)}) collective-permute-start(bf16[2,96,1536]{2,1,0:T(8,128)(2,1)S(1)} %get-tuple-element.129), channel_id=1, source_target_pairs={{0,12},{1,13},{2,14},{3,15},{4,0},{5,1},{6,2},{7,3},{8,4},{9,5},{1... | collective-permute-start | bytes 1769480 | tf_op jit(solution)/shard_map/ppermute | solution.py:64
  1008.7 8.2 collective-permute-start.35
  1048.8 37.7 %collective-permute-start.46 = (bf16[2,96,1536]{2,1,0:T(8,128)(2,1)}, bf16[2,96,1536]{2,1,0:T(8,128)(2,1)}, u32[]{:S(2)}, u32[]{:S(2)}) collective-permute-start(bf16[2,96,1536]{2,1,0:T(8,128)(2,1)} %fusion.154), channel_id=1, source_target_pairs={{0,16},{16,0},{1,17},{17,1},{2,18},{18,2},{3,19},{19,3},{4,20},{20... | collective-permute-start | bytes 1769480 | tf_op jit(solution)/shard_map/ppermute | solution.py:64
  1049.9 27.1 %collective-permute-start.45 = (bf16[1,96,3072]{2,1,0:T(8,128)(2,1)S(1)}, bf16[1,96,3072]{2,1,0:T(8,128)(2,1)S(1)}, u32[]{:S(2)}, u32[]{:S(2)}) collective-permute-start(bf16[1,96,3072]{2,1,0:T(8,128)(2,1)S(1)} %fusion.151), channel_id=1, source_target_pairs={{0,16},{16,0},{1,17},{17,1},{2,18},{18,2},{3,19},{19,3},{4,20},{20... | collective-permute-start | bytes 1769480 | tf_op jit(solution)/shard_map/ppermute | solution.py:64
  1059.8 17.3 %copy-start.49 = (f32[512,1536]{1,0:T(8,128)}, f32[512,1536]{1,0:T(8,128)S(1)}, u32[]{:S(2)}) copy-start(f32[512,1536]{1,0:T(8,128)S(1)} %fusion.59) | copy-start | bytes 9437188
  1060.8 28.9 %collective-permute-start.21 = (bf16[256,1536]{1,0:T(8,128)(2,1)}, bf16[256,1536]{1,0:T(8,128)(2,1)}, u32[]{:S(2)}, u32[]{:S(2)}) collective-permute-start(bf16[256,1536]{1,0:T(8,128)(2,1)} %slice.471), channel_id=1, source_target_pairs={{0,16},{16,0},{1,17},{17,1},{2,18},{18,2},{3,19},{19,3},{4,20},{20... | collective-permute-start | bytes 2359304 | tf_op jit(solution)/shard_map/ppermute | solution.py:64
  (115 other events, 563.2 us)
Sparse Core Ops, SparseCore 0:
  9.9 129.7 all-gather.9
  141.8 105.2 all-gather.7
  248.7 98.8 all-gather.11
  625.0 56.4 all-gather.15
  1018.8 45.4 all-gather.13

commit v4 on v3

--- a/solution.py
+++ b/solution.py
@@ -28,8 +28,10 @@
     return normalize(values) * scale_vec
 
 
-def exact_gelu(values):
-    return jax.nn.gelu(values, approximate=False)
+def gelu_parts(values):
+    below = 0.5 + 0.5 * lax.erf(values * (0.5**0.5))
+    density = jnp.exp(-0.5 * values * values) * ((2.0 * jnp.pi) ** -0.5)
+    return values * below, below + values * density
 
 
 def matmul(left, right):
@@ -58,10 +60,16 @@
     return lax.axis_size(axis)
 
 
-def swap(array, axis, pairing):
+def swap(array, axis, pairing, log=None):
     length = axis_length(axis)
     pairs = [(i, pairing(i)) for i in range(length)]
+    if log is not None:
+        log.append(array)
     return lax.ppermute(array, axis, [(i, j) for i, j in pairs if 0 <= j < length])
+
+
+def after(values, earlier):
+    return lax.optimization_barrier((values, list(earlier)))[0]
 
 
 def add_low(left, right):
@@ -90,43 +98,46 @@
     return add_low(held, swap(away, "shard", lambda i: i ^ 1))
 
 
-def down_levels(both, level):
+def level_sends(both, level, log=None):
     axis = both.ndim - 3
-    total = pick(both, level, axis).astype(WIDE)
-    for step in range(1, 4):
-        total = total + swap(
-            pick(both, (level + step) % 4, axis), "shard", lambda i: (i + 4 * step) % 16
-        ).astype(WIDE)
+    return [
+        swap(pick(both, (level + step) % 4, axis), "shard", lambda i: (i + 4 * step) % 16, log)
+        for step in range(1, 4)
+    ]
+
+
+def level_total(both, got, level):
+    total = pick(both, level, both.ndim - 3).astype(WIDE)
+    for part in got:
+        total = total + part.astype(WIDE)
     return total.astype(LOW)
 
 
-def box_total(firsts, seconds, side, level, rep):
+def box_middle(firsts, seconds, side, rep, log):
     rows = firsts[0].shape[-2]
     firsts = [part.reshape(4, 2, *part.shape[-2:]) for part in firsts]
     seconds = [part.reshape(4, 2, 2, rows // 2, part.shape[-1]) for part in seconds]
     second = add_low(
         joined([pick(part, rep, 2) for part in seconds]),
-        swap(joined([pick(part, 1 - rep, 2) for part in seconds]), "rep", lambda i: i ^ 1),
+        swap(joined([pick(part, 1 - rep, 2) for part in seconds]), "rep", lambda i: i ^ 1, log),
     )
     first = add_low(
         joined([pick(part, side, 1) for part in firsts]),
-        swap(joined([pick(part, 1 - side, 1) for part in firsts]), "shard", lambda i: i ^ 2),
+        swap(joined([pick(part, 1 - side, 1) for part in firsts]), "shard", lambda i: i ^ 2, log),
     )
     first = first.reshape(4, 2, rows // 2, first.shape[-1])
-    first = add_low(pick(first, rep, 1), swap(pick(first, 1 - rep, 1), "rep", lambda i: i ^ 1))
+    first = add_low(
+        pick(first, rep, 1),
+        swap(pick(first, 1 - rep, 1), "rep", lambda i: i ^ 1, log),
+    )
     second = add_low(
         pick(second, side, 1),
-        swap(pick(second, 1 - side, 1), "shard", lambda i: i ^ 2),
-    )
-    own = down_levels(jnp.concatenate([first, second], axis=2), level)
-    other = swap(own, "rep", lambda i: i ^ 1)
-    low, high = jnp.where(rep == 0, own, other), jnp.where(rep == 0, other, own)
-    return jnp.concatenate([low, high], axis=0)
-
-
-def plane_total(grad):
-    if axis_length("shard") != 16:
-        return lax.psum_scatter(grad, "shard", scatter_dimension=1, tiled=True)
+        swap(pick(second, 1 - side, 1), "shard", lambda i: i ^ 2, log),
+    )
+    return jnp.concatenate([first, second], axis=2)
+
+
+def plane_middle(grad):
     grad, core, side, level, _ = positions(grad)
     count, rows, width = grad.shape[0], grad.shape[1] // 16, grad.shape[2]
     parts = grad.reshape(count, 8, 2, rows, width)
@@ -138,54 +149,25 @@
         pick(held, side, 2),
         swap(pick(held, 1 - side, 2), "shard", lambda i: i ^ 2),
     )
-    return down_levels(held, level)
-
-
-def rep_pair(own):
+    return held, level_sends(held, level), level
+
+
+def rep_pair(own, earlier=()):
     other = swap(own, "rep", lambda i: i ^ 1)
+    if earlier:
+        own, other = after((own, other), earlier)
     rep = lax.axis_index("rep")
     return jnp.where(rep == 0, own, other), jnp.where(rep == 0, other, own)
 
 
-def summed_rows(grads):
-    grads = [grad.astype(LOW) for grad in grads]
-    widths = [grad.shape[1] for grad in grads]
-    if axis_length("shard") == 16 and axis_length("rep") == 2:
-        grads, core, side, level, rep = positions(grads)
-        held = across_cores(grads, core)
-        half = held.shape[-1] // 2
-        whole = box_total([held[..., :half]], [held[..., half:]], side, level, rep)
-    else:
-        share = lax.psum_scatter(joined(grads), "shard", scatter_dimension=0, tiled=True)
-        whole = lax.psum(share.astype(WIDE), "rep")
-    whole = whole.astype(WIDE)
-    out, start = [], 0
-    for width in widths:
-        out.append(whole[:, start : start + width])
-        start += width
-    return out
-
-
-def summed_halves(wide, narrow):
-    wide, narrow = wide.astype(LOW), narrow.astype(LOW)
-    width = wide.shape[1] + narrow.shape[1]
-    if axis_length("shard") == 16 and axis_length("rep") == 2:
-        (wide, narrow), core, side, level, rep = positions((wide, narrow))
-        wide, narrow = (part.reshape(8, -1, part.shape[1]) for part in (wide, narrow))
-        half = width // 2
-        whole = box_total([wide[..., :half]], [wide[..., half:], narrow], side, level, rep)
-        parts = whole.reshape(2, -1, width)
-        got = swap(pick(parts, 1 - core, 0), "shard", lambda i: i ^ 1)
-        return core_pair(pick(parts, core, 0), got, core, 1).astype(WIDE)
-    core = lax.axis_index("shard") % 2
-    grad = joined([wide, narrow])
-    grad = core_pair(grad, jnp.zeros_like(grad), core, 1)
-    share = lax.psum_scatter(grad, "shard", scatter_dimension=0, tiled=True)
-    return lax.psum(share.astype(WIDE), "rep")
-
-
-def summed_vectors(stack):
-    return jnp.sum(lax.all_gather(stack, BOTH), axis=0)
+def rep_rows(own, earlier=()):
+    low, high = rep_pair(own, earlier)
+    return jnp.concatenate([low, high], axis=0)
+
+
+def plain_rows(grads):
+    share = lax.psum_scatter(joined(grads), "shard", scatter_dimension=0, tiled=True)
+    return lax.psum(share.astype(WIDE), "rep").astype(LOW)
 
 
 def head_lanes(which):
@@ -348,6 +330,31 @@
     )(offsets, queries, window, out, logs, grads, *filled)
 
 
+def unpack_kernel(width, own_ref, got_ref, *outs):
+    core = lax.axis_index("shard") % 2
+    for half in range(2):
+        base = half * width // 2
+        whole = jnp.where(core == half, own_ref[...], got_ref[...]).astype(WIDE)
+        for pair in range(width // (4 * HD)):
+            lanes = slice(base + pair * 2 * HD, base + (pair + 1) * 2 * HD)
+            for kind in range(2):
+                start = (2 * pair + kind) * 2 * HD
+                outs[1 + kind][:, lanes] = whole[:, start : start + 2 * HD]
+        outs[0][:, base : base + width // 2] = whole[:, width:]
+
+
+def unpack(own, got):
+    rows, width = own.shape[0], own.shape[1] * 2 // 3
+    return pl.pallas_call(
+        functools.partial(unpack_kernel, width),
+        out_shape=[jax.ShapeDtypeStruct((rows, width), WIDE)] * 3,
+        cost_estimate=pl.CostEstimate(
+            flops=0, transcendentals=0, bytes_accessed=18 * rows * width
+        ),
+        name="unpack_query_key_value",
+    )(own, got)
+
+
 def core_pair(own, got, core, axis):
     return jnp.where(
         core == 0,
@@ -386,7 +393,7 @@
     key_scale = HD ** (-0.5)
     clip_total = text_states.shape[0]
     text_rows = text_states.shape[1]
-    shard_count = axis_length("shard")
+    shard_count, rep_count = axis_length("shard"), axis_length("rep")
     shard_rows = x_key.shape[0]
     place = lax.axis_index("rep") * shard_count + lax.axis_index("shard")
     core, side = place % 2, (place // 2) % 2
@@ -414,10 +421,10 @@
     gain_one, bias_one, gain_two, bias_two, gain_three, bias_three = (
         first_group[:, 4 * model_width + i].astype(WIDE) for i in range(6)
     )
-    part_query, part_pair = (
-        lax.dynamic_slice_in_dim(first_group, core * (3 * half_width) + begin, width, 1)
-        for begin, width in ((0, half_width), (half_width, model_width))
-    )
+    part_all = lax.dynamic_slice_in_dim(
+        first_group, core * (3 * half_width), 3 * half_width, 1
+    )
+    part_query, part_pair = part_all[:, :half_width], part_all[:, half_width:]
     second_group = gather_rows(jnp.concatenate([x_query, x_key, x_value, x_output], axis=1))
     full_xquery, full_xkey, full_xvalue, full_xoutput = (
         second_group[:, i * model_width : (i + 1) * model_width] for i in range(4)
@@ -453,6 +460,7 @@
     halo_rows = tok_rows + 2 * chip_rows
     normed_plain = normalize(around.astype(WIDE))
     normed_around = (normed_plain * gain_one + bias_one).astype(LOW)
+    normed_plain = normed_plain.astype(LOW)
     normed_chip = normed_around[halo_rows:]
     window = matmul(normed_around, part_pair).astype(LOW)
     queries = matmul(normed_chip, part_query).astype(LOW)
@@ -503,9 +511,8 @@
     activ, slope, grad_pre = [], [], []
     for i in range(2):
         pre_act = matmul(both_three, half_up[:, i * quarter : (i + 1) * quarter])
-        shaped, gelu_pull = jax.vjp(exact_gelu, pre_act)
-        shaped, steep = shaped.astype(LOW), gelu_pull(jnp.ones_like(pre_act))[0]
-        shaped, steep = lax.optimization_barrier((shaped, steep))
+        shaped, steep = gelu_parts(pre_act)
+        shaped, steep = lax.optimization_barrier((shaped.astype(LOW), steep))
         activ.append(shaped)
         slope.append(steep)
     for i in range(2):
@@ -517,8 +524,9 @@
     ).astype(WIDE)
     grad_down = left_t(activ, upstream).astype(LOW).reshape(2, -1, model_width)
     grad_up = left_t(both_three, grad_pre).astype(LOW)
-    own_down = plane_total(grad_down)
-    own_up = plane_total(grad_up[None])
+    if shard_count == 16:
+        down_held, down_got, down_level = plane_middle(grad_down)
+        up_held, up_got, up_level = plane_middle(grad_up[None])
     norm_three_part, grad_gain_three, grad_bias_three = norm_back(
         after_cross, gain_three, grad_norm_three
     )
@@ -537,33 +545,33 @@
     )
     grad_ck = (
         jnp.einsum("htk,thd->hdk", grad_cscore, cq_heads, preferred_element_type=WIDE) * key_scale
-    ).reshape(model_width, 2, text_rows)
+    ).reshape(model_width, 2 * text_rows)
     grad_cv = jnp.einsum(
         "htk,thd->hdk", cross_low, grad_cmix, preferred_element_type=WIDE
-    ).reshape(model_width, 2, text_rows)
-    slots = jnp.arange(clip_total, dtype=jnp.int32)
-    in_first, in_second = (
-        (slots == clip).astype(WIDE)[None, :, None] for clip in (first, second)
-    )
-    text_sums = [
-        (part[:, :1] * in_first + part[:, 1:] * in_second).reshape(model_width, -1)
-        for part in (grad_ck, grad_cv)
-    ]
-    text_sums = jnp.concatenate(text_sums, axis=1)
-    text_cols = text_sums.shape[1]
-    text_sums = jnp.pad(text_sums, ((0, 0), (0, -text_cols % 256)))
+    ).reshape(model_width, 2 * text_rows)
+    text_pair = jnp.concatenate([grad_ck, grad_cv], axis=1).astype(LOW)
+    flat_rows = clip_total * text_rows
+    text_cols = 2 * flat_rows
+    target = jnp.concatenate([slot_clip, slot_clip + clip_total]) * text_rows
+    target = target + jnp.arange(4 * text_rows, dtype=jnp.int32) % text_rows
+    spread_text = target[:, None] == jnp.arange(text_cols, dtype=jnp.int32)[None, :]
+    text_sums = matmul(text_pair, spread_text.astype(LOW)).astype(LOW)
     grad_xquery = left_t(normed_two, grad_cq)
     grad_norm_two = right_t(grad_cq, full_xquery)
     norm_two_part, grad_gain_two, grad_bias_two = norm_back(after_self, gain_two, grad_norm_two)
     grad_self_res = grad_cross_res + norm_two_part
     branch_one = grad_self_res.astype(LOW)
     grad_output = left_t(attended, branch_one)
-    fin_xoutput, fin_xquery, fin_output, text_share = summed_rows(
-        [grad_xoutput, grad_xquery, grad_output, text_sums]
-    )
-    text_whole = lax.all_gather(text_share.astype(LOW), "shard", axis=0, tiled=True)
-    flat_rows = clip_total * text_rows
-
+    text_share = lax.psum_scatter(text_sums, BOTH, scatter_dimension=0, tiled=True)
+    staged = shard_count == 16 and rep_count == 2
+    if staged:
+        grads, x_core, x_side, x_level, x_rep = positions(
+            [grad.astype(LOW) for grad in (grad_xoutput, grad_xquery, grad_output)]
+        )
+        held = across_cores(grads, x_core)
+        middle = held.shape[-1] // 2
+        x_both = box_middle([held[..., :middle]], [held[..., middle:]], x_side, x_rep, [])
+        x_got = level_sends(x_both, x_level)
     grad_attended = right_t(branch_one, full_output).astype(LOW)
     halves = jnp.transpose(grad_attended.reshape(tok_rows, 2, half_width), (1, 0, 2))
     chip_grad = core_pair(
@@ -590,61 +598,97 @@
     chip_dq, grad_window = backs
     grad_pair = left_t(normed_around, grad_window)
     grad_wq = left_t(normed_chip, chip_dq)
-    _, own_down, own_up, after_late, activ_late = lax.optimization_barrier(
-        (grad_wq, own_down, own_up, after_cross, activ)
-    )
-    down_halves = rep_pair(own_down)
-    fin_down = jnp.concatenate(down_halves, axis=0).reshape(w_down.shape).astype(WIDE)
-    up_halves = rep_pair(own_up)
-    fin_up = jnp.stack(
-        [half.reshape(w_up.shape[0], 2, shard_count, chunk) for half in up_halves], axis=1
-    )
-    fin_up = jnp.transpose(fin_up, (0, 3, 1, 2, 4)).reshape(w_up.shape).astype(WIDE)
-    mixed_both = matmul(activ_late[:, :quarter], half_down[0]) + matmul(
-        activ_late[:, quarter:], half_down[1]
-    )
-    block_out = (
-        after_late
-        + mixed_both[:tok_rows]
-        + swap(mixed_both[tok_rows:].astype(LOW), "rep", lambda i: i ^ 1).astype(WIDE)
-    ).astype(LOW)
-    fin_halves = summed_halves(grad_pair, grad_wq).reshape(shard_rows, 2, 3 * half_width)
-    fin_pair = fin_halves[:, :, :model_width].reshape(shard_rows, 2, pairs, 2, 2 * HD)
-    fin_query = fin_halves[:, :, model_width:].reshape(w_query.shape)
-    fin_key = fin_pair[:, :, :, 0].reshape(w_query.shape)
-    fin_value = fin_pair[:, :, :, 1].reshape(w_query.shape)
-    grad_around = right_t(grad_window, part_pair)
-    grad_chip = grad_around[halo_rows:] + right_t(chip_dq, part_query)
-    around_sums = [
-        jnp.sum(grad_around[:halo_rows] * normed_plain[:halo_rows], axis=0)
-        + jnp.sum(grad_chip * normed_plain[halo_rows:], axis=0),
-        jnp.sum(grad_around[:halo_rows], axis=0) + jnp.sum(grad_chip, axis=0),
+    grad_pair, grad_wq = grad_pair.astype(LOW), grad_wq.astype(LOW)
+    sent_first, sent_last = [], []
+    if staged:
+        (wide, narrow), q_core, q_side, q_level, q_rep = positions((grad_pair, grad_wq))
+        wide, narrow = (part.reshape(8, -1, part.shape[1]) for part in (wide, narrow))
+        middle = 3 * half_width // 2
+        q_both = box_middle(
+            [wide[..., :middle]], [wide[..., middle:], narrow], q_side, q_rep, sent_first
+        )
+    text_share, grad_window, chip_dq = after((text_share, grad_window, chip_dq), sent_first[:2])
+    text_whole = lax.all_gather(text_share, BOTH, axis=0, tiled=True)
+    grad_halo = right_t(grad_window[:halo_rows], part_pair)
+    halo_sums = [
+        jnp.sum(grad_halo * normed_plain[:halo_rows].astype(WIDE), axis=0),
+        jnp.sum(grad_halo, axis=0),
     ]
-    grad_halo = grad_around[:halo_rows].astype(LOW)
-    _, text_whole = lax.optimization_barrier((grad_halo, text_whole))
-    key_round, value_round = (
-        text_whole[:, :flat_rows],
-        text_whole[:, flat_rows : 2 * flat_rows],
-    )
-    col_start = lax.axis_index("shard") * shard_rows
-    text_flat = text_states.reshape(flat_rows, model_width)
-    text_slice = lax.dynamic_slice_in_dim(text_flat, col_start, shard_rows, 1)
-
-    def mixed_dims(left, right):
-        return lax.dot_general(
-            left, right, (((0,), (1,)), ((), ())), preferred_element_type=WIDE
-        )
-
-    grad_xkey = mixed_dims(text_slice, key_round)
-    grad_xvalue = mixed_dims(text_slice, value_round)
-    grad_text = mixed_dims(key_round, full_xkey) + mixed_dims(value_round, full_xvalue)
-    grad_text = grad_text.reshape(clip_total, text_rows, model_width)
+    grad_chip = right_t(
+        jnp.concatenate([chip_dq, grad_window[halo_rows:]], axis=1), part_all
+    )
+    chip_sums = [
+        jnp.sum(grad_chip * normed_plain[halo_rows:].astype(WIDE), axis=0),
+        jnp.sum(grad_chip, axis=0),
+    ]
+    around_sums = [halo_sums[i] + chip_sums[i] for i in range(2)]
+    grad_halo = grad_halo.astype(LOW)
     units = jnp.concatenate([grad_halo[tok_rows:], grad_chip.astype(LOW)], axis=0)
     units = units.reshape(3, 2, tok_rows, model_width)
     sent = jnp.concatenate([pick(units, 1 - core, 1), grad_halo[None, :tok_rows]], axis=0)
     partner = swap(sent, BOTH, lambda i: i ^ 1)
     sums = add_low(pick(units, core, 1), partner[:3])
     low_sum = add_low(grad_halo[:tok_rows], partner[3])
+    if staged:
+        q_both = after(q_both, [sums, low_sum])
+        q_got = level_sends(q_both, q_level, sent_last)
+        q_own = level_total(q_both, q_got, q_level)
+        parts = rep_rows(q_own).reshape(2, shard_rows, 3 * half_width)
+        q_swapped = swap(pick(parts, 1 - q_core, 0), "shard", lambda i: i ^ 1)
+        fin_query, fin_key, fin_value = unpack(pick(parts, q_core, 0), q_swapped)
+        x_own = level_total(x_both, after(x_got, sent_first[2:]), x_level)
+        fin_x = rep_rows(x_own, sent_last)
+    else:
+        filled = joined([grad_pair, grad_wq])
+        fin_halves = plain_rows([core_pair(filled, jnp.zeros_like(filled), core, 1)])
+        fin_x = plain_rows([grad.astype(LOW) for grad in (grad_xoutput, grad_xquery, grad_output)])
+        fin_halves = fin_halves.astype(WIDE).reshape(shard_rows, 2, 3 * half_width)
+        fin_pair = fin_halves[:, :, :model_width].reshape(shard_rows, 2, pairs, 2, 2 * HD)
+        fin_query = fin_halves[:, :, model_width:].reshape(w_query.shape)
+        fin_key = fin_pair[:, :, :, 0].reshape(w_query.shape)
+        fin_value = fin_pair[:, :, :, 1].reshape(w_query.shape)
+    fin_xoutput, fin_xquery, fin_output = (
+        fin_x[:, i * model_width : (i + 1) * model_width].astype(WIDE) for i in range(3)
+    )
+    if staged:
+        down_got, up_got = after((down_got, up_got), sent_first[2:])
+        own_down = level_total(down_held, down_got, down_level)
+        own_up = level_total(up_held, up_got, up_level)
+    else:
+        own_down = lax.psum_scatter(grad_down, "shard", scatter_dimension=1, tiled=True)
+        own_up = lax.psum_scatter(grad_up[None], "shard", scatter_dimension=1, tiled=True)
+    down_halves = rep_pair(own_down, sent_last)
+    fin_down = jnp.concatenate(down_halves, axis=0).reshape(w_down.shape).astype(WIDE)
+    up_halves = rep_pair(own_up, sent_last)
+    fin_up = jnp.stack(
+        [half.reshape(w_up.shape[0], 2, shard_count, chunk) for half in up_halves], axis=1
+    )
+    fin_up = jnp.transpose(fin_up, (0, 3, 1, 2, 4)).reshape(w_up.shape).astype(WIDE)
+    activ_late, after_late = after((activ, after_cross), [grad_chip])
+    mixed_both = matmul(activ_late[:, :quarter], half_down[0]) + matmul(
+        activ_late[:, quarter:], half_down[1]
+    )
+    y_got = swap(mixed_both[tok_rows:].astype(LOW), "rep", lambda i: i ^ 1)
+    y_own, y_got, after_late = after((mixed_both[:tok_rows], y_got, after_late), sent_last)
+    block_out = (after_late + y_own + y_got.astype(WIDE)).astype(LOW)
+    text_whole = after(text_whole, sent_last)
+    key_round, value_round = (
+        text_whole[:, :flat_rows],
+        text_whole[:, flat_rows : 2 * flat_rows],
+    )
+    col_start = lax.axis_index("shard") * shard_rows
+    text_flat = text_states.reshape(flat_rows, model_width)
+    text_slice = lax.dynamic_slice_in_dim(text_flat, col_start, shard_rows, 1)
+
+    def mixed_dims(left, right):
+        return lax.dot_general(
+            left, right, (((0,), (1,)), ((), ())), preferred_element_type=WIDE
+        )
+
+    grad_xkey = mixed_dims(text_slice, key_round)
+    grad_xvalue = mixed_dims(text_slice, value_round)
+    grad_text = mixed_dims(key_round, full_xkey) + mixed_dims(value_round, full_xvalue)
+    grad_text = grad_text.reshape(clip_total, text_rows, model_width)
     back = swap(sums[1], BOTH, lambda i: i ^ 2).astype(WIDE)
     back_half = swap(low_sum, BOTH, lambda i: i ^ 2 if i % 2 == 1 else -1)
     to_below = (
@@ -659,7 +703,7 @@
     norm_one_part, _, _ = norm_back(resid, gain_one, grad_norm_one)
     grad_gain_one, grad_bias_one = around_sums
     grad_hidden = (grad_self_res + norm_one_part).astype(LOW)
-    vectors = summed_vectors(
+    vectors = lax.all_gather(
         jnp.stack(
             [
                 grad_gain_one,
@@ -670,7 +714,10 @@
                 grad_bias_three,
             ]
         ),
-    )
+        BOTH,
+    )
+    _, vectors = lax.optimization_barrier((to_below, vectors))
+    vectors = jnp.sum(vectors, axis=0)
     fin_gain_one, fin_bias_one, fin_gain_two, fin_bias_two, fin_gain_three, fin_bias_three = (
         lax.dynamic_slice_in_dim(vectors, col_start, shard_rows, 1)
     )

time: 1130 us -> 1160 us (1.027)
  the two profiles are of different devices: /device:TPU:9 before, /device:TPU:0 now
where the time goes in v4:
time: 1160 us; the launch traced here: 1140 us
  waiting for transfers between devices  453 us (39%)
  matrix products  193 us (17%)
  starting transfers between devices  174 us (15%)
  other arithmetic  119 us (10%)
  local copies, waits for them, and re-layouts  109 us (9%)
  Pallas kernels  76 us (7%)
  between operations  19.9 us (2%)
    ppermute x47, waiting for transfers between devices, swap(): lax.ppermute(array, axis, [(i, j) for i, j in pairs if 0 <= j < length])  344 us
    ppermute x47, starting transfers between devices, swap(): lax.ppermute(array, axis, [(i, j) for i, j in pairs if 0 <= j < length])  173 us
    all_gather x3, waiting for transfers between devices, gather_rows(): return lax.all_gather(array, 'shard', axis=0, tiled=True)  79.6 us
    dot_general x12, matrix products, matmul(): return jnp.dot(left, right, preferred_element_type=WIDE)  65.5 us
    dot_general x8, matrix products, right_t(): lax.dot_general(left, right, (((1,), (1,)), ((), ())), preferred_element_...  50.3 us
    dot_general x7, matrix products, left_t(): lax.dot_general(left, right, (((0,), (0,)), ((), ())), preferred_element_...  48.7 us
    pallas_call x2, Pallas kernels, attend_back(): pl.pallas_call(functools.partial(attend_back_kernel, reach), grid=(pairs,...  47.5 us
    convert_element_type x15, other arithmetic, add_low(): return (left.astype(WIDE) + right.astype(WIDE)).astype(LOW)  40.4 us
  transfers between devices with their start and end apart: 53, of which 24 were waited for; matrix products, arithmetic and copies ran while one was open for 30% of the time, Pallas kernels for 7%

profile of v4, /device:TPU:0, one launch (start us, length us, event | category | flops | bytes accessed | tf_op | source)
XLA Modules:
  0.0 1144.2 jit_solution(8728214231756419018)
XLA Ops:
  13.4 5.5 reshape.534
  22.0 5.0 collective-permute-start.1
  27.8 33.6 %collective-permute-done.1 = bf16[256,1536]{1,0:T(8,128)(2,1)S(1)} collective-permute-done((bf16[256,1536]{1,0:T(8,128)(2,1)S(1)}, bf16[256,1536]{1,0:T(8,128)(2,1)S(1)}, u32[]{:S(2)}, u32[]{:S(2)}) %collective-permute-start.1) | collective-permute-done | bytes 786464 | tf_op jit(solution)/shard_map/ppermute | solution.py:68
  64.4 23.3 %collective-permute-done.4 = bf16[256,1536]{1,0:T(8,128)(2,1)S(1)} collective-permute-done((bf16[256,1536]{1,0:T(8,128)(2,1)S(1)}, bf16[256,1536]{1,0:T(8,128)(2,1)S(1)}, u32[]{:S(2)}, u32[]{:S(2)}) %collective-permute-start.4) | collective-permute-done | bytes 786464 | tf_op jit(solution)/shard_map/ppermute | solution.py:68
  89.6 53.7 %collective-permute-start.5 = (bf16[4,256,1536]{2,1,0:T(8,128)(2,1)}, bf16[4,256,1536]{2,1,0:T(8,128)(2,1)}, u32[]{:S(2)}, u32[]{:S(2)}) collective-permute-start(bf16[4,256,1536]{2,1,0:T(8,128)(2,1)} %pad_maximum_fusion.3), channel_id=1, source_target_pairs={{0,1},{1,0},{2,3},{3,2},{4,5},{5,4},{6,7},{7,6},{8,9},{9,8},{10,11... | collective-permute-start | bytes 9437192 | tf_op jit(solution)/shard_map/ppermute | solution.py:68
  159.3 9.2 fusion.7
  173.5 75.4 %all-gather.8.cloned.1.call-done = bf16[1536,6272]{1,0:T(8,128)(2,1)} async-done(((bf16[96,6272]{1,0:T(8,128)(2,1)}), bf16[1536,6272]{1,0:T(8,128)(2,1)}) %all-gather.8.cloned.1.call-update) | async-done | bytes 19267600 | tf_op jit(solution)/shard_map/all_gather | solution.py:80
  249.0 4.1 convert_reduce_fusion.3
  253.1 12.5 %fusion.3 = (bf16[1792,1536]{1,0:T(8,128)(2,1)}, bf16[1792,1536]{1,0:T(8,128)(2,1)S(1)}) fusion(f32[1792]{0:T(1024)S(1)} %copy-done.72, f32[1792]{0:T(1024)S(1)} %copy-done.68, bf16[512,1536]{1,0:T(8,128)(2,1)S(1)} %copy-done.5, bf16[512,1536]{1,0:T(8,128)(2,1)} %copy-done.6, bf16[512,1536]{1,0:T(8,128)(2,1)S(1)} %get-tuple-element.160, ...), kind=kLoop, calls=%fused_computation.6 | loop fusion | flops 38535168 | bytes 16541696 | tf_op jit(solution)/shard_map/convert_element_type | solution.py:463
  265.6 5.8 fusion.131.query_ref
  271.4 13.4 %convolution_convert_fusion.5.window_ref = bf16[1792,1536]{1,0:T(8,128)(2,1)} fusion(bf16[1792,1536]{1,0:T(8,128)(2,1)S(1)} %get-tuple-element.153, bf16[1536,6272]{1,0:T(8,128)(2,1)} %all-gather.8.cloned.1.call-done, s32[]{:T(128)S(6)} %add.727), kind=kOutput, calls=%fused_computation.24 | convolution fusion | flops 8458469376 | bytes 15728644 | tf_op jit(solution)/shard_map/dot_general | solution.py:38
  284.7 26.1 %attend_forward.1 = (bf16[512,768]{1,0:T(8,128)(2,1)}, f32[6,2,512]{2,1,0:T(2,128)}) custom-call(s32[1,512]{1,0:T(1,128)} %broadcast_select_fusion.10.offset_ref, bf16[512,768]{1,0:T(8,128)(2,1)} %fusion.131.query_ref, bf16[1792,1536]{1,0:T(8,128)(2,1)} %convolution_convert_fusion.5.window_ref), custom_call_target="tpu_custom_call" | custom-call | flops 9663676416 | bytes 3145728 | tf_op jit(solution)/shard_map/attend_forward/pallas_call | solution.py:218
  316.5 4.3 fusion.213
  331.9 4.3 fusion.215
  345.3 4.2 all-gather.12.cloned.1.call-done
  349.5 9.1 collective-permute-done.7
  358.5 7.8 fusion.69
  366.6 7.9 fusion.73
  374.7 10.0 convolution_convert_fusion
  384.7 6.6 fusion.77
  391.3 6.0 fusion.80
  398.5 9.0 fusion.8
  407.5 8.8 fusion.9
  420.4 4.9 dynamic-slice_bitcast_fusion
  425.3 4.7 dynamic-slice_bitcast_fusion.1
  430.6 7.5 collective-permute-done.9
  461.5 4.1 multiply_reduce_fusion.4
  472.7 4.6 fusion.89
  484.3 23.6 %attend_backward.2 = (bf16[512,768]{1,0:T(8,128)(2,1)}, bf16[1792,1536]{1,0:T(8,128)(2,1)}) custom-call(s32[1,512]{1,0:T(1,128)} %broadcast_select_fusion.10.offset_ref, bf16[512,768]{1,0:T(8,128)(2,1)} %fusion.131.query_ref, bf16[1792,1536]{1,0:T(8,128)(2,1)} %convolution_convert_fusion.5.window_ref, bf16[512,768]{1,0:T(8,128)(2,1)} %get-tuple-element.71.out_ref, ...), custom_call_target="tpu_custom_call" | custom-call | flops 12079595520 | bytes 6291456 | tf_op jit(solution)/shard_map/attend_backward/pallas_call | solution.py:304
  507.9 23.9 %attend_backward.3 = (bf16[512,768]{1,0:T(8,128)(2,1)}, bf16[1792,1536]{1,0:T(8,128)(2,1)}) custom-call(s32[1,512]{1,0:T(1,128)} %broadcast_select_fusion.10.offset_ref, bf16[512,768]{1,0:T(8,128)(2,1)} %fusion.131.query_ref, bf16[1792,1536]{1,0:T(8,128)(2,1)} %convolution_convert_fusion.5.window_ref, ...), custom_call_target="tpu_custom_call", output_to_operand_aliasing={{0}: (6, {}), {1}: (7, {})} | custom-call | flops 12079595520 | bytes 6291456 | tf_op jit(solution)/shard_map/attend_backward/pallas_call | solution.py:304
  531.7 14.1 %convolution_convert_fusion.6 = bf16[1536,1536]{1,0:T(8,128)(2,1)} fusion(bf16[1792,1536]{1,0:T(8,128)(2,1)} %copy-done.31, bf16[1792,1536]{1,0:T(8,128)(2,1)} %get-tuple-element.86), kind=kOutput, calls=%fused_computation.25 | convolution fusion | flops 8458076160 | bytes 15728640 | tf_op jit(solution)/shard_map/dot_general | solution.py:42
  545.8 4.2 convolution_convert_fusion.8
  563.1 4.1 slice.264
  571.3 5.4 dynamic-slice_bitcast_fusion.9
  580.7 18.1 %collective-permute-done.14 = bf16[4,2,96,1152]{3,2,1,0:T(8,128)(2,1)} collective-permute-done((bf16[4,2,96,1152]{3,2,1,0:T(8,128)(2,1)}, bf16[4,2,96,1152]{3,2,1,0:T(8,128)(2,1)}, u32[]{:S(2)}, u32[]{:S(2)}) %collective-permute-start.14) | collective-permute-done | bytes 1769504 | tf_op jit(solution)/shard_map/ppermute | solution.py:68
  603.3 8.7 collective-permute-done.12
  619.2 15.6 %collective-permute-done.15 = bf16[4,96,1152]{2,1,0:T(8,128)(2,1)} collective-permute-done((bf16[4,96,1152]{2,1,0:T(8,128)(2,1)S(1)}, bf16[4,96,1152]{2,1,0:T(8,128)(2,1)}, u32[]{:S(2)}, u32[]{:S(2)}) %collective-permute-start.15) | collective-permute-done | bytes 884768 | tf_op jit(solution)/shard_map/ppermute | solution.py:68
  639.3 28.7 %reduce-scatter.2.cloned.1.call-done = bf16[48,896]{1,0:T(8,128)(2,1)} async-done(((bf16[1536,896]{1,0:T(8,128)(2,1)}), bf16[48,896]{1,0:T(8,128)(2,1)}) %reduce-scatter.2.cloned.1.call-update) | async-done | bytes 86032 | tf_op jit(solution)/shard_map/reduce_scatter | solution.py:565
  669.6 7.7 fusion.208
  677.4 8.7 fusion.207
  692.4 5.3 fusion.11
  702.0 5.7 fusion.12
  711.9 4.5 fusion.22
  716.4 4.5 fusion.63
  724.9 34.4 %collective-permute-done.38 = bf16[2,4,96,1536]{3,2,1,0:T(8,128)(2,1)} collective-permute-done((bf16[2,4,96,1536]{3,2,1,0:T(8,128)(2,1)}, bf16[2,4,96,1536]{3,2,1,0:T(8,128)(2,1)}, u32[]{:S(2)}, u32[]{:S(2)}) %collective-permute-start.38) | collective-permute-done | bytes 2359328 | tf_op jit(solution)/shard_map/ppermute | solution.py:68
  764.0 53.4 %collective-permute-done.36 = bf16[1,4,96,3072]{3,2,1,0:T(8,128)(2,1)} collective-permute-done((bf16[1,4,96,3072]{3,2,1,0:T(8,128)(2,1)}, bf16[1,4,96,3072]{3,2,1,0:T(8,128)(2,1)}, u32[]{:S(2)}, u32[]{:S(2)}) %collective-permute-start.36) | collective-permute-done | bytes 2359328 | tf_op jit(solution)/shard_map/ppermute | solution.py:68
  832.7 15.3 %collective-permute-done.40 = bf16[2,96,1536]{2,1,0:T(8,128)(2,1)S(1)} collective-permute-done((bf16[2,96,1536]{2,1,0:T(8,128)(2,1)S(1)}, bf16[2,96,1536]{2,1,0:T(8,128)(2,1)S(1)}, u32[]{:S(2)}, u32[]{:S(2)}) %collective-permute-start.40) | collective-permute-done | bytes 589856 | tf_op jit(solution)/shard_map/ppermute | solution.py:68
  848.0 14.4 %collective-permute-start.44 = (bf16[1,96,3072]{2,1,0:T(8,128)(2,1)S(1)}, bf16[1,96,3072]{2,1,0:T(8,128)(2,1)S(1)}, u32[]{:S(2)}, u32[]{:S(2)}) collective-permute-start(bf16[1,96,3072]{2,1,0:T(8,128)(2,1)S(1)} %get-tuple-element.170), channel_id=1, source_target_pairs={{0,12},{1,13},{2,14},{3,15},{4,0},{5,1},{6,2},{7,3},{8,4},{9,5},{1... | collective-permute-start | bytes 1769480 | tf_op jit(solution)/shard_map/ppermute | solution.py:68
  865.4 5.4 collective-permute-start.23
  870.8 26.4 %collective-permute-done.43 = bf16[1,96,3072]{2,1,0:T(8,128)(2,1)S(1)} collective-permute-done((bf16[1,96,3072]{2,1,0:T(8,128)(2,1)S(1)}, bf16[1,96,3072]{2,1,0:T(8,128)(2,1)S(1)}, u32[]{:S(2)}, u32[]{:S(2)}) %collective-permute-start.43) | collective-permute-done | bytes 589856 | tf_op jit(solution)/shard_map/ppermute | solution.py:68
  897.2 10.5 collective-permute-start.22
  907.8 23.5 %collective-permute-start.21 = (bf16[96,2304]{1,0:T(8,128)(2,1)S(1)}, bf16[96,2304]{1,0:T(8,128)(2,1)S(1)}, u32[]{:S(2)}, u32[]{:S(2)}) collective-permute-start(bf16[96,2304]{1,0:T(8,128)(2,1)S(1)} %get-tuple-element.183), channel_id=1, source_target_pairs={{0,4},{1,5},{2,6},{3,7},{4,8},{5,9},{6,10},{7,11},{8,12},{9,13},{1... | collective-permute-start | bytes 1327112 | tf_op jit(solution)/shard_map/ppermute | solution.py:68
  933.0 4.5 add_convert_fusion
  944.7 6.1 collective-permute-done.21
  952.6 6.2 collective-permute-done.45
  962.5 9.1 collective-permute-done.46
  980.7 36.4 %collective-permute-done.24 = bf16[96,2304]{1,0:T(8,128)(2,1)S(1)} collective-permute-done((bf16[96,2304]{1,0:T(8,128)(2,1)}, bf16[96,2304]{1,0:T(8,128)(2,1)S(1)}, u32[]{:S(2)}, u32[]{:S(2)}) %collective-permute-start.24) | collective-permute-done | bytes 442400 | tf_op jit(solution)/shard_map/ppermute | solution.py:68
  1022.1 5.8 reshape.586
  1047.9 5.6 fusion.34
  1053.5 9.9 collective-permute-done.28
  1070.1 24.5 %collective-permute-start.32 = (bf16[48,4608]{1,0:T(8,128)(2,1)S(1)}, bf16[48,4608]{1,0:T(8,128)(2,1)S(1)}, u32[]{:S(2)}, u32[]{:S(2)}) collective-permute-start(bf16[48,4608]{1,0:T(8,128)(2,1)S(1)} %get-tuple-element.180), channel_id=1, source_target_pairs={{0,8},{1,9},{2,10},{3,11},{4,12},{5,13},{6,14},{7,15},{8,0},{9,1},... | collective-permute-start | bytes 1327112 | tf_op jit(solution)/shard_map/ppermute | solution.py:68
  1094.8 7.1 fusion.74
  1105.1 18.2 %collective-permute-done.32 = bf16[48,4608]{1,0:T(8,128)(2,1)S(1)} collective-permute-done((bf16[48,4608]{1,0:T(8,128)(2,1)S(1)}, bf16[48,4608]{1,0:T(8,128)(2,1)S(1)}, u32[]{:S(2)}, u32[]{:S(2)}) %collective-permute-start.32) | collective-permute-done | bytes 442400 | tf_op jit(solution)/shard_map/ppermute | solution.py:68
  1130.3 5.3 collective-permute-done.34
  (496 shorter events, 248.2 us)
Async XLA Ops:
  7.2 161.9 %all-gather.10.cloned.1.call-start = ((), (), s32[]{:S(2)}) async-start(), calls=%async_computation.2 | async-start | bytes 20054016 | tf_op jit(solution)/shard_map/all_gather | solution.py:80
  9.7 239.3 %all-gather.8.cloned.1.call-start = ((), (), s32[]{:S(2)}) async-start(), calls=%async_computation.1 | async-start | bytes 20471808 | tf_op jit(solution)/shard_map/all_gather | solution.py:80
  13.3 336.2 %all-gather.12.cloned.1.call-start = ((), (), s32[]{:S(2)}) async-start(), calls=%async_computation.3 | async-start | bytes 20054016 | tf_op jit(solution)/shard_map/all_gather | solution.py:80
  22.0 645.9 %reduce-scatter.2.cloned.1.call-start = ((), (), s32[]{:S(2)}) async-start(), calls=%async_computation.4 | async-start | bytes 2838528 | tf_op jit(solution)/shard_map/reduce_scatter | solution.py:565
  22.0 39.4 %collective-permute-start.1 = (bf16[256,1536]{1,0:T(8,128)(2,1)S(1)}, bf16[256,1536]{1,0:T(8,128)(2,1)S(1)}, u32[]{:S(2)}, u32[]{:S(2)}) collective-permute-start(bf16[256,1536]{1,0:T(8,128)(2,1)S(1)} %copy-done.2), channel_id=1, source_target_pairs={{0,4},{1,5},{2,6},{3,7},{4,8},{5,9},{6,10},{7,11},{8,12},{9,13},{1... | collective-permute-start | bytes 2359304 | tf_op jit(solution)/shard_map/ppermute | solution.py:68
  27.1 34.4 %collective-permute-start.2 = (bf16[256,1536]{1,0:T(8,128)(2,1)S(1)}, bf16[256,1536]{1,0:T(8,128)(2,1)S(1)}, u32[]{:S(2)}, u32[]{:S(2)}) collective-permute-start(bf16[256,1536]{1,0:T(8,128)(2,1)S(1)} %copy-done.2), channel_id=1, source_target_pairs={{3,11},{7,15},{11,19},{15,23},{19,27},{23,31}} | collective-permute-start | bytes 2359304 | tf_op jit(solution)/shard_map/ppermute | solution.py:68
  61.6 2.8 collective-permute-start.3
  62.5 25.2 %collective-permute-start.4 = (bf16[256,1536]{1,0:T(8,128)(2,1)S(1)}, bf16[256,1536]{1,0:T(8,128)(2,1)S(1)}, u32[]{:S(2)}, u32[]{:S(2)}) collective-permute-start(bf16[256,1536]{1,0:T(8,128)(2,1)S(1)} %get-tuple-element.207), channel_id=1, source_target_pairs={{0,2},{1,3},{2,0},{3,1},{4,6},{5,7},{6,4},{7,5},{8,10},{9,11},{10,... | collective-permute-start | bytes 2359304 | tf_op jit(solution)/shard_map/ppermute | solution.py:68
  87.7 55.6 %copy-start.95 = (s32[256]{0:T(256)S(1)}, s32[256]{0:T(256)}, u32[]{:S(2)}) copy-start(s32[256]{0:T(256)} %param.24) | copy-start | bytes 3076
  87.7 55.7 %copy-start.94 = (s32[256]{0:T(256)S(1)}, s32[256]{0:T(256)}, u32[]{:S(2)}) copy-start(s32[256]{0:T(256)} %param.23) | copy-start | bytes 3076
  89.6 62.6 %collective-permute-start.5 = (bf16[4,256,1536]{2,1,0:T(8,128)(2,1)}, bf16[4,256,1536]{2,1,0:T(8,128)(2,1)}, u32[]{:S(2)}, u32[]{:S(2)}) collective-permute-start(bf16[4,256,1536]{2,1,0:T(8,128)(2,1)} %pad_maximum_fusion.3), channel_id=1, source_target_pairs={{0,1},{1,0},{2,3},{3,2},{4,5},{5,4},{6,7},{7,6},{8,9},{9,8},{10,11... | collective-permute-start | bytes 9437192 | tf_op jit(solution)/shard_map/ppermute | solution.py:68
  143.4 8.3 collective-permute-start
  143.4 199.8 %collective-permute-start.8 = (bf16[256,1536]{1,0:T(8,128)(2,1)}, bf16[256,1536]{1,0:T(8,128)(2,1)}, u32[]{:S(2)}, u32[]{:S(2)}) collective-permute-start(bf16[256,1536]{1,0:T(8,128)(2,1)} %param.41), channel_id=1, source_target_pairs={{0,16},{16,0},{1,17},{17,1},{2,18},{18,2},{3,19},{19,3},{4,20},{20... | collective-permute-start | bytes 2359304 | tf_op jit(solution)/shard_map/ppermute | solution.py:68
  173.5 79.6 %copy-start.68 = (f32[1792]{0:T(1024)S(1)}, f32[1792]{0:T(1024)}, u32[]{:S(2)}) copy-start(f32[1792]{0:T(1024)} %copy-done.67) | copy-start | bytes 21508
  173.5 79.6 %copy-start.72 = (f32[1792]{0:T(1024)S(1)}, f32[1792]{0:T(1024)}, u32[]{:S(2)}) copy-start(f32[1792]{0:T(1024)} %add_rsqrt_fusion) | copy-start | bytes 21508
  312.0 3.7 collective-permute-start.6
  336.2 104.8 %copy-start = (f32[256,1536]{1,0:T(8,128)}, f32[256,1536]{1,0:T(8,128)S(1)}, u32[]{:S(2)}) copy-start(f32[256,1536]{1,0:T(8,128)S(1)} %get-tuple-element.90) | copy-start | bytes 4718596
  338.6 20.0 %collective-permute-start.7 = (bf16[256,1536]{1,0:T(8,128)(2,1)}, bf16[256,1536]{1,0:T(8,128)(2,1)}, u32[]{:S(2)}, u32[]{:S(2)}) collective-permute-start(bf16[256,1536]{1,0:T(8,128)(2,1)} %add_convert_fusion.4), channel_id=1, source_target_pairs={{0,16},{16,0},{1,17},{17,1},{2,18},{18,2},{3,19},{19,3},{4,20},{20... | collective-permute-start | bytes 2359304 | tf_op jit(solution)/shard_map/ppermute | solution.py:68
  419.0 19.1 %collective-permute-start.9 = (bf16[256,1536]{1,0:T(8,128)(2,1)}, bf16[256,1536]{1,0:T(8,128)(2,1)}, u32[]{:S(2)}, u32[]{:S(2)}) collective-permute-start(bf16[256,1536]{1,0:T(8,128)(2,1)} %slice.427), channel_id=1, source_target_pairs={{0,16},{16,0},{1,17},{17,1},{2,18},{18,2},{3,19},{19,3},{4,20},{20... | collective-permute-start | bytes 2359304 | tf_op jit(solution)/shard_map/ppermute | solution.py:68
  425.3 267.1 %collective-permute-start.37 = (bf16[2,8,96,1536]{3,2,1,0:T(8,128)(2,1)}, bf16[2,8,96,1536]{3,2,1,0:T(8,128)(2,1)}, u32[]{:S(2)}, u32[]{:S(2)}) collective-permute-start(bf16[2,8,96,1536]{3,2,1,0:T(8,128)(2,1)} %dynamic-slice_bitcast_fusion), channel_id=1, source_target_pairs={{0,1},{1,0},{2,3},{3,2},{4,5},{5,4},{6,7},{7,6},{8,9},{9,8},{10,11... | collective-permute-start | bytes 14155784 | tf_op jit(solution)/shard_map/ppermute | solution.py:68
  430.0 271.9 %collective-permute-start.35 = (bf16[1,8,96,3072]{3,2,1,0:T(8,128)(2,1)}, bf16[1,8,96,3072]{3,2,1,0:T(8,128)(2,1)}, u32[]{:S(2)}, u32[]{:S(2)}) collective-permute-start(bf16[1,8,96,3072]{3,2,1,0:T(8,128)(2,1)} %dynamic-slice_bitcast_fusion.1), channel_id=1, source_target_pairs={{0,1},{1,0},{2,3},{3,2},{4,5},{5,4},{6,7},{7,6},{8,9},{9,8},{10,11... | collective-permute-start | bytes 14155784 | tf_op jit(solution)/shard_map/ppermute | solution.py:68
  481.3 1.8 collective-permute-start.10
  557.9 41.0 %collective-permute-start.14 = (bf16[4,2,96,1152]{3,2,1,0:T(8,128)(2,1)}, bf16[4,2,96,1152]{3,2,1,0:T(8,128)(2,1)}, u32[]{:S(2)}, u32[]{:S(2)}) collective-permute-start(bf16[4,2,96,1152]{3,2,1,0:T(8,128)(2,1)} %pad_maximum_fusion.8), channel_id=1, source_target_pairs={{0,16},{16,0},{1,17},{17,1},{2,18},{18,2},{3,19},{19,3},{4,20},{20... | collective-permute-start | bytes 5308424 | tf_op jit(solution)/shard_map/ppermute | solution.py:68
  562.7 465.3 %all-gather.16.cloned.1.call-start = ((), (), s32[]{:S(2)}) async-start(), calls=%async_computation.6 | async-start | bytes 1622016 | tf_op jit(solution)/shard_map/all_gather | solution.py:706
  570.2 41.8 %collective-permute-start.12 = (bf16[4,192,1152]{2,1,0:T(8,128)(2,1)}, bf16[4,192,1152]{2,1,0:T(8,128)(2,1)}, u32[]{:S(2)}, u32[]{:S(2)}) collective-permute-start(bf16[4,192,1152]{2,1,0:T(8,128)(2,1)} %dynamic-slice_bitcast_fusion.12), channel_id=1, source_target_pairs={{0,2},{1,3},{2,0},{3,1},{4,6},{5,7},{6,4},{7,5},{8,10},{9,11},{10,... | collective-permute-start | bytes 5308424 | tf_op jit(solution)/shard_map/ppermute | solution.py:68
  602.2 32.6 %collective-permute-start.15 = (bf16[4,96,1152]{2,1,0:T(8,128)(2,1)S(1)}, bf16[4,96,1152]{2,1,0:T(8,128)(2,1)}, u32[]{:S(2)}, u32[]{:S(2)}) collective-permute-start(bf16[4,96,1152]{2,1,0:T(8,128)(2,1)S(1)} %dynamic-slice_bitcast_fusion.17), channel_id=1, source_target_pairs={{0,2},{1,3},{2,0},{3,1},{4,6},{5,7},{6,4},{7,5},{8,10},{9,11},{10,... | collective-permute-start | bytes 2654216 | tf_op jit(solution)/shard_map/ppermute | solution.py:68
  615.0 21.5 %collective-permute-start.13 = (bf16[4,96,1152]{2,1,0:T(8,128)(2,1)}, bf16[4,96,1152]{2,1,0:T(8,128)(2,1)}, u32[]{:S(2)}, u32[]{:S(2)}) collective-permute-start(bf16[4,96,1152]{2,1,0:T(8,128)(2,1)} %dynamic-slice_bitcast_fusion.18), channel_id=1, source_target_pairs={{0,16},{16,0},{1,17},{17,1},{2,18},{18,2},{3,19},{19,3},{4,20},{20... | collective-permute-start | bytes 2654216 | tf_op jit(solution)/shard_map/ppermute | solution.py:68
  619.0 313.0 %collective-permute-start.26 = (bf16[8,96,4608]{2,1,0:T(8,128)(2,1)}, bf16[8,96,4608]{2,1,0:T(8,128)(2,1)}, u32[]{:S(2)}, u32[]{:S(2)}) collective-permute-start(bf16[8,96,4608]{2,1,0:T(8,128)(2,1)} %pad_maximum_fusion), channel_id=1, source_target_pairs={{0,1},{1,0},{2,3},{3,2},{4,5},{5,4},{6,7},{7,6},{8,9},{9,8},{10,11... | collective-permute-start | bytes 21233672 | tf_op jit(solution)/shard_map/ppermute | solution.py:68
  691.4 130.4 %collective-permute-start.16 = (bf16[4,256,1536]{2,1,0:T(8,128)(2,1)}, bf16[4,256,1536]{2,1,0:T(8,128)(2,1)}, u32[]{:S(2)}, u32[]{:S(2)}) collective-permute-start(bf16[4,256,1536]{2,1,0:T(8,128)(2,1)} %pad_maximum_fusion.5), channel_id=1, source_target_pairs={{0,1},{1,0},{2,3},{3,2},{4,5},{5,4},{6,7},{7,6},{8,9},{9,8},{10,11... | collective-permute-start | bytes 9437192 | tf_op jit(solution)/shard_map/ppermute | solution.py:68
  692.2 355.7 %all-gather.14.cloned.1.call-start = ((), (), s32[]{:S(2)}) async-start(), calls=%async_computation.5 | async-start | bytes 2838528 | tf_op jit(solution)/shard_map/all_gather | solution.py:611
  700.6 58.6 %collective-permute-start.38 = (bf16[2,4,96,1536]{3,2,1,0:T(8,128)(2,1)}, bf16[2,4,96,1536]{3,2,1,0:T(8,128)(2,1)}, u32[]{:S(2)}, u32[]{:S(2)}) collective-permute-start(bf16[2,4,96,1536]{3,2,1,0:T(8,128)(2,1)} %dynamic-slice_bitcast_fusion.2), channel_id=1, source_target_pairs={{0,2},{1,3},{2,0},{3,1},{4,6},{5,7},{6,4},{7,5},{8,10},{9,11},{10,... | collective-permute-start | bytes 7077896 | tf_op jit(solution)/shard_map/ppermute | solution.py:68
  711.2 106.2 %collective-permute-start.36 = (bf16[1,4,96,3072]{3,2,1,0:T(8,128)(2,1)}, bf16[1,4,96,3072]{3,2,1,0:T(8,128)(2,1)}, u32[]{:S(2)}, u32[]{:S(2)}) collective-permute-start(bf16[1,4,96,3072]{3,2,1,0:T(8,128)(2,1)} %dynamic-slice_bitcast_fusion.3), channel_id=1, source_target_pairs={{0,2},{1,3},{2,0},{3,1},{4,6},{5,7},{6,4},{7,5},{8,10},{9,11},{10,... | collective-permute-start | bytes 7077896 | tf_op jit(solution)/shard_map/ppermute | solution.py:68
  722.5 96.5 %slice-start.4 = ((s8[4718592]{0:T(1024)(128)(4,1)}), s8[524288]{0:T(1024)(128)(4,1)S(1)}, s32[]{:S(2)}) async-start(s8[4718592]{0:T(1024)(128)(4,1)} %bitcast.307), calls=%async_computation.11 | async-start | bytes 1048576
  723.5 107.1 %collective-permute-start.11 = (bf16[256,1536]{1,0:T(8,128)(2,1)}, bf16[256,1536]{1,0:T(8,128)(2,1)S(1)}, u32[]{:S(2)}, u32[]{:S(2)}) collective-permute-start(bf16[256,1536]{1,0:T(8,128)(2,1)} %slice.426), channel_id=1, source_target_pairs={{0,16},{16,0},{1,17},{17,1},{2,18},{18,2},{3,19},{19,3},{4,20},{20... | collective-permute-start | bytes 2359304 | tf_op jit(solution)/shard_map/ppermute | solution.py:68
  724.9 94.1 %slice-start.5 = ((s8[4718592]{0:T(1024)(128)(4,1)}), s8[4194304]{0:T(1024)(128)(4,1)S(1)}, s32[]{:S(2)}) async-start(s8[4718592]{0:T(1024)(128)(4,1)} %bitcast.307), calls=%async_computation.12 | async-start | bytes 8388608
  762.4 61.5 %slice-start.2 = ((s8[4718592]{0:T(1024)(128)(4,1)}), s8[4194304]{0:T(1024)(128)(4,1)S(1)}, s32[]{:S(2)}) async-start(s8[4718592]{0:T(1024)(128)(4,1)} %bitcast.303), calls=%async_computation.9 | async-start | bytes 8388608
  762.6 68.9 %collective-permute-start.39 = (bf16[2,96,1536]{2,1,0:T(8,128)(2,1)S(1)}, bf16[2,96,1536]{2,1,0:T(8,128)(2,1)S(1)}, u32[]{:S(2)}, u32[]{:S(2)}) collective-permute-start(bf16[2,96,1536]{2,1,0:T(8,128)(2,1)S(1)} %get-tuple-element.175), channel_id=1, source_target_pairs={{0,4},{1,5},{2,6},{3,7},{4,8},{5,9},{6,10},{7,11},{8,12},{9,13},{1... | collective-permute-start | bytes 1769480 | tf_op jit(solution)/shard_map/ppermute | solution.py:68
  817.4 30.6 %collective-permute-start.40 = (bf16[2,96,1536]{2,1,0:T(8,128)(2,1)S(1)}, bf16[2,96,1536]{2,1,0:T(8,128)(2,1)S(1)}, u32[]{:S(2)}, u32[]{:S(2)}) collective-permute-start(bf16[2,96,1536]{2,1,0:T(8,128)(2,1)S(1)} %get-tuple-element.174), channel_id=1, source_target_pairs={{0,8},{1,9},{2,10},{3,11},{4,12},{5,13},{6,14},{7,15},{8,0},{9,1},... | collective-permute-start | bytes 1769480 | tf_op jit(solution)/shard_map/ppermute | solution.py:68
  821.8 41.9 %collective-permute-start.41 = (bf16[2,96,1536]{2,1,0:T(8,128)(2,1)S(1)}, bf16[2,96,1536]{2,1,0:T(8,128)(2,1)S(1)}, u32[]{:S(2)}, u32[]{:S(2)}) collective-permute-start(bf16[2,96,1536]{2,1,0:T(8,128)(2,1)S(1)} %get-tuple-element.173), channel_id=1, source_target_pairs={{0,12},{1,13},{2,14},{3,15},{4,0},{5,1},{6,2},{7,3},{8,4},{9,5},{1... | collective-permute-start | bytes 1769480 | tf_op jit(solution)/shard_map/ppermute | solution.py:68
  830.6 34.8 %collective-permute-start.42 = (bf16[1,96,3072]{2,1,0:T(8,128)(2,1)S(1)}, bf16[1,96,3072]{2,1,0:T(8,128)(2,1)S(1)}, u32[]{:S(2)}, u32[]{:S(2)}) collective-permute-start(bf16[1,96,3072]{2,1,0:T(8,128)(2,1)S(1)} %get-tuple-element.172), channel_id=1, source_target_pairs={{0,4},{1,5},{2,6},{3,7},{4,8},{5,9},{6,10},{7,11},{8,12},{9,13},{1... | collective-permute-start | bytes 1769480 | tf_op jit(solution)/shard_map/ppermute | solution.py:68
  831.5 65.7 %collective-permute-start.43 = (bf16[1,96,3072]{2,1,0:T(8,128)(2,1)S(1)}, bf16[1,96,3072]{2,1,0:T(8,128)(2,1)S(1)}, u32[]{:S(2)}, u32[]{:S(2)}) collective-permute-start(bf16[1,96,3072]{2,1,0:T(8,128)(2,1)S(1)} %get-tuple-element.171), channel_id=1, source_target_pairs={{0,8},{1,9},{2,10},{3,11},{4,12},{5,13},{6,14},{7,15},{8,0},{9,1},... | collective-permute-start | bytes 1769480 | tf_op jit(solution)/shard_map/ppermute | solution.py:68
  848.0 59.8 %collective-permute-start.44 = (bf16[1,96,3072]{2,1,0:T(8,128)(2,1)S(1)}, bf16[1,96,3072]{2,1,0:T(8,128)(2,1)S(1)}, u32[]{:S(2)}, u32[]{:S(2)}) collective-permute-start(bf16[1,96,3072]{2,1,0:T(8,128)(2,1)S(1)} %get-tuple-element.170), channel_id=1, source_target_pairs={{0,12},{1,13},{2,14},{3,15},{4,0},{5,1},{6,2},{7,3},{8,4},{9,5},{1... | collective-permute-start | bytes 1769480 | tf_op jit(solution)/shard_map/ppermute | solution.py:68
  862.4 70.6 %copy-start.21 = (bf16[8,96,1536]{2,1,0:T(8,128)(2,1)S(1)}, bf16[8,96,1536]{2,1,0:T(8,128)(2,1)}, u32[]{:S(2)}) copy-start(bf16[8,96,1536]{2,1,0:T(8,128)(2,1)} %get-tuple-element.154) | copy-start | bytes 7077892
  863.7 69.4 %copy-start.18 = (bf16[8,96,1536]{2,1,0:T(8,128)(2,1)S(1)}, bf16[8,96,1536]{2,1,0:T(8,128)(2,1)}, u32[]{:S(2)}) copy-start(bf16[8,96,1536]{2,1,0:T(8,128)(2,1)} %get-tuple-element.158) | copy-start | bytes 7077892
  863.7 69.4 %copy-start.19 = (bf16[8,96,1536]{2,1,0:T(8,128)(2,1)S(1)}, bf16[8,96,1536]{2,1,0:T(8,128)(2,1)}, u32[]{:S(2)}) copy-start(bf16[8,96,1536]{2,1,0:T(8,128)(2,1)} %get-tuple-element.229) | copy-start | bytes 7077892
  863.7 112.0 %collective-permute-start.18 = (bf16[256,1536]{1,0:T(8,128)(2,1)}, bf16[256,1536]{1,0:T(8,128)(2,1)}, u32[]{:S(2)}, u32[]{:S(2)}) collective-permute-start(bf16[256,1536]{1,0:T(8,128)(2,1)} %fusion.125), channel_id=1, source_target_pairs={{1,3},{3,1},{5,7},{7,5},{9,11},{11,9},{13,15},{15,13},{17,19},{19,... | collective-permute-start | bytes 2359304 | tf_op jit(solution)/shard_map/ppermute | solution.py:68
  865.4 77.3 %collective-permute-start.23 = (bf16[96,2304]{1,0:T(8,128)(2,1)}, bf16[96,2304]{1,0:T(8,128)(2,1)S(1)}, u32[]{:S(2)}, u32[]{:S(2)}) collective-permute-start(bf16[96,2304]{1,0:T(8,128)(2,1)} %get-tuple-element.181), channel_id=1, source_target_pairs={{0,12},{1,13},{2,14},{3,15},{4,0},{5,1},{6,2},{7,3},{8,4},{9,5},{1... | collective-permute-start | bytes 1327112 | tf_op jit(solution)/shard_map/ppermute | solution.py:68
  897.2 46.5 %collective-permute-start.22 = (bf16[96,2304]{1,0:T(8,128)(2,1)}, bf16[96,2304]{1,0:T(8,128)(2,1)S(1)}, u32[]{:S(2)}, u32[]{:S(2)}) collective-permute-start(bf16[96,2304]{1,0:T(8,128)(2,1)} %get-tuple-element.182), channel_id=1, source_target_pairs={{0,8},{1,9},{2,10},{3,11},{4,12},{5,13},{6,14},{7,15},{8,0},{9,1},... | collective-permute-start | bytes 1327112 | tf_op jit(solution)/shard_map/ppermute | solution.py:68
  907.8 42.9 %collective-permute-start.21 = (bf16[96,2304]{1,0:T(8,128)(2,1)S(1)}, bf16[96,2304]{1,0:T(8,128)(2,1)S(1)}, u32[]{:S(2)}, u32[]{:S(2)}) collective-permute-start(bf16[96,2304]{1,0:T(8,128)(2,1)S(1)} %get-tuple-element.183), channel_id=1, source_target_pairs={{0,4},{1,5},{2,6},{3,7},{4,8},{5,9},{6,10},{7,11},{8,12},{9,13},{1... | collective-permute-start | bytes 1327112 | tf_op jit(solution)/shard_map/ppermute | solution.py:68
  932.0 43.8 %collective-permute-start.17 = (bf16[256,1536]{1,0:T(8,128)(2,1)}, bf16[256,1536]{1,0:T(8,128)(2,1)S(1)}, u32[]{:S(2)}, u32[]{:S(2)}) collective-permute-start(bf16[256,1536]{1,0:T(8,128)(2,1)} %slice_bitcast_fusion.4), channel_id=1, source_target_pairs={{0,2},{1,3},{2,0},{3,1},{4,6},{5,7},{6,4},{7,5},{8,10},{9,11},{10,... | collective-permute-start | bytes 2359304 | tf_op jit(solution)/shard_map/ppermute | solution.py:68
  942.6 16.2 %collective-permute-start.45 = (bf16[1,96,3072]{2,1,0:T(8,128)(2,1)S(1)}, bf16[1,96,3072]{2,1,0:T(8,128)(2,1)S(1)}, u32[]{:S(2)}, u32[]{:S(2)}) collective-permute-start(bf16[1,96,3072]{2,1,0:T(8,128)(2,1)S(1)} %fusion.148), channel_id=1, source_target_pairs={{0,16},{16,0},{1,17},{17,1},{2,18},{18,2},{3,19},{19,3},{4,20},{20... | collective-permute-start | bytes 1769480 | tf_op jit(solution)/shard_map/ppermute | solution.py:68
  943.7 27.9 %collective-permute-start.46 = (bf16[2,96,1536]{2,1,0:T(8,128)(2,1)S(1)}, bf16[2,96,1536]{2,1,0:T(8,128)(2,1)}, u32[]{:S(2)}, u32[]{:S(2)}) collective-permute-start(bf16[2,96,1536]{2,1,0:T(8,128)(2,1)S(1)} %fusion.145), channel_id=1, source_target_pairs={{0,16},{16,0},{1,17},{17,1},{2,18},{18,2},{3,19},{19,3},{4,20},{20... | collective-permute-start | bytes 1769480 | tf_op jit(solution)/shard_map/ppermute | solution.py:68
  950.7 87.4 %collective-permute-start.27 = (bf16[4,96,2304]{2,1,0:T(8,128)(2,1)}, bf16[4,96,2304]{2,1,0:T(8,128)(2,1)}, u32[]{:S(2)}, u32[]{:S(2)}) collective-permute-start(bf16[4,96,2304]{2,1,0:T(8,128)(2,1)} %dynamic-slice_bitcast_fusion.11), channel_id=1, source_target_pairs={{0,2},{1,3},{2,0},{3,1},{4,6},{5,7},{6,4},{7,5},{8,10},{9,11},{10,... | collective-permute-start | bytes 5308424 | tf_op jit(solution)/shard_map/ppermute | solution.py:68
  958.8 83.2 %collective-permute-start.29 = (bf16[4,2,48,2304]{3,2,0,1:T(8,128)(2,1)}, bf16[4,2,48,2304]{3,2,0,1:T(8,128)(2,1)}, u32[]{:S(2)}, u32[]{:S(2)}) collective-permute-start(bf16[4,2,48,2304]{3,2,0,1:T(8,128)(2,1)} %bitcast.292), channel_id=1, source_target_pairs={{0,16},{16,0},{1,17},{17,1},{2,18},{18,2},{3,19},{19,3},{4,20},{20... | collective-permute-start | bytes 5308424 | tf_op jit(solution)/shard_map/ppermute | solution.py:68
  971.6 45.4 %collective-permute-start.24 = (bf16[96,2304]{1,0:T(8,128)(2,1)}, bf16[96,2304]{1,0:T(8,128)(2,1)S(1)}, u32[]{:S(2)}, u32[]{:S(2)}) collective-permute-start(bf16[96,2304]{1,0:T(8,128)(2,1)} %fusion.155), channel_id=1, source_target_pairs={{0,16},{16,0},{1,17},{17,1},{2,18},{18,2},{3,19},{19,3},{4,20},{20... | collective-permute-start | bytes 1327112 | tf_op jit(solution)/shard_map/ppermute | solution.py:68
  978.3 54.3 %collective-permute-start.19 = (bf16[256,1536]{1,0:T(8,128)(2,1)}, bf16[256,1536]{1,0:T(8,128)(2,1)S(1)}, u32[]{:S(2)}, u32[]{:S(2)}) collective-permute-start(bf16[256,1536]{1,0:T(8,128)(2,1)} %fusion.122), channel_id=1, source_target_pairs={{4,0},{5,1},{6,2},{7,3},{8,4},{9,5},{10,6},{11,7},{12,8},{13,9},{1... | collective-permute-start | bytes 2359304 | tf_op jit(solution)/shard_map/ppermute | solution.py:68
  979.7 52.9 %collective-permute-start.20 = (bf16[256,1536]{1,0:T(8,128)(2,1)}, bf16[256,1536]{1,0:T(8,128)(2,1)S(1)}, u32[]{:S(2)}, u32[]{:S(2)}) collective-permute-start(bf16[256,1536]{1,0:T(8,128)(2,1)} %collective-permute-done.18), channel_id=1, source_target_pairs={{11,3},{15,7},{19,11},{23,15},{27,19},{31,23}} | collective-permute-start | bytes 2359304 | tf_op jit(solution)/shard_map/ppermute | solution.py:68
  1018.1 12.0 %collective-permute-start.25 = (bf16[96,2304]{1,0:T(8,128)(2,1)}, bf16[96,2304]{1,0:T(8,128)(2,1)}, u32[]{:S(2)}, u32[]{:S(2)}) collective-permute-start(bf16[96,2304]{1,0:T(8,128)(2,1)} %get-tuple-element.199), channel_id=1, source_target_pairs={{0,1},{1,0},{2,3},{3,2},{4,5},{5,4},{6,7},{7,6},{8,9},{9,8},{10,11... | collective-permute-start | bytes 1327112 | tf_op jit(solution)/shard_map/ppermute | solution.py:68
  1041.2 22.2 %collective-permute-start.28 = (bf16[4,48,2304]{2,1,0:T(8,128)(2,1)S(1)}, bf16[4,48,2304]{2,1,0:T(8,128)(2,1)}, u32[]{:S(2)}, u32[]{:S(2)}) collective-permute-start(bf16[4,48,2304]{2,1,0:T(8,128)(2,1)S(1)} %dynamic-slice_bitcast_fusion.16), channel_id=1, source_target_pairs={{0,16},{16,0},{1,17},{17,1},{2,18},{18,2},{3,19},{19,3},{4,20},{20... | collective-permute-start | bytes 2654216 | tf_op jit(solution)/shard_map/ppermute | solution.py:68
  1046.1 22.1 %collective-permute-start.30 = (bf16[4,48,2304]{2,1,0:T(8,128)(2,1)}, bf16[4,48,2304]{2,1,0:T(8,128)(2,1)}, u32[]{:S(2)}, u32[]{:S(2)}) collective-permute-start(bf16[4,48,2304]{2,1,0:T(8,128)(2,1)} %dynamic-slice_bitcast_fusion.15), channel_id=1, source_target_pairs={{0,2},{1,3},{2,0},{3,1},{4,6},{5,7},{6,4},{7,5},{8,10},{9,11},{10,... | collective-permute-start | bytes 2654216 | tf_op jit(solution)/shard_map/ppermute | solution.py:68
  1069.7 35.4 %collective-permute-start.31 = (bf16[48,4608]{1,0:T(8,128)(2,1)S(1)}, bf16[48,4608]{1,0:T(8,128)(2,1)S(1)}, u32[]{:S(2)}, u32[]{:S(2)}) collective-permute-start(bf16[48,4608]{1,0:T(8,128)(2,1)S(1)} %get-tuple-element.179), channel_id=1, source_target_pairs={{0,4},{1,5},{2,6},{3,7},{4,8},{5,9},{6,10},{7,11},{8,12},{9,13},{1... | collective-permute-start | bytes 1327112 | tf_op jit(solution)/shard_map/ppermute | solution.py:68
  1070.1 53.3 %collective-permute-start.32 = (bf16[48,4608]{1,0:T(8,128)(2,1)S(1)}, bf16[48,4608]{1,0:T(8,128)(2,1)S(1)}, u32[]{:S(2)}, u32[]{:S(2)}) collective-permute-start(bf16[48,4608]{1,0:T(8,128)(2,1)S(1)} %get-tuple-element.180), channel_id=1, source_target_pairs={{0,8},{1,9},{2,10},{3,11},{4,12},{5,13},{6,14},{7,15},{8,0},{9,1},... | collective-permute-start | bytes 1327112 | tf_op jit(solution)/shard_map/ppermute | solution.py:68
  1094.5 28.8 %collective-permute-start.33 = (bf16[48,4608]{1,0:T(8,128)(2,1)S(1)}, bf16[48,4608]{1,0:T(8,128)(2,1)S(1)}, u32[]{:S(2)}, u32[]{:S(2)}) collective-permute-start(bf16[48,4608]{1,0:T(8,128)(2,1)S(1)} %get-tuple-element.178), channel_id=1, source_target_pairs={{0,12},{1,13},{2,14},{3,15},{4,0},{5,1},{6,2},{7,3},{8,4},{9,5},{1... | collective-permute-start | bytes 1327112 | tf_op jit(solution)/shard_map/ppermute | solution.py:68
  1123.6 12.1 %collective-permute-start.34 = (bf16[48,4608]{1,0:T(8,128)(2,1)S(1)}, bf16[48,4608]{1,0:T(8,128)(2,1)S(1)}, u32[]{:S(2)}, u32[]{:S(2)}) collective-permute-start(bf16[48,4608]{1,0:T(8,128)(2,1)S(1)} %fusion.152), channel_id=1, source_target_pairs={{0,16},{16,0},{1,17},{17,1},{2,18},{18,2},{3,19},{19,3},{4,20},{20... | collective-permute-start | bytes 1327112 | tf_op jit(solution)/shard_map/ppermute | solution.py:68
  (110 other events, 753.4 us)
Sparse Core Ops, SparseCore 0:
  9.8 140.1 all-gather.9
  152.2 96.7 all-gather.7
  250.6 98.8 all-gather.11
  562.8 105.1 reduce-scatter.1
  692.3 56.9 all-gather.15
  752.1 69.0 all-gather.13

commit v5 on v4

--- a/solution.py
+++ b/solution.py
@@ -353,6 +353,31 @@
         ),
         name="unpack_query_key_value",
     )(own, got)
+
+
+def interleave_kernel(count, chunk, own_ref, other_ref, out_ref):
+    rep = lax.axis_index("rep")
+    own, other = own_ref[...].astype(WIDE), other_ref[...].astype(WIDE)
+    halves = jnp.where(rep == 0, own, other), jnp.where(rep == 0, other, own)
+    for index in range(count):
+        parts = [
+            half[:, (j * count + index) * chunk : (j * count + index + 1) * chunk]
+            for half in halves
+            for j in range(2)
+        ]
+        out_ref[:, 4 * chunk * index : 4 * chunk * (index + 1)] = jnp.concatenate(parts, axis=1)
+
+
+def interleave(own, other, count, chunk):
+    rows, width = own.shape
+    return pl.pallas_call(
+        functools.partial(interleave_kernel, count, chunk),
+        out_shape=jax.ShapeDtypeStruct((rows, 2 * width), WIDE),
+        cost_estimate=pl.CostEstimate(
+            flops=0, transcendentals=0, bytes_accessed=12 * rows * width
+        ),
+        name="interleave_up",
+    )(own, other)
 
 
 def core_pair(own, got, core, axis):
@@ -614,9 +639,7 @@
         jnp.sum(grad_halo * normed_plain[:halo_rows].astype(WIDE), axis=0),
         jnp.sum(grad_halo, axis=0),
     ]
-    grad_chip = right_t(
-        jnp.concatenate([chip_dq, grad_window[halo_rows:]], axis=1), part_all
-    )
+    grad_chip = right_t(chip_dq, part_query) + right_t(grad_window[halo_rows:], part_pair)
     chip_sums = [
         jnp.sum(grad_chip * normed_plain[halo_rows:].astype(WIDE), axis=0),
         jnp.sum(grad_chip, axis=0),
@@ -630,14 +653,47 @@
     sums = add_low(pick(units, core, 1), partner[:3])
     low_sum = add_low(grad_halo[:tok_rows], partner[3])
     if staged:
+        down_got = after(down_got, [chip_dq])
+        up_got = after(up_got, sent_first[2:])
+        own_down = level_total(down_held, down_got, down_level)
+        own_up = level_total(up_held, up_got, up_level)
+    else:
+        own_down = lax.psum_scatter(grad_down, "shard", scatter_dimension=1, tiled=True)
+        own_up = lax.psum_scatter(grad_up[None], "shard", scatter_dimension=1, tiled=True)
+    activ_late, after_late = after((activ, after_cross), sent_first[2:] if staged else [grad_chip])
+    mixed_both = matmul(activ_late[:, :quarter], half_down[0]) + matmul(
+        activ_late[:, quarter:], half_down[1]
+    )
+    y_got = swap(mixed_both[tok_rows:].astype(LOW), "rep", lambda i: i ^ 1)
+    if staged:
         q_both = after(q_both, [sums, low_sum])
         q_got = level_sends(q_both, q_level, sent_last)
+    text_whole = after(text_whole, sent_last)
+    key_round, value_round = (
+        text_whole[:, :flat_rows],
+        text_whole[:, flat_rows : 2 * flat_rows],
+    )
+    col_start = lax.axis_index("shard") * shard_rows
+    text_flat = text_states.reshape(flat_rows, model_width)
+    text_slice = lax.dynamic_slice_in_dim(text_flat, col_start, shard_rows, 1)
+
+    def mixed_dims(left, right):
+        return lax.dot_general(
+            left, right, (((0,), (1,)), ((), ())), preferred_element_type=WIDE
+        )
+
+    grad_xkey = mixed_dims(text_slice, key_round)
+    grad_xvalue = mixed_dims(text_slice, value_round)
+    grad_text = mixed_dims(key_round, full_xkey) + mixed_dims(value_round, full_xvalue)
+    grad_text = grad_text.reshape(clip_total, text_rows, model_width)
+    filler = sent_last + [grad_text, grad_xkey, grad_xvalue] if staged else []
+    if staged:
         q_own = level_total(q_both, q_got, q_level)
         parts = rep_rows(q_own).reshape(2, shard_rows, 3 * half_width)
         q_swapped = swap(pick(parts, 1 - q_core, 0), "shard", lambda i: i ^ 1)
         fin_query, fin_key, fin_value = unpack(pick(parts, q_core, 0), q_swapped)
-        x_own = level_total(x_both, after(x_got, sent_first[2:]), x_level)
-        fin_x = rep_rows(x_own, sent_last)
+        x_own = level_total(x_both, after(x_got, sent_first[2:] + [own_down, own_up, mixed_both]), x_level)
+        fin_x = rep_rows(x_own, filler)
     else:
         filled = joined([grad_pair, grad_wq])
         fin_halves = plain_rows([core_pair(filled, jnp.zeros_like(filled), core, 1)])
@@ -650,55 +706,27 @@
     fin_xoutput, fin_xquery, fin_output = (
         fin_x[:, i * model_width : (i + 1) * model_width].astype(WIDE) for i in range(3)
     )
-    if staged:
-        down_got, up_got = after((down_got, up_got), sent_first[2:])
-        own_down = level_total(down_held, down_got, down_level)
-        own_up = level_total(up_held, up_got, up_level)
-    else:
-        own_down = lax.psum_scatter(grad_down, "shard", scatter_dimension=1, tiled=True)
-        own_up = lax.psum_scatter(grad_up[None], "shard", scatter_dimension=1, tiled=True)
-    down_halves = rep_pair(own_down, sent_last)
+    down_halves = rep_pair(own_down, filler)
     fin_down = jnp.concatenate(down_halves, axis=0).reshape(w_down.shape).astype(WIDE)
-    up_halves = rep_pair(own_up, sent_last)
-    fin_up = jnp.stack(
-        [half.reshape(w_up.shape[0], 2, shard_count, chunk) for half in up_halves], axis=1
-    )
-    fin_up = jnp.transpose(fin_up, (0, 3, 1, 2, 4)).reshape(w_up.shape).astype(WIDE)
-    activ_late, after_late = after((activ, after_cross), [grad_chip])
-    mixed_both = matmul(activ_late[:, :quarter], half_down[0]) + matmul(
-        activ_late[:, quarter:], half_down[1]
-    )
-    y_got = swap(mixed_both[tok_rows:].astype(LOW), "rep", lambda i: i ^ 1)
+    other_up = swap(own_up, "rep", lambda i: i ^ 1)
+    own_up, other_up = after((own_up, other_up), filler)
+    fin_up = interleave(own_up[0], other_up[0], shard_count, chunk)
     y_own, y_got, after_late = after((mixed_both[:tok_rows], y_got, after_late), sent_last)
     block_out = (after_late + y_own + y_got.astype(WIDE)).astype(LOW)
-    text_whole = after(text_whole, sent_last)
-    key_round, value_round = (
-        text_whole[:, :flat_rows],
-        text_whole[:, flat_rows : 2 * flat_rows],
-    )
-    col_start = lax.axis_index("shard") * shard_rows
-    text_flat = text_states.reshape(flat_rows, model_width)
-    text_slice = lax.dynamic_slice_in_dim(text_flat, col_start, shard_rows, 1)
-
-    def mixed_dims(left, right):
-        return lax.dot_general(
-            left, right, (((0,), (1,)), ((), ())), preferred_element_type=WIDE
-        )
-
-    grad_xkey = mixed_dims(text_slice, key_round)
-    grad_xvalue = mixed_dims(text_slice, value_round)
-    grad_text = mixed_dims(key_round, full_xkey) + mixed_dims(value_round, full_xvalue)
-    grad_text = grad_text.reshape(clip_total, text_rows, model_width)
     back = swap(sums[1], BOTH, lambda i: i ^ 2).astype(WIDE)
     back_half = swap(low_sum, BOTH, lambda i: i ^ 2 if i % 2 == 1 else -1)
     to_below = (
         sums[0].astype(WIDE) + jnp.where(side == 0, back_half.astype(WIDE), back)
     ).astype(LOW)
+    down_part = swap(to_below, BOTH, lambda i: i - 4)
+    far_part = swap(back_half, BOTH, lambda i: i - 8 if i % 4 == 3 else -1)
+    if staged:
+        down_part, far_part = after((down_part, far_part), [q_own])
     grad_norm_one = (
         sums[2].astype(WIDE)
         + jnp.where(side == 0, back, 0.0)
-        + swap(to_below, BOTH, lambda i: i - 4).astype(WIDE)
-        + swap(back_half, BOTH, lambda i: i - 8 if i % 4 == 3 else -1).astype(WIDE)
+        + down_part.astype(WIDE)
+        + far_part.astype(WIDE)
     )
     norm_one_part, _, _ = norm_back(resid, gain_one, grad_norm_one)
     grad_gain_one, grad_bias_one = around_sums

time: 1160 us -> 1110 us (0.957)
  waiting for transfers between devices: 453 us -> 412 us
    reduce_scatter x1, waiting for transfers between devices: 28.7 us -> 0.01 us  [on_device(): lax.psum_scatter(text_sums, BOTH, scatter_dimension=0, tiled=True)]
    ppermute x47, waiting for transfers between devices: 344 us -> 329 us  [swap(): lax.ppermute(array, axis, [(i, j) for i, j in pairs if 0 <= j < length])]
    dot_general x8 -> x9, matrix products: 50.3 us -> 54.8 us  [right_t(): lax.dot_general(left, right, (((1,), (1,)), ((), ())), preferred_element_...]
    unnamed x249 -> x245, local copies, waits for them, and re-layouts: 23.3 us -> 26.3 us
    squeeze x19 -> x18, local copies, waits for them, and re-layouts: 35.2 us -> 35.4 us  [pick(): return lax.dynamic_index_in_dim(array, index, axis, False)]
  transfers between devices with their start and end apart: 53 -> 53, of which waited for: 24 -> 20; matrix products, arithmetic and copies ran while one was open for 30% -> 30% of each run, Pallas kernels for 7% -> 7%
where the time goes in v5:
time: 1110 us; the launch traced here: 1100 us
  waiting for transfers between devices  412 us (37%)
  matrix products  199 us (18%)
  starting transfers between devices  169 us (15%)
  other arithmetic  122 us (11%)
  local copies, waits for them, and re-layouts  100 us (9%)
  Pallas kernels  79.2 us (7%)
  between operations  19.5 us (2%)
    ppermute x47, waiting for transfers between devices, swap(): lax.ppermute(array, axis, [(i, j) for i, j in pairs if 0 <= j < length])  329 us
    ppermute x47, starting transfers between devices, swap(): lax.ppermute(array, axis, [(i, j) for i, j in pairs if 0 <= j < length])  169 us
    all_gather x3, waiting for transfers between devices, gather_rows(): return lax.all_gather(array, 'shard', axis=0, tiled=True)  83.4 us
    dot_general x12, matrix products, matmul(): return jnp.dot(left, right, preferred_element_type=WIDE)  65.2 us
    dot_general x9, matrix products, right_t(): lax.dot_general(left, right, (((1,), (1,)), ((), ())), preferred_element_...  54.8 us
    dot_general x7, matrix products, left_t(): lax.dot_general(left, right, (((0,), (0,)), ((), ())), preferred_element_...  49 us
    pallas_call x2, Pallas kernels, attend_back(): pl.pallas_call(functools.partial(attend_back_kernel, reach), grid=(pairs,...  47.4 us
    convert_element_type x15, other arithmetic, add_low(): return (left.astype(WIDE) + right.astype(WIDE)).astype(LOW)  35.6 us
  transfers between devices with their start and end apart: 53, of which 20 were waited for; matrix products, arithmetic and copies ran while one was open for 30% of the time, Pallas kernels for 7%

profile of v5, /device:TPU:0, one launch (start us, length us, event | category | flops | bytes accessed | tf_op | source)
XLA Modules:
  0.0 1100.1 jit_solution(2687777351389258313)
XLA Ops:
  19.1 5.2 collective-permute-start.1
  25.0 33.7 %collective-permute-done.1 = bf16[256,1536]{1,0:T(8,128)(2,1)S(1)} collective-permute-done((bf16[256,1536]{1,0:T(8,128)(2,1)S(1)}, bf16[256,1536]{1,0:T(8,128)(2,1)S(1)}, u32[]{:S(2)}, u32[]{:S(2)}) %collective-permute-start.1) | collective-permute-done | bytes 786464 | tf_op jit(solution)/shard_map/ppermute | solution.py:68
  61.6 24.6 %collective-permute-done.4 = bf16[256,1536]{1,0:T(8,128)(2,1)S(1)} collective-permute-done((bf16[256,1536]{1,0:T(8,128)(2,1)S(1)}, bf16[256,1536]{1,0:T(8,128)(2,1)S(1)}, u32[]{:S(2)}, u32[]{:S(2)}) %collective-permute-start.4) | collective-permute-done | bytes 786464 | tf_op jit(solution)/shard_map/ppermute | solution.py:68
  88.1 52.5 %collective-permute-start.5 = (bf16[4,256,1536]{2,1,0:T(8,128)(2,1)}, bf16[4,256,1536]{2,1,0:T(8,128)(2,1)}, u32[]{:S(2)}, u32[]{:S(2)}) collective-permute-start(bf16[4,256,1536]{2,1,0:T(8,128)(2,1)} %pad_maximum_fusion.3), channel_id=1, source_target_pairs={{0,1},{1,0},{2,3},{3,2},{4,5},{5,4},{6,7},{7,6},{8,9},{9,8},{10,11... | collective-permute-start | bytes 9437192 | tf_op jit(solution)/shard_map/ppermute | solution.py:68
  156.1 9.2 fusion.7
  170.2 79.1 %all-gather.8.cloned.1.call-done = bf16[1536,6272]{1,0:T(8,128)(2,1)} async-done(((bf16[96,6272]{1,0:T(8,128)(2,1)}), bf16[1536,6272]{1,0:T(8,128)(2,1)}) %all-gather.8.cloned.1.call-update) | async-done | bytes 19267600 | tf_op jit(solution)/shard_map/all_gather | solution.py:80
  249.3 4.1 convert_reduce_fusion.3
  253.4 12.5 %fusion.3 = (bf16[1792,1536]{1,0:T(8,128)(2,1)}, bf16[1792,1536]{1,0:T(8,128)(2,1)S(1)}) fusion(f32[1792]{0:T(1024)S(1)} %copy-done.70, f32[1792]{0:T(1024)S(1)} %copy-done.66, bf16[512,1536]{1,0:T(8,128)(2,1)S(1)} %copy-done.5, bf16[512,1536]{1,0:T(8,128)(2,1)} %copy-done.6, bf16[512,1536]{1,0:T(8,128)(2,1)S(1)} %get-tuple-element.164, ...), kind=kLoop, calls=%fused_computation.6 | loop fusion | flops 38535168 | bytes 16541696 | tf_op jit(solution)/shard_map/convert_element_type | solution.py:488
  265.9 5.8 fusion.130.query_ref
  271.7 13.3 %convolution_convert_fusion.5.window_ref = bf16[1792,1536]{1,0:T(8,128)(2,1)} fusion(bf16[1792,1536]{1,0:T(8,128)(2,1)S(1)} %get-tuple-element.157, bf16[1536,6272]{1,0:T(8,128)(2,1)} %all-gather.8.cloned.1.call-done, s32[]{:T(128)S(6)} %add.731), kind=kOutput, calls=%fused_computation.24 | convolution fusion | flops 8458469376 | bytes 15728644 | tf_op jit(solution)/shard_map/dot_general | solution.py:38
  285.0 26.1 %attend_forward.1 = (bf16[512,768]{1,0:T(8,128)(2,1)}, f32[6,2,512]{2,1,0:T(2,128)}) custom-call(s32[1,512]{1,0:T(1,128)} %broadcast_select_fusion.8.offset_ref, bf16[512,768]{1,0:T(8,128)(2,1)} %fusion.130.query_ref, bf16[1792,1536]{1,0:T(8,128)(2,1)} %convolution_convert_fusion.5.window_ref), custom_call_target="tpu_custom_call" | custom-call | flops 9663676416 | bytes 3145728 | tf_op jit(solution)/shard_map/attend_forward/pallas_call | solution.py:218
  316.8 4.3 fusion.212
  322.0 3.8 fusion.92
  326.0 3.7 fusion.213
  332.2 4.3 fusion.214
  345.5 4.3 all-gather.12.cloned.1.call-done
  349.8 8.9 collective-permute-done.7
  358.8 7.8 fusion.69
  366.8 7.9 fusion.73
  374.9 10.0 convolution_convert_fusion.1
  384.9 6.6 fusion.77
  391.5 6.0 fusion.80
  398.7 9.0 fusion.8
  407.7 9.0 fusion.9
  420.9 4.9 dynamic-slice_bitcast_fusion.1
  425.7 4.8 dynamic-slice_bitcast_fusion
  431.0 7.5 collective-permute-done.9
  445.7 4.7 fusion.95
  462.4 3.7 convolution_convert_fusion.3
  466.2 4.7 multiply_reduce_fusion.4
  473.9 3.8 convolution_convert_fusion.2
  477.8 3.7 fusion.89
  486.3 7.6 dynamic-slice_bitcast_fusion.7
  495.1 23.7 %attend_backward.2 = (bf16[512,768]{1,0:T(8,128)(2,1)}, bf16[1792,1536]{1,0:T(8,128)(2,1)}) custom-call(s32[1,512]{1,0:T(1,128)} %broadcast_select_fusion.8.offset_ref, bf16[512,768]{1,0:T(8,128)(2,1)} %fusion.130.query_ref, bf16[1792,1536]{1,0:T(8,128)(2,1)} %convolution_convert_fusion.5.window_ref, bf16[512,768]{1,0:T(8,128)(2,1)} %get-tuple-element.73.out_ref, ...), custom_call_target="tpu_custom_call" | custom-call | flops 12079595520 | bytes 6291456 | tf_op jit(solution)/shard_map/attend_backward/pallas_call | solution.py:304
  518.8 23.7 %attend_backward.3 = (bf16[512,768]{1,0:T(8,128)(2,1)}, bf16[1792,1536]{1,0:T(8,128)(2,1)}) custom-call(s32[1,512]{1,0:T(1,128)} %broadcast_select_fusion.8.offset_ref, bf16[512,768]{1,0:T(8,128)(2,1)} %fusion.130.query_ref, bf16[1792,1536]{1,0:T(8,128)(2,1)} %convolution_convert_fusion.5.window_ref, ...), custom_call_target="tpu_custom_call", output_to_operand_aliasing={{0}: (6, {}), {1}: (7, {})} | custom-call | flops 12079595520 | bytes 6291456 | tf_op jit(solution)/shard_map/attend_backward/pallas_call | solution.py:304
  542.5 14.5 %convolution_convert_fusion.6 = bf16[1536,1536]{1,0:T(8,128)(2,1)} fusion(bf16[1792,1536]{1,0:T(8,128)(2,1)} %copy-done.34, bf16[1792,1536]{1,0:T(8,128)(2,1)} %get-tuple-element.89), kind=kOutput, calls=%fused_computation.25 | convolution fusion | flops 8458076160 | bytes 15728640 | tf_op jit(solution)/shard_map/dot_general | solution.py:42
  557.0 4.2 convolution_convert_fusion.8
  561.3 4.0 slice.263
  581.0 3.6 pad_maximum_fusion
  590.0 21.6 %collective-permute-done.11 = bf16[4,192,1152]{2,1,0:T(8,128)(2,1)} collective-permute-done((bf16[4,192,1152]{2,1,0:T(8,128)(2,1)}, bf16[4,192,1152]{2,1,0:T(8,128)(2,1)}, u32[]{:S(2)}, u32[]{:S(2)}) %collective-permute-start.11) | collective-permute-done | bytes 1769504 | tf_op jit(solution)/shard_map/ppermute | solution.py:68
  621.6 4.5 fusion.20
  626.1 4.5 fusion.63
  635.7 10.2 fusion.206
  647.8 5.1 fusion.50
  652.9 4.8 fusion.207
  664.7 5.5 fusion.12
  674.3 4.3 fusion.11
  689.3 43.0 %collective-permute-done.35 = bf16[2,4,96,1536]{3,2,1,0:T(8,128)(2,1)} collective-permute-done((bf16[2,4,96,1536]{3,2,1,0:T(8,128)(2,1)}, bf16[2,4,96,1536]{3,2,1,0:T(8,128)(2,1)}, u32[]{:S(2)}, u32[]{:S(2)}) %collective-permute-start.35) | collective-permute-done | bytes 2359328 | tf_op jit(solution)/shard_map/ppermute | solution.py:68
  737.1 51.0 %collective-permute-done.40 = bf16[1,4,96,3072]{3,2,1,0:T(8,128)(2,1)} collective-permute-done((bf16[1,4,96,3072]{3,2,1,0:T(8,128)(2,1)}, bf16[1,4,96,3072]{3,2,1,0:T(8,128)(2,1)}, u32[]{:S(2)}, u32[]{:S(2)}) %collective-permute-start.40) | collective-permute-done | bytes 2359328 | tf_op jit(solution)/shard_map/ppermute | solution.py:68
  802.4 16.6 %collective-permute-done.37 = bf16[2,96,1536]{2,1,0:T(8,128)(2,1)S(1)} collective-permute-done((bf16[2,96,1536]{2,1,0:T(8,128)(2,1)S(1)}, bf16[2,96,1536]{2,1,0:T(8,128)(2,1)S(1)}, u32[]{:S(2)}, u32[]{:S(2)}) %collective-permute-start.37) | collective-permute-done | bytes 589856 | tf_op jit(solution)/shard_map/ppermute | solution.py:68
  818.9 15.0 %collective-permute-start.43 = (bf16[1,96,3072]{2,1,0:T(8,128)(2,1)S(1)}, bf16[1,96,3072]{2,1,0:T(8,128)(2,1)S(1)}, u32[]{:S(2)}, u32[]{:S(2)}) collective-permute-start(bf16[1,96,3072]{2,1,0:T(8,128)(2,1)S(1)} %get-tuple-element.174), channel_id=1, source_target_pairs={{0,12},{1,13},{2,14},{3,15},{4,0},{5,1},{6,2},{7,3},{8,4},{9,5},{1... | collective-permute-start | bytes 1769480 | tf_op jit(solution)/shard_map/ppermute | solution.py:68
  839.7 26.8 %collective-permute-done.42 = bf16[1,96,3072]{2,1,0:T(8,128)(2,1)S(1)} collective-permute-done((bf16[1,96,3072]{2,1,0:T(8,128)(2,1)S(1)}, bf16[1,96,3072]{2,1,0:T(8,128)(2,1)S(1)}, u32[]{:S(2)}, u32[]{:S(2)}) %collective-permute-start.42) | collective-permute-done | bytes 589856 | tf_op jit(solution)/shard_map/ppermute | solution.py:68
  866.6 11.0 collective-permute-start.22
  877.5 23.4 %collective-permute-start.21 = (bf16[96,2304]{1,0:T(8,128)(2,1)}, bf16[96,2304]{1,0:T(8,128)(2,1)}, u32[]{:S(2)}, u32[]{:S(2)}) collective-permute-start(bf16[96,2304]{1,0:T(8,128)(2,1)} %get-tuple-element.187), channel_id=1, source_target_pairs={{0,4},{1,5},{2,6},{3,7},{4,8},{5,9},{6,10},{7,11},{8,12},{9,13},{1... | collective-permute-start | bytes 1327112 | tf_op jit(solution)/shard_map/ppermute | solution.py:68
  903.7 4.5 add_convert_fusion
  912.6 7.9 collective-permute-done.21
  928.4 18.8 %collective-permute-done.24 = bf16[96,2304]{1,0:T(8,128)(2,1)S(1)} collective-permute-done((bf16[96,2304]{1,0:T(8,128)(2,1)S(1)}, bf16[96,2304]{1,0:T(8,128)(2,1)S(1)}, u32[]{:S(2)}, u32[]{:S(2)}) %collective-permute-start.24) | collective-permute-done | bytes 442400 | tf_op jit(solution)/shard_map/ppermute | solution.py:68
  964.0 30.5 %collective-permute-done.27 = bf16[4,96,2304]{2,1,0:T(8,128)(2,1)} collective-permute-done((bf16[4,96,2304]{2,1,0:T(8,128)(2,1)}, bf16[4,96,2304]{2,1,0:T(8,128)(2,1)}, u32[]{:S(2)}, u32[]{:S(2)}) %collective-permute-start.27) | collective-permute-done | bytes 1769504 | tf_op jit(solution)/shard_map/ppermute | solution.py:68
  1001.4 5.8 fusion.32
  1007.2 7.1 fusion.74
  1024.9 25.6 %collective-permute-start.32 = (bf16[48,4608]{1,0:T(8,128)(2,1)}, bf16[48,4608]{1,0:T(8,128)(2,1)}, u32[]{:S(2)}, u32[]{:S(2)}) collective-permute-start(bf16[48,4608]{1,0:T(8,128)(2,1)} %get-tuple-element.184), channel_id=1, source_target_pairs={{0,8},{1,9},{2,10},{3,11},{4,12},{5,13},{6,14},{7,15},{8,0},{9,1},... | collective-permute-start | bytes 1327112 | tf_op jit(solution)/shard_map/ppermute | solution.py:68
  1055.2 6.1 collective-permute-done.31
  1061.3 16.8 %collective-permute-done.32 = bf16[48,4608]{1,0:T(8,128)(2,1)} collective-permute-done((bf16[48,4608]{1,0:T(8,128)(2,1)}, bf16[48,4608]{1,0:T(8,128)(2,1)}, u32[]{:S(2)}, u32[]{:S(2)}) %collective-permute-start.32) | collective-permute-done | bytes 442400 | tf_op jit(solution)/shard_map/ppermute | solution.py:68
  1082.4 9.4 collective-permute-done.44
  (487 shorter events, 229.9 us)
Async XLA Ops:
  7.2 158.7 %all-gather.10.cloned.1.call-start = ((), (), s32[]{:S(2)}) async-start(), calls=%async_computation.2 | async-start | bytes 20054016 | tf_op jit(solution)/shard_map/all_gather | solution.py:80
  9.7 239.7 %all-gather.8.cloned.1.call-start = ((), (), s32[]{:S(2)}) async-start(), calls=%async_computation.1 | async-start | bytes 20471808 | tf_op jit(solution)/shard_map/all_gather | solution.py:80
  14.2 335.6 %all-gather.12.cloned.1.call-start = ((), (), s32[]{:S(2)}) async-start(), calls=%async_computation.3 | async-start | bytes 20054016 | tf_op jit(solution)/shard_map/all_gather | solution.py:80
  19.0 616.6 %reduce-scatter.2.cloned.1.call-start = ((), (), s32[]{:S(2)}) async-start(), calls=%async_computation.4 | async-start | bytes 2838528 | tf_op jit(solution)/shard_map/reduce_scatter | solution.py:590
  19.1 39.6 %collective-permute-start.1 = (bf16[256,1536]{1,0:T(8,128)(2,1)S(1)}, bf16[256,1536]{1,0:T(8,128)(2,1)S(1)}, u32[]{:S(2)}, u32[]{:S(2)}) collective-permute-start(bf16[256,1536]{1,0:T(8,128)(2,1)S(1)} %copy-done.2), channel_id=1, source_target_pairs={{0,4},{1,5},{2,6},{3,7},{4,8},{5,9},{6,10},{7,11},{8,12},{9,13},{1... | collective-permute-start | bytes 2359304 | tf_op jit(solution)/shard_map/ppermute | solution.py:68
  24.3 34.4 %collective-permute-start.2 = (bf16[256,1536]{1,0:T(8,128)(2,1)S(1)}, bf16[256,1536]{1,0:T(8,128)(2,1)S(1)}, u32[]{:S(2)}, u32[]{:S(2)}) collective-permute-start(bf16[256,1536]{1,0:T(8,128)(2,1)S(1)} %copy-done.2), channel_id=1, source_target_pairs={{3,11},{7,15},{11,19},{15,23},{19,27},{23,31}} | collective-permute-start | bytes 2359304 | tf_op jit(solution)/shard_map/ppermute | solution.py:68
  58.8 2.8 collective-permute-start.3
  59.7 26.4 %collective-permute-start.4 = (bf16[256,1536]{1,0:T(8,128)(2,1)S(1)}, bf16[256,1536]{1,0:T(8,128)(2,1)S(1)}, u32[]{:S(2)}, u32[]{:S(2)}) collective-permute-start(bf16[256,1536]{1,0:T(8,128)(2,1)S(1)} %get-tuple-element.209), channel_id=1, source_target_pairs={{0,2},{1,3},{2,0},{3,1},{4,6},{5,7},{6,4},{7,5},{8,10},{9,11},{10,... | collective-permute-start | bytes 2359304 | tf_op jit(solution)/shard_map/ppermute | solution.py:68
  86.1 54.4 %copy-start.95 = (s32[256]{0:T(256)S(1)}, s32[256]{0:T(256)}, u32[]{:S(2)}) copy-start(s32[256]{0:T(256)} %param.24) | copy-start | bytes 3076
  86.1 54.5 %copy-start.94 = (s32[256]{0:T(256)S(1)}, s32[256]{0:T(256)}, u32[]{:S(2)}) copy-start(s32[256]{0:T(256)} %param.23) | copy-start | bytes 3076
  88.1 61.4 %collective-permute-start.5 = (bf16[4,256,1536]{2,1,0:T(8,128)(2,1)}, bf16[4,256,1536]{2,1,0:T(8,128)(2,1)}, u32[]{:S(2)}, u32[]{:S(2)}) collective-permute-start(bf16[4,256,1536]{2,1,0:T(8,128)(2,1)} %pad_maximum_fusion.3), channel_id=1, source_target_pairs={{0,1},{1,0},{2,3},{3,2},{4,5},{5,4},{6,7},{7,6},{8,9},{9,8},{10,11... | collective-permute-start | bytes 9437192 | tf_op jit(solution)/shard_map/ppermute | solution.py:68
  140.6 8.3 collective-permute-start
  140.7 202.8 %collective-permute-start.8 = (bf16[256,1536]{1,0:T(8,128)(2,1)}, bf16[256,1536]{1,0:T(8,128)(2,1)}, u32[]{:S(2)}, u32[]{:S(2)}) collective-permute-start(bf16[256,1536]{1,0:T(8,128)(2,1)} %param.41), channel_id=1, source_target_pairs={{0,16},{16,0},{1,17},{17,1},{2,18},{18,2},{3,19},{19,3},{4,20},{20... | collective-permute-start | bytes 2359304 | tf_op jit(solution)/shard_map/ppermute | solution.py:68
  170.2 83.2 %copy-start.66 = (f32[1792]{0:T(1024)S(1)}, f32[1792]{0:T(1024)}, u32[]{:S(2)}) copy-start(f32[1792]{0:T(1024)} %copy-done.65) | copy-start | bytes 21508
  170.2 83.2 %copy-start.70 = (f32[1792]{0:T(1024)S(1)}, f32[1792]{0:T(1024)}, u32[]{:S(2)}) copy-start(f32[1792]{0:T(1024)} %add_rsqrt_fusion) | copy-start | bytes 21508
  312.3 3.7 collective-permute-start.6
  336.5 104.9 %copy-start = (f32[256,1536]{1,0:T(8,128)}, f32[256,1536]{1,0:T(8,128)S(1)}, u32[]{:S(2)}) copy-start(f32[256,1536]{1,0:T(8,128)S(1)} %get-tuple-element.92) | copy-start | bytes 4718596
  338.8 20.0 %collective-permute-start.7 = (bf16[256,1536]{1,0:T(8,128)(2,1)}, bf16[256,1536]{1,0:T(8,128)(2,1)}, u32[]{:S(2)}, u32[]{:S(2)}) collective-permute-start(bf16[256,1536]{1,0:T(8,128)(2,1)} %add_convert_fusion.4), channel_id=1, source_target_pairs={{0,16},{16,0},{1,17},{17,1},{2,18},{18,2},{3,19},{19,3},{4,20},{20... | collective-permute-start | bytes 2359304 | tf_op jit(solution)/shard_map/ppermute | solution.py:68
  419.4 19.1 %collective-permute-start.9 = (bf16[256,1536]{1,0:T(8,128)(2,1)}, bf16[256,1536]{1,0:T(8,128)(2,1)}, u32[]{:S(2)}, u32[]{:S(2)}) collective-permute-start(bf16[256,1536]{1,0:T(8,128)(2,1)} %slice.429), channel_id=1, source_target_pairs={{0,16},{16,0},{1,17},{17,1},{2,18},{18,2},{3,19},{19,3},{4,20},{20... | collective-permute-start | bytes 2359304 | tf_op jit(solution)/shard_map/ppermute | solution.py:68
  425.7 239.0 %collective-permute-start.34 = (bf16[2,8,96,1536]{3,2,1,0:T(8,128)(2,1)}, bf16[2,8,96,1536]{3,2,1,0:T(8,128)(2,1)}, u32[]{:S(2)}, u32[]{:S(2)}) collective-permute-start(bf16[2,8,96,1536]{3,2,1,0:T(8,128)(2,1)} %dynamic-slice_bitcast_fusion.1), channel_id=1, source_target_pairs={{0,1},{1,0},{2,3},{3,2},{4,5},{5,4},{6,7},{7,6},{8,9},{9,8},{10,11... | collective-permute-start | bytes 14155784 | tf_op jit(solution)/shard_map/ppermute | solution.py:68
  430.5 243.8 %collective-permute-start.39 = (bf16[1,8,96,3072]{3,2,1,0:T(8,128)(2,1)}, bf16[1,8,96,3072]{3,2,1,0:T(8,128)(2,1)}, u32[]{:S(2)}, u32[]{:S(2)}) collective-permute-start(bf16[1,8,96,3072]{3,2,1,0:T(8,128)(2,1)} %dynamic-slice_bitcast_fusion), channel_id=1, source_target_pairs={{0,1},{1,0},{2,3},{3,2},{4,5},{5,4},{6,7},{7,6},{8,9},{9,8},{10,11... | collective-permute-start | bytes 14155784 | tf_op jit(solution)/shard_map/ppermute | solution.py:68
  483.4 10.5 collective-permute-start.10
  486.2 464.7 %all-gather.16.cloned.1.call-start = ((), (), s32[]{:S(2)}) async-start(), calls=%async_computation.6 | async-start | bytes 1622016 | tf_op jit(solution)/shard_map/all_gather | solution.py:734
  569.6 42.0 %collective-permute-start.11 = (bf16[4,192,1152]{2,1,0:T(8,128)(2,1)}, bf16[4,192,1152]{2,1,0:T(8,128)(2,1)}, u32[]{:S(2)}, u32[]{:S(2)}) collective-permute-start(bf16[4,192,1152]{2,1,0:T(8,128)(2,1)} %dynamic-slice_bitcast_fusion.12), channel_id=1, source_target_pairs={{0,2},{1,3},{2,0},{3,1},{4,6},{5,7},{6,4},{7,5},{8,10},{9,11},{10,... | collective-permute-start | bytes 5308424 | tf_op jit(solution)/shard_map/ppermute | solution.py:68
  576.1 41.1 %collective-permute-start.12 = (bf16[4,2,96,1152]{3,2,0,1:T(8,128)(2,1)}, bf16[4,2,96,1152]{3,2,0,1:T(8,128)(2,1)}, u32[]{:S(2)}, u32[]{:S(2)}) collective-permute-start(bf16[4,2,96,1152]{3,2,0,1:T(8,128)(2,1)} %pad_maximum_fusion.8), channel_id=1, source_target_pairs={{0,16},{16,0},{1,17},{17,1},{2,18},{18,2},{3,19},{19,3},{4,20},{20... | collective-permute-start | bytes 5308424 | tf_op jit(solution)/shard_map/ppermute | solution.py:68
  587.8 315.4 %collective-permute-start.26 = (bf16[8,96,4608]{2,1,0:T(8,128)(2,1)}, bf16[8,96,4608]{2,1,0:T(8,128)(2,1)}, u32[]{:S(2)}, u32[]{:S(2)}) collective-permute-start(bf16[8,96,4608]{2,1,0:T(8,128)(2,1)} %pad_maximum_fusion), channel_id=1, source_target_pairs={{0,1},{1,0},{2,3},{3,2},{4,5},{5,4},{6,7},{7,6},{8,9},{9,8},{10,11... | collective-permute-start | bytes 21233672 | tf_op jit(solution)/shard_map/ppermute | solution.py:68
  633.3 51.0 %collective-permute-start.15 = (bf16[4,96,1152]{2,1,0:T(8,128)(2,1)}, bf16[4,96,1152]{2,1,0:T(8,128)(2,1)}, u32[]{:S(2)}, u32[]{:S(2)}) collective-permute-start(bf16[4,96,1152]{2,1,0:T(8,128)(2,1)} %dynamic-slice_bitcast_fusion.17), channel_id=1, source_target_pairs={{0,2},{1,3},{2,0},{3,1},{4,6},{5,7},{6,4},{7,5},{8,10},{9,11},{10,... | collective-permute-start | bytes 2654216 | tf_op jit(solution)/shard_map/ppermute | solution.py:68
  634.2 51.6 %collective-permute-start.14 = (bf16[4,96,1152]{2,1,0:T(8,128)(2,1)}, bf16[4,96,1152]{2,1,0:T(8,128)(2,1)}, u32[]{:S(2)}, u32[]{:S(2)}) collective-permute-start(bf16[4,96,1152]{2,1,0:T(8,128)(2,1)} %dynamic-slice_bitcast_fusion.18), channel_id=1, source_target_pairs={{0,16},{16,0},{1,17},{17,1},{2,18},{18,2},{3,19},{19,3},{4,20},{20... | collective-permute-start | bytes 2654216 | tf_op jit(solution)/shard_map/ppermute | solution.py:68
  658.6 342.8 %all-gather.14.cloned.1.call-start = ((), (), s32[]{:S(2)}) async-start(), calls=%async_computation.5 | async-start | bytes 2838528 | tf_op jit(solution)/shard_map/all_gather | solution.py:636
  673.0 59.3 %collective-permute-start.35 = (bf16[2,4,96,1536]{3,2,1,0:T(8,128)(2,1)}, bf16[2,4,96,1536]{3,2,1,0:T(8,128)(2,1)}, u32[]{:S(2)}, u32[]{:S(2)}) collective-permute-start(bf16[2,4,96,1536]{3,2,1,0:T(8,128)(2,1)} %dynamic-slice_bitcast_fusion.3), channel_id=1, source_target_pairs={{0,2},{1,3},{2,0},{3,1},{4,6},{5,7},{6,4},{7,5},{8,10},{9,11},{10,... | collective-permute-start | bytes 7077896 | tf_op jit(solution)/shard_map/ppermute | solution.py:68
  681.5 106.7 %collective-permute-start.40 = (bf16[1,4,96,3072]{3,2,1,0:T(8,128)(2,1)}, bf16[1,4,96,3072]{3,2,1,0:T(8,128)(2,1)}, u32[]{:S(2)}, u32[]{:S(2)}) collective-permute-start(bf16[1,4,96,3072]{3,2,1,0:T(8,128)(2,1)} %dynamic-slice_bitcast_fusion.2), channel_id=1, source_target_pairs={{0,2},{1,3},{2,0},{3,1},{4,6},{5,7},{6,4},{7,5},{8,10},{9,11},{10,... | collective-permute-start | bytes 7077896 | tf_op jit(solution)/shard_map/ppermute | solution.py:68
  684.3 109.0 %collective-permute-start.16 = (bf16[4,256,1536]{2,1,0:T(8,128)(2,1)}, bf16[4,256,1536]{2,1,0:T(8,128)(2,1)}, u32[]{:S(2)}, u32[]{:S(2)}) collective-permute-start(bf16[4,256,1536]{2,1,0:T(8,128)(2,1)} %pad_maximum_fusion.5), channel_id=1, source_target_pairs={{0,1},{1,0},{2,3},{3,2},{4,5},{5,4},{6,7},{7,6},{8,9},{9,8},{10,11... | collective-permute-start | bytes 9437192 | tf_op jit(solution)/shard_map/ppermute | solution.py:68
  685.8 114.9 %collective-permute-start.13 = (bf16[256,1536]{1,0:T(8,128)(2,1)}, bf16[256,1536]{1,0:T(8,128)(2,1)}, u32[]{:S(2)}, u32[]{:S(2)}) collective-permute-start(bf16[256,1536]{1,0:T(8,128)(2,1)} %slice.428), channel_id=1, source_target_pairs={{0,16},{16,0},{1,17},{17,1},{2,18},{18,2},{3,19},{19,3},{4,20},{20... | collective-permute-start | bytes 2359304 | tf_op jit(solution)/shard_map/ppermute | solution.py:68
  687.9 102.7 %slice-start.4 = ((s8[4718592]{0:T(1024)(128)(4,1)}), s8[524288]{0:T(1024)(128)(4,1)S(1)}, s32[]{:S(2)}) async-start(s8[4718592]{0:T(1024)(128)(4,1)} %bitcast.306), calls=%async_computation.11 | async-start | bytes 1048576
  689.3 101.3 %slice-start.5 = ((s8[4718592]{0:T(1024)(128)(4,1)}), s8[4194304]{0:T(1024)(128)(4,1)S(1)}, s32[]{:S(2)}) async-start(s8[4718592]{0:T(1024)(128)(4,1)} %bitcast.306), calls=%async_computation.12 | async-start | bytes 8388608
  735.4 59.4 %slice-start.2 = ((s8[4718592]{0:T(1024)(128)(4,1)}), s8[4194304]{0:T(1024)(128)(4,1)S(1)}, s32[]{:S(2)}) async-start(s8[4718592]{0:T(1024)(128)(4,1)} %bitcast.302), calls=%async_computation.9 | async-start | bytes 8388608
  735.6 65.8 %collective-permute-start.36 = (bf16[2,96,1536]{2,1,0:T(8,128)(2,1)S(1)}, bf16[2,96,1536]{2,1,0:T(8,128)(2,1)S(1)}, u32[]{:S(2)}, u32[]{:S(2)}) collective-permute-start(bf16[2,96,1536]{2,1,0:T(8,128)(2,1)S(1)} %get-tuple-element.179), channel_id=1, source_target_pairs={{0,4},{1,5},{2,6},{3,7},{4,8},{5,9},{6,10},{7,11},{8,12},{9,13},{1... | collective-permute-start | bytes 1769480 | tf_op jit(solution)/shard_map/ppermute | solution.py:68
  788.2 30.8 %collective-permute-start.37 = (bf16[2,96,1536]{2,1,0:T(8,128)(2,1)S(1)}, bf16[2,96,1536]{2,1,0:T(8,128)(2,1)S(1)}, u32[]{:S(2)}, u32[]{:S(2)}) collective-permute-start(bf16[2,96,1536]{2,1,0:T(8,128)(2,1)S(1)} %get-tuple-element.178), channel_id=1, source_target_pairs={{0,8},{1,9},{2,10},{3,11},{4,12},{5,13},{6,14},{7,15},{8,0},{9,1},... | collective-permute-start | bytes 1769480 | tf_op jit(solution)/shard_map/ppermute | solution.py:68
  793.3 43.3 %collective-permute-start.38 = (bf16[2,96,1536]{2,1,0:T(8,128)(2,1)S(1)}, bf16[2,96,1536]{2,1,0:T(8,128)(2,1)S(1)}, u32[]{:S(2)}, u32[]{:S(2)}) collective-permute-start(bf16[2,96,1536]{2,1,0:T(8,128)(2,1)S(1)} %get-tuple-element.177), channel_id=1, source_target_pairs={{0,12},{1,13},{2,14},{3,15},{4,0},{5,1},{6,2},{7,3},{8,4},{9,5},{1... | collective-permute-start | bytes 1769480 | tf_op jit(solution)/shard_map/ppermute | solution.py:68
  800.7 37.5 %collective-permute-start.41 = (bf16[1,96,3072]{2,1,0:T(8,128)(2,1)S(1)}, bf16[1,96,3072]{2,1,0:T(8,128)(2,1)S(1)}, u32[]{:S(2)}, u32[]{:S(2)}) collective-permute-start(bf16[1,96,3072]{2,1,0:T(8,128)(2,1)S(1)} %get-tuple-element.176), channel_id=1, source_target_pairs={{0,4},{1,5},{2,6},{3,7},{4,8},{5,9},{6,10},{7,11},{8,12},{9,13},{1... | collective-permute-start | bytes 1769480 | tf_op jit(solution)/shard_map/ppermute | solution.py:68
  801.4 65.2 %collective-permute-start.42 = (bf16[1,96,3072]{2,1,0:T(8,128)(2,1)S(1)}, bf16[1,96,3072]{2,1,0:T(8,128)(2,1)S(1)}, u32[]{:S(2)}, u32[]{:S(2)}) collective-permute-start(bf16[1,96,3072]{2,1,0:T(8,128)(2,1)S(1)} %get-tuple-element.175), channel_id=1, source_target_pairs={{0,8},{1,9},{2,10},{3,11},{4,12},{5,13},{6,14},{7,15},{8,0},{9,1},... | collective-permute-start | bytes 1769480 | tf_op jit(solution)/shard_map/ppermute | solution.py:68
  818.9 58.6 %collective-permute-start.43 = (bf16[1,96,3072]{2,1,0:T(8,128)(2,1)S(1)}, bf16[1,96,3072]{2,1,0:T(8,128)(2,1)S(1)}, u32[]{:S(2)}, u32[]{:S(2)}) collective-permute-start(bf16[1,96,3072]{2,1,0:T(8,128)(2,1)S(1)} %get-tuple-element.174), channel_id=1, source_target_pairs={{0,12},{1,13},{2,14},{3,15},{4,0},{5,1},{6,2},{7,3},{8,4},{9,5},{1... | collective-permute-start | bytes 1769480 | tf_op jit(solution)/shard_map/ppermute | solution.py:68
  834.0 69.7 %copy-start.19 = (bf16[8,96,1536]{2,1,0:T(8,128)(2,1)S(1)}, bf16[8,96,1536]{2,1,0:T(8,128)(2,1)}, u32[]{:S(2)}) copy-start(bf16[8,96,1536]{2,1,0:T(8,128)(2,1)} %get-tuple-element.158) | copy-start | bytes 7077892
  836.5 67.2 %copy-start.17 = (bf16[8,96,1536]{2,1,0:T(8,128)(2,1)S(1)}, bf16[8,96,1536]{2,1,0:T(8,128)(2,1)}, u32[]{:S(2)}) copy-start(bf16[8,96,1536]{2,1,0:T(8,128)(2,1)} %get-tuple-element.162) | copy-start | bytes 7077892
  836.5 67.2 %copy-start.18 = (bf16[8,96,1536]{2,1,0:T(8,128)(2,1)S(1)}, bf16[8,96,1536]{2,1,0:T(8,128)(2,1)}, u32[]{:S(2)}) copy-start(bf16[8,96,1536]{2,1,0:T(8,128)(2,1)} %get-tuple-element.231) | copy-start | bytes 7077892
  836.5 86.2 %collective-permute-start.18 = (bf16[256,1536]{1,0:T(8,128)(2,1)}, bf16[256,1536]{1,0:T(8,128)(2,1)}, u32[]{:S(2)}, u32[]{:S(2)}) collective-permute-start(bf16[256,1536]{1,0:T(8,128)(2,1)} %fusion.123), channel_id=1, source_target_pairs={{1,3},{3,1},{5,7},{7,5},{9,11},{11,9},{13,15},{15,13},{17,19},{19,... | collective-permute-start | bytes 2359304 | tf_op jit(solution)/shard_map/ppermute | solution.py:68
  838.3 72.3 %collective-permute-start.23 = (bf16[96,2304]{1,0:T(8,128)(2,1)}, bf16[96,2304]{1,0:T(8,128)(2,1)}, u32[]{:S(2)}, u32[]{:S(2)}) collective-permute-start(bf16[96,2304]{1,0:T(8,128)(2,1)} %get-tuple-element.185), channel_id=1, source_target_pairs={{0,12},{1,13},{2,14},{3,15},{4,0},{5,1},{6,2},{7,3},{8,4},{9,5},{1... | collective-permute-start | bytes 1327112 | tf_op jit(solution)/shard_map/ppermute | solution.py:68
  866.6 44.8 %collective-permute-start.22 = (bf16[96,2304]{1,0:T(8,128)(2,1)}, bf16[96,2304]{1,0:T(8,128)(2,1)}, u32[]{:S(2)}, u32[]{:S(2)}) collective-permute-start(bf16[96,2304]{1,0:T(8,128)(2,1)} %get-tuple-element.186), channel_id=1, source_target_pairs={{0,8},{1,9},{2,10},{3,11},{4,12},{5,13},{6,14},{7,15},{8,0},{9,1},... | collective-permute-start | bytes 1327112 | tf_op jit(solution)/shard_map/ppermute | solution.py:68
  877.5 43.0 %collective-permute-start.21 = (bf16[96,2304]{1,0:T(8,128)(2,1)}, bf16[96,2304]{1,0:T(8,128)(2,1)}, u32[]{:S(2)}, u32[]{:S(2)}) collective-permute-start(bf16[96,2304]{1,0:T(8,128)(2,1)} %get-tuple-element.187), channel_id=1, source_target_pairs={{0,4},{1,5},{2,6},{3,7},{4,8},{5,9},{6,10},{7,11},{8,12},{9,13},{1... | collective-permute-start | bytes 1327112 | tf_op jit(solution)/shard_map/ppermute | solution.py:68
  903.3 19.5 %collective-permute-start.17 = (bf16[256,1536]{1,0:T(8,128)(2,1)S(1)}, bf16[256,1536]{1,0:T(8,128)(2,1)S(1)}, u32[]{:S(2)}, u32[]{:S(2)}) collective-permute-start(bf16[256,1536]{1,0:T(8,128)(2,1)S(1)} %slice_bitcast_fusion.4), channel_id=1, source_target_pairs={{0,2},{1,3},{2,0},{3,1},{4,6},{5,7},{6,4},{7,5},{8,10},{9,11},{10,... | collective-permute-start | bytes 2359304 | tf_op jit(solution)/shard_map/ppermute | solution.py:68
  910.6 141.2 %collective-permute-start.45 = (bf16[1,96,3072]{2,1,0:T(8,128)(2,1)}, bf16[1,96,3072]{2,1,0:T(8,128)(2,1)}, u32[]{:S(2)}, u32[]{:S(2)}) collective-permute-start(bf16[1,96,3072]{2,1,0:T(8,128)(2,1)} %fusion.144), channel_id=1, source_target_pairs={{0,16},{16,0},{1,17},{17,1},{2,18},{18,2},{3,19},{19,3},{4,20},{20... | collective-permute-start | bytes 1769480 | tf_op jit(solution)/shard_map/ppermute | solution.py:68
  911.4 108.3 %collective-permute-start.46 = (bf16[2,96,1536]{2,1,0:T(8,128)(2,1)}, bf16[2,96,1536]{2,1,0:T(8,128)(2,1)}, u32[]{:S(2)}, u32[]{:S(2)}) collective-permute-start(bf16[2,96,1536]{2,1,0:T(8,128)(2,1)} %fusion.147), channel_id=1, source_target_pairs={{0,16},{16,0},{1,17},{17,1},{2,18},{18,2},{3,19},{19,3},{4,20},{20... | collective-permute-start | bytes 1769480 | tf_op jit(solution)/shard_map/ppermute | solution.py:68
  922.2 25.0 %collective-permute-start.24 = (bf16[96,2304]{1,0:T(8,128)(2,1)S(1)}, bf16[96,2304]{1,0:T(8,128)(2,1)S(1)}, u32[]{:S(2)}, u32[]{:S(2)}) collective-permute-start(bf16[96,2304]{1,0:T(8,128)(2,1)S(1)} %fusion.154), channel_id=1, source_target_pairs={{0,16},{16,0},{1,17},{17,1},{2,18},{18,2},{3,19},{19,3},{4,20},{20... | collective-permute-start | bytes 1327112 | tf_op jit(solution)/shard_map/ppermute | solution.py:68
  925.3 32.0 %collective-permute-start.19 = (bf16[256,1536]{1,0:T(8,128)(2,1)}, bf16[256,1536]{1,0:T(8,128)(2,1)}, u32[]{:S(2)}, u32[]{:S(2)}) collective-permute-start(bf16[256,1536]{1,0:T(8,128)(2,1)} %fusion.120), channel_id=1, source_target_pairs={{4,0},{5,1},{6,2},{7,3},{8,4},{9,5},{10,6},{11,7},{12,8},{13,9},{1... | collective-permute-start | bytes 2359304 | tf_op jit(solution)/shard_map/ppermute | solution.py:68
  926.6 31.3 %collective-permute-start.20 = (bf16[256,1536]{1,0:T(8,128)(2,1)}, bf16[256,1536]{1,0:T(8,128)(2,1)}, u32[]{:S(2)}, u32[]{:S(2)}) collective-permute-start(bf16[256,1536]{1,0:T(8,128)(2,1)} %collective-permute-done.18), channel_id=1, source_target_pairs={{11,3},{15,7},{19,11},{23,15},{27,19},{31,23}} | collective-permute-start | bytes 2359304 | tf_op jit(solution)/shard_map/ppermute | solution.py:68
  948.3 4.8 collective-permute-start.25
  953.1 41.4 %collective-permute-start.27 = (bf16[4,96,2304]{2,1,0:T(8,128)(2,1)}, bf16[4,96,2304]{2,1,0:T(8,128)(2,1)}, u32[]{:S(2)}, u32[]{:S(2)}) collective-permute-start(bf16[4,96,2304]{2,1,0:T(8,128)(2,1)} %dynamic-slice_bitcast_fusion.11), channel_id=1, source_target_pairs={{0,2},{1,3},{2,0},{3,1},{4,6},{5,7},{6,4},{7,5},{8,10},{9,11},{10,... | collective-permute-start | bytes 5308424 | tf_op jit(solution)/shard_map/ppermute | solution.py:68
  957.3 41.0 %collective-permute-start.29 = (bf16[4,2,48,2304]{3,2,0,1:T(8,128)(2,1)}, bf16[4,2,48,2304]{3,2,0,1:T(8,128)(2,1)S(1)}, u32[]{:S(2)}, u32[]{:S(2)}) collective-permute-start(bf16[4,2,48,2304]{3,2,0,1:T(8,128)(2,1)} %bitcast.346), channel_id=1, source_target_pairs={{0,16},{16,0},{1,17},{17,1},{2,18},{18,2},{3,19},{19,3},{4,20},{20... | collective-permute-start | bytes 5308424 | tf_op jit(solution)/shard_map/ppermute | solution.py:68
  996.5 23.1 %collective-permute-start.28 = (bf16[4,48,2304]{2,1,0:T(8,128)(2,1)S(1)}, bf16[4,48,2304]{2,1,0:T(8,128)(2,1)S(1)}, u32[]{:S(2)}, u32[]{:S(2)}) collective-permute-start(bf16[4,48,2304]{2,1,0:T(8,128)(2,1)S(1)} %dynamic-slice_bitcast_fusion.16), channel_id=1, source_target_pairs={{0,16},{16,0},{1,17},{17,1},{2,18},{18,2},{3,19},{19,3},{4,20},{20... | collective-permute-start | bytes 2654216 | tf_op jit(solution)/shard_map/ppermute | solution.py:68
  1001.0 21.2 %collective-permute-start.30 = (bf16[4,48,2304]{2,1,0:T(8,128)(2,1)}, bf16[4,48,2304]{2,1,0:T(8,128)(2,1)}, u32[]{:S(2)}, u32[]{:S(2)}) collective-permute-start(bf16[4,48,2304]{2,1,0:T(8,128)(2,1)} %dynamic-slice_bitcast_fusion.15), channel_id=1, source_target_pairs={{0,2},{1,3},{2,0},{3,1},{4,6},{5,7},{6,4},{7,5},{8,10},{9,11},{10,... | collective-permute-start | bytes 2654216 | tf_op jit(solution)/shard_map/ppermute | solution.py:68
  1024.6 36.7 %collective-permute-start.31 = (bf16[48,4608]{1,0:T(8,128)(2,1)}, bf16[48,4608]{1,0:T(8,128)(2,1)}, u32[]{:S(2)}, u32[]{:S(2)}) collective-permute-start(bf16[48,4608]{1,0:T(8,128)(2,1)} %get-tuple-element.183), channel_id=1, source_target_pairs={{0,4},{1,5},{2,6},{3,7},{4,8},{5,9},{6,10},{7,11},{8,12},{9,13},{1... | collective-permute-start | bytes 1327112 | tf_op jit(solution)/shard_map/ppermute | solution.py:68
  1024.9 53.3 %collective-permute-start.32 = (bf16[48,4608]{1,0:T(8,128)(2,1)}, bf16[48,4608]{1,0:T(8,128)(2,1)}, u32[]{:S(2)}, u32[]{:S(2)}) collective-permute-start(bf16[48,4608]{1,0:T(8,128)(2,1)} %get-tuple-element.184), channel_id=1, source_target_pairs={{0,8},{1,9},{2,10},{3,11},{4,12},{5,13},{6,14},{7,15},{8,0},{9,1},... | collective-permute-start | bytes 1327112 | tf_op jit(solution)/shard_map/ppermute | solution.py:68
  1050.5 27.7 %collective-permute-start.33 = (bf16[48,4608]{1,0:T(8,128)(2,1)S(1)}, bf16[48,4608]{1,0:T(8,128)(2,1)}, u32[]{:S(2)}, u32[]{:S(2)}) collective-permute-start(bf16[48,4608]{1,0:T(8,128)(2,1)S(1)} %get-tuple-element.182), channel_id=1, source_target_pairs={{0,12},{1,13},{2,14},{3,15},{4,0},{5,1},{6,2},{7,3},{8,4},{9,5},{1... | collective-permute-start | bytes 1327112 | tf_op jit(solution)/shard_map/ppermute | solution.py:68
  1079.7 12.1 %collective-permute-start.44 = (bf16[48,4608]{1,0:T(8,128)(2,1)S(1)}, bf16[48,4608]{1,0:T(8,128)(2,1)S(1)}, u32[]{:S(2)}, u32[]{:S(2)}) collective-permute-start(bf16[48,4608]{1,0:T(8,128)(2,1)S(1)} %fusion.151), channel_id=1, source_target_pairs={{0,16},{16,0},{1,17},{17,1},{2,18},{18,2},{3,19},{19,3},{4,20},{20... | collective-permute-start | bytes 1327112 | tf_op jit(solution)/shard_map/ppermute | solution.py:68
  (108 other events, 743.4 us)
Sparse Core Ops, SparseCore 0:
  9.8 140.5 all-gather.9
  152.5 96.7 all-gather.7
  250.9 98.8 all-gather.11
  486.4 100.8 reduce-scatter.1
  658.7 56.9 all-gather.15
  718.4 70.7 all-gather.13

commit v6 on v5

--- a/solution.py
+++ b/solution.py
@@ -90,10 +90,84 @@
     return grads, index % 2, (index // 2) % 2, index // 4, rep
 
 
+def away_kernel(_, *refs):
+    out_ref, start = refs[-1], 0
+    for ref in refs[:-1]:
+        out_ref[0, :, start : start + ref.shape[1]] = ref[...]
+        start += ref.shape[1]
+
+
+def away_rows(grads, core):
+    rows = grads[0].shape[0] // 16
+    width = sum(grad.shape[1] for grad in grads)
+    return pl.pallas_call(
+        away_kernel,
+        grid_spec=pltpu.PrefetchScalarGridSpec(
+            num_scalar_prefetch=1,
+            grid=(8,),
+            in_specs=[
+                pl.BlockSpec((rows, grad.shape[1]), lambda i, c: (2 * i + 1 - c[0], 0))
+                for grad in grads
+            ],
+            out_specs=pl.BlockSpec((1, rows, width), lambda i, c: (i, 0, 0)),
+        ),
+        out_shape=jax.ShapeDtypeStruct((8, rows, width), LOW),
+        cost_estimate=pl.CostEstimate(
+            flops=0, transcendentals=0, bytes_accessed=32 * rows * width
+        ),
+    )(core[None], *grads)
+
+
+def first_sends_kernel(_, wide_ref, *refs):
+    pieces, side_ref, rep_ref = refs[:-2], refs[-2], refs[-1]
+    half = side_ref.shape[-1]
+    side_ref[0] = wide_ref[:, :half]
+    rest = wide_ref.shape[1] - half
+    for side in range(2):
+        rep_ref[0, side, :, :rest] = pieces[side][:, half:]
+        rep_ref[0, side, :, rest:] = pieces[2 + side][...]
+
+
+def first_sends(wide, narrow, side, rep):
+    rows = wide.shape[0] // 8
+    half = (wide.shape[1] + narrow.shape[1]) // 2
+
+    def part(array, which):
+        return pl.BlockSpec(
+            (rows // 2, array.shape[1]), lambda z, p: (4 * z + 2 * which + 1 - p[1], 0)
+        )
+
+    return pl.pallas_call(
+        first_sends_kernel,
+        grid_spec=pltpu.PrefetchScalarGridSpec(
+            num_scalar_prefetch=1,
+            grid=(4,),
+            in_specs=[
+                pl.BlockSpec((rows, wide.shape[1]), lambda z, p: (2 * z + 1 - p[0], 0)),
+                part(wide, 0),
+                part(wide, 1),
+                part(narrow, 0),
+                part(narrow, 1),
+            ],
+            out_specs=[
+                pl.BlockSpec((1, rows, half), lambda z, p: (z, 0, 0)),
+                pl.BlockSpec((1, 2, rows // 2, half), lambda z, p: (z, 0, 0, 0)),
+            ],
+        ),
+        out_shape=[
+            jax.ShapeDtypeStruct((4, rows, half), LOW),
+            jax.ShapeDtypeStruct((4, 2, rows // 2, half), LOW),
+        ],
+        cost_estimate=pl.CostEstimate(
+            flops=0, transcendentals=0, bytes_accessed=32 * rows * half
+        ),
+    )(jnp.stack([side, rep]), wide, wide, wide, narrow, narrow)
+
+
 def across_cores(grads, core):
     rows = grads[0].shape[0] // 16
     parts = [grad.reshape(8, 2, rows, grad.shape[1]) for grad in grads]
-    away = joined([pick(part, 1 - core, 1) for part in parts])
+    away = away_rows(grads, core)
     held = joined([pick(part, core, 1) for part in parts])
     return add_low(held, swap(away, "shard", lambda i: i ^ 1))
 
@@ -113,17 +187,22 @@
     return total.astype(LOW)
 
 
-def box_middle(firsts, seconds, side, rep, log):
+def box_middle(firsts, seconds, side, rep, log, sends=None):
     rows = firsts[0].shape[-2]
     firsts = [part.reshape(4, 2, *part.shape[-2:]) for part in firsts]
     seconds = [part.reshape(4, 2, 2, rows // 2, part.shape[-1]) for part in seconds]
+    if sends is None:
+        sends = (
+            joined([pick(part, 1 - side, 1) for part in firsts]),
+            joined([pick(part, 1 - rep, 2) for part in seconds]),
+        )
     second = add_low(
         joined([pick(part, rep, 2) for part in seconds]),
-        swap(joined([pick(part, 1 - rep, 2) for part in seconds]), "rep", lambda i: i ^ 1, log),
+        swap(sends[1], "rep", lambda i: i ^ 1, log),
     )
     first = add_low(
         joined([pick(part, side, 1) for part in firsts]),
-        swap(joined([pick(part, 1 - side, 1) for part in firsts]), "shard", lambda i: i ^ 2, log),
+        swap(sends[0], "shard", lambda i: i ^ 2, log),
     )
     first = first.reshape(4, 2, rows // 2, first.shape[-1])
     first = add_low(
@@ -141,9 +220,9 @@
     grad, core, side, level, _ = positions(grad)
     count, rows, width = grad.shape[0], grad.shape[1] // 16, grad.shape[2]
     parts = grad.reshape(count, 8, 2, rows, width)
+    away = pick(parts, 1 - core, 2)
     held = add_low(
-        pick(parts, core, 2),
-        swap(pick(parts, 1 - core, 2), "shard", lambda i: i ^ 1),
+        pick(parts, core, 2), swap(away, "shard", lambda i: i ^ 1)
     ).reshape(count, 4, 2, rows, width)
     held = add_low(
         pick(held, side, 2),
@@ -594,7 +673,7 @@
             [grad.astype(LOW) for grad in (grad_xoutput, grad_xquery, grad_output)]
         )
         held = across_cores(grads, x_core)
-        middle = held.shape[-1] // 2
+        middle = held.shape[-1] // 4
         x_both = box_middle([held[..., :middle]], [held[..., middle:]], x_side, x_rep, [])
         x_got = level_sends(x_both, x_level)
     grad_attended = right_t(branch_one, full_output).astype(LOW)
@@ -627,10 +706,11 @@
     sent_first, sent_last = [], []
     if staged:
         (wide, narrow), q_core, q_side, q_level, q_rep = positions((grad_pair, grad_wq))
+        q_sends = first_sends(wide, narrow, q_side, q_rep)
         wide, narrow = (part.reshape(8, -1, part.shape[1]) for part in (wide, narrow))
         middle = 3 * half_width // 2
         q_both = box_middle(
-            [wide[..., :middle]], [wide[..., middle:], narrow], q_side, q_rep, sent_first
+            [wide[..., :middle]], [wide[..., middle:], narrow], q_side, q_rep, sent_first, q_sends
         )
     text_share, grad_window, chip_dq = after((text_share, grad_window, chip_dq), sent_first[:2])
     text_whole = lax.all_gather(text_share, BOTH, axis=0, tiled=True)
@@ -741,11 +821,11 @@
                 grad_gain_three,
                 grad_bias_three,
             ]
-        ),
+        ).astype(LOW),
         BOTH,
     )
-    _, vectors = lax.optimization_barrier((to_below, vectors))
-    vectors = jnp.sum(vectors, axis=0)
+    vectors = after(vectors, [to_below, fin_query])
+    vectors = jnp.sum(vectors.astype(WIDE), axis=0)
     fin_gain_one, fin_bias_one, fin_gain_two, fin_bias_two, fin_gain_three, fin_bias_three = (
         lax.dynamic_slice_in_dim(vectors, col_start, shard_rows, 1)
     )

time: 1110 us -> 1230 us (1.11)
  blocking collectives: 0 us -> 133 us
  starting transfers between devices: 169 us -> 150 us
  local copies, waits for them, and re-layouts: 100 us -> 81.8 us
  Pallas kernels: 79.2 us -> 93.7 us
  waiting for transfers between devices: 412 us -> 426 us
    all_gather x0 -> x1, blocking collectives: none -> 133 us  [on_device(): lax.all_gather(jnp.stack([grad_gain_one, grad_bias_one, grad_gain_two, gr...]
    reduce_scatter x1, waiting for transfers between devices: 0.01 us -> 31.8 us  [on_device(): lax.psum_scatter(text_sums, BOTH, scatter_dimension=0, tiled=True)]
    ppermute x47, starting transfers between devices: 169 us -> 149 us  [swap(): lax.ppermute(array, axis, [(i, j) for i, j in pairs if 0 <= j < length])]
    ppermute x47, waiting for transfers between devices: 329 us -> 311 us  [swap(): lax.ppermute(array, axis, [(i, j) for i, j in pairs if 0 <= j < length])]
    pallas_call x0 -> x2, Pallas kernels: none -> 14 us  [the longest x1 8.31 us: away_rows(): pl.pallas_call(away_kernel, grid_spec=pltpu.PrefetchScalarGridSpec(num_sc...]
    unnamed x245 -> x229, local copies, waits for them, and re-layouts: 26.3 us -> 20.1 us
  transfers between devices with their start and end apart: 53 -> 52, of which waited for: 20 -> 20; matrix products, arithmetic and copies ran while one was open for 30% -> 26% of each run, Pallas kernels for 7% -> 8%
where the time goes in v6:
time: 1230 us; the launch traced here: 1210 us
  waiting for transfers between devices  426 us (35%)
  matrix products  199 us (16%)
  starting transfers between devices  150 us (12%)
  blocking collectives  133 us (11%)
  other arithmetic  112 us (9%)
  Pallas kernels  93.7 us (8%)
  local copies, waits for them, and re-layouts  81.8 us (7%)
  between operations  19.4 us (2%)
    ppermute x47, waiting for transfers between devices, swap(): lax.ppermute(array, axis, [(i, j) for i, j in pairs if 0 <= j < length])  311 us
    ppermute x47, starting transfers between devices, swap(): lax.ppermute(array, axis, [(i, j) for i, j in pairs if 0 <= j < length])  149 us
    all_gather x1, blocking collectives, on_device(): lax.all_gather(jnp.stack([grad_gain_one, grad_bias_one, grad_gain_two, gr...  133 us
    all_gather x3, waiting for transfers between devices, gather_rows(): return lax.all_gather(array, 'shard', axis=0, tiled=True)  83.1 us
    dot_general x12, matrix products, matmul(): return jnp.dot(left, right, preferred_element_type=WIDE)  65.3 us
    dot_general x9, matrix products, right_t(): lax.dot_general(left, right, (((1,), (1,)), ((), ())), preferred_element_...  54 us
    dot_general x7, matrix products, left_t(): lax.dot_general(left, right, (((0,), (0,)), ((), ())), preferred_element_...  48.2 us
    pallas_call x2, Pallas kernels, attend_back(): pl.pallas_call(functools.partial(attend_back_kernel, reach), grid=(pairs,...  47.7 us
  transfers between devices with their start and end apart: 52, of which 20 were waited for; matrix products, arithmetic and copies ran while one was open for 26% of the time, Pallas kernels for 8%

profile of v6, /device:TPU:0, one launch (start us, length us, event | category | flops | bytes accessed | tf_op | source)
XLA Modules:
  0.0 1214.0 jit_solution(9214110706356628151)
XLA Ops:
  19.1 5.1 collective-permute-start.1
  25.0 33.7 %collective-permute-done.1 = bf16[256,1536]{1,0:T(8,128)(2,1)S(1)} collective-permute-done((bf16[256,1536]{1,0:T(8,128)(2,1)S(1)}, bf16[256,1536]{1,0:T(8,128)(2,1)S(1)}, u32[]{:S(2)}, u32[]{:S(2)}) %collective-permute-start.1) | collective-permute-done | bytes 786464 | tf_op jit(solution)/shard_map/ppermute | solution.py:68
  61.9 25.1 %collective-permute-done.4 = bf16[256,1536]{1,0:T(8,128)(2,1)S(1)} collective-permute-done((bf16[256,1536]{1,0:T(8,128)(2,1)S(1)}, bf16[256,1536]{1,0:T(8,128)(2,1)S(1)}, u32[]{:S(2)}, u32[]{:S(2)}) %collective-permute-start.4) | collective-permute-done | bytes 786464 | tf_op jit(solution)/shard_map/ppermute | solution.py:68
  88.9 51.7 %collective-permute-start.5 = (bf16[4,256,1536]{2,1,0:T(8,128)(2,1)}, bf16[4,256,1536]{2,1,0:T(8,128)(2,1)}, u32[]{:S(2)}, u32[]{:S(2)}) collective-permute-start(bf16[4,256,1536]{2,1,0:T(8,128)(2,1)} %pad_maximum_fusion.2), channel_id=1, source_target_pairs={{0,1},{1,0},{2,3},{3,2},{4,5},{5,4},{6,7},{7,6},{8,9},{9,8},{10,11... | collective-permute-start | bytes 9437192 | tf_op jit(solution)/shard_map/ppermute | solution.py:68
  156.2 9.2 fusion.7
  170.4 79.2 %all-gather.5.cloned.1.call-done = bf16[1536,6272]{1,0:T(8,128)(2,1)} async-done(((bf16[96,6272]{1,0:T(8,128)(2,1)}), bf16[1536,6272]{1,0:T(8,128)(2,1)}) %all-gather.5.cloned.1.call-update) | async-done | bytes 19267600 | tf_op jit(solution)/shard_map/all_gather | solution.py:80
  249.6 4.2 convert_reduce_fusion.4
  253.9 13.1 %fusion.3 = (bf16[1792,1536]{1,0:T(8,128)(2,1)}, bf16[1792,1536]{1,0:T(8,128)(2,1)S(1)}) fusion(f32[1792]{0:T(1024)} %add_rsqrt_fusion, f32[1792]{0:T(1024)} %copy-done.61, bf16[512,1536]{1,0:T(8,128)(2,1)S(1)} %copy-done.5, bf16[512,1536]{1,0:T(8,128)(2,1)} %copy-done.6, bf16[512,1536]{1,0:T(8,128)(2,1)S(1)} %get-tuple-element.162, ...), kind=kLoop, calls=%fused_computation.6 | loop fusion | flops 38535168 | bytes 16541696 | tf_op jit(solution)/shard_map/convert_element_type | solution.py:567
  266.9 5.8 fusion.129.query_ref
  272.7 13.1 %convolution_convert_fusion.5.window_ref = bf16[1792,1536]{1,0:T(8,128)(2,1)} fusion(bf16[1792,1536]{1,0:T(8,128)(2,1)S(1)} %get-tuple-element.159, bf16[1536,6272]{1,0:T(8,128)(2,1)} %all-gather.5.cloned.1.call-done, s32[]{:T(128)S(6)} %add.728), kind=kOutput, calls=%fused_computation.24 | convolution fusion | flops 8458469376 | bytes 15728644 | tf_op jit(solution)/shard_map/dot_general | solution.py:38
  285.8 26.2 %attend_forward.1 = (bf16[512,768]{1,0:T(8,128)(2,1)}, f32[6,2,512]{2,1,0:T(2,128)}) custom-call(s32[1,512]{1,0:T(1,128)} %broadcast_select_fusion.8.offset_ref, bf16[512,768]{1,0:T(8,128)(2,1)} %fusion.129.query_ref, bf16[1792,1536]{1,0:T(8,128)(2,1)} %convolution_convert_fusion.5.window_ref), custom_call_target="tpu_custom_call" | custom-call | flops 9663676416 | bytes 3145728 | tf_op jit(solution)/shard_map/attend_forward/pallas_call | solution.py:297
  317.6 4.2 fusion.211
  322.7 3.9 fusion.92
  333.0 4.2 fusion.213
  346.2 3.9 all-gather.9.cloned.1.call-done
  350.1 9.4 collective-permute-done.7
  359.5 7.9 fusion.68
  367.6 7.9 fusion.72
  375.8 10.0 convolution_convert_fusion.1
  385.8 6.6 fusion.76
  392.4 6.0 fusion.79
  399.6 9.1 fusion.8
  408.7 8.8 fusion.9
  421.5 4.9 dynamic-slice_bitcast_fusion.1
  426.4 4.8 dynamic-slice_bitcast_fusion
  431.7 7.5 collective-permute-done.9
  459.9 4.7 multiply_reduce_fusion.4
  468.7 4.6 fusion.89
  486.1 23.6 %attend_backward.2 = (bf16[512,768]{1,0:T(8,128)(2,1)}, bf16[1792,1536]{1,0:T(8,128)(2,1)}) custom-call(s32[1,512]{1,0:T(1,128)} %broadcast_select_fusion.8.offset_ref, bf16[512,768]{1,0:T(8,128)(2,1)} %fusion.129.query_ref, bf16[1792,1536]{1,0:T(8,128)(2,1)} %convolution_convert_fusion.5.window_ref, bf16[512,768]{1,0:T(8,128)(2,1)} %get-tuple-element.75.out_ref, ...), custom_call_target="tpu_custom_call" | custom-call | flops 12079595520 | bytes 6291456 | tf_op jit(solution)/shard_map/attend_backward/pallas_call | solution.py:383
  509.7 24.1 %attend_backward.3 = (bf16[512,768]{1,0:T(8,128)(2,1)}, bf16[1792,1536]{1,0:T(8,128)(2,1)}) custom-call(s32[1,512]{1,0:T(1,128)} %broadcast_select_fusion.8.offset_ref, bf16[512,768]{1,0:T(8,128)(2,1)} %fusion.129.query_ref, bf16[1792,1536]{1,0:T(8,128)(2,1)} %convolution_convert_fusion.5.window_ref, ...), custom_call_target="tpu_custom_call", output_to_operand_aliasing={{0}: (6, {}), {1}: (7, {})} | custom-call | flops 12079595520 | bytes 6291456 | tf_op jit(solution)/shard_map/attend_backward/pallas_call | solution.py:383
  533.8 14.0 %convolution_convert_fusion.6.wide_ref.refs_0_.refs_1_ = bf16[1536,1536]{1,0:T(8,128)(2,1)} fusion(bf16[1792,1536]{1,0:T(8,128)(2,1)} %copy-done.26, bf16[1792,1536]{1,0:T(8,128)(2,1)} %get-tuple-element.93), kind=kOutput, calls=%fused_computation.25 | convolution fusion | flops 8458076160 | bytes 15728640 | tf_op jit(solution)/shard_map/dot_general | solution.py:42
  547.8 4.2 convolution_convert_fusion.8.refs_2_.refs_3_
  552.6 5.7 shard_map.348
  567.4 8.3 shard_map.349
  580.2 5.0 dynamic-slice_bitcast_fusion.4
  585.2 4.2 slice.263
  591.6 8.1 collective-permute-done.12
  603.0 16.6 %collective-permute-done.11 = bf16[4,192,1152]{2,1,0:T(8,128)(2,1)} collective-permute-done((bf16[4,192,1152]{2,1,0:T(8,128)(2,1)}, bf16[4,192,1152]{2,1,0:T(8,128)(2,1)}, u32[]{:S(2)}, u32[]{:S(2)}) %collective-permute-start.11) | collective-permute-done | bytes 1769504 | tf_op jit(solution)/shard_map/ppermute | solution.py:68
  622.7 4.5 fusion.21
  627.2 4.6 fusion.62
  634.5 6.3 collective-permute-done.15
  641.4 31.8 %reduce-scatter.2.cloned.1.call-done = bf16[48,896]{1,0:T(8,128)(2,1)} async-done(((bf16[1536,896]{1,0:T(8,128)(2,1)}), bf16[48,896]{1,0:T(8,128)(2,1)}) %reduce-scatter.2.cloned.1.call-update) | async-done | bytes 86032 | tf_op jit(solution)/shard_map/reduce_scatter | solution.py:669
  673.2 10.2 fusion.206
  685.3 5.5 fusion.51
  705.0 5.7 fusion.11
  718.3 133.3 %all_gather.20 = bf16[32,6,1536]{2,1,0:T(8,128)(2,1)} all-gather(bf16[1,6,1536]{2,1,0:T(8,128)(2,1)S(1)} %stack.90), channel_id=1, replica_groups=mesh['rep'=2,'shard'=16] {'rep','shard'}, dimensions={0}, use_global_device_ids=true | all-gather | bytes 608256 | tf_op jit(solution)/shard_map/all_gather | solution.py:814
  867.6 5.5 collective-permute-done.36
  873.1 24.8 %collective-permute-done.37 = bf16[2,96,1536]{2,1,0:T(8,128)(2,1)S(1)} collective-permute-done((bf16[2,96,1536]{2,1,0:T(8,128)(2,1)S(1)}, bf16[2,96,1536]{2,1,0:T(8,128)(2,1)S(1)}, u32[]{:S(2)}, u32[]{:S(2)}) %collective-permute-start.37) | collective-permute-done | bytes 589856 | tf_op jit(solution)/shard_map/ppermute | solution.py:68
  897.9 9.4 collective-permute-start.43
  911.6 36.4 %collective-permute-done.42 = bf16[1,96,3072]{2,1,0:T(8,128)(2,1)S(1)} collective-permute-done((bf16[1,96,3072]{2,1,0:T(8,128)(2,1)S(1)}, bf16[1,96,3072]{2,1,0:T(8,128)(2,1)S(1)}, u32[]{:S(2)}, u32[]{:S(2)}) %collective-permute-start.42) | collective-permute-done | bytes 589856 | tf_op jit(solution)/shard_map/ppermute | solution.py:68
  948.0 5.8 collective-permute-start.22
  953.8 23.2 %collective-permute-start.21 = (bf16[96,2304]{1,0:T(8,128)(2,1)}, bf16[96,2304]{1,0:T(8,128)(2,1)S(1)}, u32[]{:S(2)}, u32[]{:S(2)}) collective-permute-start(bf16[96,2304]{1,0:T(8,128)(2,1)} %get-tuple-element.181), channel_id=1, source_target_pairs={{0,4},{1,5},{2,6},{3,7},{4,8},{5,9},{6,10},{7,11},{8,12},{9,13},{1... | collective-permute-start | bytes 1327112 | tf_op jit(solution)/shard_map/ppermute | solution.py:68
  979.3 4.5 add_convert_fusion
  989.1 8.9 collective-permute-done.22
  1003.9 20.9 %collective-permute-done.24 = bf16[96,2304]{1,0:T(8,128)(2,1)S(1)} collective-permute-done((bf16[96,2304]{1,0:T(8,128)(2,1)S(1)}, bf16[96,2304]{1,0:T(8,128)(2,1)S(1)}, u32[]{:S(2)}, u32[]{:S(2)}) %collective-permute-start.24) | collective-permute-done | bytes 442400 | tf_op jit(solution)/shard_map/ppermute | solution.py:68
  1042.2 57.0 %collective-permute-done.28 = bf16[4,48,1152]{2,1,0:T(8,128)(2,1)S(1)} collective-permute-done((bf16[4,48,1152]{2,1,0:T(8,128)(2,1)}, bf16[4,48,1152]{2,1,0:T(8,128)(2,1)S(1)}, u32[]{:S(2)}, u32[]{:S(2)}) %collective-permute-start.28) | collective-permute-done | bytes 442400 | tf_op jit(solution)/shard_map/ppermute | solution.py:68
  1110.2 5.1 fusion.33
  1115.4 7.1 fusion.73
  1122.5 16.7 %collective-permute-done.30 = bf16[4,48,3456]{2,1,0:T(8,128)(2,1)S(1)} collective-permute-done((bf16[4,48,3456]{2,1,0:T(8,128)(2,1)S(1)}, bf16[4,48,3456]{2,1,0:T(8,128)(2,1)S(1)}, u32[]{:S(2)}, u32[]{:S(2)}) %collective-permute-start.30) | collective-permute-done | bytes 1327136 | tf_op jit(solution)/shard_map/ppermute | solution.py:68
  1140.6 15.2 %collective-permute-start.31 = (bf16[48,4608]{1,0:T(8,128)(2,1)}, bf16[48,4608]{1,0:T(8,128)(2,1)}, u32[]{:S(2)}, u32[]{:S(2)}) collective-permute-start(bf16[48,4608]{1,0:T(8,128)(2,1)} %get-tuple-element.177), channel_id=1, source_target_pairs={{0,4},{1,5},{2,6},{3,7},{4,8},{5,9},{6,10},{7,11},{8,12},{9,13},{1... | collective-permute-start | bytes 1327112 | tf_op jit(solution)/shard_map/ppermute | solution.py:68
  1155.7 8.1 collective-permute-start.32
  1168.6 6.1 collective-permute-done.31
  1174.7 17.6 %collective-permute-done.32 = bf16[48,4608]{1,0:T(8,128)(2,1)} collective-permute-done((bf16[48,4608]{1,0:T(8,128)(2,1)}, bf16[48,4608]{1,0:T(8,128)(2,1)}, u32[]{:S(2)}, u32[]{:S(2)}) %collective-permute-start.32) | collective-permute-done | bytes 442400 | tf_op jit(solution)/shard_map/ppermute | solution.py:68
  1195.7 10.2 collective-permute-done.44
  (466 shorter events, 221.6 us)
Async XLA Ops:
  7.2 158.9 %all-gather.7.cloned.1.call-start = ((), (), s32[]{:S(2)}) async-start(), calls=%async_computation.2 | async-start | bytes 20054016 | tf_op jit(solution)/shard_map/all_gather | solution.py:80
  9.8 239.8 %all-gather.5.cloned.1.call-start = ((), (), s32[]{:S(2)}) async-start(), calls=%async_computation.1 | async-start | bytes 20471808 | tf_op jit(solution)/shard_map/all_gather | solution.py:80
  14.3 335.9 %all-gather.9.cloned.1.call-start = ((), (), s32[]{:S(2)}) async-start(), calls=%async_computation.3 | async-start | bytes 20054016 | tf_op jit(solution)/shard_map/all_gather | solution.py:80
  19.0 654.1 %reduce-scatter.2.cloned.1.call-start = ((), (), s32[]{:S(2)}) async-start(), calls=%async_computation.4 | async-start | bytes 2838528 | tf_op jit(solution)/shard_map/reduce_scatter | solution.py:669
  19.1 39.6 %collective-permute-start.1 = (bf16[256,1536]{1,0:T(8,128)(2,1)S(1)}, bf16[256,1536]{1,0:T(8,128)(2,1)S(1)}, u32[]{:S(2)}, u32[]{:S(2)}) collective-permute-start(bf16[256,1536]{1,0:T(8,128)(2,1)S(1)} %copy-done.2), channel_id=1, source_target_pairs={{0,4},{1,5},{2,6},{3,7},{4,8},{5,9},{6,10},{7,11},{8,12},{9,13},{1... | collective-permute-start | bytes 2359304 | tf_op jit(solution)/shard_map/ppermute | solution.py:68
  24.2 34.4 %collective-permute-start.2 = (bf16[256,1536]{1,0:T(8,128)(2,1)S(1)}, bf16[256,1536]{1,0:T(8,128)(2,1)S(1)}, u32[]{:S(2)}, u32[]{:S(2)}) collective-permute-start(bf16[256,1536]{1,0:T(8,128)(2,1)S(1)} %copy-done.2), channel_id=1, source_target_pairs={{3,11},{7,15},{11,19},{15,23},{19,27},{23,31}} | collective-permute-start | bytes 2359304 | tf_op jit(solution)/shard_map/ppermute | solution.py:68
  58.8 3.0 collective-permute-start.3
  60.0 26.9 %collective-permute-start.4 = (bf16[256,1536]{1,0:T(8,128)(2,1)S(1)}, bf16[256,1536]{1,0:T(8,128)(2,1)S(1)}, u32[]{:S(2)}, u32[]{:S(2)}) collective-permute-start(bf16[256,1536]{1,0:T(8,128)(2,1)S(1)} %get-tuple-element.201), channel_id=1, source_target_pairs={{0,2},{1,3},{2,0},{3,1},{4,6},{5,7},{6,4},{7,5},{8,10},{9,11},{10,... | collective-permute-start | bytes 2359304 | tf_op jit(solution)/shard_map/ppermute | solution.py:68
  86.9 53.7 %copy-start.89 = (s32[256]{0:T(256)S(1)}, s32[256]{0:T(256)}, u32[]{:S(2)}) copy-start(s32[256]{0:T(256)} %param.24) | copy-start | bytes 3076
  86.9 53.7 %copy-start.88 = (s32[256]{0:T(256)S(1)}, s32[256]{0:T(256)}, u32[]{:S(2)}) copy-start(s32[256]{0:T(256)} %param.23) | copy-start | bytes 3076
  88.9 60.7 %collective-permute-start.5 = (bf16[4,256,1536]{2,1,0:T(8,128)(2,1)}, bf16[4,256,1536]{2,1,0:T(8,128)(2,1)}, u32[]{:S(2)}, u32[]{:S(2)}) collective-permute-start(bf16[4,256,1536]{2,1,0:T(8,128)(2,1)} %pad_maximum_fusion.2), channel_id=1, source_target_pairs={{0,1},{1,0},{2,3},{3,2},{4,5},{5,4},{6,7},{7,6},{8,9},{9,8},{10,11... | collective-permute-start | bytes 9437192 | tf_op jit(solution)/shard_map/ppermute | solution.py:68
  140.6 8.3 collective-permute-start
  140.7 203.5 %collective-permute-start.8 = (bf16[256,1536]{1,0:T(8,128)(2,1)}, bf16[256,1536]{1,0:T(8,128)(2,1)}, u32[]{:S(2)}, u32[]{:S(2)}) collective-permute-start(bf16[256,1536]{1,0:T(8,128)(2,1)} %param.41), channel_id=1, source_target_pairs={{0,16},{16,0},{1,17},{17,1},{2,18},{18,2},{3,19},{19,3},{4,20},{20... | collective-permute-start | bytes 2359304 | tf_op jit(solution)/shard_map/ppermute | solution.py:68
  313.2 3.6 collective-permute-start.6
  337.2 104.9 %copy-start = (f32[256,1536]{1,0:T(8,128)}, f32[256,1536]{1,0:T(8,128)S(1)}, u32[]{:S(2)}) copy-start(f32[256,1536]{1,0:T(8,128)S(1)} %get-tuple-element.96) | copy-start | bytes 4718596
  339.5 20.0 %collective-permute-start.7 = (bf16[256,1536]{1,0:T(8,128)(2,1)}, bf16[256,1536]{1,0:T(8,128)(2,1)}, u32[]{:S(2)}, u32[]{:S(2)}) collective-permute-start(bf16[256,1536]{1,0:T(8,128)(2,1)} %add_convert_fusion.4), channel_id=1, source_target_pairs={{0,16},{16,0},{1,17},{17,1},{2,18},{18,2},{3,19},{19,3},{4,20},{20... | collective-permute-start | bytes 2359304 | tf_op jit(solution)/shard_map/ppermute | solution.py:68
  420.0 19.1 %collective-permute-start.9 = (bf16[256,1536]{1,0:T(8,128)(2,1)}, bf16[256,1536]{1,0:T(8,128)(2,1)}, u32[]{:S(2)}, u32[]{:S(2)}) collective-permute-start(bf16[256,1536]{1,0:T(8,128)(2,1)} %slice.429), channel_id=1, source_target_pairs={{0,16},{16,0},{1,17},{17,1},{2,18},{18,2},{3,19},{19,3},{4,20},{20... | collective-permute-start | bytes 2359304 | tf_op jit(solution)/shard_map/ppermute | solution.py:68
  426.4 271.4 %collective-permute-start.34 = (bf16[2,8,96,1536]{3,2,1,0:T(8,128)(2,1)}, bf16[2,8,96,1536]{3,2,1,0:T(8,128)(2,1)}, u32[]{:S(2)}, u32[]{:S(2)}) collective-permute-start(bf16[2,8,96,1536]{3,2,1,0:T(8,128)(2,1)} %dynamic-slice_bitcast_fusion.1), channel_id=1, source_target_pairs={{0,1},{1,0},{2,3},{3,2},{4,5},{5,4},{6,7},{7,6},{8,9},{9,8},{10,11... | collective-permute-start | bytes 14155784 | tf_op jit(solution)/shard_map/ppermute | solution.py:68
  431.2 273.9 %collective-permute-start.39 = (bf16[1,8,96,3072]{3,2,1,0:T(8,128)(2,1)}, bf16[1,8,96,3072]{3,2,1,0:T(8,128)(2,1)}, u32[]{:S(2)}, u32[]{:S(2)}) collective-permute-start(bf16[1,8,96,3072]{3,2,1,0:T(8,128)(2,1)} %dynamic-slice_bitcast_fusion), channel_id=1, source_target_pairs={{0,1},{1,0},{2,3},{3,2},{4,5},{5,4},{6,7},{7,6},{8,9},{9,8},{10,11... | collective-permute-start | bytes 14155784 | tf_op jit(solution)/shard_map/ppermute | solution.py:68
  477.6 7.3 collective-permute-start.10
  558.3 41.3 %collective-permute-start.12 = (bf16[4,2,96,1152]{3,2,1,0:T(8,128)(2,1)}, bf16[4,2,96,1152]{3,2,1,0:T(8,128)(2,1)}, u32[]{:S(2)}, u32[]{:S(2)}) collective-permute-start(bf16[4,2,96,1152]{3,2,1,0:T(8,128)(2,1)} %get-tuple-element.90), channel_id=1, source_target_pairs={{0,16},{16,0},{1,17},{17,1},{2,18},{18,2},{3,19},{19,3},{4,20},{20... | collective-permute-start | bytes 5308424 | tf_op jit(solution)/shard_map/ppermute | solution.py:68
  566.1 533.3 %all-gather.11.cloned.1.call-start = ((), (), s32[]{:S(2)}) async-start(), calls=%async_computation.5 | async-start | bytes 2838528 | tf_op jit(solution)/shard_map/all_gather | solution.py:716
  575.7 403.6 %collective-permute-start.26 = (bf16[8,96,4608]{2,1,0:T(8,128)(2,1)}, bf16[8,96,4608]{2,1,0:T(8,128)(2,1)}, u32[]{:S(2)}, u32[]{:S(2)}) collective-permute-start(bf16[8,96,4608]{2,1,0:T(8,128)(2,1)} %shard_map.349), channel_id=1, source_target_pairs={{0,1},{1,0},{2,3},{3,2},{4,5},{5,4},{6,7},{7,6},{8,9},{9,8},{10,11... | collective-permute-start | bytes 21233672 | tf_op jit(solution)/shard_map/ppermute | solution.py:68
  575.9 43.7 %collective-permute-start.11 = (bf16[4,192,1152]{2,1,0:T(8,128)(2,1)}, bf16[4,192,1152]{2,1,0:T(8,128)(2,1)}, u32[]{:S(2)}, u32[]{:S(2)}) collective-permute-start(bf16[4,192,1152]{2,1,0:T(8,128)(2,1)} %get-tuple-element.89), channel_id=1, source_target_pairs={{0,2},{1,3},{2,0},{3,1},{4,6},{5,7},{6,4},{7,5},{8,10},{9,11},{10,... | collective-permute-start | bytes 5308424 | tf_op jit(solution)/shard_map/ppermute | solution.py:68
  591.6 28.1 %copy-start.17 = (bf16[8,192,1152]{2,1,0:T(8,128)(2,1)S(1)}, bf16[8,192,1152]{2,1,0:T(8,128)(2,1)}, u32[]{:S(2)}) copy-start(bf16[8,192,1152]{2,1,0:T(8,128)(2,1)} %slice.263) | copy-start | bytes 10616836
  601.7 39.1 %collective-permute-start.15 = (bf16[4,96,1152]{2,1,0:T(8,128)(2,1)S(1)}, bf16[4,96,1152]{2,1,0:T(8,128)(2,1)S(1)}, u32[]{:S(2)}, u32[]{:S(2)}) collective-permute-start(bf16[4,96,1152]{2,1,0:T(8,128)(2,1)S(1)} %dynamic-slice_bitcast_fusion.11), channel_id=1, source_target_pairs={{0,2},{1,3},{2,0},{3,1},{4,6},{5,7},{6,4},{7,5},{8,10},{9,11},{10,... | collective-permute-start | bytes 2654216 | tf_op jit(solution)/shard_map/ppermute | solution.py:68
  634.5 80.9 %collective-permute-start.14 = (bf16[4,96,1152]{2,1,0:T(8,128)(2,1)}, bf16[4,96,1152]{2,1,0:T(8,128)(2,1)}, u32[]{:S(2)}, u32[]{:S(2)}) collective-permute-start(bf16[4,96,1152]{2,1,0:T(8,128)(2,1)} %dynamic-slice_bitcast_fusion.12), channel_id=1, source_target_pairs={{0,16},{16,0},{1,17},{17,1},{2,18},{18,2},{3,19},{19,3},{4,20},{20... | collective-permute-start | bytes 2654216 | tf_op jit(solution)/shard_map/ppermute | solution.py:68
  640.8 226.2 %collective-permute-start.13 = (bf16[256,1536]{1,0:T(8,128)(2,1)}, bf16[256,1536]{1,0:T(8,128)(2,1)}, u32[]{:S(2)}, u32[]{:S(2)}) collective-permute-start(bf16[256,1536]{1,0:T(8,128)(2,1)} %slice.428), channel_id=1, source_target_pairs={{0,16},{16,0},{1,17},{17,1},{2,18},{18,2},{3,19},{19,3},{4,20},{20... | collective-permute-start | bytes 2359304 | tf_op jit(solution)/shard_map/ppermute | solution.py:68
  703.5 148.1 %collective-permute-start.35 = (bf16[2,4,96,1536]{3,2,1,0:T(8,128)(2,1)}, bf16[2,4,96,1536]{3,2,1,0:T(8,128)(2,1)}, u32[]{:S(2)}, u32[]{:S(2)}) collective-permute-start(bf16[2,4,96,1536]{3,2,1,0:T(8,128)(2,1)} %dynamic-slice_bitcast_fusion.3), channel_id=1, source_target_pairs={{0,2},{1,3},{2,0},{3,1},{4,6},{5,7},{6,4},{7,5},{8,10},{9,11},{10,... | collective-permute-start | bytes 7077896 | tf_op jit(solution)/shard_map/ppermute | solution.py:68
  712.4 142.6 %collective-permute-start.40 = (bf16[1,4,96,3072]{3,2,1,0:T(8,128)(2,1)}, bf16[1,4,96,3072]{3,2,1,0:T(8,128)(2,1)}, u32[]{:S(2)}, u32[]{:S(2)}) collective-permute-start(bf16[1,4,96,3072]{3,2,1,0:T(8,128)(2,1)} %dynamic-slice_bitcast_fusion.2), channel_id=1, source_target_pairs={{0,2},{1,3},{2,0},{3,1},{4,6},{5,7},{6,4},{7,5},{8,10},{9,11},{10,... | collective-permute-start | bytes 7077896 | tf_op jit(solution)/shard_map/ppermute | solution.py:68
  715.4 142.6 %collective-permute-start.16 = (bf16[4,256,1536]{2,1,0:T(8,128)(2,1)}, bf16[4,256,1536]{2,1,0:T(8,128)(2,1)}, u32[]{:S(2)}, u32[]{:S(2)}) collective-permute-start(bf16[4,256,1536]{2,1,0:T(8,128)(2,1)} %pad_maximum_fusion.4), channel_id=1, source_target_pairs={{0,1},{1,0},{2,3},{3,2},{4,5},{5,4},{6,7},{7,6},{8,9},{9,8},{10,11... | collective-permute-start | bytes 9437192 | tf_op jit(solution)/shard_map/ppermute | solution.py:68
  718.3 136.7 %slice-start.2 = ((s8[4718592]{0:T(1024)(128)(4,1)}), s8[4194304]{0:T(1024)(128)(4,1)S(1)}, s32[]{:S(2)}) async-start(s8[4718592]{0:T(1024)(128)(4,1)} %bitcast.299), calls=%async_computation.8 | async-start | bytes 8388608
  854.9 18.2 %collective-permute-start.36 = (bf16[2,96,1536]{2,1,0:T(8,128)(2,1)S(1)}, bf16[2,96,1536]{2,1,0:T(8,128)(2,1)S(1)}, u32[]{:S(2)}, u32[]{:S(2)}) collective-permute-start(bf16[2,96,1536]{2,1,0:T(8,128)(2,1)S(1)} %get-tuple-element.175), channel_id=1, source_target_pairs={{0,4},{1,5},{2,6},{3,7},{4,8},{5,9},{6,10},{7,11},{8,12},{9,13},{1... | collective-permute-start | bytes 1769480 | tf_op jit(solution)/shard_map/ppermute | solution.py:68
  855.0 42.9 %collective-permute-start.37 = (bf16[2,96,1536]{2,1,0:T(8,128)(2,1)S(1)}, bf16[2,96,1536]{2,1,0:T(8,128)(2,1)S(1)}, u32[]{:S(2)}, u32[]{:S(2)}) collective-permute-start(bf16[2,96,1536]{2,1,0:T(8,128)(2,1)S(1)} %get-tuple-element.174), channel_id=1, source_target_pairs={{0,8},{1,9},{2,10},{3,11},{4,12},{5,13},{6,14},{7,15},{8,0},{9,1},... | collective-permute-start | bytes 1769480 | tf_op jit(solution)/shard_map/ppermute | solution.py:68
  858.0 51.9 %collective-permute-start.38 = (bf16[2,96,1536]{2,1,0:T(8,128)(2,1)S(1)}, bf16[2,96,1536]{2,1,0:T(8,128)(2,1)S(1)}, u32[]{:S(2)}, u32[]{:S(2)}) collective-permute-start(bf16[2,96,1536]{2,1,0:T(8,128)(2,1)S(1)} %get-tuple-element.173), channel_id=1, source_target_pairs={{0,12},{1,13},{2,14},{3,15},{4,0},{5,1},{6,2},{7,3},{8,4},{9,5},{1... | collective-permute-start | bytes 1769480 | tf_op jit(solution)/shard_map/ppermute | solution.py:68
  865.9 41.4 %copy-start.1 = (f32[256,1536]{1,0:T(8,128)S(1)}, f32[256,1536]{1,0:T(8,128)}, u32[]{:S(2)}) copy-start(f32[256,1536]{1,0:T(8,128)} %copy-done) | copy-start | bytes 4718596
  865.9 41.4 %slice-start.7 = ((f32[512,1536]{1,0:T(8,128)}), f32[256,1536]{1,0:T(8,128)S(1)}, s32[]{:S(2)}) async-start(f32[512,1536]{1,0:T(8,128)} %copy-done.24), calls=%async_computation.13 | async-start | bytes 3145728 | tf_op jit(solution)/shard_map/slice | solution.py:794
  867.0 44.6 %collective-permute-start.41 = (bf16[1,96,3072]{2,1,0:T(8,128)(2,1)S(1)}, bf16[1,96,3072]{2,1,0:T(8,128)(2,1)S(1)}, u32[]{:S(2)}, u32[]{:S(2)}) collective-permute-start(bf16[1,96,3072]{2,1,0:T(8,128)(2,1)S(1)} %get-tuple-element.172), channel_id=1, source_target_pairs={{0,4},{1,5},{2,6},{3,7},{4,8},{5,9},{6,10},{7,11},{8,12},{9,13},{1... | collective-permute-start | bytes 1769480 | tf_op jit(solution)/shard_map/ppermute | solution.py:68
  873.1 74.9 %collective-permute-start.42 = (bf16[1,96,3072]{2,1,0:T(8,128)(2,1)S(1)}, bf16[1,96,3072]{2,1,0:T(8,128)(2,1)S(1)}, u32[]{:S(2)}, u32[]{:S(2)}) collective-permute-start(bf16[1,96,3072]{2,1,0:T(8,128)(2,1)S(1)} %get-tuple-element.171), channel_id=1, source_target_pairs={{0,8},{1,9},{2,10},{3,11},{4,12},{5,13},{6,14},{7,15},{8,0},{9,1},... | collective-permute-start | bytes 1769480 | tf_op jit(solution)/shard_map/ppermute | solution.py:68
  897.9 55.9 %collective-permute-start.43 = (bf16[1,96,3072]{2,1,0:T(8,128)(2,1)S(1)}, bf16[1,96,3072]{2,1,0:T(8,128)(2,1)S(1)}, u32[]{:S(2)}, u32[]{:S(2)}) collective-permute-start(bf16[1,96,3072]{2,1,0:T(8,128)(2,1)S(1)} %get-tuple-element.170), channel_id=1, source_target_pairs={{0,12},{1,13},{2,14},{3,15},{4,0},{5,1},{6,2},{7,3},{8,4},{9,5},{1... | collective-permute-start | bytes 1769480 | tf_op jit(solution)/shard_map/ppermute | solution.py:68
  907.3 72.0 %copy-start.16 = (bf16[8,96,1536]{2,1,0:T(8,128)(2,1)S(1)}, bf16[8,96,1536]{2,1,0:T(8,128)(2,1)}, u32[]{:S(2)}) copy-start(bf16[8,96,1536]{2,1,0:T(8,128)(2,1)} %get-tuple-element.225) | copy-start | bytes 7077892
  909.8 69.5 %copy-start.14 = (bf16[8,96,1536]{2,1,0:T(8,128)(2,1)S(1)}, bf16[8,96,1536]{2,1,0:T(8,128)(2,1)}, u32[]{:S(2)}) copy-start(bf16[8,96,1536]{2,1,0:T(8,128)(2,1)} %dynamic-slice_bitcast_fusion.6) | copy-start | bytes 7077892
  909.8 69.5 %copy-start.15 = (bf16[8,96,1536]{2,1,0:T(8,128)(2,1)S(1)}, bf16[8,96,1536]{2,1,0:T(8,128)(2,1)}, u32[]{:S(2)}) copy-start(bf16[8,96,1536]{2,1,0:T(8,128)(2,1)} %get-tuple-element.224) | copy-start | bytes 7077892
  909.8 90.5 %collective-permute-start.18 = (bf16[256,1536]{1,0:T(8,128)(2,1)S(1)}, bf16[256,1536]{1,0:T(8,128)(2,1)}, u32[]{:S(2)}, u32[]{:S(2)}) collective-permute-start(bf16[256,1536]{1,0:T(8,128)(2,1)S(1)} %fusion.122), channel_id=1, source_target_pairs={{1,3},{3,1},{5,7},{7,5},{9,11},{11,9},{13,15},{15,13},{17,19},{19,... | collective-permute-start | bytes 2359304 | tf_op jit(solution)/shard_map/ppermute | solution.py:68
  911.6 76.5 %collective-permute-start.23 = (bf16[96,2304]{1,0:T(8,128)(2,1)}, bf16[96,2304]{1,0:T(8,128)(2,1)S(1)}, u32[]{:S(2)}, u32[]{:S(2)}) collective-permute-start(bf16[96,2304]{1,0:T(8,128)(2,1)} %get-tuple-element.179), channel_id=1, source_target_pairs={{0,12},{1,13},{2,14},{3,15},{4,0},{5,1},{6,2},{7,3},{8,4},{9,5},{1... | collective-permute-start | bytes 1327112 | tf_op jit(solution)/shard_map/ppermute | solution.py:68
  948.0 49.9 %collective-permute-start.22 = (bf16[96,2304]{1,0:T(8,128)(2,1)}, bf16[96,2304]{1,0:T(8,128)(2,1)S(1)}, u32[]{:S(2)}, u32[]{:S(2)}) collective-permute-start(bf16[96,2304]{1,0:T(8,128)(2,1)} %get-tuple-element.180), channel_id=1, source_target_pairs={{0,8},{1,9},{2,10},{3,11},{4,12},{5,13},{6,14},{7,15},{8,0},{9,1},... | collective-permute-start | bytes 1327112 | tf_op jit(solution)/shard_map/ppermute | solution.py:68
  953.8 45.2 %collective-permute-start.21 = (bf16[96,2304]{1,0:T(8,128)(2,1)}, bf16[96,2304]{1,0:T(8,128)(2,1)S(1)}, u32[]{:S(2)}, u32[]{:S(2)}) collective-permute-start(bf16[96,2304]{1,0:T(8,128)(2,1)} %get-tuple-element.181), channel_id=1, source_target_pairs={{0,4},{1,5},{2,6},{3,7},{4,8},{5,9},{6,10},{7,11},{8,12},{9,13},{1... | collective-permute-start | bytes 1327112 | tf_op jit(solution)/shard_map/ppermute | solution.py:68
  979.3 19.9 %collective-permute-start.17 = (bf16[256,1536]{1,0:T(8,128)(2,1)S(1)}, bf16[256,1536]{1,0:T(8,128)(2,1)S(1)}, u32[]{:S(2)}, u32[]{:S(2)}) collective-permute-start(bf16[256,1536]{1,0:T(8,128)(2,1)S(1)} %slice_bitcast_fusion.4), channel_id=1, source_target_pairs={{0,2},{1,3},{2,0},{3,1},{4,6},{5,7},{6,4},{7,5},{8,10},{9,11},{10,... | collective-permute-start | bytes 2359304 | tf_op jit(solution)/shard_map/ppermute | solution.py:68
  988.1 177.1 %collective-permute-start.45 = (bf16[1,96,3072]{2,1,0:T(8,128)(2,1)}, bf16[1,96,3072]{2,1,0:T(8,128)(2,1)}, u32[]{:S(2)}, u32[]{:S(2)}) collective-permute-start(bf16[1,96,3072]{2,1,0:T(8,128)(2,1)} %fusion.143), channel_id=1, source_target_pairs={{0,16},{16,0},{1,17},{17,1},{2,18},{18,2},{3,19},{19,3},{4,20},{20... | collective-permute-start | bytes 1769480 | tf_op jit(solution)/shard_map/ppermute | solution.py:68
  998.0 124.5 %collective-permute-start.46 = (bf16[2,96,1536]{2,1,0:T(8,128)(2,1)}, bf16[2,96,1536]{2,1,0:T(8,128)(2,1)}, u32[]{:S(2)}, u32[]{:S(2)}) collective-permute-start(bf16[2,96,1536]{2,1,0:T(8,128)(2,1)} %fusion.146), channel_id=1, source_target_pairs={{0,16},{16,0},{1,17},{17,1},{2,18},{18,2},{3,19},{19,3},{4,20},{20... | collective-permute-start | bytes 1769480 | tf_op jit(solution)/shard_map/ppermute | solution.py:68
  999.0 28.5 %collective-permute-start.27 = (bf16[4,96,1152]{2,1,0:T(8,128)(2,1)S(1)}, bf16[4,96,1152]{2,1,0:T(8,128)(2,1)S(1)}, u32[]{:S(2)}, u32[]{:S(2)}) collective-permute-start(bf16[4,96,1152]{2,1,0:T(8,128)(2,1)S(1)} %dynamic-slice_bitcast_fusion.10), channel_id=1, source_target_pairs={{0,2},{1,3},{2,0},{3,1},{4,6},{5,7},{6,4},{7,5},{8,10},{9,11},{10,... | collective-permute-start | bytes 2654216 | tf_op jit(solution)/shard_map/ppermute | solution.py:68
  999.3 25.6 %collective-permute-start.24 = (bf16[96,2304]{1,0:T(8,128)(2,1)S(1)}, bf16[96,2304]{1,0:T(8,128)(2,1)S(1)}, u32[]{:S(2)}, u32[]{:S(2)}) collective-permute-start(bf16[96,2304]{1,0:T(8,128)(2,1)S(1)} %fusion.154), channel_id=1, source_target_pairs={{0,16},{16,0},{1,17},{17,1},{2,18},{18,2},{3,19},{19,3},{4,20},{20... | collective-permute-start | bytes 1327112 | tf_op jit(solution)/shard_map/ppermute | solution.py:68
  1002.6 32.4 %collective-permute-start.19 = (bf16[256,1536]{1,0:T(8,128)(2,1)}, bf16[256,1536]{1,0:T(8,128)(2,1)}, u32[]{:S(2)}, u32[]{:S(2)}) collective-permute-start(bf16[256,1536]{1,0:T(8,128)(2,1)} %fusion.119), channel_id=1, source_target_pairs={{4,0},{5,1},{6,2},{7,3},{8,4},{9,5},{10,6},{11,7},{12,8},{13,9},{1... | collective-permute-start | bytes 2359304 | tf_op jit(solution)/shard_map/ppermute | solution.py:68
  1024.8 11.3 collective-permute-start.20
  1027.5 2.0 collective-permute-start.25
  1029.6 76.2 %collective-permute-start.29 = (bf16[4,2,48,3456]{3,2,0,1:T(8,128)(2,1)}, bf16[4,2,48,3456]{3,2,0,1:T(8,128)(2,1)}, u32[]{:S(2)}, u32[]{:S(2)}) collective-permute-start(bf16[4,2,48,3456]{3,2,0,1:T(8,128)(2,1)} %bitcast.283), channel_id=1, source_target_pairs={{0,16},{16,0},{1,17},{17,1},{2,18},{18,2},{3,19},{19,3},{4,20},{20... | collective-permute-start | bytes 7962632 | tf_op jit(solution)/shard_map/ppermute | solution.py:68
  1035.1 64.2 %collective-permute-start.28 = (bf16[4,48,1152]{2,1,0:T(8,128)(2,1)}, bf16[4,48,1152]{2,1,0:T(8,128)(2,1)S(1)}, u32[]{:S(2)}, u32[]{:S(2)}) collective-permute-start(bf16[4,48,1152]{2,1,0:T(8,128)(2,1)} %dynamic-slice_bitcast_fusion.20), channel_id=1, source_target_pairs={{0,16},{16,0},{1,17},{17,1},{2,18},{18,2},{3,19},{19,3},{4,20},{20... | collective-permute-start | bytes 1327112 | tf_op jit(solution)/shard_map/ppermute | solution.py:68
  1041.1 58.1 %copy-start.31 = (bf16[4,96,1152]{2,1,0:T(8,128)(2,1)S(1)}, bf16[4,96,1152]{2,1,0:T(8,128)(2,1)}, u32[]{:S(2)}) copy-start(bf16[4,96,1152]{2,1,0:T(8,128)(2,1)} %copy-done.30) | copy-start | bytes 2654212
  1042.2 63.6 %copy-start.13 = (bf16[4,2,1,48,3456]{4,3,2,1,0:T(8,128)(2,1)S(1)}, bf16[4,2,1,48,3456]{4,3,2,1,0:T(8,128)(2,1)}, u32[]{:S(2)}) copy-start(bf16[4,2,1,48,3456]{4,3,2,1,0:T(8,128)(2,1)} %get-tuple-element.160) | copy-start | bytes 7962628
  1108.4 30.7 %collective-permute-start.30 = (bf16[4,48,3456]{2,1,0:T(8,128)(2,1)S(1)}, bf16[4,48,3456]{2,1,0:T(8,128)(2,1)S(1)}, u32[]{:S(2)}, u32[]{:S(2)}) collective-permute-start(bf16[4,48,3456]{2,1,0:T(8,128)(2,1)S(1)} %dynamic-slice_bitcast_fusion.8), channel_id=1, source_target_pairs={{0,2},{1,3},{2,0},{3,1},{4,6},{5,7},{6,4},{7,5},{8,10},{9,11},{10,... | collective-permute-start | bytes 3981320 | tf_op jit(solution)/shard_map/ppermute | solution.py:68
  1140.6 34.1 %collective-permute-start.31 = (bf16[48,4608]{1,0:T(8,128)(2,1)}, bf16[48,4608]{1,0:T(8,128)(2,1)}, u32[]{:S(2)}, u32[]{:S(2)}) collective-permute-start(bf16[48,4608]{1,0:T(8,128)(2,1)} %get-tuple-element.177), channel_id=1, source_target_pairs={{0,4},{1,5},{2,6},{3,7},{4,8},{5,9},{6,10},{7,11},{8,12},{9,13},{1... | collective-permute-start | bytes 1327112 | tf_op jit(solution)/shard_map/ppermute | solution.py:68
  1155.7 36.6 %collective-permute-start.32 = (bf16[48,4608]{1,0:T(8,128)(2,1)}, bf16[48,4608]{1,0:T(8,128)(2,1)}, u32[]{:S(2)}, u32[]{:S(2)}) collective-permute-start(bf16[48,4608]{1,0:T(8,128)(2,1)} %get-tuple-element.178), channel_id=1, source_target_pairs={{0,8},{1,9},{2,10},{3,11},{4,12},{5,13},{6,14},{7,15},{8,0},{9,1},... | collective-permute-start | bytes 1327112 | tf_op jit(solution)/shard_map/ppermute | solution.py:68
  1163.8 28.5 %collective-permute-start.33 = (bf16[48,4608]{1,0:T(8,128)(2,1)S(1)}, bf16[48,4608]{1,0:T(8,128)(2,1)}, u32[]{:S(2)}, u32[]{:S(2)}) collective-permute-start(bf16[48,4608]{1,0:T(8,128)(2,1)S(1)} %get-tuple-element.176), channel_id=1, source_target_pairs={{0,12},{1,13},{2,14},{3,15},{4,0},{5,1},{6,2},{7,3},{8,4},{9,5},{1... | collective-permute-start | bytes 1327112 | tf_op jit(solution)/shard_map/ppermute | solution.py:68
  1193.9 12.1 collective-permute-start.44
  (99 other events, 458.1 us)
Sparse Core Ops, SparseCore 0:
  9.8 140.8 all-gather.6
  152.8 96.7 all-gather.4
  251.2 98.8 all-gather.8
  566.2 106.8 reduce-scatter.1
  718.3 62.1 all-gather.10
